TPU v7x, 32 devices: a whole 2x2x4 slice. The times are simulated.
32 devices in a mesh: dp: 4 (over z), row: 4 (over y, x), col: 2 (over core).
Axes of the slice: x: 2, y: 2, z: 4, core: 2. Of those that a mesh axis runs over, the one named last changes fastest.
Arguments:
- inputs: bfloat16 [4096, 1024], P(('dp', 'row'), 'col'), may hold values from -53 to 53
- prefix: int32 [4], P('dp'), may hold values from 102 to 512
- picks: int32 [4096, 4, 32], P(('dp', 'col')), may hold values from 0 to 65535, as said below
- gain_attn: bfloat16 [1024], replicated, may hold values from 0.25 to 1.75
- w_qkv: bfloat16 [3, 1024, 1024], P(None, 'col', 'row'), may hold values from -0.1875 to 0.1875
- w_attn_out: bfloat16 [1024, 1024], P('row', 'col'), may hold values from -1.5 to 1.5
- gain_mem: bfloat16 [1024], replicated, may hold values from 0.25 to 1.75
- w_query: bfloat16 [1024, 4096], P('col', 'row'), may hold values from -0.1875 to 0.1875
- w_gate: bfloat16 [1024, 1024], P('col', 'row'), may hold values from -0.1875 to 0.1875
- w_proj: bfloat16 [1024, 1024], P('row', 'col'), may hold values from -0.5 to 0.5
- subkeys: bfloat16 [4, 2, 256, 512], replicated, may hold values from -0.1875 to 0.1875
- values: bfloat16 [65536, 1024], P(('dp', 'row', 'col')), may hold values from -6 to 6
- cotangent: bfloat16 [4096, 1024], P(('dp', 'row'), 'col'), may hold values from -6 to 6
Outputs:
- output: bfloat16 [4096, 1024], P(('dp', 'row'), 'col')
- grad_inputs: float32 [4096, 1024], P(('dp', 'row'), 'col')
- grad_gain_attn: float32 [1024], replicated
- grad_w_qkv: float32 [3, 1024, 1024], P(None, 'col', 'row')
- grad_w_attn_out: float32 [1024, 1024], P('row', 'col')
- grad_gain_mem: float32 [1024], replicated
- grad_w_query: float32 [1024, 4096], P('col', 'row')
- grad_w_gate: float32 [1024, 1024], P('col', 'row')
- grad_w_proj: float32 [1024, 1024], P('row', 'col')
- grad_subkeys: float32 [4, 2, 256, 512], replicated
- grad_values: float32 [65536, 1024], P(('dp', 'row', 'col'))
Inputs may be any that keep to these rules, and one draw needn't show every extreme that they name: `picks`: for each memory head and each aligned block of 128 tokens, each device's run of 2048 value rows is picked exactly 128 times.
All inputs are finite; a program needn't handle non-finite values.
Results may differ from a plain program's by a relative error of at most 0.018.
Values may be sent and summed in bfloat16 or wider, within the bound.
A program may use at most 256 MiB of HBM per device.

v0:
```python
import jax
import jax.numpy as jnp
from jax import lax
from jax.sharding import PartitionSpec as P

D = 1024
HDIM = 64
HALF = 512
SUBKEYS = 256
TOPK = 32
FBLK = 128


EPSILON = 1e-06


def row_gather(operand):
    return lax.all_gather(operand, "row", axis=0, tiled=True)


def col_gather(operand):
    return lax.all_gather(operand, "col", axis=0, tiled=True)


def feature_total(operand):
    return lax.psum(operand, "col")


def col_reduce(gathered, product):
    return lax.psum_scatter(product(gathered), "col", scatter_dimension=0, tiled=True)


def row_reduce(gathered, product):
    return lax.psum_scatter(product(gathered), "row", scatter_dimension=0, tiled=True)


def norm_forward(residual, gain_slice):
    sum_squares = feature_total(jnp.sum(residual * residual, axis=1))
    inv_scale = lax.rsqrt(sum_squares / D + EPSILON)
    unit_rows = residual * inv_scale[:, None]
    return (unit_rows, inv_scale, (unit_rows * gain_slice).astype(jnp.bfloat16))


def norm_backward(grad_normed, unit_rows, inv_scale, gain_slice):
    grad_unit = grad_normed * gain_slice
    inner_mean = feature_total(jnp.sum(grad_unit * unit_rows, axis=1)) / D
    grad_input = inv_scale[:, None] * (grad_unit - unit_rows * inner_mean[:, None])
    return (grad_input, jnp.sum(grad_normed * unit_rows, axis=0))


def allowed_mask(query_count, key_count, first_pos, prefix_len):
    query_pos = first_pos + lax.iota(jnp.int32, query_count)
    key_pos = lax.iota(jnp.int32, key_count)
    return (key_pos[None, :] <= query_pos[:, None]) | (key_pos[None, :] < prefix_len)


def head_scores(query_head, key_head, allowed):
    raw_scores = jnp.einsum(
        "qd,kd->qk", query_head, key_head, preferred_element_type=jnp.float32
    ) * HDIM ** (-0.5)
    return jnp.where(allowed, raw_scores, -jnp.inf)


def attend_forward(own_qkv, kv_rows, allowed):
    head_count = own_qkv.shape[2] // HDIM
    outputs = []
    log_sums = []
    for head_index in range(head_count):
        columns = slice(head_index * HDIM, (head_index + 1) * HDIM)
        scores = head_scores(own_qkv[:, 0, columns], kv_rows[:, 0, columns], allowed)
        peak_score = jnp.max(scores, axis=1, keepdims=True)
        exp_scores = jnp.exp(scores - peak_score)
        row_sum = jnp.sum(exp_scores, axis=1, keepdims=True)
        probabilities = (exp_scores / row_sum).astype(jnp.bfloat16)
        outputs.append(
            jnp.dot(probabilities, kv_rows[:, 1, columns], preferred_element_type=jnp.float32)
        )
        log_sums.append(peak_score[:, 0] + jnp.log(row_sum[:, 0]))
    return (jnp.concatenate(outputs, axis=1), jnp.stack(log_sums))


def attend_backward(own_qkv, kv_rows, allowed, log_sums, grad_out):
    head_count = own_qkv.shape[2] // HDIM
    grad_queries = []
    grad_keys = []
    grad_values = []
    for head_index in range(head_count):
        columns = slice(head_index * HDIM, (head_index + 1) * HDIM)
        query_head = own_qkv[:, 0, columns]
        key_head = kv_rows[:, 0, columns]
        value_head = kv_rows[:, 1, columns]
        grad_head = grad_out[:, columns]
        scores = head_scores(query_head, key_head, allowed)
        probabilities = jnp.exp(scores - log_sums[head_index][:, None])
        grad_probs = jnp.einsum(
            "qd,kd->qk", grad_head, value_head, preferred_element_type=jnp.float32
        )
        inner_sum = jnp.sum(probabilities * grad_probs, axis=1, keepdims=True)
        grad_scores = (probabilities * (grad_probs - inner_sum)).astype(jnp.bfloat16)
        grad_queries.append(
            jnp.dot(grad_scores, key_head, preferred_element_type=jnp.float32) * HDIM ** (-0.5)
        )
        grad_keys.append(
            jnp.einsum("qk,qd->kd", grad_scores, query_head, preferred_element_type=jnp.float32)
            * HDIM ** (-0.5)
        )
        grad_values.append(
            jnp.einsum(
                "qk,qd->kd",
                probabilities.astype(jnp.bfloat16),
                grad_head,
                preferred_element_type=jnp.float32,
            )
        )
    stacked = jnp.stack(
        [jnp.concatenate(grad_keys, axis=1), jnp.concatenate(grad_values, axis=1)], axis=1
    )
    return (jnp.concatenate(grad_queries, axis=1), stacked)


def fetch_rows(wanted, sort_order, value_shard):
    dp_count = lax.axis_size("dp")
    grid_count = lax.axis_size("row") * lax.axis_size("col")
    rows_dev = value_shard.shape[0]
    requests = jnp.take(wanted, sort_order).reshape(dp_count, grid_count, -1)
    arrived = lax.all_to_all(
        lax.all_to_all(requests, "dp", split_axis=0, concat_axis=0, tiled=True),
        ("row", "col"),
        split_axis=1,
        concat_axis=1,
        tiled=True,
    )
    local_rows = arrived % rows_dev
    found_rows = jnp.take(value_shard, local_rows, axis=0)
    returned = lax.all_to_all(
        lax.all_to_all(found_rows, "dp", split_axis=0, concat_axis=0, tiled=True),
        ("row", "col"),
        split_axis=1,
        concat_axis=1,
        tiled=True,
    )
    unsort = jnp.argsort(sort_order)
    return (jnp.take(returned.reshape(-1, value_shard.shape[1]), unsort, axis=0), local_rows)


def memory_forward(query_rows, picks, subkeys, values):
    head_count = query_rows.shape[1] // (2 * HALF)
    row_count = lax.axis_size("row")
    head_first = lax.axis_index("row") * head_count
    rows_dev = values.shape[0]
    own_tokens = query_rows.shape[0]
    head_id = head_first + 0
    keys_head = lax.dynamic_index_in_dim(subkeys, head_id, 0, keepdims=False)
    picks_head = lax.dynamic_index_in_dim(picks, head_id, 1, keepdims=False)
    first_scores = jnp.einsum(
        "td,ad->ta", query_rows[:, :HALF], keys_head[0], preferred_element_type=jnp.float32
    )
    second_scores = jnp.einsum(
        "td,ad->ta", query_rows[:, HALF:], keys_head[1], preferred_element_type=jnp.float32
    )
    upper_index = picks_head // SUBKEYS
    lower_index = picks_head % SUBKEYS
    pick_scores = jnp.take_along_axis(first_scores, upper_index, axis=1) + jnp.take_along_axis(
        second_scores, lower_index, axis=1
    )
    pick_weights = jax.nn.softmax(pick_scores, axis=1)
    weights_low = pick_weights.astype(jnp.bfloat16)
    block_parts = []
    block_state = []
    for block_index in range(own_tokens // FBLK):
        wanted = picks_head[block_index * FBLK : (block_index + 1) * FBLK].reshape(-1)
        sort_order = jnp.argsort(wanted // rows_dev, stable=True)
        fetched, local_rows = fetch_rows(wanted, sort_order, values)
        grouped = fetched.reshape(FBLK, TOPK, row_count, -1)
        block_weights = weights_low[block_index * FBLK : (block_index + 1) * FBLK]
        block_parts.append(
            jnp.einsum("tk,tkcf->ctf", block_weights, grouped, preferred_element_type=jnp.float32)
        )
        block_state.append((wanted, sort_order, local_rows))
    totals = jnp.concatenate(block_parts, axis=1)
    kept_state = [
        (
            head_id,
            keys_head,
            query_rows,
            upper_index,
            lower_index,
            pick_weights,
            weights_low,
            block_state,
        )
    ]
    memory = lax.psum_scatter(totals, "row", scatter_dimension=0, tiled=True)[0]
    return (memory, kept_state)


def memory_backward(grad_memory, kept_state, values, subkeys):
    gathered = row_gather(grad_memory[None])
    own_tokens = gathered.shape[1]
    grad_tokens = jnp.moveaxis(gathered, 0, 1).reshape(own_tokens, -1)
    dp_count = lax.axis_size("dp")
    grid_count = lax.axis_size("row") * lax.axis_size("col")
    rows_dev = values.shape[0]
    row_ids = lax.iota(jnp.int32, rows_dev)
    grad_values = jnp.zeros(values.shape, jnp.float32)
    grad_subkeys = jnp.zeros(subkeys.shape, jnp.float32)
    grad_queries = []
    for (
        head_id,
        keys_head,
        query_head,
        upper_index,
        lower_index,
        pick_weights,
        weights_low,
        block_state,
    ) in kept_state:
        block_grads = []
        for block_index, (wanted, sort_order, local_rows) in enumerate(block_state):
            token_rows = grad_tokens[block_index * FBLK : (block_index + 1) * FBLK]
            send_rows = jnp.take(token_rows, sort_order // TOPK, axis=0).reshape(
                dp_count, grid_count, -1, token_rows.shape[1]
            )
            block_weights = weights_low[block_index * FBLK : (block_index + 1) * FBLK].reshape(-1)
            send_weights = jnp.take(block_weights, sort_order).reshape(dp_count, grid_count, -1)
            arrived_rows, arrived_weights = (
                lax.all_to_all(
                    lax.all_to_all(send_rows, "dp", split_axis=0, concat_axis=0, tiled=True),
                    ("row", "col"),
                    split_axis=1,
                    concat_axis=1,
                    tiled=True,
                ),
                lax.all_to_all(
                    lax.all_to_all(send_weights, "dp", split_axis=0, concat_axis=0, tiled=True),
                    ("row", "col"),
                    split_axis=1,
                    concat_axis=1,
                    tiled=True,
                ),
            )
            flat_local = local_rows.reshape(-1)
            picker = jnp.where(
                flat_local[:, None] == row_ids[None, :],
                arrived_weights.reshape(-1)[:, None],
                jnp.zeros((), jnp.bfloat16),
            )
            grad_values = grad_values + jnp.einsum(
                "pr,pf->rf",
                picker,
                arrived_rows.reshape(-1, arrived_rows.shape[-1]),
                preferred_element_type=jnp.float32,
            )
            stored = jnp.take(values, local_rows, axis=0)
            products = jnp.einsum(
                "abcf,abcf->abc", arrived_rows, stored, preferred_element_type=jnp.float32
            )
            returned = lax.all_to_all(
                lax.all_to_all(products, "dp", split_axis=0, concat_axis=0, tiled=True),
                ("row", "col"),
                split_axis=1,
                concat_axis=1,
                tiled=True,
            )
            unsort = jnp.argsort(sort_order)
            block_grads.append(jnp.take(returned.reshape(-1), unsort).reshape(FBLK, TOPK))
        grad_weights = jnp.concatenate(block_grads, axis=0)
        grad_scores = pick_weights * (
            grad_weights - jnp.sum(pick_weights * grad_weights, axis=1, keepdims=True)
        )
        token_index = lax.broadcasted_iota(jnp.int32, upper_index.shape, 0)
        grad_first = (
            jnp.zeros((own_tokens, SUBKEYS), jnp.float32)
            .at[token_index, upper_index]
            .add(grad_scores)
            .astype(jnp.bfloat16)
        )
        grad_second = (
            jnp.zeros((own_tokens, SUBKEYS), jnp.float32)
            .at[token_index, lower_index]
            .add(grad_scores)
            .astype(jnp.bfloat16)
        )
        grad_queries.append(
            jnp.concatenate(
                [
                    jnp.dot(grad_first, keys_head[0], preferred_element_type=jnp.float32),
                    jnp.dot(grad_second, keys_head[1], preferred_element_type=jnp.float32),
                ],
                axis=1,
            )
        )
        grad_keys_head = jnp.stack(
            [
                jnp.einsum(
                    "ta,td->ad",
                    grad_first,
                    query_head[:, :HALF],
                    preferred_element_type=jnp.float32,
                ),
                jnp.einsum(
                    "ta,td->ad",
                    grad_second,
                    query_head[:, HALF:],
                    preferred_element_type=jnp.float32,
                ),
            ]
        )
        grad_subkeys = lax.dynamic_update_index_in_dim(grad_subkeys, grad_keys_head, head_id, 0)
    return (grad_queries[0].astype(jnp.bfloat16), grad_values, grad_subkeys)


def per_device(
    inputs,
    prefix,
    picks,
    gain_attn,
    w_qkv,
    w_attn_out,
    gain_mem,
    w_query,
    w_gate,
    w_proj,
    subkeys,
    values,
    cotangent,
):
    width_part = inputs.shape[1]
    own_tokens = picks.shape[0]
    seq_tokens = own_tokens * lax.axis_size("col")
    query_width = w_query.shape[1]
    col_first = lax.axis_index("col") * width_part
    gain_one = lax.dynamic_slice_in_dim(gain_attn, col_first, width_part).astype(jnp.float32)
    gain_two = lax.dynamic_slice_in_dim(gain_mem, col_first, width_part).astype(jnp.float32)

    def project_qkv(piece_rows):
        return jnp.einsum("tc,jcf->tjf", piece_rows, w_qkv, preferred_element_type=jnp.float32)

    def proj_attn(piece_rows):
        return jnp.dot(piece_rows, w_attn_out, preferred_element_type=jnp.float32)

    def project_memory(piece_rows):
        return jnp.concatenate(
            [
                jnp.dot(piece_rows, w_query, preferred_element_type=jnp.float32),
                jnp.dot(piece_rows, w_gate, preferred_element_type=jnp.float32),
            ],
            axis=1,
        )

    def proj_mem(piece_rows):
        return jnp.dot(piece_rows, w_proj, preferred_element_type=jnp.float32)

    def back_proj(piece_rows):
        return jnp.einsum("tc,fc->tf", piece_rows, w_proj, preferred_element_type=jnp.float32)

    def back_memory_in(piece_rows):
        return jnp.einsum(
            "tq,cq->tc", piece_rows[:, :query_width], w_query, preferred_element_type=jnp.float32
        ) + jnp.einsum(
            "tf,cf->tc", piece_rows[:, query_width:], w_gate, preferred_element_type=jnp.float32
        )

    def back_attn(piece_rows):
        return jnp.einsum("tc,fc->tf", piece_rows, w_attn_out, preferred_element_type=jnp.float32)

    def back_qkv(piece_rows):
        return jnp.einsum("tjf,jcf->tc", piece_rows, w_qkv, preferred_element_type=jnp.float32)

    residual = inputs.astype(jnp.float32)
    unit_one, scale_one, normed_one = norm_forward(residual, gain_one)
    gathered_one = row_gather(normed_one)
    own_qkv = col_reduce(gathered_one, project_qkv).astype(jnp.bfloat16)
    kv_rows = col_gather(own_qkv[:, 1:])
    allowed = allowed_mask(own_tokens, seq_tokens, lax.axis_index("col") * own_tokens, prefix[0])
    attended_sum, log_sums = attend_forward(own_qkv, kv_rows, allowed)
    attended = attended_sum.astype(jnp.bfloat16)
    attended_all = col_gather(attended)
    hidden = residual + row_reduce(attended_all, proj_attn)
    unit_two, scale_two, normed_two = norm_forward(hidden, gain_two)
    gathered_two = row_gather(normed_two)
    mixed_sum = col_reduce(gathered_two, project_memory)
    query_rows = mixed_sum[:, :query_width].astype(jnp.bfloat16)
    gate_value = mixed_sum[:, query_width:]
    memory, kept_state = memory_forward(query_rows, picks, subkeys, values)
    sigmoid_gate = jax.nn.sigmoid(gate_value)
    silu_gate = gate_value * sigmoid_gate
    gated_value = (memory * silu_gate).astype(jnp.bfloat16)
    gated_all = col_gather(gated_value)
    output = (hidden + row_reduce(gated_all, proj_mem)).astype(jnp.bfloat16)
    grad_rows = row_gather(cotangent)
    grad_w_proj = jnp.einsum("tf,tc->fc", gated_all, grad_rows, preferred_element_type=jnp.float32)
    grad_gated = col_reduce(grad_rows, back_proj)
    grad_memory = (grad_gated * silu_gate).astype(jnp.bfloat16)
    grad_gate = (
        grad_gated * memory * sigmoid_gate * (1.0 + gate_value * (1.0 - sigmoid_gate))
    ).astype(jnp.bfloat16)
    grad_query, grad_values, grad_subkeys = memory_backward(
        grad_memory, kept_state, values, subkeys
    )
    grad_mixed = col_gather(jnp.concatenate([grad_query, grad_gate], axis=1))
    grad_w_query = jnp.einsum(
        "tc,tq->cq", gathered_two, grad_mixed[:, :query_width], preferred_element_type=jnp.float32
    )
    grad_w_gate = jnp.einsum(
        "tc,tf->cf", gathered_two, grad_mixed[:, query_width:], preferred_element_type=jnp.float32
    )
    grad_normed_two = row_reduce(grad_mixed, back_memory_in)
    grad_from_two, grad_gain_two = norm_backward(grad_normed_two, unit_two, scale_two, gain_two)
    grad_hidden = cotangent.astype(jnp.float32) + grad_from_two
    grad_hidden_all = row_gather(grad_hidden.astype(jnp.bfloat16))
    grad_w_attn_out = jnp.einsum(
        "tf,tc->fc", attended_all, grad_hidden_all, preferred_element_type=jnp.float32
    )
    grad_attended = col_reduce(grad_hidden_all, back_attn).astype(jnp.bfloat16)
    grad_query_own, grad_kv_all = attend_backward(
        own_qkv, kv_rows, allowed, log_sums, grad_attended
    )
    grad_kv_own = lax.psum_scatter(grad_kv_all, "col", scatter_dimension=0, tiled=True)
    grad_qkv = jnp.concatenate([grad_query_own[:, None], grad_kv_own], axis=1).astype(jnp.bfloat16)
    grad_qkv_all = col_gather(grad_qkv)
    grad_w_qkv = jnp.einsum(
        "tc,tjf->jcf", gathered_one, grad_qkv_all, preferred_element_type=jnp.float32
    )
    grad_normed_one = row_reduce(grad_qkv_all, back_qkv)
    grad_from_one, grad_gain_one = norm_backward(grad_normed_one, unit_one, scale_one, gain_one)
    grad_inputs = grad_hidden + grad_from_one
    weight_sums = (
        lax.psum(grad_w_qkv.astype(jnp.bfloat16), "dp").astype(jnp.float32),
        lax.psum(grad_w_attn_out.astype(jnp.bfloat16), "dp").astype(jnp.float32),
        lax.psum(grad_w_query.astype(jnp.bfloat16), "dp").astype(jnp.float32),
        lax.psum(grad_w_gate.astype(jnp.bfloat16), "dp").astype(jnp.float32),
        lax.psum(grad_w_proj.astype(jnp.bfloat16), "dp").astype(jnp.float32),
    )
    gain_full_one = lax.dynamic_update_slice_in_dim(
        jnp.zeros(gain_attn.shape, jnp.float32), grad_gain_one, col_first, 0
    )
    gain_full_two = lax.dynamic_update_slice_in_dim(
        jnp.zeros(gain_mem.shape, jnp.float32), grad_gain_two, col_first, 0
    )
    small_sums = lax.psum((gain_full_one, gain_full_two, grad_subkeys), ("dp", "row", "col"))
    return (
        output,
        grad_inputs,
        small_sums[0],
        weight_sums[0],
        weight_sums[1],
        small_sums[1],
        weight_sums[2],
        weight_sums[3],
        weight_sums[4],
        small_sums[2],
        grad_values,
    )


def solution(mesh):
    placed = (
        P(("dp", "row"), "col"),
        P("dp"),
        P(("dp", "col"), None, None),
        P(),
        P(None, "col", "row"),
        P("row", "col"),
        P(),
        P("col", "row"),
        P("col", "row"),
        P("row", "col"),
        P(),
        P(("dp", "row", "col"), None),
        P(("dp", "row"), "col"),
    )
    return jax.shard_map(
        per_device,
        mesh=mesh,
        in_specs=placed,
        out_specs=(
            P(("dp", "row"), "col"),
            P(("dp", "row"), "col"),
            P(),
            P(None, "col", "row"),
            P("row", "col"),
            P(),
            P("col", "row"),
            P("col", "row"),
            P("row", "col"),
            P(),
            P(("dp", "row", "col"), None),
        ),
        check_vma=False,
    )
```

profile of v0, /device:TPU:0, one launch (start us, length us, event | category | flops | bytes accessed | tf_op | source)
XLA Modules:
  0.0 4143.7 jit_solution(14106048706521889177)
XLA Ops:
  14.2 29.2 all-gather.10.cloned.1.call-done
  85.9 36.4 reduce-scatter.15.cloned.1.call-done
  127.5 26.0 all-gather.14.cloned.1.call-done
  170.8 40.5 gather_fusion.11
  218.0 40.4 gather_fusion.8
  265.0 40.5 gather_fusion.5
  314.8 40.2 gather_fusion
  358.4 129.5 %gather_fusion.4 = f32[16384]{0:T(1024)S(1)} fusion(f32[512,256]{1,0:T(8,128)S(1)} %fusion.82, s32[16384]{0:T(1024)S(1)} %reshape.711), kind=kCustom, calls=%fused_computation.16.clone | custom fusion | bytes 262144 | tf_op jit(solution)/shard_map/jit(take_along_axis)/gather | solution.py:163
  489.5 129.5 %gather_fusion.3 = f32[16384]{0:T(1024)S(1)} fusion(f32[512,256]{1,0:T(8,128)S(1)} %fusion.85, s32[16384]{0:T(1024)S(1)} %reshape.706), kind=kCustom, calls=%fused_computation.3.clone | custom fusion | bytes 262144 | tf_op jit(solution)/shard_map/jit(take_along_axis)/gather | solution.py:163
  621.7 25.6 gather_fusion.25
  655.5 34.3 gather_fusion.24
  690.1 25.6 gather_fusion.23
  718.5 25.6 gather_fusion.22
  856.3 158.1 %all-to-all-done.28 = bf16[4,8,128,1024]{3,2,1,0:T(8,128)(2,1)} async-done(((bf16[4,8,128,1024]{3,2,1,0:T(8,128)(2,1)}), bf16[4,8,128,1024]{3,2,1,0:T(8,128)(2,1)}, u32[]{:S(2)}, u32[]{:S(2)}) %all-to-all-start.28) | async-done | bytes 8388640 | tf_op jit(solution)/shard_map/all_to_all | solution.py:228
  1045.9 157.4 %all-to-all-done.24 = bf16[4,8,128,1024]{3,2,1,0:T(8,128)(2,1)} async-done(((bf16[4,8,128,1024]{3,2,1,0:T(8,128)(2,1)}), bf16[4,8,128,1024]{3,2,1,0:T(8,128)(2,1)}, u32[]{:S(2)}, u32[]{:S(2)}) %all-to-all-start.24) | async-done | bytes 8388640 | tf_op jit(solution)/shard_map/all_to_all | solution.py:228
  1235.0 156.7 %all-to-all-done.20 = bf16[4,8,128,1024]{3,2,1,0:T(8,128)(2,1)} async-done(((bf16[4,8,128,1024]{3,2,1,0:T(8,128)(2,1)}), bf16[4,8,128,1024]{3,2,1,0:T(8,128)(2,1)}, u32[]{:S(2)}, u32[]{:S(2)}) %all-to-all-start.20) | async-done | bytes 8388640 | tf_op jit(solution)/shard_map/all_to_all | solution.py:228
  1405.7 174.2 %all-to-all-done.16 = bf16[4,8,128,1024]{3,2,1,0:T(8,128)(2,1)} async-done(((bf16[4,8,128,1024]{3,2,1,0:T(8,128)(2,1)}), bf16[4,8,128,1024]{3,2,1,0:T(8,128)(2,1)}, u32[]{:S(2)}, u32[]{:S(2)}) %all-to-all-start.16) | async-done | bytes 8388640 | tf_op jit(solution)/shard_map/all_to_all | solution.py:228
  1593.2 85.7 %all-to-all-done.29 = bf16[4,8,128,1024]{3,2,0,1:T(8,128)(2,1)} async-done(((bf16[4,8,128,1024]{3,2,0,1:T(8,128)(2,1)}), bf16[4,8,128,1024]{3,2,0,1:T(8,128)(2,1)}, u32[]{:S(2)}, u32[]{:S(2)}) %all-to-all-start.29) | async-done | bytes 8388640 | tf_op jit(solution)/shard_map/all_to_all | solution.py:227
  1692.3 85.7 %all-to-all-done.25 = bf16[4,8,128,1024]{3,2,0,1:T(8,128)(2,1)} async-done(((bf16[4,8,128,1024]{3,2,0,1:T(8,128)(2,1)}), bf16[4,8,128,1024]{3,2,0,1:T(8,128)(2,1)}, u32[]{:S(2)}, u32[]{:S(2)}) %all-to-all-start.25) | async-done | bytes 8388640 | tf_op jit(solution)/shard_map/all_to_all | solution.py:227
  1791.6 85.8 %all-to-all-done.21 = bf16[4,8,128,1024]{3,2,0,1:T(8,128)(2,1)} async-done(((bf16[4,8,128,1024]{3,2,0,1:T(8,128)(2,1)}), bf16[4,8,128,1024]{3,2,0,1:T(8,128)(2,1)}, u32[]{:S(2)}, u32[]{:S(2)}) %all-to-all-start.21) | async-done | bytes 8388640 | tf_op jit(solution)/shard_map/all_to_all | solution.py:227
  1882.3 23.5 gather_fusion.12
  1905.9 23.5 gather_fusion.9
  1929.5 23.5 gather_fusion.6
  1953.0 23.6 gather_fusion.1
  2076.9 191.9 %all_to_all.201 = bf16[4,8,128,1024]{3,2,1,0:T(8,128)(2,1)} all-to-all(bf16[4,8,128,1024]{3,2,1,0:T(8,128)(2,1)} %get-tuple-element.127), channel_id=1, replica_groups=mesh['dp'=4,'row'=4,'col'=2] {'dp'}, dimensions={0} | all-to-all | bytes 16777216 | tf_op jit(solution)/shard_map/all_to_all | solution.py:136
  2268.9 186.6 %all_to_all.202 = bf16[4,8,128,1024]{3,2,1,0:T(8,128)(2,1)} all-to-all(bf16[4,8,128,1024]{3,2,1,0:T(8,128)(2,1)S(1)} %copy-done.1), channel_id=1, replica_groups=mesh['dp'=4,'row'=4,'col'=2] {'dp'}, dimensions={0} | all-to-all | bytes 16777216 | tf_op jit(solution)/shard_map/all_to_all | solution.py:136
  2455.4 185.8 %all_to_all.203 = bf16[4,8,128,1024]{3,2,1,0:T(8,128)(2,1)} all-to-all(bf16[4,8,128,1024]{3,2,1,0:T(8,128)(2,1)S(1)} %bitcast.332), channel_id=1, replica_groups=mesh['dp'=4,'row'=4,'col'=2] {'dp'}, dimensions={0} | all-to-all | bytes 16777216 | tf_op jit(solution)/shard_map/all_to_all | solution.py:136
  2655.2 173.8 %all-to-all-done.2 = bf16[4,8,128,1024]{3,2,1,0:T(8,128)(2,1)} async-done(((bf16[4,8,128,1024]{3,2,1,0:T(8,128)(2,1)}), bf16[4,8,128,1024]{3,2,1,0:T(8,128)(2,1)}, u32[]{:S(2)}, u32[]{:S(2)}) %all-to-all-start.2) | async-done | bytes 8388640 | tf_op jit(solution)/shard_map/all_to_all | solution.py:136
  2842.2 85.8 %all-to-all-done.15 = bf16[4,8,128,1024]{3,2,0,1:T(8,128)(2,1)} async-done(((bf16[4,8,128,1024]{3,2,0,1:T(8,128)(2,1)}), bf16[4,8,128,1024]{3,2,0,1:T(8,128)(2,1)}, u32[]{:S(2)}, u32[]{:S(2)}) %all-to-all-start.15) | async-done | bytes 8388640 | tf_op jit(solution)/shard_map/all_to_all | solution.py:135
  2941.4 85.6 %all-to-all-done.11 = bf16[4,8,128,1024]{3,2,0,1:T(8,128)(2,1)} async-done(((bf16[4,8,128,1024]{3,2,0,1:T(8,128)(2,1)}), bf16[4,8,128,1024]{3,2,0,1:T(8,128)(2,1)}, u32[]{:S(2)}, u32[]{:S(2)}) %all-to-all-start.11) | async-done | bytes 8388640 | tf_op jit(solution)/shard_map/all_to_all | solution.py:135
  3056.4 23.0 gather_fusion.21
  3079.5 23.0 gather_fusion.19
  3102.5 23.0 gather_fusion.17
  3125.6 23.0 gather_fusion.15
  3172.6 25.5 gather_fusion.13
  3236.1 25.3 gather_fusion.10
  3300.2 25.3 gather_fusion.7
  3364.7 25.3 gather_fusion.2
  3425.2 113.3 %scatter_custom_fusion.1 = f32[131072]{0:T(1024)S(1)} fusion(s32[16384]{0:T(1024)S(1)} %reshape.652, f32[16384]{0:T(1024)S(1)} %reshape.648, f32[]{:T(128)} %constant.227.clone.1), kind=kCustom, calls=%fused_computation.208 | custom fusion | flops 16384 | bytes 524292
  3538.6 113.3 %scatter_custom_fusion = f32[131072]{0:T(1024)S(1)} fusion(s32[16384]{0:T(1024)S(1)} %reshape.646, f32[16384]{0:T(1024)S(1)} %reshape.648, f32[]{:T(128)} %constant.227.clone.1), kind=kCustom, calls=%fused_computation.210 | custom fusion | flops 16384 | bytes 524292
  3675.5 36.5 reduce-scatter.23.cloned.1.call-done
  3719.0 26.6 all-gather.20.cloned.1.call-done
  3891.8 23.2 fusion.4
  3917.1 23.0 fusion.6
  3956.8 23.3 fusion.8
  3984.4 29.3 add_add_fusion
  4028.1 38.6 all-reduce.1
  4069.2 62.6 %all-reduce.6.cloned.1.call-done = f32[4,2,256,512]{3,2,1,0:T(8,128)} async-done(((f32[4,2,256,512]{3,2,1,0:T(8,128)}), f32[4,2,256,512]{3,2,1,0:T(8,128)}) %all-reduce.6.cloned.1.call-update) | async-done | bytes 4194320 | tf_op jit(solution)/shard_map/psum | solution.py:441
  (691 shorter events, 912.2 us)
Async XLA Ops:
  7.2 36.2 all-gather.10.cloned.1.call-start
  14.2 44.5 %reduce-scatter.13.cloned.1.call-start = ((), (), s32[]{:S(2)}) async-start(), calls=%async_computation.51 | async-start | bytes 4718592 | tf_op jit(solution)/shard_map/reduce_scatter | solution.py:30
  47.5 24.0 all-gather.12.cloned.1.call-start
  61.1 61.2 %reduce-scatter.15.cloned.1.call-start = ((), (), s32[]{:S(2)}) async-start(), calls=%async_computation.53 | async-start | bytes 2621440 | tf_op jit(solution)/shard_map/reduce_scatter | solution.py:34
  85.8 67.7 %all-gather.14.cloned.1.call-start = ((), (), s32[]{:S(2)}) async-start(), calls=%async_computation.54 | async-start | bytes 1310720 | tf_op jit(solution)/shard_map/all_gather | solution.py:18
  126.9 178.8 %all-gather.16.cloned.1.call-start = ((), (), s32[]{:S(2)}) async-start(), calls=%async_computation.57 | async-start | bytes 1310720 | tf_op jit(solution)/shard_map/all_gather | solution.py:18
  127.4 227.6 %reduce-scatter.17.cloned.1.call-start = ((), (), s32[]{:S(2)}) async-start(), calls=%async_computation.55 | async-start | bytes 7864320 | tf_op jit(solution)/shard_map/reduce_scatter | solution.py:30
  161.3 491.9 %reduce-scatter.21.cloned.1.call-start = ((), (), s32[]{:S(2)}) async-start(), calls=%async_computation.58 | async-start | bytes 1572864 | tf_op jit(solution)/shard_map/reduce_scatter | solution.py:30
  648.6 95.5 %all-to-all-start.12 = ((s32[4,8,128]{2,1,0:T(8,128)}), s32[4,8,128]{2,1,0:T(8,128)S(1)}, u32[]{:S(2)}, u32[]{:S(2)}) async-start(s32[4,8,128]{2,1,0:T(8,128)} %select_bitcast_fusion), calls=%async_computation.15 | async-start | bytes 32768 | tf_op jit(solution)/shard_map/all_to_all | solution.py:127
  653.2 131.9 %all-gather.24.cloned.1.call-start = ((), (), s32[]{:S(2)}) async-start(), calls=%async_computation.67 | async-start | bytes 1310720 | tf_op jit(solution)/shard_map/all_gather | solution.py:18
  744.1 10.7 all-to-all-start.8
  754.9 8.8 all-to-all-start.4
  763.7 8.8 all-to-all-start
  772.5 8.0 all-to-all-start.13
  780.6 8.0 all-to-all-start.9
  788.6 23.9 all-to-all-start.5
  812.5 11.5 all-to-all-start.1
  824.6 189.8 %all-to-all-start.28 = ((bf16[4,8,128,1024]{3,2,1,0:T(8,128)(2,1)}), bf16[4,8,128,1024]{3,2,1,0:T(8,128)(2,1)}, u32[]{:S(2)}, u32[]{:S(2)}) async-start(bf16[4,8,128,1024]{3,2,1,0:T(8,128)(2,1)} %bitcast.334), calls=%async_computation.33 | async-start | bytes 16777216 | tf_op jit(solution)/shard_map/all_to_all | solution.py:228
  1014.4 188.9 %all-to-all-start.24 = ((bf16[4,8,128,1024]{3,2,1,0:T(8,128)(2,1)}), bf16[4,8,128,1024]{3,2,1,0:T(8,128)(2,1)}, u32[]{:S(2)}, u32[]{:S(2)}) async-start(bf16[4,8,128,1024]{3,2,1,0:T(8,128)(2,1)} %bitcast.335), calls=%async_computation.29 | async-start | bytes 16777216 | tf_op jit(solution)/shard_map/all_to_all | solution.py:228
  1203.3 188.4 %all-to-all-start.20 = ((bf16[4,8,128,1024]{3,2,1,0:T(8,128)(2,1)}), bf16[4,8,128,1024]{3,2,1,0:T(8,128)(2,1)}, u32[]{:S(2)}, u32[]{:S(2)}) async-start(bf16[4,8,128,1024]{3,2,1,0:T(8,128)(2,1)} %bitcast.333), calls=%async_computation.25 | async-start | bytes 16777216 | tf_op jit(solution)/shard_map/all_to_all | solution.py:228
  1391.7 188.2 %all-to-all-start.16 = ((bf16[4,8,128,1024]{3,2,1,0:T(8,128)(2,1)}), bf16[4,8,128,1024]{3,2,1,0:T(8,128)(2,1)}, u32[]{:S(2)}, u32[]{:S(2)}) async-start(bf16[4,8,128,1024]{3,2,1,0:T(8,128)(2,1)} %bitcast.336), calls=%async_computation.21 | async-start | bytes 16777216 | tf_op jit(solution)/shard_map/all_to_all | solution.py:228
  1579.9 99.0 %all-to-all-start.29 = ((bf16[4,8,128,1024]{3,2,0,1:T(8,128)(2,1)}), bf16[4,8,128,1024]{3,2,0,1:T(8,128)(2,1)}, u32[]{:S(2)}, u32[]{:S(2)}) async-start(bf16[4,8,128,1024]{3,2,0,1:T(8,128)(2,1)} %copy.202), calls=%async_computation.34 | async-start | bytes 16777216 | tf_op jit(solution)/shard_map/all_to_all | solution.py:227
  1678.9 99.0 %all-to-all-start.25 = ((bf16[4,8,128,1024]{3,2,0,1:T(8,128)(2,1)}), bf16[4,8,128,1024]{3,2,0,1:T(8,128)(2,1)}, u32[]{:S(2)}, u32[]{:S(2)}) async-start(bf16[4,8,128,1024]{3,2,0,1:T(8,128)(2,1)} %copy.198), calls=%async_computation.30 | async-start | bytes 16777216 | tf_op jit(solution)/shard_map/all_to_all | solution.py:227
  1777.9 99.4 %all-to-all-start.21 = ((bf16[4,8,128,1024]{3,2,0,1:T(8,128)(2,1)}), bf16[4,8,128,1024]{3,2,0,1:T(8,128)(2,1)}, u32[]{:S(2)}, u32[]{:S(2)}) async-start(bf16[4,8,128,1024]{3,2,0,1:T(8,128)(2,1)} %copy.194), calls=%async_computation.26 | async-start | bytes 16777216 | tf_op jit(solution)/shard_map/all_to_all | solution.py:227
  1877.3 110.4 %all-to-all-start.17 = ((bf16[4,8,128,1024]{3,2,0,1:T(8,128)(2,1)}), bf16[4,8,128,1024]{3,2,0,1:T(8,128)(2,1)}, u32[]{:S(2)}, u32[]{:S(2)}) async-start(bf16[4,8,128,1024]{3,2,0,1:T(8,128)(2,1)} %copy.190), calls=%async_computation.22 | async-start | bytes 16777216 | tf_op jit(solution)/shard_map/all_to_all | solution.py:227
  1987.7 14.3 all-to-all-start.30
  2002.0 16.1 all-to-all-start.26
  2018.1 16.1 all-to-all-start.22
  2034.2 10.7 all-to-all-start.18
  2044.9 8.8 all-to-all-start.31
  2641.2 187.8 %all-to-all-start.2 = ((bf16[4,8,128,1024]{3,2,1,0:T(8,128)(2,1)}), bf16[4,8,128,1024]{3,2,1,0:T(8,128)(2,1)}, u32[]{:S(2)}, u32[]{:S(2)}) async-start(bf16[4,8,128,1024]{3,2,1,0:T(8,128)(2,1)} %get-tuple-element.115), calls=%async_computation.4 | async-start | bytes 16777216 | tf_op jit(solution)/shard_map/all_to_all | solution.py:136
  2829.0 99.0 %all-to-all-start.15 = ((bf16[4,8,128,1024]{3,2,0,1:T(8,128)(2,1)}), bf16[4,8,128,1024]{3,2,0,1:T(8,128)(2,1)}, u32[]{:S(2)}, u32[]{:S(2)}) async-start(bf16[4,8,128,1024]{3,2,0,1:T(8,128)(2,1)} %copy.185), calls=%async_computation.18 | async-start | bytes 16777216 | tf_op jit(solution)/shard_map/all_to_all | solution.py:135
  2928.0 99.0 %all-to-all-start.11 = ((bf16[4,8,128,1024]{3,2,0,1:T(8,128)(2,1)}), bf16[4,8,128,1024]{3,2,0,1:T(8,128)(2,1)}, u32[]{:S(2)}, u32[]{:S(2)}) async-start(bf16[4,8,128,1024]{3,2,0,1:T(8,128)(2,1)} %copy.178), calls=%async_computation.14 | async-start | bytes 16777216 | tf_op jit(solution)/shard_map/all_to_all | solution.py:135
  3027.0 130.4 %all-to-all-start.7 = ((bf16[4,8,128,1024]{3,2,0,1:T(8,128)(2,1)}), bf16[4,8,128,1024]{3,2,0,1:T(8,128)(2,1)}, u32[]{:S(2)}, u32[]{:S(2)}) async-start(bf16[4,8,128,1024]{3,2,0,1:T(8,128)(2,1)} %copy.171), calls=%async_computation.10 | async-start | bytes 16777216 | tf_op jit(solution)/shard_map/all_to_all | solution.py:135
  3157.4 198.9 %all-to-all-start.3 = ((bf16[4,8,128,1024]{3,2,0,1:T(8,128)(2,1)}), bf16[4,8,128,1024]{3,2,0,1:T(8,128)(2,1)}, u32[]{:S(2)}, u32[]{:S(2)}) async-start(bf16[4,8,128,1024]{3,2,0,1:T(8,128)(2,1)} %copy.160), calls=%async_computation.5 | async-start | bytes 16777216 | tf_op jit(solution)/shard_map/all_to_all | solution.py:135
  3162.4 491.2 %reduce-scatter.31.cloned.1.call-start = ((), (), s32[]{:S(2)}) async-start(), calls=%async_computation.68 | async-start | bytes 2621440
  3423.4 245.9 %all-gather.18.cloned.1.call-start = ((), (), s32[]{:S(2)}) async-start(), calls=%async_computation.59 | async-start | bytes 3932160 | tf_op jit(solution)/shard_map/all_gather | solution.py:22
  3658.2 53.8 %reduce-scatter.23.cloned.1.call-start = ((), (), s32[]{:S(2)}) async-start(), calls=%async_computation.60 | async-start | bytes 2621440 | tf_op jit(solution)/shard_map/reduce_scatter | solution.py:34
  3675.4 70.1 %all-gather.20.cloned.1.call-start = ((), (), s32[]{:S(2)}) async-start(), calls=%async_computation.61 | async-start | bytes 1310720 | tf_op jit(solution)/shard_map/all_gather | solution.py:18
  3718.9 37.9 reduce-scatter.25.cloned.1.call-start
  3748.3 35.5 reduce-scatter.27.cloned.1.call-start
  3772.7 25.5 all-gather.22.cloned.1.call-start
  3786.0 228.1 %all-reduce.8.cloned.1.call-start = ((), (), s32[]{:S(2)}) async-start(), calls=%async_computation.69 | async-start | bytes 5242880 | tf_op jit(solution)/shard_map/psum | solution.py:429
  3829.1 9.1 all-to-all-start.32
  3838.2 8.4 all-to-all-start.39
  3865.9 158.2 %reduce-scatter.29.cloned.1.call-start = ((), (), s32[]{:S(2)}) async-start(), calls=%async_computation.65 | async-start | bytes 2621440 | tf_op jit(solution)/shard_map/reduce_scatter | solution.py:34
  3874.6 192.1 %reduce-scatter.19.cloned.1.call-start = ((), (), s32[]{:S(2)}) async-start(), calls=%async_computation.56 | async-start | bytes 2621440 | tf_op jit(solution)/shard_map/reduce_scatter | solution.py:34
  3916.9 214.9 %all-reduce.6.cloned.1.call-start = ((), (), s32[]{:S(2)}) async-start(), calls=%async_computation.66 | async-start | bytes 8388608 | tf_op jit(solution)/shard_map/psum | solution.py:441
  (145 other events, 5154.3 us)
Sparse Core Ops, SparseCore 0:
  14.3 29.0 all-gather.9
  47.7 10.9 reduce-scatter.12
  61.2 10.2 all-gather.11
  85.9 36.3 reduce-scatter.14
  127.0 26.4 all-gather.13
  155.2 26.4 all-gather.15
  184.6 12.8 reduce-scatter.16
  308.5 8.4 reduce-scatter.20
  656.4 26.8 all-gather.23
  3423.5 34.7 reduce-scatter.30
  3658.3 10.8 all-gather.17
  3675.6 36.3 reduce-scatter.22
  3719.1 26.4 all-gather.19
  3748.4 8.3 reduce-scatter.24
  3772.9 10.8 reduce-scatter.26
  3786.1 11.0 all-gather.21
  3802.0 105.7 all-reduce.7
  3910.6 34.1 reduce-scatter.28
  3947.7 35.1 reduce-scatter.18
  3988.9 142.7 all-reduce.5
where the time goes:
time: 4160 us; the launch traced here: 4140 us
  waiting for transfers between devices  1570 us (38%)
  local copies, waits for them, and re-layouts  1120 us (27%)
  blocking collectives  652 us (16%)
  other arithmetic  467 us (11%)
  matrix products  167 us (4%)
  starting transfers between devices  147 us (4%)
    all_to_all x4, waiting for transfers between devices, memory_backward(): lax.all_to_all(send_rows, 'dp', split_axis=0, concat_axis=0, tiled=True)  646 us
    all_to_all x3, blocking collectives, fetch_rows(): lax.all_to_all(found_rows, 'dp', split_axis=0, concat_axis=0, tiled=True)  564 us
    unnamed x11, other arithmetic  258 us
    all_to_all x4, waiting for transfers between devices, memory_backward(): lax.all_to_all(lax.all_to_all(send_rows, 'dp', split_axis=0, concat_axis=...  257 us
    all_to_all x1, waiting for transfers between devices, fetch_rows(): lax.all_to_all(found_rows, 'dp', split_axis=0, concat_axis=0, tiled=True)  174 us
    all_to_all x4, waiting for transfers between devices, fetch_rows(): lax.all_to_all(lax.all_to_all(found_rows, 'dp', split_axis=0, concat_axis...  171 us
    gather x4, local copies, waits for them, and re-layouts, fetch_rows(): requests = jnp.take(wanted, sort_order).reshape(dp_count, grid_count, -1)  162 us
    gather x5, local copies, waits for them, and re-layouts, memory_forward(): jnp.take_along_axis(first_scores, upper_index, axis=1)  130 us
  transfers between devices with their start and end apart: 53, of which 35 were waited for; matrix products, arithmetic and copies ran while one was open for 39% of the time, Pallas kernels for 0%

commit v1 on v0

--- a/solution.py
+++ b/solution.py
@@ -1,6 +1,9 @@
+import functools
+
 import jax
 import jax.numpy as jnp
 from jax import lax
+from jax.experimental import pallas as pl
 from jax.sharding import PartitionSpec as P
 
 D = 1024
@@ -118,196 +121,310 @@
     return (jnp.concatenate(grad_queries, axis=1), stacked)
 
 
-def fetch_rows(wanted, sort_order, value_shard):
+def flat_picks(picks_head):
+    blocks = picks_head.shape[0] // FBLK
+    return jnp.swapaxes(picks_head.reshape(blocks, FBLK, TOPK), 1, 2).reshape(blocks, TOPK * FBLK)
+
+
+def one_hot(row_values, size):
+    hot = lax.broadcasted_iota(jnp.int32, (size, row_values.shape[1]), 0) == row_values
+    return jnp.where(hot, 1.0, 0.0).astype(jnp.bfloat16)
+
+
+def route_kernel(rows_dev, owners, cap, picks_ref, rank_ref, meta_ref):
+    lane = lax.broadcasted_iota(jnp.int32, (FBLK, FBLK), 0)
+    before = jnp.where(lane < lax.broadcasted_iota(jnp.int32, (FBLK, FBLK), 1), 1.0, 0.0).astype(
+        jnp.bfloat16
+    )
+    picks = picks_ref[0]
+    owner = picks // rows_dev
+    local = picks % rows_dev
+    hot = one_hot(owner, owners)
+    running = jnp.zeros((owners, 1), jnp.float32)
+    ranks = []
+    for chunk in range(picks.shape[1] // FBLK):
+        part = hot[:, chunk * FBLK : (chunk + 1) * FBLK]
+        earlier = jnp.dot(part, before, preferred_element_type=jnp.float32)
+        wide = part.astype(jnp.float32)
+        ranks.append(jnp.sum(wide * (earlier + running), axis=0, keepdims=True))
+        running = running + jnp.sum(wide, axis=1, keepdims=True)
+    rank = jnp.concatenate(ranks, axis=1).astype(jnp.int32)
+    rank_ref[0] = rank
+    slot_hot = one_hot(rank, cap)
+    token = lax.broadcasted_iota(jnp.int32, picks.shape, 1) % FBLK
+    outs = []
+    for payload in (local % SUBKEYS, local // SUBKEYS, token):
+        scaled = hot * payload.astype(jnp.float32).astype(jnp.bfloat16)
+        outs.append(
+            lax.dot_general(
+                scaled, slot_hot, (((1,), (1,)), ((), ())), preferred_element_type=jnp.float32
+            ).astype(jnp.int32)
+        )
+    meta_ref[0] = (outs[1] * FBLK + outs[2]) * SUBKEYS + outs[0]
+
+
+def route(flat, rows_dev, owners, cap):
+    blocks, count = flat.shape
+    rank, meta = pl.pallas_call(
+        functools.partial(route_kernel, rows_dev, owners, cap),
+        grid=(blocks,),
+        in_specs=[pl.BlockSpec((1, 1, count), lambda i: (i, 0, 0))],
+        out_specs=[
+            pl.BlockSpec((1, 1, count), lambda i: (i, 0, 0)),
+            pl.BlockSpec((1, owners, cap), lambda i: (i, 0, 0)),
+        ],
+        out_shape=[
+            jax.ShapeDtypeStruct((blocks, 1, count), jnp.int32),
+            jax.ShapeDtypeStruct((blocks, owners, cap), jnp.int32),
+        ],
+        name="route",
+    )(flat[:, None, :])
+    return rank, meta
+
+
+def weigh_kernel(rows_dev, owners, cap, query_ref, keys_ref, picks_ref, rank_ref, weights_ref, slots_ref):
+    picks = picks_ref[0]
+    first = lax.dot_general(
+        keys_ref[0], query_ref[:, :HALF], (((1,), (1,)), ((), ())), preferred_element_type=jnp.float32
+    )
+    second = lax.dot_general(
+        keys_ref[1], query_ref[:, HALF:], (((1,), (1,)), ((), ())), preferred_element_type=jnp.float32
+    )
+    upper = picks // SUBKEYS
+    lower = picks % SUBKEYS
+    key_id = lax.broadcasted_iota(jnp.int32, (SUBKEYS, FBLK), 0)
+    rows = []
+    for pick in range(TOPK):
+        columns = slice(pick * FBLK, (pick + 1) * FBLK)
+        chosen = jnp.where(key_id == upper[:, columns], first, 0.0) + jnp.where(
+            key_id == lower[:, columns], second, 0.0
+        )
+        rows.append(jnp.sum(chosen, axis=0, keepdims=True))
+    scores = jnp.concatenate(rows, axis=0)
+    powers = jnp.exp(scores - jnp.max(scores, axis=0, keepdims=True))
+    weights = powers / jnp.sum(powers, axis=0, keepdims=True)
+    weights_ref[0] = weights
+    flat = jnp.concatenate([weights[pick : pick + 1] for pick in range(TOPK)], axis=1)
+    scaled = one_hot(picks // rows_dev, owners) * flat.astype(jnp.bfloat16)
+    slots_ref[0] = lax.dot_general(
+        scaled,
+        one_hot(rank_ref[0], cap),
+        (((1,), (1,)), ((), ())),
+        preferred_element_type=jnp.float32,
+    ).astype(jnp.bfloat16)
+
+
+def weigh(query_rows, keys_head, flat, rank, rows_dev, owners, cap):
+    blocks, count = flat.shape
+    return pl.pallas_call(
+        functools.partial(weigh_kernel, rows_dev, owners, cap),
+        grid=(blocks,),
+        in_specs=[
+            pl.BlockSpec((FBLK, 2 * HALF), lambda i: (i, 0)),
+            pl.BlockSpec((2, SUBKEYS, HALF), lambda i: (0, 0, 0)),
+            pl.BlockSpec((1, 1, count), lambda i: (i, 0, 0)),
+            pl.BlockSpec((1, 1, count), lambda i: (i, 0, 0)),
+        ],
+        out_specs=[
+            pl.BlockSpec((1, TOPK, FBLK), lambda i: (i, 0, 0)),
+            pl.BlockSpec((1, owners, cap), lambda i: (i, 0, 0)),
+        ],
+        out_shape=[
+            jax.ShapeDtypeStruct((blocks, TOPK, FBLK), jnp.float32),
+            jax.ShapeDtypeStruct((blocks, owners, cap), jnp.bfloat16),
+        ],
+        name="weigh",
+    )(query_rows, keys_head, flat[:, None, :], rank)
+
+
+def spread_kernel(areas, key_ref, low_ref, weight_ref, out_ref):
+    key = key_ref[0]
+    at_key = lax.broadcasted_iota(jnp.int32, (areas * FBLK, key.shape[1]), 0) == key
+    left = jnp.where(at_key, weight_ref[0].astype(jnp.float32), 0.0).astype(jnp.bfloat16)
+    stacked = lax.dot_general(
+        left,
+        one_hot(low_ref[0], SUBKEYS),
+        (((1,), (1,)), ((), ())),
+        preferred_element_type=jnp.float32,
+    ).astype(jnp.bfloat16)
+    for area in range(areas):
+        out_ref[:, area * SUBKEYS : (area + 1) * SUBKEYS] = stacked[area * FBLK : (area + 1) * FBLK]
+
+
+def spread(key, low, weight, rows_dev):
+    blocks, slots = key.shape
+    areas = rows_dev // SUBKEYS
+    row = pl.BlockSpec((1, 1, slots), lambda i: (i, 0, 0))
+    return pl.pallas_call(
+        functools.partial(spread_kernel, areas),
+        grid=(blocks,),
+        in_specs=[row, row, row],
+        out_specs=pl.BlockSpec((FBLK, rows_dev), lambda i: (i, 0)),
+        out_shape=jax.ShapeDtypeStruct((blocks * FBLK, rows_dev), jnp.bfloat16),
+        name="spread",
+    )(key[:, None], low[:, None], weight[:, None])
+
+
+def collect_kernel(areas, grid_ref, key_ref, low_ref, out_ref):
+    key = key_ref[0]
+    low_hot = one_hot(low_ref[0], SUBKEYS)
+    total = jnp.zeros(key.shape, jnp.float32)
+    for area in range(areas):
+        product = jnp.dot(
+            grid_ref[:, area * SUBKEYS : (area + 1) * SUBKEYS],
+            low_hot,
+            preferred_element_type=jnp.float32,
+        )
+        spot = lax.broadcasted_iota(jnp.int32, product.shape, 0) + area * FBLK
+        total = total + jnp.sum(jnp.where(spot == key, product, 0.0), axis=0, keepdims=True)
+    out_ref[0] = total
+
+
+def collect(grid_products, key, low, rows_dev):
+    blocks, slots = key.shape
+    row = pl.BlockSpec((1, 1, slots), lambda i: (i, 0, 0))
+    return pl.pallas_call(
+        functools.partial(collect_kernel, rows_dev // SUBKEYS),
+        grid=(blocks,),
+        in_specs=[pl.BlockSpec((FBLK, rows_dev), lambda i: (i, 0)), row, row],
+        out_specs=row,
+        out_shape=jax.ShapeDtypeStruct((blocks, 1, slots), jnp.float32),
+        name="collect",
+    )(grid_products, key[:, None], low[:, None])[:, 0]
+
+
+def unweigh_kernel(rows_dev, owners, back_ref, picks_ref, rank_ref, weights_ref, first_ref, second_ref):
+    picks = picks_ref[0]
+    hot = one_hot(picks // rows_dev, owners)
+    back = back_ref[0]
+    high = back.astype(jnp.bfloat16)
+    rest = back - high.astype(jnp.float32)
+    middle = rest.astype(jnp.bfloat16)
+    lowest = (rest - middle.astype(jnp.float32)).astype(jnp.bfloat16)
+    spread_back = (
+        jnp.dot(high, hot, preferred_element_type=jnp.float32)
+        + jnp.dot(middle, hot, preferred_element_type=jnp.float32)
+        + jnp.dot(lowest, hot, preferred_element_type=jnp.float32)
+    )
+    slot = lax.broadcasted_iota(jnp.int32, spread_back.shape, 0)
+    flat = jnp.sum(jnp.where(slot == rank_ref[0], spread_back, 0.0), axis=0, keepdims=True)
+    grads = jnp.concatenate(
+        [flat[:, pick * FBLK : (pick + 1) * FBLK] for pick in range(TOPK)], axis=0
+    )
+    weights = weights_ref[0]
+    grads = weights * (grads - jnp.sum(weights * grads, axis=0, keepdims=True))
+    upper = picks // SUBKEYS
+    lower = picks % SUBKEYS
+    key_id = lax.broadcasted_iota(jnp.int32, (SUBKEYS, FBLK), 0)
+    first = jnp.zeros((SUBKEYS, FBLK), jnp.float32)
+    second = jnp.zeros((SUBKEYS, FBLK), jnp.float32)
+    for pick in range(TOPK):
+        columns = slice(pick * FBLK, (pick + 1) * FBLK)
+        value = grads[pick : pick + 1]
+        first = first + jnp.where(key_id == upper[:, columns], value, 0.0)
+        second = second + jnp.where(key_id == lower[:, columns], value, 0.0)
+    first_ref[...] = first.astype(jnp.bfloat16)
+    second_ref[...] = second.astype(jnp.bfloat16)
+
+
+def unweigh(back, flat, rank, weights, rows_dev, owners):
+    blocks, count = flat.shape
+    cap = back.shape[1]
+    return pl.pallas_call(
+        functools.partial(unweigh_kernel, rows_dev, owners),
+        grid=(blocks,),
+        in_specs=[
+            pl.BlockSpec((1, cap, owners), lambda i: (i, 0, 0)),
+            pl.BlockSpec((1, 1, count), lambda i: (i, 0, 0)),
+            pl.BlockSpec((1, 1, count), lambda i: (i, 0, 0)),
+            pl.BlockSpec((1, TOPK, FBLK), lambda i: (i, 0, 0)),
+        ],
+        out_specs=[
+            pl.BlockSpec((SUBKEYS, FBLK), lambda i: (0, i)),
+            pl.BlockSpec((SUBKEYS, FBLK), lambda i: (0, i)),
+        ],
+        out_shape=[jax.ShapeDtypeStruct((SUBKEYS, blocks * FBLK), jnp.bfloat16)] * 2,
+        name="unweigh",
+    )(back, flat[:, None, :], rank, weights)
+
+
+EVERYONE = ("dp", "row", "col")
+
+
+def exchange(operand):
+    return lax.all_to_all(operand, EVERYONE, split_axis=0, concat_axis=0, tiled=True)
+
+
+def by_block(arrived, dp_count, row_count, col_count):
+    _, blocks, cap = arrived.shape
+    wide = arrived.reshape(dp_count, row_count, col_count, blocks, cap)
+    return jnp.transpose(wide, (0, 2, 3, 1, 4)).reshape(
+        dp_count * col_count * blocks, row_count * cap
+    )
+
+
+def by_source(blocked, dp_count, row_count, col_count, blocks, cap):
+    wide = blocked.reshape(dp_count, col_count, blocks, row_count, cap)
+    return jnp.transpose(wide, (0, 3, 1, 2, 4)).reshape(
+        dp_count * row_count * col_count, blocks, cap
+    )
+
+
+def memory_all(query_rows, grad_memory, picks, subkeys, values):
     dp_count = lax.axis_size("dp")
-    grid_count = lax.axis_size("row") * lax.axis_size("col")
-    rows_dev = value_shard.shape[0]
-    requests = jnp.take(wanted, sort_order).reshape(dp_count, grid_count, -1)
-    arrived = lax.all_to_all(
-        lax.all_to_all(requests, "dp", split_axis=0, concat_axis=0, tiled=True),
-        ("row", "col"),
-        split_axis=1,
-        concat_axis=1,
-        tiled=True,
-    )
-    local_rows = arrived % rows_dev
-    found_rows = jnp.take(value_shard, local_rows, axis=0)
-    returned = lax.all_to_all(
-        lax.all_to_all(found_rows, "dp", split_axis=0, concat_axis=0, tiled=True),
-        ("row", "col"),
-        split_axis=1,
-        concat_axis=1,
-        tiled=True,
-    )
-    unsort = jnp.argsort(sort_order)
-    return (jnp.take(returned.reshape(-1, value_shard.shape[1]), unsort, axis=0), local_rows)
-
-
-def memory_forward(query_rows, picks, subkeys, values):
-    head_count = query_rows.shape[1] // (2 * HALF)
     row_count = lax.axis_size("row")
-    head_first = lax.axis_index("row") * head_count
+    col_count = lax.axis_size("col")
+    owners = dp_count * row_count * col_count
     rows_dev = values.shape[0]
+    cap = FBLK * TOPK // owners
     own_tokens = query_rows.shape[0]
-    head_id = head_first + 0
+    blocks = own_tokens // FBLK
+    head_id = lax.axis_index("row")
     keys_head = lax.dynamic_index_in_dim(subkeys, head_id, 0, keepdims=False)
     picks_head = lax.dynamic_index_in_dim(picks, head_id, 1, keepdims=False)
-    first_scores = jnp.einsum(
-        "td,ad->ta", query_rows[:, :HALF], keys_head[0], preferred_element_type=jnp.float32
-    )
-    second_scores = jnp.einsum(
-        "td,ad->ta", query_rows[:, HALF:], keys_head[1], preferred_element_type=jnp.float32
-    )
-    upper_index = picks_head // SUBKEYS
-    lower_index = picks_head % SUBKEYS
-    pick_scores = jnp.take_along_axis(first_scores, upper_index, axis=1) + jnp.take_along_axis(
-        second_scores, lower_index, axis=1
-    )
-    pick_weights = jax.nn.softmax(pick_scores, axis=1)
-    weights_low = pick_weights.astype(jnp.bfloat16)
-    block_parts = []
-    block_state = []
-    for block_index in range(own_tokens // FBLK):
-        wanted = picks_head[block_index * FBLK : (block_index + 1) * FBLK].reshape(-1)
-        sort_order = jnp.argsort(wanted // rows_dev, stable=True)
-        fetched, local_rows = fetch_rows(wanted, sort_order, values)
-        grouped = fetched.reshape(FBLK, TOPK, row_count, -1)
-        block_weights = weights_low[block_index * FBLK : (block_index + 1) * FBLK]
-        block_parts.append(
-            jnp.einsum("tk,tkcf->ctf", block_weights, grouped, preferred_element_type=jnp.float32)
-        )
-        block_state.append((wanted, sort_order, local_rows))
-    totals = jnp.concatenate(block_parts, axis=1)
-    kept_state = [
-        (
-            head_id,
-            keys_head,
-            query_rows,
-            upper_index,
-            lower_index,
-            pick_weights,
-            weights_low,
-            block_state,
-        )
-    ]
-    memory = lax.psum_scatter(totals, "row", scatter_dimension=0, tiled=True)[0]
-    return (memory, kept_state)
-
-
-def memory_backward(grad_memory, kept_state, values, subkeys):
-    gathered = row_gather(grad_memory[None])
-    own_tokens = gathered.shape[1]
-    grad_tokens = jnp.moveaxis(gathered, 0, 1).reshape(own_tokens, -1)
-    dp_count = lax.axis_size("dp")
-    grid_count = lax.axis_size("row") * lax.axis_size("col")
-    rows_dev = values.shape[0]
-    row_ids = lax.iota(jnp.int32, rows_dev)
-    grad_values = jnp.zeros(values.shape, jnp.float32)
-    grad_subkeys = jnp.zeros(subkeys.shape, jnp.float32)
-    grad_queries = []
-    for (
-        head_id,
-        keys_head,
-        query_head,
-        upper_index,
-        lower_index,
-        pick_weights,
-        weights_low,
-        block_state,
-    ) in kept_state:
-        block_grads = []
-        for block_index, (wanted, sort_order, local_rows) in enumerate(block_state):
-            token_rows = grad_tokens[block_index * FBLK : (block_index + 1) * FBLK]
-            send_rows = jnp.take(token_rows, sort_order // TOPK, axis=0).reshape(
-                dp_count, grid_count, -1, token_rows.shape[1]
+    flat = flat_picks(picks_head)
+    rank, meta = route(flat, rows_dev, owners, cap)
+    sizes = (dp_count, row_count, col_count)
+    meta_in = by_block(exchange(jnp.swapaxes(meta, 0, 1)), *sizes)
+    key = meta_in // SUBKEYS
+    low = meta_in % SUBKEYS
+    weights, slots = weigh(query_rows, keys_head, flat, rank, rows_dev, owners, cap)
+    weight_in = by_block(exchange(jnp.swapaxes(slots, 0, 1)), *sizes)
+    table = spread(key, low, weight_in, rows_dev)
+    partial = jnp.dot(table, values, preferred_element_type=jnp.float32).astype(jnp.bfloat16)
+    grid = partial.reshape(dp_count, col_count, own_tokens, row_count, -1)
+    grid = jnp.transpose(grid, (0, 3, 1, 2, 4)).reshape(owners, own_tokens, -1)
+    memory = lax.psum_scatter(grid, EVERYONE, scatter_dimension=0, tiled=True)[0]
+    memory = memory.astype(jnp.float32)
+    wide = lax.all_gather(grad_memory, "row", axis=1, tiled=True)
+    grad_all = lax.all_gather(wide, ("dp", "col"), axis=0, tiled=True)
+    grad_values = lax.dot_general(
+        table, grad_all, (((0,), (0,)), ((), ())), preferred_element_type=jnp.float32
+    )
+    products = lax.dot_general(
+        grad_all, values, (((1,), (1,)), ((), ())), preferred_element_type=jnp.float32
+    ).astype(jnp.bfloat16)
+    found = collect(products, key, low, rows_dev)
+    back = exchange(by_source(found, *sizes, blocks, cap))
+    first_t, second_t = unweigh(
+        jnp.transpose(back, (1, 2, 0)), flat, rank, weights, rows_dev, owners
+    )
+    grad_query = jnp.concatenate(
+        [
+            lax.dot_general(
+                part, keys_head[i], (((0,), (0,)), ((), ())), preferred_element_type=jnp.float32
             )
-            block_weights = weights_low[block_index * FBLK : (block_index + 1) * FBLK].reshape(-1)
-            send_weights = jnp.take(block_weights, sort_order).reshape(dp_count, grid_count, -1)
-            arrived_rows, arrived_weights = (
-                lax.all_to_all(
-                    lax.all_to_all(send_rows, "dp", split_axis=0, concat_axis=0, tiled=True),
-                    ("row", "col"),
-                    split_axis=1,
-                    concat_axis=1,
-                    tiled=True,
-                ),
-                lax.all_to_all(
-                    lax.all_to_all(send_weights, "dp", split_axis=0, concat_axis=0, tiled=True),
-                    ("row", "col"),
-                    split_axis=1,
-                    concat_axis=1,
-                    tiled=True,
-                ),
-            )
-            flat_local = local_rows.reshape(-1)
-            picker = jnp.where(
-                flat_local[:, None] == row_ids[None, :],
-                arrived_weights.reshape(-1)[:, None],
-                jnp.zeros((), jnp.bfloat16),
-            )
-            grad_values = grad_values + jnp.einsum(
-                "pr,pf->rf",
-                picker,
-                arrived_rows.reshape(-1, arrived_rows.shape[-1]),
-                preferred_element_type=jnp.float32,
-            )
-            stored = jnp.take(values, local_rows, axis=0)
-            products = jnp.einsum(
-                "abcf,abcf->abc", arrived_rows, stored, preferred_element_type=jnp.float32
-            )
-            returned = lax.all_to_all(
-                lax.all_to_all(products, "dp", split_axis=0, concat_axis=0, tiled=True),
-                ("row", "col"),
-                split_axis=1,
-                concat_axis=1,
-                tiled=True,
-            )
-            unsort = jnp.argsort(sort_order)
-            block_grads.append(jnp.take(returned.reshape(-1), unsort).reshape(FBLK, TOPK))
-        grad_weights = jnp.concatenate(block_grads, axis=0)
-        grad_scores = pick_weights * (
-            grad_weights - jnp.sum(pick_weights * grad_weights, axis=1, keepdims=True)
-        )
-        token_index = lax.broadcasted_iota(jnp.int32, upper_index.shape, 0)
-        grad_first = (
-            jnp.zeros((own_tokens, SUBKEYS), jnp.float32)
-            .at[token_index, upper_index]
-            .add(grad_scores)
-            .astype(jnp.bfloat16)
-        )
-        grad_second = (
-            jnp.zeros((own_tokens, SUBKEYS), jnp.float32)
-            .at[token_index, lower_index]
-            .add(grad_scores)
-            .astype(jnp.bfloat16)
-        )
-        grad_queries.append(
-            jnp.concatenate(
-                [
-                    jnp.dot(grad_first, keys_head[0], preferred_element_type=jnp.float32),
-                    jnp.dot(grad_second, keys_head[1], preferred_element_type=jnp.float32),
-                ],
-                axis=1,
-            )
-        )
-        grad_keys_head = jnp.stack(
-            [
-                jnp.einsum(
-                    "ta,td->ad",
-                    grad_first,
-                    query_head[:, :HALF],
-                    preferred_element_type=jnp.float32,
-                ),
-                jnp.einsum(
-                    "ta,td->ad",
-                    grad_second,
-                    query_head[:, HALF:],
-                    preferred_element_type=jnp.float32,
-                ),
-            ]
-        )
-        grad_subkeys = lax.dynamic_update_index_in_dim(grad_subkeys, grad_keys_head, head_id, 0)
-    return (grad_queries[0].astype(jnp.bfloat16), grad_values, grad_subkeys)
+            for i, part in enumerate((first_t, second_t))
+        ],
+        axis=1,
+    ).astype(jnp.bfloat16)
+    grad_keys = jnp.stack(
+        [
+            jnp.dot(first_t, query_rows[:, :HALF], preferred_element_type=jnp.float32),
+            jnp.dot(second_t, query_rows[:, HALF:], preferred_element_type=jnp.float32),
+        ]
+    )
+    return memory, grad_query, grad_values, grad_keys
 
 
 def per_device(
@@ -382,22 +499,25 @@
     mixed_sum = col_reduce(gathered_two, project_memory)
     query_rows = mixed_sum[:, :query_width].astype(jnp.bfloat16)
     gate_value = mixed_sum[:, query_width:]
-    memory, kept_state = memory_forward(query_rows, picks, subkeys, values)
     sigmoid_gate = jax.nn.sigmoid(gate_value)
     silu_gate = gate_value * sigmoid_gate
+    grad_rows = row_gather(cotangent)
+    grad_gated = col_reduce(grad_rows, back_proj)
+    grad_memory = (grad_gated * silu_gate).astype(jnp.bfloat16)
+    memory, grad_query, grad_values, grad_keys = memory_all(
+        query_rows, grad_memory, picks, subkeys, values
+    )
     gated_value = (memory * silu_gate).astype(jnp.bfloat16)
     gated_all = col_gather(gated_value)
     output = (hidden + row_reduce(gated_all, proj_mem)).astype(jnp.bfloat16)
-    grad_rows = row_gather(cotangent)
     grad_w_proj = jnp.einsum("tf,tc->fc", gated_all, grad_rows, preferred_element_type=jnp.float32)
-    grad_gated = col_reduce(grad_rows, back_proj)
-    grad_memory = (grad_gated * silu_gate).astype(jnp.bfloat16)
     grad_gate = (
         grad_gated * memory * sigmoid_gate * (1.0 + gate_value * (1.0 - sigmoid_gate))
     ).astype(jnp.bfloat16)
-    grad_query, grad_values, grad_subkeys = memory_backward(
-        grad_memory, kept_state, values, subkeys
-    )
+    grad_keys = lax.psum_scatter(grad_keys.reshape(-1, HALF), ("dp", "col"), scatter_dimension=0, tiled=True)
+    grad_subkeys = lax.all_gather(
+        grad_keys.astype(jnp.bfloat16), ("row", "dp", "col"), axis=0, tiled=True
+    ).astype(jnp.float32).reshape(subkeys.shape)
     grad_mixed = col_gather(jnp.concatenate([grad_query, grad_gate], axis=1))
     grad_w_query = jnp.einsum(
         "tc,tq->cq", gathered_two, grad_mixed[:, :query_width], preferred_element_type=jnp.float32
@@ -438,7 +558,7 @@
     gain_full_two = lax.dynamic_update_slice_in_dim(
         jnp.zeros(gain_mem.shape, jnp.float32), grad_gain_two, col_first, 0
     )
-    small_sums = lax.psum((gain_full_one, gain_full_two, grad_subkeys), ("dp", "row", "col"))
+    small_sums = lax.psum((gain_full_one, gain_full_two), ("dp", "row", "col"))
     return (
         output,
         grad_inputs,
@@ -449,7 +569,7 @@
         weight_sums[2],
         weight_sums[3],
         weight_sums[4],
-        small_sums[2],
+        grad_subkeys,
         grad_values,
     )
 

time: 4160 us -> 1050 us (0.25)
  local copies, waits for them, and re-layouts: 1120 us -> 44.4 us
  waiting for transfers between devices: 1570 us -> 648 us
  blocking collectives: 652 us -> 54.9 us
  other arithmetic: 467 us -> 48.5 us
  starting transfers between devices: 147 us -> 11.8 us
  Pallas kernels: 0 us -> 80.4 us
    all_to_all x33 -> x3, waiting for transfers between devices: 1310 us -> 17.3 us  [exchange(): lax.all_to_all(operand, EVERYONE, split_axis=0, concat_axis=0, tiled=True)]
    gather x34 -> x0, local copies, waits for them, and re-layouts: 893 us -> none  [the longest x4 162 us: fetch_rows(): requests = jnp.take(wanted, sort_order).reshape(dp_count, grid_count, -1)]
    all_to_all x7 -> x0, blocking collectives: 599 us -> none  [the longest x3 564 us: fetch_rows(): lax.all_to_all(found_rows, 'dp', split_axis=0, concat_axis=0, tiled=True)]
    unnamed x11 -> x0, other arithmetic: 258 us -> none
    reduce_scatter x0 -> x2, waiting for transfers between devices: none -> 180 us  [the longest x1 147 us: memory_all(): lax.psum_scatter(grid, EVERYONE, scatter_dimension=0, tiled=True)[0]]
    all_to_all x36 -> x1, local copies, waits for them, and re-layouts: 140 us -> 0.84 us  [exchange(): lax.all_to_all(operand, EVERYONE, split_axis=0, concat_axis=0, tiled=True)]
    all_to_all x33 -> x3, starting transfers between devices: 145 us -> 10.2 us  [exchange(): lax.all_to_all(operand, EVERYONE, split_axis=0, concat_axis=0, tiled=True)]
    all_gather x0 -> x3, waiting for transfers between devices: none -> 128 us  [the longest x1 83.6 us: memory_all(): grad_all = lax.all_gather(wide, ('dp', 'col'), axis=0, tiled=True)]
  transfers between devices with their start and end apart: 53 -> 25, of which waited for: 35 -> 19; matrix products, arithmetic and copies ran while one was open for 39% -> 13% of each run, Pallas kernels for 0% -> 4%
where the time goes in v1:
time: 1050 us; the launch traced here: 1040 us
  waiting for transfers between devices  648 us (62%)
  matrix products  136 us (13%)
  Pallas kernels  80.4 us (8%)
  blocking collectives  54.9 us (5%)
  other arithmetic  48.5 us (5%)
  local copies, waits for them, and re-layouts  44.4 us (4%)
  between operations  16.1 us (2%)
  starting transfers between devices  11.8 us (1%)
    reduce_scatter x1, waiting for transfers between devices, memory_all(): lax.psum_scatter(grid, EVERYONE, scatter_dimension=0, tiled=True)[0]  147 us
    psum x1, waiting for transfers between devices, per_device(): lax.psum(grad_w_qkv.astype(jnp.bfloat16), 'dp').astype(jnp.float32)  102 us
    reduce_scatter x4, waiting for transfers between devices, row_reduce(): lax.psum_scatter(product(gathered), 'row', scatter_dimension=0, tiled=True)  100 us
    all_gather x1, waiting for transfers between devices, memory_all(): grad_all = lax.all_gather(wide, ('dp', 'col'), axis=0, tiled=True)  83.6 us
    all_gather x4, waiting for transfers between devices, row_gather(): return lax.all_gather(operand, 'row', axis=0, tiled=True)  82.4 us
    psum x1, blocking collectives, per_device(): small_sums = lax.psum((gain_full_one, gain_full_two), ('dp', 'row', 'col'))  39.7 us
    reduce_scatter x1, waiting for transfers between devices, per_device(): lax.psum_scatter(grad_keys.reshape(-1, HALF), ('dp', 'col'), scatter_dime...  33 us
    pallas_call x1, Pallas kernels, collect(): pl.pallas_call(functools.partial(collect_kernel, rows_dev // SUBKEYS), gr...  26.6 us
  transfers between devices with their start and end apart: 25, of which 19 were waited for; matrix products, arithmetic and copies ran while one was open for 13% of the time, Pallas kernels for 4%

profile of v1, /device:TPU:0, one launch (start us, length us, event | category | flops | bytes accessed | tf_op | source)
XLA Modules:
  0.0 1040.0 jit_solution(2342147210053276957)
XLA Ops:
  8.5 2.6 psum.77
  13.7 29.2 %all-gather.11.cloned.1.call-done = bf16[1024,512]{1,0:T(8,128)(2,1)} async-done(((bf16[256,512]{1,0:T(8,128)(2,1)}), bf16[1024,512]{1,0:T(8,128)(2,1)}) %all-gather.11.cloned.1.call-update) | async-done | bytes 1048592 | tf_op jit(solution)/shard_map/all_gather | solution.py:21
  42.9 4.1 fusion.30
  47.1 11.1 %reduce-scatter.12.cloned.1.call-done = f32[512,3,256]{2,0,1:T(8,128)} async-done(((f32[1024,3,256]{2,0,1:T(8,128)}), f32[512,3,256]{2,0,1:T(8,128)}) %reduce-scatter.12.cloned.1.call-update) | async-done | bytes 1572880 | tf_op jit(solution)/shard_map/reduce_scatter | solution.py:33
  61.3 9.7 all-gather.13.cloned.1.call-done
  84.4 36.4 %reduce-scatter.14.cloned.1.call-done = f32[256,512]{1,0:T(8,128)} async-done(((f32[1024,512]{1,0:T(8,128)}), f32[256,512]{1,0:T(8,128)}) %reduce-scatter.14.cloned.1.call-update) | async-done | bytes 524304 | tf_op jit(solution)/shard_map/reduce_scatter | solution.py:37
  121.9 2.5 psum.78
  125.3 26.6 %all-gather.15.cloned.1.call-done = bf16[1024,512]{1,0:T(8,128)(2,1)} async-done(((bf16[256,512]{1,0:T(8,128)(2,1)}), bf16[1024,512]{1,0:T(8,128)(2,1)}) %all-gather.15.cloned.1.call-update) | async-done | bytes 1048592 | tf_op jit(solution)/shard_map/all_gather | solution.py:21
  155.1 2.8 pad_maximum_fusion
  160.2 6.5 route.1
  168.3 4.6 all-to-all-start
  173.7 6.6 all-to-all-done
  186.0 12.4 %weigh.1 = (f32[4,32,128]{2,1,0:T(8,128)}, bf16[4,32,128]{2,1,0:T(8,128)(2,1)}) custom-call(bf16[512,1024]{1,0:T(8,128)(2,1)} %slice.132.query_ref, bf16[2,256,512]{2,1,0:T(8,128)(2,1)} %dynamic-slice_bitcast_fusion.keys_ref, s32[4,1,4096]{2,1,0:T(1,128)} %bitcast.177, s32[4,1,4096]{2,1,0:T(1,128)} %get-tuple-element.18.rank_ref), custom_call_target="tpu_custom_call" | custom-call | tf_op jit(solution)/shard_map/weigh/pallas_call | solution.py:219
  199.8 2.6 all-to-all-start.1
  202.5 2.7 fusion.79
  205.2 4.4 all-to-all-done.1
  210.3 23.4 %spread.1 = bf16[4096,2048]{1,0:T(8,128)(2,1)} custom-call(s32[32,1,512]{2,1,0:T(1,128)} %and_select_fusion.1.key_ref, s32[32,1,512]{2,1,0:T(1,128)} %get-tuple-element.69.low_ref, bf16[32,1,512]{2,1,0:T(2,128)(2,1)} %broadcast_in_dim_reshape.10.weight_ref), custom_call_target="tpu_custom_call" | custom-call | tf_op jit(solution)/shard_map/spread/pallas_call | solution.py:258
  233.7 23.4 %convolution_convert_fusion.1 = bf16[4096,1024]{1,0:T(8,128)(2,1)} fusion(bf16[4096,2048]{1,0:T(8,128)(2,1)} %spread.1, bf16[2048,1024]{1,0:T(8,128)(2,1)} %param.24), kind=kOutput, calls=%fused_computation.1 | convolution fusion | flops 17184063488 | bytes 29360128 | tf_op jit(solution)/shard_map/dot_general | solution.py:394
  257.1 14.6 %reshape.216 = bf16[4,2,512,4,256]{4,3,2,1,0:T(4,128)(2,1)} reshape(bf16[4096,1024]{1,0:T(8,128)(2,1)} %convolution_convert_fusion.1) | data formatting | bytes 16777216 | tf_op jit(solution)/shard_map/reshape | solution.py:395
  271.7 8.3 copy.53
  280.2 147.1 %reduce-scatter.18.cloned.1.call-done = bf16[1,512,256]{2,1,0:T(8,128)(2,1)} async-done(((bf16[32,512,256]{2,1,0:T(8,128)(2,1)}), bf16[1,512,256]{2,1,0:T(8,128)(2,1)}) %reduce-scatter.18.cloned.1.call-update) | async-done | bytes 262160 | tf_op jit(solution)/shard_map/reduce_scatter | solution.py:397
  429.8 22.3 %all-gather.19.cloned.1.call-done = bf16[512,1024]{1,0:T(8,128)(2,1)} async-done(((bf16[512,256]{1,0:T(8,128)(2,1)}), bf16[512,1024]{1,0:T(8,128)(2,1)}) %all-gather.19.cloned.1.call-update) | async-done | bytes 1048592 | tf_op jit(solution)/shard_map/all_gather | solution.py:399
  452.2 83.6 %all-gather.21.cloned.1.call-done = bf16[4096,1024]{1,0:T(8,128)(2,1)} async-done(((bf16[512,1024]{1,0:T(8,128)(2,1)}), bf16[4096,1024]{1,0:T(8,128)(2,1)}) %all-gather.21.cloned.1.call-update) | async-done | bytes 8388624 | tf_op jit(solution)/shard_map/all_gather | solution.py:400
  535.8 23.5 %convolution_convert_fusion.grid_ref = bf16[4096,2048]{1,0:T(8,128)(2,1)} fusion(bf16[4096,1024]{1,0:T(8,128)(2,1)} %all-gather.21.cloned.1.call-done, bf16[2048,1024]{1,0:T(8,128)(2,1)} %param.24), kind=kOutput, calls=%fused_computation | convolution fusion | flops 17188257792 | bytes 29360128 | tf_op jit(solution)/shard_map/dot_general | solution.py:404
  559.4 26.6 %collect.1 = f32[32,1,512]{2,1,0:T(1,128)} custom-call(bf16[4096,2048]{1,0:T(8,128)(2,1)} %convolution_convert_fusion.grid_ref, s32[32,1,512]{2,1,0:T(1,128)} %and_select_fusion.1.key_ref, s32[32,1,512]{2,1,0:T(1,128)} %get-tuple-element.69.low_ref), custom_call_target="tpu_custom_call" | custom-call | tf_op jit(solution)/shard_map/collect/pallas_call | solution.py:286
  587.5 3.1 all-to-all-start.2
  591.8 6.3 all-to-all-done.2
  598.9 11.5 %unweigh.1 = (bf16[256,512]{1,0:T(8,128)(2,1)}, bf16[256,512]{1,0:T(8,128)(2,1)}) custom-call(f32[4,128,32]{2,1,0:T(8,128)} %bitcast.175, s32[4,1,4096]{2,1,0:T(1,128)} %bitcast.178, s32[4,1,4096]{2,1,0:T(1,128)} %get-tuple-element.18.rank_ref, f32[4,32,128]{2,1,0:T(8,128)} %get-tuple-element.20.weights_ref), custom_call_target="tpu_custom_call" | custom-call | tf_op jit(solution)/shard_map/unweigh/pallas_call | solution.py:333
  614.3 8.2 all-gather.23.cloned.1.call-done
  622.4 3.1 fusion.7
  625.6 2.9 convolution_add_fusion
  628.5 36.5 %reduce-scatter.24.cloned.1.call-done = f32[256,512]{1,0:T(8,128)} async-done(((f32[1024,512]{1,0:T(8,128)}), f32[256,512]{1,0:T(8,128)}) %reduce-scatter.24.cloned.1.call-update) | async-done | bytes 524304 | tf_op jit(solution)/shard_map/reduce_scatter | solution.py:37
  666.3 2.7 psum.79
  671.0 26.6 %all-gather.25.cloned.1.call-done = bf16[1024,512]{1,0:T(8,128)(2,1)} async-done(((bf16[256,512]{1,0:T(8,128)(2,1)}), bf16[1024,512]{1,0:T(8,128)(2,1)}) %all-gather.25.cloned.1.call-update) | async-done | bytes 1048592 | tf_op jit(solution)/shard_map/all_gather | solution.py:21
  697.6 2.7 fusion.80
  700.4 8.4 reduce-scatter.26.cloned.1.call-done
  738.9 33.0 %reduce-scatter.32.cloned.1.call-done = f32[64,512]{1,0:T(8,128)} async-done(((f32[512,512]{1,0:T(8,128)}), f32[64,512]{1,0:T(8,128)}) %reduce-scatter.32.cloned.1.call-update) | async-done | bytes 131088 | tf_op jit(solution)/shard_map/reduce_scatter | solution.py:517
  773.6 2.8 all_gather.40
  777.2 2.6 convolution_convert_fusion.5
  785.6 3.6 fusion.16
  790.3 3.8 convolution_bitcast_fusion
  797.0 24.1 %fusion.81 = f32[2048,1024]{1,0:T(8,128)} fusion(bf16[4096,2048]{1,0:T(8,128)(2,1)} %spread.1, bf16[4096,1024]{1,0:T(8,128)(2,1)} %all-gather.21.cloned.1.call-done), kind=kOutput, calls=%fused_computation.180 | convolution fusion | flops 17179869184 | bytes 33554432 | tf_op jit(solution)/shard_map/dot_general | solution.py:401
  821.1 22.0 %all-gather.29.cloned.1.call-done = bf16[2048,512]{1,0:T(8,128)(2,1)} async-done(((bf16[64,512]{1,0:T(8,128)(2,1)}), bf16[2048,512]{1,0:T(8,128)(2,1)}) %all-gather.29.cloned.1.call-update) | async-done | bytes 2097168 | tf_op jit(solution)/shard_map/all_gather | solution.py:518
  843.1 4.2 convert.53
  847.4 101.9 %all-reduce.4.cloned.1.call-done = (bf16[3,512,256]{1,2,0:T(8,128)(2,1)}, bf16[256,512]{1,0:T(8,128)(2,1)}, bf16[512,1024]{1,0:T(8,128)(2,1)}, bf16[512,256]{1,0:T(8,128)(2,1)}, bf16[256,512]{1,0:T(8,128)(2,1)}) async-done(((bf16[3,512,256]{1,2,0:T(8,128)(2,1)}, bf16[256,512]{1,0:T(8,128)(2,1)}, bf16[512,1024]{1,0:T(8,128)(2,1)}, bf16[512,256]{1,0:T(8,128)(2,1)}, bf16[256,512]{1,0:T(8,128)(2,1)}), ...) | async-done | bytes 2621456 | tf_op jit(solution)/shard_map/psum | solution.py:549
  956.2 2.9 convert_element_type.163
  959.1 27.4 %reduce-scatter.30.cloned.1.call-done = f32[256,512]{1,0:T(8,128)} async-done(((f32[1024,512]{1,0:T(8,128)}), f32[256,512]{1,0:T(8,128)}) %reduce-scatter.30.cloned.1.call-update) | async-done | bytes 524304 | tf_op jit(solution)/shard_map/reduce_scatter | solution.py:37
  990.5 39.7 %all-reduce = (f32[1024]{0:T(1024)}, f32[1024]{0:T(1024)}) all-reduce(f32[1024]{0:T(1024)S(1)} %dynamic_update_slice.6, f32[1024]{0:T(1024)S(1)} %dynamic_update_slice.7), channel_id=1, replica_groups=mesh['dp'=4,'row'=4,'col'=2] {'dp','row','col'}, use_global_device_ids=true, to_apply=%region_31.32 | all-reduce | flops 2048 | bytes 16384 | tf_op jit(solution)/shard_map/psum | solution.py:561
  (239 shorter events, 106.5 us)
Async XLA Ops:
  7.2 165.7 %copy-start = (bf16[4,2,256,512]{3,2,1,0:T(8,128)(2,1)S(1)}, bf16[4,2,256,512]{3,2,1,0:T(8,128)(2,1)}, u32[]{:S(2)}) copy-start(bf16[4,2,256,512]{3,2,1,0:T(8,128)(2,1)} %param.23) | copy-start | bytes 6291460
  7.2 35.7 %all-gather.11.cloned.1.call-start = ((), (), s32[]{:S(2)}) async-start(), calls=%async_computation.14 | async-start | bytes 1310720 | tf_op jit(solution)/shard_map/all_gather | solution.py:21
  11.1 35.9 %copy-start.39 = (f32[256]{0:T(256)}, f32[256]{0:T(256)S(1)}, u32[]{:S(2)}) copy-start(f32[256]{0:T(256)S(1)} %add_rsqrt_fusion.1) | copy-start | bytes 3076
  11.9 35.1 %copy-start.37 = (f32[512]{0:T(512)}, f32[512]{0:T(512)S(1)}, u32[]{:S(2)}) copy-start(f32[512]{0:T(512)S(1)} %dynamic-slice_convert_fusion.1) | copy-start | bytes 6148
  13.7 44.5 %reduce-scatter.12.cloned.1.call-start = ((), (), s32[]{:S(2)}) async-start(), calls=%async_computation.15 | async-start | bytes 4718592 | tf_op jit(solution)/shard_map/reduce_scatter | solution.py:33
  47.0 24.1 %all-gather.13.cloned.1.call-start = ((), (), s32[]{:S(2)}) async-start(), calls=%async_computation.16 | async-start | bytes 1572864 | tf_op jit(solution)/shard_map/all_gather | solution.py:25
  59.7 16.4 %copy-start.19 = (bf16[512,3,256]{2,0,1:T(8,128)(2,1)}, bf16[512,3,256]{2,0,1:T(8,128)(2,1)S(1)}, u32[]{:S(2)}) copy-start(bf16[512,3,256]{2,0,1:T(8,128)(2,1)S(1)} %convert_element_type.131) | copy-start | bytes 2359300
  60.6 60.1 %reduce-scatter.14.cloned.1.call-start = ((), (), s32[]{:S(2)}) async-start(), calls=%async_computation.17 | async-start | bytes 2621440 | tf_op jit(solution)/shard_map/reduce_scatter | solution.py:37
  73.0 4.4 copy-start.7
  74.2 3.9 copy-start.5
  75.6 3.2 copy-start.3
  79.6 2.9 copy-start.32
  82.4 38.3 %copy-start.16 = (bf16[256,512]{1,0:T(8,128)(2,1)S(1)}, bf16[256,512]{1,0:T(8,128)(2,1)}, u32[]{:S(2)}) copy-start(bf16[256,512]{1,0:T(8,128)(2,1)} %param.13) | copy-start | bytes 786436
  84.2 67.7 %all-gather.15.cloned.1.call-start = ((), (), s32[]{:S(2)}) async-start(), calls=%async_computation.18 | async-start | bytes 1310720 | tf_op jit(solution)/shard_map/all_gather | solution.py:21
  125.3 56.7 %reduce-scatter.16.cloned.1.call-start = ((), (), s32[]{:S(2)}) async-start(), calls=%async_computation.19 | async-start | bytes 7864320 | tf_op jit(solution)/shard_map/reduce_scatter | solution.py:33
  157.9 44.6 %all-gather.17.cloned.1.call-start = ((), (), s32[]{:S(2)}) async-start(), calls=%async_computation.22 | async-start | bytes 1310720 | tf_op jit(solution)/shard_map/all_gather | solution.py:21
  168.3 12.0 %all-to-all-start = ((s32[32,4,128]{2,1,0:T(4,128)}), s32[32,4,128]{2,1,0:T(4,128)S(1)}, u32[]{:S(2)}, u32[]{:S(2)}) async-start(s32[32,4,128]{2,1,0:T(4,128)} %copy.46), calls=%async_computation.2 | async-start | bytes 131072 | tf_op jit(solution)/shard_map/all_to_all | solution.py:355
  184.9 17.5 %copy-start.33 = (bf16[256,512]{1,0:T(8,128)(2,1)S(1)}, bf16[256,512]{1,0:T(8,128)(2,1)}, u32[]{:S(2)}) copy-start(bf16[256,512]{1,0:T(8,128)(2,1)} %param.22) | copy-start | bytes 786436
  199.8 9.8 all-to-all-start.1
  202.4 77.8 %reduce-scatter.22.cloned.1.call-start = ((), (), s32[]{:S(2)}) async-start(), calls=%async_computation.23 | async-start | bytes 1572864 | tf_op jit(solution)/shard_map/reduce_scatter | solution.py:33
  205.2 222.1 %reduce-scatter.18.cloned.1.call-start = ((), (), s32[]{:S(2)}) async-start(), calls=%async_computation.20 | async-start | bytes 8650752 | tf_op jit(solution)/shard_map/reduce_scatter | solution.py:397
  280.0 172.2 %all-gather.19.cloned.1.call-start = ((), (), s32[]{:S(2)}) async-start(), calls=%async_computation.24 | async-start | bytes 1310720 | tf_op jit(solution)/shard_map/all_gather | solution.py:399
  429.8 106.1 %all-gather.21.cloned.1.call-start = ((), (), s32[]{:S(2)}) async-start(), calls=%async_computation.25 | async-start | bytes 9437184 | tf_op jit(solution)/shard_map/all_gather | solution.py:400
  587.5 10.5 %all-to-all-start.2 = ((f32[32,4,128]{2,1,0:T(4,128)}), f32[32,4,128]{2,1,0:T(4,128)S(1)}, u32[]{:S(2)}, u32[]{:S(2)}) async-start(f32[32,4,128]{2,1,0:T(4,128)} %copy.55), calls=%async_computation.8 | async-start | bytes 131072 | tf_op jit(solution)/shard_map/all_to_all | solution.py:355
  590.6 31.8 %all-gather.23.cloned.1.call-start = ((), (), s32[]{:S(2)}) async-start(), calls=%async_computation.26 | async-start | bytes 3932160 | tf_op jit(solution)/shard_map/all_gather | solution.py:25
  614.2 11.4 %copy-start.28 = (bf16[512,256]{1,0:T(8,128)(2,1)S(1)}, bf16[512,256]{1,0:T(8,128)(2,1)}, u32[]{:S(2)}) copy-start(bf16[512,256]{1,0:T(8,128)(2,1)} %param.21) | copy-start | bytes 786436
  614.2 50.8 %reduce-scatter.24.cloned.1.call-start = ((), (), s32[]{:S(2)}) async-start(), calls=%async_computation.27 | async-start | bytes 2621440 | tf_op jit(solution)/shard_map/reduce_scatter | solution.py:37
  628.5 40.5 %copy-start.24 = (bf16[256,512]{1,0:T(8,128)(2,1)S(1)}, bf16[256,512]{1,0:T(8,128)(2,1)}, u32[]{:S(2)}) copy-start(bf16[256,512]{1,0:T(8,128)(2,1)} %param.25) | copy-start | bytes 786436
  628.5 69.1 %all-gather.25.cloned.1.call-start = ((), (), s32[]{:S(2)}) async-start(), calls=%async_computation.28 | async-start | bytes 1310720 | tf_op jit(solution)/shard_map/all_gather | solution.py:21
  670.9 37.9 %reduce-scatter.26.cloned.1.call-start = ((), (), s32[]{:S(2)}) async-start(), calls=%async_computation.29 | async-start | bytes 1572864 | tf_op jit(solution)/shard_map/reduce_scatter | solution.py:33
  700.3 36.3 %reduce-scatter.28.cloned.1.call-start = ((), (), s32[]{:S(2)}) async-start(), calls=%async_computation.30 | async-start | bytes 3145728 | tf_op jit(solution)/shard_map/reduce_scatter | solution.py:539
  708.8 3.5 copy-start.4
  710.1 2.8 copy-start.6
  724.9 47.1 %reduce-scatter.32.cloned.1.call-start = ((), (), s32[]{:S(2)}) async-start(), calls=%async_computation.33 | async-start | bytes 1179648 | tf_op jit(solution)/shard_map/reduce_scatter | solution.py:517
  729.6 56.0 %all-gather.27.cloned.1.call-start = ((), (), s32[]{:S(2)}) async-start(), calls=%async_computation.31 | async-start | bytes 2359296 | tf_op jit(solution)/shard_map/all_gather | solution.py:25
  729.7 4.0 copy-start.12
  729.7 5.5 copy-start.14
  738.9 104.2 %all-gather.29.cloned.1.call-start = ((), (), s32[]{:S(2)}) async-start(), calls=%async_computation.34 | async-start | bytes 2162688 | tf_op jit(solution)/shard_map/all_gather | solution.py:518
  773.6 175.8 %all-reduce.4.cloned.1.call-start = ((), (), s32[]{:S(2)}) async-start(), calls=%async_computation.35 | async-start | bytes 5242880 | tf_op jit(solution)/shard_map/psum | solution.py:549
  773.6 6.2 copy-start.31
  777.2 5.0 copy-start.36
  789.2 197.3 %reduce-scatter.30.cloned.1.call-start = ((), (), s32[]{:S(2)}) async-start(), calls=%async_computation.32 | async-start | bytes 2621440 | tf_op jit(solution)/shard_map/reduce_scatter | solution.py:37
  794.1 236.1 %reduce-scatter.20.cloned.1.call-start = ((), (), s32[]{:S(2)}) async-start(), calls=%async_computation.21 | async-start | bytes 2621440 | tf_op jit(solution)/shard_map/reduce_scatter | solution.py:37
  949.3 5.5 copy-start.35
  956.2 30.3 %copy-start.17 = (bf16[256,512]{1,0:T(8,128)(2,1)S(1)}, bf16[256,512]{1,0:T(8,128)(2,1)}, u32[]{:S(2)}) copy-start(bf16[256,512]{1,0:T(8,128)(2,1)} %param.13) | copy-start | bytes 786436
  956.2 30.3 %copy-start.38 = (f32[512]{0:T(512)S(1)}, f32[512]{0:T(512)}, u32[]{:S(2)}) copy-start(f32[512]{0:T(512)} %copy-done.37) | copy-start | bytes 6148
  956.2 30.3 %copy-start.40 = (f32[256]{0:T(256)S(1)}, f32[256]{0:T(256)}, u32[]{:S(2)}) copy-start(f32[256]{0:T(256)} %copy-done.39) | copy-start | bytes 3076
  956.2 74.0 %copy-start.18 = (f32[256,512]{1,0:T(8,128)S(1)}, f32[256,512]{1,0:T(8,128)}, u32[]{:S(2)}) copy-start(f32[256,512]{1,0:T(8,128)} %reduce-scatter.24.cloned.1.call-done) | copy-start | bytes 1572868
  (20 other events, 30.4 us)
Sparse Core Ops, SparseCore 0:
  13.8 29.0 all-gather.10
  47.1 10.9 reduce-scatter.11
  60.7 10.2 all-gather.12
  84.4 36.3 reduce-scatter.13
  125.4 26.4 all-gather.14
  158.0 13.0 reduce-scatter.15
  173.0 27.7 all-gather.16
  206.0 9.6 reduce-scatter.21
  280.1 147.1 reduce-scatter.17
  429.9 22.2 all-gather.18
  453.8 82.0 all-gather.20
  614.3 8.0 all-gather.22
  628.6 36.3 reduce-scatter.23
  671.1 26.5 all-gather.24
  700.4 8.3 reduce-scatter.25
  725.0 10.8 reduce-scatter.27
  738.0 33.8 reduce-scatter.31
  774.0 7.9 all-gather.26
  785.5 57.5 all-gather.28
  846.2 103.0 all-reduce.3
  952.3 34.1 reduce-scatter.29
  989.4 35.5 reduce-scatter.19

commit v2 on v1

--- a/solution.py
+++ b/solution.py
@@ -4,6 +4,7 @@
 import jax.numpy as jnp
 from jax import lax
 from jax.experimental import pallas as pl
+from jax.experimental.pallas import tpu as pltpu
 from jax.sharding import PartitionSpec as P
 
 D = 1024
@@ -17,108 +18,500 @@
 EPSILON = 1e-06
 
 
-def row_gather(operand):
-    return lax.all_gather(operand, "row", axis=0, tiled=True)
-
-
-def col_gather(operand):
-    return lax.all_gather(operand, "col", axis=0, tiled=True)
-
-
-def feature_total(operand):
-    return lax.psum(operand, "col")
-
-
-def col_reduce(gathered, product):
-    return lax.psum_scatter(product(gathered), "col", scatter_dimension=0, tiled=True)
-
-
-def row_reduce(gathered, product):
-    return lax.psum_scatter(product(gathered), "row", scatter_dimension=0, tiled=True)
-
-
-def norm_forward(residual, gain_slice):
-    sum_squares = feature_total(jnp.sum(residual * residual, axis=1))
-    inv_scale = lax.rsqrt(sum_squares / D + EPSILON)
-    unit_rows = residual * inv_scale[:, None]
-    return (unit_rows, inv_scale, (unit_rows * gain_slice).astype(jnp.bfloat16))
-
-
-def norm_backward(grad_normed, unit_rows, inv_scale, gain_slice):
-    grad_unit = grad_normed * gain_slice
-    inner_mean = feature_total(jnp.sum(grad_unit * unit_rows, axis=1)) / D
-    grad_input = inv_scale[:, None] * (grad_unit - unit_rows * inner_mean[:, None])
-    return (grad_input, jnp.sum(grad_normed * unit_rows, axis=0))
+MESH = pl.DeviceIdType.MESH
+VMEM = pl.BlockSpec(memory_space=pltpu.VMEM)
+ANY = pl.BlockSpec(memory_space=pl.ANY)
+DMA = pltpu.SemaphoreType.DMA
+
+
+def here():
+    return lax.axis_index("dp"), lax.axis_index("row"), lax.axis_index("col")
+
+
+def grid_sizes():
+    return lax.axis_size("dp"), lax.axis_size("row"), lax.axis_size("col")
+
+
+def remote(src, dst, send_sem, recv_sem, device):
+    return pltpu.make_async_remote_copy(
+        src_ref=src,
+        dst_ref=dst,
+        send_sem=send_sem,
+        recv_sem=recv_sem,
+        device_id=device,
+        device_id_type=MESH,
+    )
+
+
+def arrived(dst, sem):
+    pltpu.make_async_copy(dst, dst, sem).wait()
+
+
+def greet_plane(spot, sizes):
+    barrier = pltpu.get_barrier_semaphore()
+    dp, row, col = spot
+    _, rows, cols = sizes
+    for j in range(rows):
+        for k in range(cols):
+            if j + k > 0:
+                pl.semaphore_signal(
+                    barrier,
+                    inc=1,
+                    device_id=(dp, lax.rem(row + j, rows), lax.rem(col + k, cols)),
+                    device_id_type=MESH,
+                )
+    pl.semaphore_wait(barrier, rows * cols - 1)
+
+
+def greet_partner(spot, sizes):
+    barrier = pltpu.get_barrier_semaphore()
+    dp, row, col = spot
+    pl.semaphore_signal(barrier, inc=1, device_id=(dp, row, 1 - col), device_id_type=MESH)
+    pl.semaphore_wait(barrier, 1)
+
+
+def device_of(index, sizes):
+    _, rows, cols = sizes
+    return (
+        lax.div(index, rows * cols),
+        lax.rem(lax.div(index, cols), rows),
+        lax.rem(index, cols),
+    )
+
+
+def index_of(spot, sizes):
+    return (spot[0] * sizes[1] + spot[1]) * sizes[2] + spot[2]
+
+
+def greet_all(spot, sizes):
+    barrier = pltpu.get_barrier_semaphore()
+    count = sizes[0] * sizes[1] * sizes[2]
+    me = index_of(spot, sizes)
+
+    def greet(step, carry):
+        pl.semaphore_signal(
+            barrier,
+            inc=1,
+            device_id=device_of(lax.rem(me + step, count), sizes),
+            device_id_type=MESH,
+        )
+        return carry
+
+    lax.fori_loop(1, count, greet, 0)
+    pl.semaphore_wait(barrier, count - 1)
+
+
+class Gather:
+    def __init__(self, spot, sizes, src, dst, send, recv):
+        self.spot, self.sizes, self.src, self.dst = spot, sizes, src, dst
+        self.send, self.recv = send, recv
+        self.tokens, self.width = src.shape
+        dp, row, col = spot
+        _, rows, cols = sizes
+        self.half = rows // cols
+        self.target = lax.div(row, self.half)
+        self.slot = lax.rem(row, self.half) * cols + col
+        first = pl.multiple_of(lax.rem(row, self.half) * self.tokens, self.tokens)
+        left = pl.multiple_of(col * self.width, self.width)
+        self.there = dst.at[pl.ds(first, self.tokens), pl.ds(left, self.width)]
+
+    def copy(self, step):
+        dp, row, _ = self.spot
+        device = (dp, lax.rem(row + step, self.sizes[1]), self.target)
+        return remote(self.src, self.there, self.send.at[step], self.recv.at[self.slot], device)
+
+    def start(self):
+        col = self.spot[2]
+
+        for step in range(1, self.sizes[1]):
+            self.copy(step).start()
+
+        @pl.when(self.target == col)
+        def _():
+            pltpu.make_async_copy(self.src, self.there, self.recv.at[self.slot]).start()
+
+        @pl.when(self.target != col)
+        def _():
+            self.copy(0).start()
+
+    def wait(self):
+        cols = self.sizes[2]
+        for i in range(self.half):
+            for k in range(cols):
+                arrived(
+                    self.dst.at[pl.ds(i * self.tokens, self.tokens), pl.ds(k * self.width, self.width)],
+                    self.recv.at[i * cols + k],
+                )
+        for step in range(1, self.sizes[1]):
+            self.copy(step).wait_send()
+
+        @pl.when(self.target != self.spot[2])
+        def _():
+            self.copy(0).wait_send()
+
+
+class Scatter:
+    def __init__(self, spot, sizes, src, landing, send, recv):
+        self.spot, self.sizes, self.src, self.landing = spot, sizes, src, landing
+        self.send, self.recv = send, recv
+        _, self.tokens, self.width = landing.shape
+        self.half = sizes[1] // sizes[2]
+
+    def parts(self):
+        dp, row, col = self.spot
+        cols = self.sizes[2]
+        for i in range(self.half):
+            for k in range(cols):
+                piece = self.src.at[
+                    pl.ds(i * self.tokens, self.tokens), pl.ds(k * self.width, self.width)
+                ]
+                target = col * self.half + i
+                mine = jnp.logical_and(target == row, col == k)
+                there = self.landing.at[row]
+                copy = remote(
+                    piece, there, self.send.at[i * cols + k], self.recv.at[row], (dp, target, k)
+                )
+                yield mine, copy, pltpu.make_async_copy(piece, there, self.recv.at[row])
+
+    def start(self):
+        for mine, copy, own in self.parts():
+            pl.when(jnp.logical_not(mine))(copy.start)
+            pl.when(mine)(own.start)
+
+    def wait(self):
+        for q in range(self.sizes[1]):
+            arrived(self.landing.at[q], self.recv.at[q])
+
+    def wait_send(self):
+        for mine, copy, _ in self.parts():
+            pl.when(jnp.logical_not(mine))(copy.wait_send)
+
+
+def plane_sems(sizes):
+    rows, cols = sizes[1], sizes[2]
+    return [DMA((rows,)), DMA((rows,))]
+
+
+def start_kernel(sizes, *refs):
+    x, dy, wqkv, wquery, wgate, wproj, wattn = refs[:7]
+    xs, dys, wqkv_all, wquery_all, wgate_all, wproj_all, wattn_all = refs[7:14]
+    xsend, xrecv, ysend, yrecv, wsend, wrecv, wlocal = refs[14:]
+    spot = here()
+    dp, row, col = spot
+    greet_plane(spot, sizes)
+    gather_x = Gather(spot, sizes, x, xs, xsend, xrecv)
+    gather_y = Gather(spot, sizes, dy, dys, ysend, yrecv)
+    gather_x.start()
+    gather_y.start()
+    copies = []
+    for n, (src, dst, dim) in enumerate(
+        (
+            (wqkv, wqkv_all, 1),
+            (wquery, wquery_all, 0),
+            (wgate, wgate_all, 0),
+            (wproj, wproj_all, 1),
+            (wattn, wattn_all, 1),
+        )
+    ):
+        size = src.shape[dim]
+        window = [slice(None)] * len(src.shape)
+        window[dim] = pl.ds(pl.multiple_of(col * size, size), size)
+        there = dst.at[tuple(window)]
+        away = remote(src, there, wsend.at[n], wrecv.at[n], (dp, row, 1 - col))
+        own = pltpu.make_async_copy(src, there, wlocal.at[n])
+        away.start()
+        own.start()
+        copies += [away, own]
+    for copy in copies:
+        copy.wait()
+    gather_x.wait()
+    gather_y.wait()
+
+
+def start_all(sizes, x, dy, wqkv, wquery, wgate, wproj, wattn):
+    tokens, width = x.shape
+    half = sizes[1] // sizes[2]
+    cols = sizes[2]
+    low = jnp.bfloat16
+
+    def twice(operand, dim):
+        shape = list(operand.shape)
+        shape[dim] *= cols
+        return jax.ShapeDtypeStruct(tuple(shape), low)
+
+    whole = jax.ShapeDtypeStruct((half * tokens, cols * width), low)
+    return pl.pallas_call(
+        functools.partial(start_kernel, sizes),
+        in_specs=[VMEM] * 7,
+        out_specs=[ANY] * 7,
+        out_shape=[
+            whole,
+            whole,
+            twice(wqkv, 1),
+            twice(wquery, 0),
+            twice(wgate, 0),
+            twice(wproj, 1),
+            twice(wattn, 1),
+        ],
+        scratch_shapes=plane_sems(sizes) * 2 + [DMA((5,))] * 3,
+        compiler_params=pltpu.CompilerParams(collective_id=0, has_side_effects=True),
+        name="start_all",
+    )(x, dy, wqkv, wquery, wgate, wproj, wattn)
+
+
+def swap_kernel(sizes, src, dst, send, recv, own):
+    spot = here()
+    dp, row, col = spot
+    greet_partner(spot, sizes)
+    size = src.shape[1]
+    there = dst.at[:, pl.ds(pl.multiple_of(col * size, size), size)]
+    away = remote(src, there, send, recv, (dp, row, 1 - col))
+    local = pltpu.make_async_copy(src, there, own)
+    away.start()
+    local.start()
+    away.wait()
+    local.wait()
+
+
+def swap_tokens(sizes, src):
+    shape = (src.shape[0], src.shape[1] * sizes[2], src.shape[2])
+    return pl.pallas_call(
+        functools.partial(swap_kernel, sizes),
+        in_specs=[VMEM],
+        out_specs=VMEM,
+        out_shape=jax.ShapeDtypeStruct(shape, src.dtype),
+        scratch_shapes=[DMA, DMA, DMA],
+        compiler_params=pltpu.CompilerParams(collective_id=1, has_side_effects=True),
+        name="swap_tokens",
+    )(src)
+
+
+def pair_sum_kernel(sizes, src, out, landing, send, recv):
+    spot = here()
+    dp, row, col = spot
+    greet_partner(spot, sizes)
+    size = landing.shape[1]
+    other = pl.multiple_of((1 - col) * size, size)
+    away = remote(src.at[:, pl.ds(other, size)], landing, send, recv, (dp, row, 1 - col))
+    away.start()
+    away.wait()
+    own = src[:, pl.ds(pl.multiple_of(col * size, size), size)]
+    out[...] = (own + landing[...]).astype(out.dtype)
+
+
+def pair_sum(sizes, src):
+    shape = (src.shape[0], src.shape[1] // sizes[2], src.shape[2])
+    return pl.pallas_call(
+        functools.partial(pair_sum_kernel, sizes),
+        in_specs=[VMEM],
+        out_specs=VMEM,
+        out_shape=jax.ShapeDtypeStruct(shape, jnp.bfloat16),
+        scratch_shapes=[pltpu.VMEM(shape, src.dtype), DMA, DMA],
+        compiler_params=pltpu.CompilerParams(collective_id=2, has_side_effects=True),
+        name="pair_sum",
+    )(src)
+
+
+def fold(column):
+    return jnp.broadcast_to(column, (column.shape[0], 128))
+
+
+def join_kernel(
+    sizes, part, x, gain, hidden, normed_all, landing, mine, theirs, block,
+    ssend, srecv, gsend, grecv, psend, precv,
+):
+    spot = here()
+    dp, row, col = spot
+    greet_plane(spot, sizes)
+    scatter = Scatter(spot, sizes, part, landing, ssend, srecv)
+    scatter.start()
+    scatter.wait()
+    total = x[...].astype(jnp.float32)
+    for q in range(sizes[1]):
+        total = total + landing[q].astype(jnp.float32)
+    hidden[...] = total
+    mine[...] = fold(jnp.sum(total * total, axis=1, keepdims=True))
+    pair = remote(mine, theirs, psend, precv, (dp, row, 1 - col))
+    pair.start()
+    pair.wait()
+    squares = mine[:, :1] + theirs[:, :1]
+    scale = lax.rsqrt(squares / D + EPSILON)
+    block[...] = (hidden[...] * scale * gain[...].astype(jnp.float32)).astype(jnp.bfloat16)
+    gather = Gather(spot, sizes, block, normed_all, gsend, grecv)
+    gather.start()
+    scatter.wait_send()
+    gather.wait()
+
+
+def join(sizes, part, x, gain):
+    tokens, width = x.shape
+    rows = sizes[1]
+    return pl.pallas_call(
+        functools.partial(join_kernel, sizes),
+        in_specs=[VMEM] * 3,
+        out_specs=[VMEM, VMEM],
+        out_shape=[
+            jax.ShapeDtypeStruct((tokens, width), jnp.float32),
+            jax.ShapeDtypeStruct(part.shape, jnp.bfloat16),
+        ],
+        scratch_shapes=[
+            pltpu.VMEM((rows, tokens, width), jnp.bfloat16),
+            pltpu.VMEM((tokens, 128), jnp.float32),
+            pltpu.VMEM((tokens, 128), jnp.float32),
+            pltpu.VMEM((tokens, width), jnp.bfloat16),
+        ]
+        + plane_sems(sizes) * 2
+        + [DMA, DMA],
+        compiler_params=pltpu.CompilerParams(collective_id=3, has_side_effects=True),
+        name="join",
+    )(part, x, gain[None])
+
+
+def norm_back(sizes, spot, landing, base, above, gain, mine, theirs, psend, precv):
+    dp, row, col = spot
+    normed_grad = landing[0].astype(jnp.float32)
+    for q in range(1, sizes[1]):
+        normed_grad = normed_grad + landing[q].astype(jnp.float32)
+    values = base[...].astype(jnp.float32)
+    unit_grad = normed_grad * gain[...].astype(jnp.float32)
+    mine[0] = fold(jnp.sum(values * values, axis=1, keepdims=True))
+    mine[1] = fold(jnp.sum(unit_grad * values, axis=1, keepdims=True))
+    pair = remote(mine, theirs, psend, precv, (dp, row, 1 - col))
+    pair.start()
+    pair.wait()
+    scale = lax.rsqrt((mine[0, :, :1] + theirs[0, :, :1]) / D + EPSILON)
+    inner = scale * (mine[1, :, :1] + theirs[1, :, :1]) / D
+    unit = values * scale
+    grad = above[...].astype(jnp.float32) + scale * (unit_grad - unit * inner)
+    return grad, jnp.sum(normed_grad * unit, axis=0, keepdims=True)
+
+
+def middle_kernel(
+    sizes, part, out_part, hidden, dy, gain, output, grad, grad_all, gain_grad,
+    landing, out_landing, mine, theirs, block, ssend, srecv, osend, orecv, gsend, grecv, psend, precv,
+):
+    spot = here()
+    greet_plane(spot, sizes)
+    scatter = Scatter(spot, sizes, part, landing, ssend, srecv)
+    scatter.start()
+    out_scatter = Scatter(spot, sizes, out_part, out_landing, osend, orecv)
+    out_scatter.start()
+    scatter.wait()
+    total, gains = norm_back(sizes, spot, landing, hidden, dy, gain, mine, theirs, psend, precv)
+    gain_grad[...] = gains
+    grad[...] = total
+    block[...] = total.astype(jnp.bfloat16)
+    gather = Gather(spot, sizes, block, grad_all, gsend, grecv)
+    gather.start()
+    out_scatter.wait()
+    result = hidden[...]
+    for q in range(sizes[1]):
+        result = result + out_landing[q].astype(jnp.float32)
+    output[...] = result.astype(jnp.bfloat16)
+    scatter.wait_send()
+    out_scatter.wait_send()
+    gather.wait()
+
+
+def middle(sizes, part, out_part, hidden, dy, gain):
+    tokens, width = hidden.shape
+    rows = sizes[1]
+    low, wide = jnp.bfloat16, jnp.float32
+    return pl.pallas_call(
+        functools.partial(middle_kernel, sizes),
+        in_specs=[VMEM] * 5,
+        out_specs=[VMEM] * 4,
+        out_shape=[
+            jax.ShapeDtypeStruct((tokens, width), low),
+            jax.ShapeDtypeStruct((tokens, width), wide),
+            jax.ShapeDtypeStruct(part.shape, low),
+            jax.ShapeDtypeStruct((1, width), wide),
+        ],
+        scratch_shapes=[
+            pltpu.VMEM((rows, tokens, width), low),
+            pltpu.VMEM((rows, tokens, width), low),
+            pltpu.VMEM((2, tokens, 128), wide),
+            pltpu.VMEM((2, tokens, 128), wide),
+            pltpu.VMEM((tokens, width), low),
+        ]
+        + plane_sems(sizes) * 3
+        + [DMA, DMA],
+        compiler_params=pltpu.CompilerParams(collective_id=4, has_side_effects=True),
+        name="middle",
+    )(part, out_part, hidden, dy, gain[None])
+
+
+def last_kernel(
+    sizes, part, x, above, gain, other_gain, grad, gain_sums,
+    landing, mine, theirs, own_gain, gain_landing, ssend, srecv, psend, precv, bsend, brecv,
+):
+    spot = here()
+    count = sizes[0] * sizes[1] * sizes[2]
+    me = index_of(spot, sizes)
+    greet_all(spot, sizes)
+    scatter = Scatter(spot, sizes, part, landing, ssend, srecv)
+    scatter.start()
+    scatter.wait()
+    total, gains = norm_back(sizes, spot, landing, x, above, gain, mine, theirs, psend, precv)
+    lines = gains.shape[1] // 128
+    for line in range(lines):
+        columns = slice(line * 128, (line + 1) * 128)
+        own_gain[line : line + 1] = gains[:, columns]
+        own_gain[lines + line : lines + line + 1] = other_gain[:, columns]
+
+    def tell(step, carry):
+        device = device_of(lax.rem(me + step, count), sizes)
+        remote(own_gain, gain_landing.at[me], bsend, brecv, device).start()
+        return carry
+
+    lax.fori_loop(1, count, tell, 0)
+    gain_landing[me] = own_gain[...]
+    grad[...] = total
+    scatter.wait_send()
+    arrived(gain_landing.at[pl.ds(0, count - 1)], brecv)
+    for col in range(sizes[2]):
+
+        def add(index, sums):
+            return sums + gain_landing[index * sizes[2] + col]
+
+        gain_sums[col] = lax.fori_loop(
+            0, sizes[0] * sizes[1], add, jnp.zeros(own_gain.shape, jnp.float32)
+        )
+    arrived(gain_landing.at[pl.ds(0, count - 1)], bsend)
+
+
+def last(sizes, part, x, above, gain, other_gain):
+    tokens, width = x.shape
+    rows = sizes[1]
+    lines = 2 * width // 128
+    count = sizes[0] * sizes[1] * sizes[2]
+    wide = jnp.float32
+    return pl.pallas_call(
+        functools.partial(last_kernel, sizes),
+        in_specs=[VMEM] * 5,
+        out_specs=[VMEM] * 2,
+        out_shape=[
+            jax.ShapeDtypeStruct((tokens, width), wide),
+            jax.ShapeDtypeStruct((sizes[2], lines, 128), wide),
+        ],
+        scratch_shapes=[
+            pltpu.VMEM((rows, tokens, width), jnp.bfloat16),
+            pltpu.VMEM((2, tokens, 128), wide),
+            pltpu.VMEM((2, tokens, 128), wide),
+            pltpu.VMEM((lines, 128), wide),
+            pltpu.VMEM((count, lines, 128), wide),
+        ]
+        + plane_sems(sizes)
+        + [DMA, DMA, DMA, DMA],
+        compiler_params=pltpu.CompilerParams(collective_id=5, has_side_effects=True),
+        name="last",
+    )(part, x, above, gain[None], other_gain)
 
 
 def allowed_mask(query_count, key_count, first_pos, prefix_len):
     query_pos = first_pos + lax.iota(jnp.int32, query_count)
     key_pos = lax.iota(jnp.int32, key_count)
     return (key_pos[None, :] <= query_pos[:, None]) | (key_pos[None, :] < prefix_len)
-
-
-def head_scores(query_head, key_head, allowed):
-    raw_scores = jnp.einsum(
-        "qd,kd->qk", query_head, key_head, preferred_element_type=jnp.float32
-    ) * HDIM ** (-0.5)
-    return jnp.where(allowed, raw_scores, -jnp.inf)
-
-
-def attend_forward(own_qkv, kv_rows, allowed):
-    head_count = own_qkv.shape[2] // HDIM
-    outputs = []
-    log_sums = []
-    for head_index in range(head_count):
-        columns = slice(head_index * HDIM, (head_index + 1) * HDIM)
-        scores = head_scores(own_qkv[:, 0, columns], kv_rows[:, 0, columns], allowed)
-        peak_score = jnp.max(scores, axis=1, keepdims=True)
-        exp_scores = jnp.exp(scores - peak_score)
-        row_sum = jnp.sum(exp_scores, axis=1, keepdims=True)
-        probabilities = (exp_scores / row_sum).astype(jnp.bfloat16)
-        outputs.append(
-            jnp.dot(probabilities, kv_rows[:, 1, columns], preferred_element_type=jnp.float32)
-        )
-        log_sums.append(peak_score[:, 0] + jnp.log(row_sum[:, 0]))
-    return (jnp.concatenate(outputs, axis=1), jnp.stack(log_sums))
-
-
-def attend_backward(own_qkv, kv_rows, allowed, log_sums, grad_out):
-    head_count = own_qkv.shape[2] // HDIM
-    grad_queries = []
-    grad_keys = []
-    grad_values = []
-    for head_index in range(head_count):
-        columns = slice(head_index * HDIM, (head_index + 1) * HDIM)
-        query_head = own_qkv[:, 0, columns]
-        key_head = kv_rows[:, 0, columns]
-        value_head = kv_rows[:, 1, columns]
-        grad_head = grad_out[:, columns]
-        scores = head_scores(query_head, key_head, allowed)
-        probabilities = jnp.exp(scores - log_sums[head_index][:, None])
-        grad_probs = jnp.einsum(
-            "qd,kd->qk", grad_head, value_head, preferred_element_type=jnp.float32
-        )
-        inner_sum = jnp.sum(probabilities * grad_probs, axis=1, keepdims=True)
-        grad_scores = (probabilities * (grad_probs - inner_sum)).astype(jnp.bfloat16)
-        grad_queries.append(
-            jnp.dot(grad_scores, key_head, preferred_element_type=jnp.float32) * HDIM ** (-0.5)
-        )
-        grad_keys.append(
-            jnp.einsum("qk,qd->kd", grad_scores, query_head, preferred_element_type=jnp.float32)
-            * HDIM ** (-0.5)
-        )
-        grad_values.append(
-            jnp.einsum(
-                "qk,qd->kd",
-                probabilities.astype(jnp.bfloat16),
-                grad_head,
-                preferred_element_type=jnp.float32,
-            )
-        )
-    stacked = jnp.stack(
-        [jnp.concatenate(grad_keys, axis=1), jnp.concatenate(grad_values, axis=1)], axis=1
-    )
-    return (jnp.concatenate(grad_queries, axis=1), stacked)
 
 
 def flat_picks(picks_head):
@@ -427,6 +820,78 @@
     return memory, grad_query, grad_values, grad_keys
 
 
+def head_scores(query_head, key_head, allowed):
+    raw_scores = jnp.einsum(
+        "qd,kd->qk", query_head, key_head, preferred_element_type=jnp.float32
+    ) * HDIM ** (-0.5)
+    return jnp.where(allowed, raw_scores, -jnp.inf)
+
+
+def attend_forward(queries, keys, values, allowed):
+    outputs = []
+    log_sums = []
+    for head_index in range(queries.shape[1] // HDIM):
+        columns = slice(head_index * HDIM, (head_index + 1) * HDIM)
+        scores = head_scores(queries[:, columns], keys[:, columns], allowed)
+        peak_score = jnp.max(scores, axis=1, keepdims=True)
+        exp_scores = jnp.exp(scores - peak_score)
+        row_sum = jnp.sum(exp_scores, axis=1, keepdims=True)
+        probabilities = (exp_scores / row_sum).astype(jnp.bfloat16)
+        outputs.append(
+            jnp.dot(probabilities, values[:, columns], preferred_element_type=jnp.float32)
+        )
+        log_sums.append(peak_score[:, 0] + jnp.log(row_sum[:, 0]))
+    return (jnp.concatenate(outputs, axis=1), jnp.stack(log_sums))
+
+
+def attend_backward(queries, keys, values, allowed, log_sums, grad_out):
+    grad_queries = []
+    grad_keys = []
+    grad_values = []
+    for head_index in range(queries.shape[1] // HDIM):
+        columns = slice(head_index * HDIM, (head_index + 1) * HDIM)
+        query_head = queries[:, columns]
+        key_head = keys[:, columns]
+        value_head = values[:, columns]
+        grad_head = grad_out[:, columns]
+        scores = head_scores(query_head, key_head, allowed)
+        probabilities = jnp.exp(scores - log_sums[head_index][:, None])
+        grad_probs = jnp.einsum(
+            "qd,kd->qk", grad_head, value_head, preferred_element_type=jnp.float32
+        )
+        inner_sum = jnp.sum(probabilities * grad_probs, axis=1, keepdims=True)
+        grad_scores = (probabilities * (grad_probs - inner_sum)).astype(jnp.bfloat16)
+        grad_queries.append(
+            jnp.dot(grad_scores, key_head, preferred_element_type=jnp.float32) * HDIM ** (-0.5)
+        )
+        grad_keys.append(
+            jnp.einsum("qk,qd->kd", grad_scores, query_head, preferred_element_type=jnp.float32)
+            * HDIM ** (-0.5)
+        )
+        grad_values.append(
+            jnp.einsum(
+                "qk,qd->kd",
+                probabilities.astype(jnp.bfloat16),
+                grad_head,
+                preferred_element_type=jnp.float32,
+            )
+        )
+    stacked = jnp.stack([jnp.concatenate(grad_keys, axis=1), jnp.concatenate(grad_values, axis=1)])
+    return (jnp.concatenate(grad_queries, axis=1), stacked)
+
+
+def dense(left, right):
+    return jnp.dot(left, right, preferred_element_type=jnp.float32)
+
+
+def dense_nt(left, right):
+    return lax.dot_general(left, right, (((1,), (1,)), ((), ())), preferred_element_type=jnp.float32)
+
+
+def dense_tn(left, right):
+    return lax.dot_general(left, right, (((0,), (0,)), ((), ())), preferred_element_type=jnp.float32)
+
+
 def per_device(
     inputs,
     prefix,
@@ -442,133 +907,91 @@
     values,
     cotangent,
 ):
+    low = jnp.bfloat16
+    sizes = grid_sizes()
     width_part = inputs.shape[1]
     own_tokens = picks.shape[0]
-    seq_tokens = own_tokens * lax.axis_size("col")
-    query_width = w_query.shape[1]
-    col_first = lax.axis_index("col") * width_part
-    gain_one = lax.dynamic_slice_in_dim(gain_attn, col_first, width_part).astype(jnp.float32)
-    gain_two = lax.dynamic_slice_in_dim(gain_mem, col_first, width_part).astype(jnp.float32)
-
-    def project_qkv(piece_rows):
-        return jnp.einsum("tc,jcf->tjf", piece_rows, w_qkv, preferred_element_type=jnp.float32)
-
-    def proj_attn(piece_rows):
-        return jnp.dot(piece_rows, w_attn_out, preferred_element_type=jnp.float32)
-
-    def project_memory(piece_rows):
-        return jnp.concatenate(
-            [
-                jnp.dot(piece_rows, w_query, preferred_element_type=jnp.float32),
-                jnp.dot(piece_rows, w_gate, preferred_element_type=jnp.float32),
-            ],
-            axis=1,
-        )
-
-    def proj_mem(piece_rows):
-        return jnp.dot(piece_rows, w_proj, preferred_element_type=jnp.float32)
-
-    def back_proj(piece_rows):
-        return jnp.einsum("tc,fc->tf", piece_rows, w_proj, preferred_element_type=jnp.float32)
-
-    def back_memory_in(piece_rows):
-        return jnp.einsum(
-            "tq,cq->tc", piece_rows[:, :query_width], w_query, preferred_element_type=jnp.float32
-        ) + jnp.einsum(
-            "tf,cf->tc", piece_rows[:, query_width:], w_gate, preferred_element_type=jnp.float32
-        )
-
-    def back_attn(piece_rows):
-        return jnp.einsum("tc,fc->tf", piece_rows, w_attn_out, preferred_element_type=jnp.float32)
-
-    def back_qkv(piece_rows):
-        return jnp.einsum("tjf,jcf->tc", piece_rows, w_qkv, preferred_element_type=jnp.float32)
-
-    residual = inputs.astype(jnp.float32)
-    unit_one, scale_one, normed_one = norm_forward(residual, gain_one)
-    gathered_one = row_gather(normed_one)
-    own_qkv = col_reduce(gathered_one, project_qkv).astype(jnp.bfloat16)
-    kv_rows = col_gather(own_qkv[:, 1:])
-    allowed = allowed_mask(own_tokens, seq_tokens, lax.axis_index("col") * own_tokens, prefix[0])
-    attended_sum, log_sums = attend_forward(own_qkv, kv_rows, allowed)
-    attended = attended_sum.astype(jnp.bfloat16)
-    attended_all = col_gather(attended)
-    hidden = residual + row_reduce(attended_all, proj_attn)
-    unit_two, scale_two, normed_two = norm_forward(hidden, gain_two)
-    gathered_two = row_gather(normed_two)
-    mixed_sum = col_reduce(gathered_two, project_memory)
-    query_rows = mixed_sum[:, :query_width].astype(jnp.bfloat16)
-    gate_value = mixed_sum[:, query_width:]
+    seq_tokens = own_tokens * sizes[2]
+    col = lax.axis_index("col")
+    col_first = col * width_part
+    gain_one = lax.dynamic_slice_in_dim(gain_attn, col_first, width_part)
+    gain_two = lax.dynamic_slice_in_dim(gain_mem, col_first, width_part)
+
+    x_own, dy_own, qkv_w, query_w, gate_w, proj_w, attn_w = start_all(
+        sizes, inputs, cotangent, w_qkv, w_query, w_gate, w_proj, w_attn_out
+    )
+    residual = x_own.astype(jnp.float32)
+    scale_one = lax.rsqrt(jnp.sum(residual * residual, axis=1, keepdims=True) / D + EPSILON)
+    normed_one = (residual * scale_one * gain_attn.astype(jnp.float32)).astype(low)
+    qkv = jnp.einsum("tc,jcf->jtf", normed_one, qkv_w, preferred_element_type=jnp.float32).astype(low)
+    kv_all = swap_tokens(sizes, qkv[1:])
+    allowed = allowed_mask(own_tokens, seq_tokens, col * own_tokens, prefix[0])
+    attended_sum, log_sums = attend_forward(qkv[0], kv_all[0], kv_all[1], allowed)
+    attended = attended_sum.astype(low)
+    hidden, normed_two = join(sizes, dense(attended, attn_w).astype(low), inputs, gain_two)
+    query_rows = dense(normed_two, query_w).astype(low)
+    gate_value = dense(normed_two, gate_w)
     sigmoid_gate = jax.nn.sigmoid(gate_value)
     silu_gate = gate_value * sigmoid_gate
-    grad_rows = row_gather(cotangent)
-    grad_gated = col_reduce(grad_rows, back_proj)
-    grad_memory = (grad_gated * silu_gate).astype(jnp.bfloat16)
+    grad_gated = dense_nt(dy_own, proj_w)
+    grad_memory = (grad_gated * silu_gate).astype(low)
     memory, grad_query, grad_values, grad_keys = memory_all(
         query_rows, grad_memory, picks, subkeys, values
     )
-    gated_value = (memory * silu_gate).astype(jnp.bfloat16)
-    gated_all = col_gather(gated_value)
-    output = (hidden + row_reduce(gated_all, proj_mem)).astype(jnp.bfloat16)
-    grad_w_proj = jnp.einsum("tf,tc->fc", gated_all, grad_rows, preferred_element_type=jnp.float32)
+    gated_value = (memory * silu_gate).astype(low)
+    out_part = dense(gated_value, proj_w).astype(low)
     grad_gate = (
         grad_gated * memory * sigmoid_gate * (1.0 + gate_value * (1.0 - sigmoid_gate))
-    ).astype(jnp.bfloat16)
-    grad_keys = lax.psum_scatter(grad_keys.reshape(-1, HALF), ("dp", "col"), scatter_dimension=0, tiled=True)
-    grad_subkeys = lax.all_gather(
-        grad_keys.astype(jnp.bfloat16), ("row", "dp", "col"), axis=0, tiled=True
-    ).astype(jnp.float32).reshape(subkeys.shape)
-    grad_mixed = col_gather(jnp.concatenate([grad_query, grad_gate], axis=1))
-    grad_w_query = jnp.einsum(
-        "tc,tq->cq", gathered_two, grad_mixed[:, :query_width], preferred_element_type=jnp.float32
-    )
-    grad_w_gate = jnp.einsum(
-        "tc,tf->cf", gathered_two, grad_mixed[:, query_width:], preferred_element_type=jnp.float32
-    )
-    grad_normed_two = row_reduce(grad_mixed, back_memory_in)
-    grad_from_two, grad_gain_two = norm_backward(grad_normed_two, unit_two, scale_two, gain_two)
-    grad_hidden = cotangent.astype(jnp.float32) + grad_from_two
-    grad_hidden_all = row_gather(grad_hidden.astype(jnp.bfloat16))
-    grad_w_attn_out = jnp.einsum(
-        "tf,tc->fc", attended_all, grad_hidden_all, preferred_element_type=jnp.float32
-    )
-    grad_attended = col_reduce(grad_hidden_all, back_attn).astype(jnp.bfloat16)
-    grad_query_own, grad_kv_all = attend_backward(
-        own_qkv, kv_rows, allowed, log_sums, grad_attended
-    )
-    grad_kv_own = lax.psum_scatter(grad_kv_all, "col", scatter_dimension=0, tiled=True)
-    grad_qkv = jnp.concatenate([grad_query_own[:, None], grad_kv_own], axis=1).astype(jnp.bfloat16)
-    grad_qkv_all = col_gather(grad_qkv)
-    grad_w_qkv = jnp.einsum(
-        "tc,tjf->jcf", gathered_one, grad_qkv_all, preferred_element_type=jnp.float32
-    )
-    grad_normed_one = row_reduce(grad_qkv_all, back_qkv)
-    grad_from_one, grad_gain_one = norm_backward(grad_normed_one, unit_one, scale_one, gain_one)
-    grad_inputs = grad_hidden + grad_from_one
-    weight_sums = (
-        lax.psum(grad_w_qkv.astype(jnp.bfloat16), "dp").astype(jnp.float32),
-        lax.psum(grad_w_attn_out.astype(jnp.bfloat16), "dp").astype(jnp.float32),
-        lax.psum(grad_w_query.astype(jnp.bfloat16), "dp").astype(jnp.float32),
-        lax.psum(grad_w_gate.astype(jnp.bfloat16), "dp").astype(jnp.float32),
-        lax.psum(grad_w_proj.astype(jnp.bfloat16), "dp").astype(jnp.float32),
-    )
-    gain_full_one = lax.dynamic_update_slice_in_dim(
-        jnp.zeros(gain_attn.shape, jnp.float32), grad_gain_one, col_first, 0
-    )
-    gain_full_two = lax.dynamic_update_slice_in_dim(
-        jnp.zeros(gain_mem.shape, jnp.float32), grad_gain_two, col_first, 0
-    )
-    small_sums = lax.psum((gain_full_one, gain_full_two), ("dp", "row", "col"))
+    ).astype(low)
+    grad_part = (dense_nt(grad_query, query_w) + dense_nt(grad_gate, gate_w)).astype(low)
+    output, grad_hidden, grad_hidden_all, gain_two_grad = middle(
+        sizes, grad_part, out_part, hidden, cotangent, gain_two
+    )
+    grad_attended = dense_nt(grad_hidden_all, attn_w).astype(low)
+    grad_query_own, grad_kv_part = attend_backward(
+        qkv[0], kv_all[0], kv_all[1], allowed, log_sums, grad_attended
+    )
+    grad_kv = pair_sum(sizes, grad_kv_part)
+    grad_q = grad_query_own.astype(low)
+    x_part = (
+        dense_nt(grad_q, qkv_w[0]) + dense_nt(grad_kv[0], qkv_w[1]) + dense_nt(grad_kv[1], qkv_w[2])
+    ).astype(low)
+    grad_inputs, gain_sums = last(sizes, x_part, inputs, grad_hidden, gain_one, gain_two_grad)
+    gain_rows = gain_sums.reshape(sizes[2], 2, width_part)
+    grad_gain_one = gain_rows[:, 0].reshape(-1)
+    grad_gain_two = gain_rows[:, 1].reshape(-1)
+
+    def col_sum(grad, dim):
+        return lax.psum_scatter(grad.astype(low), "col", scatter_dimension=dim, tiled=True)
+
+    def weight_sum(grad, dim):
+        return lax.psum(col_sum(grad, dim), "dp").astype(jnp.float32)
+
+    grad_w_proj = weight_sum(dense_tn(gated_value, dy_own), 1)
+    grad_w_query = weight_sum(dense_tn(normed_two, grad_query), 0)
+    grad_w_gate = weight_sum(dense_tn(normed_two, grad_gate), 0)
+    grad_w_attn_out = weight_sum(dense_tn(attended, grad_hidden_all), 1)
+    grad_w_qkv = weight_sum(
+        jnp.stack([dense_tn(normed_one, part) for part in (grad_q, grad_kv[0], grad_kv[1])]), 1
+    )
+    grad_keys = lax.psum_scatter(
+        grad_keys.astype(low).reshape(-1, HALF), ("dp", "col"), scatter_dimension=0, tiled=True
+    )
+    grad_subkeys = (
+        lax.all_gather(grad_keys, ("row", "dp", "col"), axis=0, tiled=True)
+        .astype(jnp.float32)
+        .reshape(subkeys.shape)
+    )
     return (
         output,
         grad_inputs,
-        small_sums[0],
-        weight_sums[0],
-        weight_sums[1],
-        small_sums[1],
-        weight_sums[2],
-        weight_sums[3],
-        weight_sums[4],
+        grad_gain_one,
+        grad_w_qkv,
+        grad_w_attn_out,
+        grad_gain_two,
+        grad_w_query,
+        grad_w_gate,
+        grad_w_proj,
         grad_subkeys,
         grad_values,
     )

time: 1050 us -> 865 us (0.82)
  waiting for transfers between devices: 648 us -> 393 us
  Pallas kernels: 80.4 us -> 219 us
  blocking collectives: 54.9 us -> 10.3 us
  other arithmetic: 48.5 us -> 26.6 us
    pallas_call x0 -> x6, Pallas kernels: none -> 139 us  [the longest x1 40 us: middle(): pl.pallas_call(functools.partial(middle_kernel, sizes), in_specs=[VMEM] *...]
    reduce_scatter x10 -> x6, waiting for transfers between devices: 153 us -> 20.8 us  [the longest x5 20.7 us: col_sum(): lax.psum_scatter(grad.astype(low), 'col', scatter_dimension=dim, tiled=True)]
    all_gather x8 -> x1, waiting for transfers between devices: 122 us -> 6.75 us  [per_device(): lax.all_gather(grad_keys, ('row', 'dp', 'col'), axis=0, tiled=True)]
    psum x5 -> x0, blocking collectives: 50 us -> none  [the longest x1 39.7 us: per_device(): small_sums = lax.psum((gain_full_one, gain_full_two), ('dp', 'row', 'col'))]
    convert_element_type x13 -> x6, other arithmetic: 20.4 us -> 9.22 us  [the longest x5 8.39 us: weight_sum(): return lax.psum(col_sum(grad, dim), 'dp').astype(jnp.float32)]
    dot_general x19 -> x23, matrix products: 40.6 us -> 40.1 us  [the longest x7 13.6 us: dense_tn(): lax.dot_general(left, right, (((0,), (0,)), ((), ())), preferred_element_...]
  transfers between devices with their start and end apart: 25 -> 13, of which waited for: 19 -> 9; matrix products, arithmetic and copies ran while one was open for 13% -> 9% of each run, Pallas kernels for 4% -> 8%
where the time goes in v2:
time: 865 us; the launch traced here: 854 us
  waiting for transfers between devices  393 us (45%)
  Pallas kernels  219 us (25%)
  matrix products  138 us (16%)
  local copies, waits for them, and re-layouts  43 us (5%)
  other arithmetic  26.6 us (3%)
  between operations  15.6 us (2%)
  blocking collectives  10.3 us (1%)
  starting transfers between devices  9.01 us (1%)
    reduce_scatter x1, waiting for transfers between devices, memory_all(): lax.psum_scatter(grid, EVERYONE, scatter_dimension=0, tiled=True)[0]  143 us
    psum x1, waiting for transfers between devices, weight_sum(): return lax.psum(col_sum(grad, dim), 'dp').astype(jnp.float32)  102 us
    all_gather x1, waiting for transfers between devices, memory_all(): grad_all = lax.all_gather(wide, ('dp', 'col'), axis=0, tiled=True)  83.6 us
    pallas_call x1, Pallas kernels, middle(): pl.pallas_call(functools.partial(middle_kernel, sizes), in_specs=[VMEM] *...  40 us
    pallas_call x1, Pallas kernels, join(): pl.pallas_call(functools.partial(join_kernel, sizes), in_specs=[VMEM] * 3...  32.6 us
    pallas_call x1, Pallas kernels, start_all(): pl.pallas_call(functools.partial(start_kernel, sizes), in_specs=[VMEM] *...  30.2 us
    pallas_call x1, Pallas kernels, last(): pl.pallas_call(functools.partial(last_kernel, sizes), in_specs=[VMEM] * 5...  27 us
    pallas_call x1, Pallas kernels, collect(): pl.pallas_call(functools.partial(collect_kernel, rows_dev // SUBKEYS), gr...  26.6 us
  transfers between devices with their start and end apart: 13, of which 9 were waited for; matrix products, arithmetic and copies ran while one was open for 9% of the time, Pallas kernels for 8%

profile of v2, /device:TPU:0, one launch (start us, length us, event | category | flops | bytes accessed | tf_op | source)
XLA Modules:
  0.0 854.3 jit_solution(6444497745374423587)
XLA Ops:
  8.0 30.2 %start_all.1 = (bf16[512,1024]{1,0:T(8,128)(2,1)}, bf16[512,1024]{1,0:T(8,128)(2,1)}, bf16[3,1024,256]{2,1,0:T(8,128)(2,1)}, bf16[1024,1024]{1,0:T(8,128)(2,1)},...) custom-call(bf16[256,512]{1,0:T(8,128)(2,1)} %x.3, bf16[256,512]{1,0:T(8,128)(2,1)} %dy.1, ...), custom_call_target="tpu_custom_call" | custom-call | tf_op jit(solution)/shard_map/start_all/pallas_call | solution.py:243
  39.8 2.8 fusion.12
  44.1 4.0 swap_tokens.1
  49.4 2.1 fusion.110
  51.4 2.0 fusion.111
  53.4 2.1 fusion.112
  55.6 2.0 fusion.113
  59.8 6.5 route.1
  67.1 2.0 fusion.7
  78.2 32.6 %join.1 = (f32[256,512]{1,0:T(8,128)}, bf16[512,1024]{1,0:T(8,128)(2,1)}) custom-call(bf16[512,1024]{1,0:T(8,128)(2,1)} %convolution_convert_fusion.5.part, bf16[256,512]{1,0:T(8,128)(2,1)} %x.3, bf16[1,512]{1,0:T(2,128)(2,1)} %broadcast_in_dim.16.gain), custom_call_target="tpu_custom_call" | custom-call | tf_op jit(solution)/shard_map/join/pallas_call | solution.py:349
  110.8 4.2 convolution_convert_fusion.4.query_ref
  114.9 12.4 %weigh.1 = (f32[4,32,128]{2,1,0:T(8,128)}, bf16[4,32,128]{2,1,0:T(8,128)(2,1)}) custom-call(bf16[512,1024]{1,0:T(8,128)(2,1)} %convolution_convert_fusion.4.query_ref, bf16[2,256,512]{2,1,0:T(8,128)(2,1)} %dynamic-slice_bitcast_fusion.keys_ref, s32[4,1,4096]{2,1,0:T(1,128)} %bitcast.129, s32[4,1,4096]{2,1,0:T(1,128)} %get-tuple-element.40.rank_ref), custom_call_target="tpu_custom_call" | custom-call | tf_op jit(solution)/shard_map/weigh/pallas_call | solution.py:612
  128.7 5.4 all-to-all-start.2
  134.8 6.6 all-to-all-done.2
  141.3 2.6 all-to-all-start
  144.6 6.7 all-to-all-done
  153.0 23.3 %spread.1 = bf16[4096,2048]{1,0:T(8,128)(2,1)} custom-call(s32[32,1,512]{2,1,0:T(1,128)} %and_select_fusion.1.key_ref, s32[32,1,512]{2,1,0:T(1,128)} %get-tuple-element.58.low_ref, bf16[32,1,512]{2,1,0:T(2,128)(2,1)} %broadcast_in_dim_reshape.10.weight_ref), custom_call_target="tpu_custom_call" | custom-call | tf_op jit(solution)/shard_map/spread/pallas_call | solution.py:651
  176.3 23.4 %convolution_convert_fusion.1 = bf16[4096,1024]{1,0:T(8,128)(2,1)} fusion(bf16[4096,2048]{1,0:T(8,128)(2,1)} %spread.1, bf16[2048,1024]{1,0:T(8,128)(2,1)} %param.24), kind=kOutput, calls=%fused_computation.1 | convolution fusion | flops 17184063488 | bytes 29360128 | tf_op jit(solution)/shard_map/dot_general | solution.py:787
  199.7 14.5 %reshape.223 = bf16[4,2,512,4,256]{4,3,2,1,0:T(4,128)(2,1)} reshape(bf16[4096,1024]{1,0:T(8,128)(2,1)} %convolution_convert_fusion.1) | data formatting | bytes 16777216 | tf_op jit(solution)/shard_map/reshape | solution.py:788
  214.2 8.3 copy.86
  223.6 2.5 fusion.114
  226.0 143.4 %reduce-scatter.8.cloned.1.call-done = bf16[1,512,256]{2,1,0:T(8,128)(2,1)} async-done(((bf16[32,512,256]{2,1,0:T(8,128)(2,1)}), bf16[1,512,256]{2,1,0:T(8,128)(2,1)}) %reduce-scatter.8.cloned.1.call-update) | async-done | bytes 262160 | tf_op jit(solution)/shard_map/reduce_scatter | solution.py:790
  369.5 2.9 fusion.38
  372.5 22.3 %all-gather.4.cloned.1.call-done = bf16[512,1024]{1,0:T(8,128)(2,1)} async-done(((bf16[512,256]{1,0:T(8,128)(2,1)}), bf16[512,1024]{1,0:T(8,128)(2,1)}) %all-gather.4.cloned.1.call-update) | async-done | bytes 1048592 | tf_op jit(solution)/shard_map/all_gather | solution.py:792
  394.9 83.6 %all-gather.6.cloned.1.call-done = bf16[4096,1024]{1,0:T(8,128)(2,1)} async-done(((bf16[512,1024]{1,0:T(8,128)(2,1)}), bf16[4096,1024]{1,0:T(8,128)(2,1)}) %all-gather.6.cloned.1.call-update) | async-done | bytes 8388624 | tf_op jit(solution)/shard_map/all_gather | solution.py:793
  478.5 23.6 %convolution_convert_fusion.grid_ref = bf16[4096,2048]{1,0:T(8,128)(2,1)} fusion(bf16[4096,1024]{1,0:T(8,128)(2,1)} %all-gather.6.cloned.1.call-done, bf16[2048,1024]{1,0:T(8,128)(2,1)} %param.24), kind=kOutput, calls=%fused_computation | convolution fusion | flops 17188257792 | bytes 29360128 | tf_op jit(solution)/shard_map/dot_general | solution.py:797
  502.0 26.6 %collect.1 = f32[32,1,512]{2,1,0:T(1,128)} custom-call(bf16[4096,2048]{1,0:T(8,128)(2,1)} %convolution_convert_fusion.grid_ref, s32[32,1,512]{2,1,0:T(1,128)} %and_select_fusion.1.key_ref, s32[32,1,512]{2,1,0:T(1,128)} %get-tuple-element.58.low_ref), custom_call_target="tpu_custom_call" | custom-call | tf_op jit(solution)/shard_map/collect/pallas_call | solution.py:679
  529.6 10.3 %all_to_all.15 = f32[32,4,128]{2,1,0:T(4,128)S(1)} all-to-all(f32[32,4,128]{2,1,0:T(4,128)S(1)} %copy.81), channel_id=1, replica_groups=mesh['dp'=4,'row'=4,'col'=2] {'dp','row','col'}, dimensions={0} | all-to-all | bytes 131072 | tf_op jit(solution)/shard_map/all_to_all | solution.py:748
  540.7 11.5 %unweigh.1 = (bf16[256,512]{1,0:T(8,128)(2,1)}, bf16[256,512]{1,0:T(8,128)(2,1)}) custom-call(f32[4,128,32]{2,1,0:T(8,128)} %bitcast.127, s32[4,1,4096]{2,1,0:T(1,128)} %bitcast.130, s32[4,1,4096]{2,1,0:T(1,128)} %get-tuple-element.40.rank_ref, f32[4,32,128]{2,1,0:T(8,128)} %get-tuple-element.42.weights_ref), custom_call_target="tpu_custom_call" | custom-call | tf_op jit(solution)/shard_map/unweigh/pallas_call | solution.py:726
  556.0 2.8 convolution_convert_fusion.7
  559.0 2.6 convolution_convert_fusion.8
  561.6 2.9 convolution_convert_fusion.3.out_part
  568.0 40.0 %middle.1 = (bf16[256,512]{1,0:T(8,128)(2,1)}, f32[256,512]{1,0:T(8,128)}, bf16[512,1024]{1,0:T(8,128)(2,1)}, f32[1,512]{1,0:T(1,128)}) custom-call(bf16[512,1024]{1,0:T(8,128)(2,1)} %add_convert_fusion.1.part, bf16[512,1024]{1,0:T(8,128)(2,1)} %convolution_convert_fusion.3.out_part, f32[256,512]{1,0:T(8,128)} %get-tuple-element.46.hidden, ...), custom_call_target="tpu_custom_call" | custom-call | tf_op jit(solution)/shard_map/middle/pallas_call | solution.py:420
  608.1 2.0 convolution_convert_fusion.17
  610.1 2.2 fusion.22
  626.1 5.2 pair_sum.1
  631.3 1.9 fusion.21
  638.6 1.9 fusion.13
  643.5 3.8 convolution_convert_fusion.2
  648.6 6.8 reduce-scatter.10.cloned.1.call-done
  655.5 13.9 %reduce-scatter.14.cloned.1.call-done = bf16[512,1024]{1,0:T(8,128)(2,1)} async-done(((bf16[1024,1024]{1,0:T(8,128)(2,1)}), bf16[512,1024]{1,0:T(8,128)(2,1)}) %reduce-scatter.14.cloned.1.call-update) | async-done | bytes 1048592 | tf_op jit(solution)/shard_map/reduce_scatter | solution.py:965
  669.4 24.1 %fusion.115 = f32[2048,1024]{1,0:T(8,128)} fusion(bf16[4096,2048]{1,0:T(8,128)(2,1)} %spread.1, bf16[4096,1024]{1,0:T(8,128)(2,1)} %all-gather.6.cloned.1.call-done), kind=kOutput, calls=%fused_computation.196 | convolution fusion | flops 17179869184 | bytes 33554432 | tf_op jit(solution)/shard_map/dot_general | solution.py:794
  696.5 27.0 %last.1 = (f32[256,512]{1,0:T(8,128)}, f32[2,8,128]{2,1,0:T(8,128)}) custom-call(bf16[512,1024]{1,0:T(8,128)(2,1)} %add_convert_fusion.part, bf16[256,512]{1,0:T(8,128)(2,1)} %x.3, f32[256,512]{1,0:T(8,128)} %get-tuple-element.49.above, bf16[1,512]{1,0:T(2,128)(2,1)} %broadcast_in_dim.17.gain, f32[1,512]{1,0:T(1,128)} %get-tuple-element.50.other_gain), custom_call_target="tpu_custom_call" | custom-call | tf_op jit(solution)/shard_map/last/pallas_call | solution.py:489
  724.8 6.7 all-gather.8.cloned.1.call-done
  731.5 4.2 convert.68
  735.7 101.9 %all-reduce.3.cloned.1.call-done = (bf16[3,512,256]{2,1,0:T(8,128)(2,1)}, bf16[256,512]{1,0:T(8,128)(2,1)}, bf16[512,1024]{1,0:T(8,128)(2,1)}, bf16[512,256]{1,0:T(8,128)(2,1)}, bf16[256,512]{1,0:T(8,128)(2,1)}) async-done(((bf16[3,512,256]{2,1,0:T(8,128)(2,1)}, bf16[256,512]{1,0:T(8,128)(2,1)}, bf16[512,1024]{1,0:T(8,128)(2,1)}, bf16[512,256]{1,0:T(8,128)(2,1)}, bf16[256,512]{1,0:T(8,128)(2,1)}), ...) | async-done | bytes 2621456 | tf_op jit(solution)/shard_map/psum | solution.py:968
  837.6 1.9 convert_element_type.159
  839.5 1.9 convert_element_type.163
  (194 shorter events, 64.7 us)
Async XLA Ops:
  7.2 59.1 %copy-start = (bf16[4,2,256,512]{3,2,1,0:T(8,128)(2,1)S(1)}, bf16[4,2,256,512]{3,2,1,0:T(8,128)(2,1)}, u32[]{:S(2)}) copy-start(bf16[4,2,256,512]{3,2,1,0:T(8,128)(2,1)} %param.23) | copy-start | bytes 6291460
  49.4 6.2 copy-start.13
  55.6 2.0 copy-start.32
  66.3 2.9 copy-start.7
  69.2 1.6 copy-start.5
  69.9 6.2 copy-start.36
  71.3 1.6 copy-start.3
  71.9 4.2 copy-start.38
  73.4 1.6 copy-start.1
  74.1 2.0 copy-start.40
  110.7 23.3 %copy-start.30 = (s32[4,32,128]{2,1,0:T(8,128)S(1)}, s32[4,32,128]{2,1,0:T(8,128)}, u32[]{:S(2)}) copy-start(s32[4,32,128]{2,1,0:T(8,128)} %get-tuple-element.39) | copy-start | bytes 196612
  128.7 12.6 %all-to-all-start.2 = ((bf16[32,4,128]{2,1,0:T(4,128)(2,1)}), bf16[32,4,128]{2,1,0:T(4,128)(2,1)S(1)}, u32[]{:S(2)}, u32[]{:S(2)}) async-start(bf16[32,4,128]{2,1,0:T(4,128)(2,1)} %copy.83), calls=%async_computation.2 | async-start | bytes 65536 | tf_op jit(solution)/shard_map/all_to_all | solution.py:748
  141.3 10.0 %all-to-all-start = ((s32[32,4,128]{2,1,0:T(4,128)}), s32[32,4,128]{2,1,0:T(4,128)S(1)}, u32[]{:S(2)}, u32[]{:S(2)}) async-start(s32[32,4,128]{2,1,0:T(4,128)} %copy.78), calls=%async_computation | async-start | bytes 131072 | tf_op jit(solution)/shard_map/all_to_all | solution.py:748
  143.9 225.6 %reduce-scatter.8.cloned.1.call-start = ((), (), s32[]{:S(2)}) async-start(), calls=%async_computation.12 | async-start | bytes 8650752 | tf_op jit(solution)/shard_map/reduce_scatter | solution.py:790
  222.5 172.3 %all-gather.4.cloned.1.call-start = ((), (), s32[]{:S(2)}) async-start(), calls=%async_computation.10 | async-start | bytes 1310720 | tf_op jit(solution)/shard_map/all_gather | solution.py:792
  372.4 106.1 %all-gather.6.cloned.1.call-start = ((), (), s32[]{:S(2)}) async-start(), calls=%async_computation.11 | async-start | bytes 9437184 | tf_op jit(solution)/shard_map/all_gather | solution.py:793
  394.8 252.5 %reduce-scatter.20.cloned.1.call-start = ((), (), s32[]{:S(2)}) async-start(), calls=%async_computation.18 | async-start | bytes 589824 | tf_op jit(solution)/shard_map/reduce_scatter | solution.py:977
  556.0 92.6 %reduce-scatter.18.cloned.1.call-start = ((), (), s32[]{:S(2)}) async-start(), calls=%async_computation.17 | async-start | bytes 786432 | tf_op jit(solution)/shard_map/reduce_scatter | solution.py:965
  558.9 89.8 %reduce-scatter.16.cloned.1.call-start = ((), (), s32[]{:S(2)}) async-start(), calls=%async_computation.16 | async-start | bytes 786432 | tf_op jit(solution)/shard_map/reduce_scatter | solution.py:965
  561.5 87.1 %reduce-scatter.12.cloned.1.call-start = ((), (), s32[]{:S(2)}) async-start(), calls=%async_computation.14 | async-start | bytes 786432 | tf_op jit(solution)/shard_map/reduce_scatter | solution.py:965
  561.6 2.9 copy-start.28
  561.6 3.2 copy-start.26
  561.6 3.6 copy-start.33
  564.9 1.7 copy-start.25
  565.2 1.3 copy-start.23
  608.1 4.2 copy-start.8
  612.3 1.6 copy-start.6
  614.5 1.6 copy-start.4
  616.7 1.6 copy-start.2
  631.3 3.7 copy-start.12
  631.3 3.7 copy-start.14
  631.3 4.2 copy-start.34
  631.3 4.2 copy-start.37
  631.3 4.2 copy-start.39
  631.3 4.2 copy-start.41
  631.3 4.2 copy-start.43
  636.8 18.6 %reduce-scatter.10.cloned.1.call-start = ((), (), s32[]{:S(2)}) async-start(), calls=%async_computation.13 | async-start | bytes 2359296 | tf_op jit(solution)/shard_map/reduce_scatter | solution.py:965
  637.1 3.4 copy-start.16
  637.1 3.4 copy-start.20
  641.9 1.6 copy-start.21
  643.2 26.1 %reduce-scatter.14.cloned.1.call-start = ((), (), s32[]{:S(2)}) async-start(), calls=%async_computation.15 | async-start | bytes 3145728 | tf_op jit(solution)/shard_map/reduce_scatter | solution.py:965
  647.3 84.2 %all-gather.8.cloned.1.call-start = ((), (), s32[]{:S(2)}) async-start(), calls=%async_computation.19 | async-start | bytes 2162688 | tf_op jit(solution)/shard_map/all_gather | solution.py:981
  647.9 189.7 %all-reduce.3.cloned.1.call-start = ((), (), s32[]{:S(2)}) async-start(), calls=%async_computation.20 | async-start | bytes 5242880 | tf_op jit(solution)/shard_map/psum | solution.py:968
  669.4 24.2 %copy-start.18 = (bf16[3,1024,256]{2,1,0:T(8,128)(2,1)S(1)}, bf16[3,1024,256]{2,1,0:T(8,128)(2,1)}, u32[]{:S(2)}) copy-start(bf16[3,1024,256]{2,1,0:T(8,128)(2,1)} %get-tuple-element.34) | copy-start | bytes 4718596
  837.6 5.6 copy-start.22
  839.5 5.0 copy-start.19
  844.5 1.6 copy-start.27
  844.5 2.3 copy-start.24
  (9 other events, 9.0 us)
Sparse Core Ops, SparseCore 0:
  222.7 146.7 reduce-scatter.7
  372.5 22.2 all-gather.3
  396.4 82.0 all-gather.5
  556.1 27.9 reduce-scatter.19
  586.1 6.1 reduce-scatter.17
  594.5 9.0 reduce-scatter.15
  637.0 5.5 reduce-scatter.11
  645.3 10.0 reduce-scatter.9
  658.3 11.0 reduce-scatter.13
  672.2 59.3 all-gather.7
  734.3 103.2 all-reduce.2

commit v3 on v2

--- a/solution.py
+++ b/solution.py
@@ -630,60 +630,408 @@
     )(query_rows, keys_head, flat[:, None, :], rank)
 
 
-def spread_kernel(areas, key_ref, low_ref, weight_ref, out_ref):
-    key = key_ref[0]
-    at_key = lax.broadcasted_iota(jnp.int32, (areas * FBLK, key.shape[1]), 0) == key
-    left = jnp.where(at_key, weight_ref[0].astype(jnp.float32), 0.0).astype(jnp.bfloat16)
-    stacked = lax.dot_general(
-        left,
-        one_hot(low_ref[0], SUBKEYS),
-        (((1,), (1,)), ((), ())),
-        preferred_element_type=jnp.float32,
-    ).astype(jnp.bfloat16)
-    for area in range(areas):
-        out_ref[:, area * SUBKEYS : (area + 1) * SUBKEYS] = stacked[area * FBLK : (area + 1) * FBLK]
-
-
-def spread(key, low, weight, rows_dev):
-    blocks, slots = key.shape
-    areas = rows_dev // SUBKEYS
-    row = pl.BlockSpec((1, 1, slots), lambda i: (i, 0, 0))
+def own_block(tokens_ref, dp, col, row, width):
+    left = pl.multiple_of(row * width, width)
+    return tokens_ref.at[dp, col, :, pl.ds(left, width)]
+
+
+def send_rows(spot, sizes, src, landing, send, recv):
+    count = sizes[0] * sizes[1] * sizes[2]
+    me = index_of(spot, sizes)
+
+    def one(step, carry):
+        other = lax.rem(me + step, count)
+        remote(src.at[other], landing.at[me], send, recv, device_of(other, sizes)).start()
+        return carry
+
+    lax.fori_loop(1, count, one, 0)
+    landing[me] = src[me]
+
+
+def all_rows(landing, sem):
+    return arrived(landing.at[pl.ds(0, landing.shape[0] - 1)], sem)
+
+
+def slot_row(sizes, table, dp, col, block):
+    pieces = []
+    for row in range(sizes[1]):
+        index = (dp * sizes[1] + row) * sizes[2] + col
+        pieces.append(table[index, block : block + 1, :])
+    return jnp.concatenate(pieces, axis=1)
+
+
+def read_kernel(
+    sizes, blocks, grads, meta, slots, values,
+    grads_all, table, own_part, other_part, meta_in,
+    slots_in, tables, parts, msend, mrecv, ssend, srecv, zsend, zrecv, xsend, xrecv, csend, crecv,
+    local, tsem, psem, qsend, qrecv,
+):
+    spot = here()
+    dp, row, col = spot
+    dps, rows, cols = sizes
+    tokens, width = grads.shape
+    areas = values.shape[0] // SUBKEYS
+    greet_all(spot, sizes)
+    send_rows(spot, sizes, meta, meta_in, msend, mrecv)
+    send_rows(spot, sizes, slots, slots_in, ssend, srecv)
+
+    def block_at(j, k, c):
+        return own_block(grads_all, lax.rem(dp + j, dps), c, lax.rem(row + k, rows), width)
+
+    def cross(src, j, k):
+        remote(src, block_at(j, k, col), csend, crecv, (dp, row, 1 - col)).start()
+
+    def sideways(src, j):
+        for k in range(1, rows):
+            remote(
+                src, block_at(j, 0, col), xsend, xrecv.at[j, rows - k],
+                (dp, lax.rem(row + k, rows), col),
+            ).start()
+
+    for k in range(1, dps):
+        remote(
+            grads, block_at(0, 0, col), zsend, zrecv.at[dps - k], (lax.rem(dp + k, dps), row, col)
+        ).start()
+    sideways(grads, 0)
+    cross(grads, 0, 0)
+    keep = pltpu.make_async_copy(grads, block_at(0, 0, col), local)
+    keep.start()
+
+    def from_above(j):
+        src = block_at(j, 0, col)
+        arrived(src, zrecv.at[j])
+        sideways(src, j)
+        cross(src, j, 0)
+
+    def from_side(j):
+        for k in range(1, rows):
+            src = block_at(j, k, col)
+            arrived(src, xrecv.at[j, k])
+            cross(src, j, k)
+
+    all_rows(meta_in, mrecv)
+    all_rows(slots_in, srecv)
+
+    def chunk(turn, kk):
+        source_dp = lax.rem(dp + 1 + turn, dps)
+        source_col = 1 - col if kk == 0 else col
+        table_out = pltpu.make_async_copy(
+            tables.at[kk], table.at[source_dp, source_col], tsem.at[kk]
+        )
+
+        @pl.when(turn > 0)
+        def _():
+            table_out.wait()
+
+        for block in range(blocks):
+            row_meta = slot_row(sizes, meta_in, source_dp, source_col, block)
+            key = row_meta // SUBKEYS
+            low = row_meta % SUBKEYS
+            weight = slot_row(sizes, slots_in, source_dp, source_col, block)
+            at_key = lax.broadcasted_iota(jnp.int32, (areas * FBLK, key.shape[1]), 0) == key
+            left = jnp.where(at_key, weight, 0.0).astype(jnp.bfloat16)
+            stacked = lax.dot_general(
+                left,
+                one_hot(low, SUBKEYS),
+                (((1,), (1,)), ((), ())),
+                preferred_element_type=jnp.float32,
+            ).astype(jnp.bfloat16)
+            for area in range(areas):
+                tables[
+                    kk,
+                    block * FBLK : (block + 1) * FBLK,
+                    area * SUBKEYS : (area + 1) * SUBKEYS,
+                ] = stacked[area * FBLK : (area + 1) * FBLK]
+        table_out.start()
+        if kk == 0:
+            part_out = remote(
+                parts.at[0], other_part.at[source_dp], qsend, qrecv, (dp, row, 1 - col)
+            )
+        else:
+            part_out = pltpu.make_async_copy(parts.at[1], own_part.at[source_dp], psem)
+
+        @pl.when(turn > 0)
+        def _():
+            if kk == 0:
+                part_out.wait_send()
+            else:
+                part_out.wait()
+
+        def strip(n, carry):
+            columns = pl.ds(pl.multiple_of(n * 256, 256), 256)
+            parts[kk, :, columns] = jnp.dot(
+                tables[kk], values[:, columns], preferred_element_type=jnp.float32
+            ).astype(jnp.bfloat16)
+            return carry
+
+        lax.fori_loop(0, values.shape[1] // 256, strip, 0)
+        part_out.start()
+
+    def step(turn, carry):
+        chunk(turn, 0)
+
+        @pl.when(jnp.logical_and(turn > 0, 2 * turn < dps))
+        def _():
+            from_above(2 * turn)
+
+        @pl.when(turn > 0)
+        def _():
+            from_side(turn - 1)
+
+        chunk(turn, 1)
+
+        @pl.when(2 * turn + 1 < dps)
+        def _():
+            from_above(2 * turn + 1)
+
+        return carry
+
+    lax.fori_loop(0, dps, step, 0)
+    from_side(dps - 1)
+    keep.wait()
+    for kk in range(2):
+        pltpu.make_async_copy(tables.at[kk], table.at[0, 0], tsem.at[kk]).wait()
+    pltpu.make_async_copy(parts.at[1], own_part.at[0], psem).wait()
+    remote(parts.at[0], other_part.at[0], qsend, qrecv, (dp, row, 1 - col)).wait_send()
+    arrived(other_part, qrecv)
+    arrived(grads_all.at[:, 0], crecv)
+    arrived(grads_all.at[:, 0], csend)
+    arrived(grads_all.at[pl.ds(0, dps - 1), 0, :, pl.ds(0, width)], zsend)
+    arrived(grads_all.at[:, 0, :, pl.ds(0, (rows - 1) * width)], xsend)
+    all_rows(meta_in, msend)
+    all_rows(slots_in, ssend)
+
+
+def read_memory(sizes, grads, meta, slots, values):
+    dps, rows, cols = sizes
+    tokens, width = grads.shape
+    rows_dev, features = values.shape
+    blocks = tokens // FBLK
+    low = jnp.bfloat16
+    shape = jax.ShapeDtypeStruct
     return pl.pallas_call(
-        functools.partial(spread_kernel, areas),
-        grid=(blocks,),
-        in_specs=[row, row, row],
-        out_specs=pl.BlockSpec((FBLK, rows_dev), lambda i: (i, 0)),
-        out_shape=jax.ShapeDtypeStruct((blocks * FBLK, rows_dev), jnp.bfloat16),
-        name="spread",
-    )(key[:, None], low[:, None], weight[:, None])
-
-
-def collect_kernel(areas, grid_ref, key_ref, low_ref, out_ref):
-    key = key_ref[0]
-    low_hot = one_hot(low_ref[0], SUBKEYS)
-    total = jnp.zeros(key.shape, jnp.float32)
-    for area in range(areas):
-        product = jnp.dot(
-            grid_ref[:, area * SUBKEYS : (area + 1) * SUBKEYS],
-            low_hot,
-            preferred_element_type=jnp.float32,
-        )
-        spot = lax.broadcasted_iota(jnp.int32, product.shape, 0) + area * FBLK
-        total = total + jnp.sum(jnp.where(spot == key, product, 0.0), axis=0, keepdims=True)
-    out_ref[0] = total
-
-
-def collect(grid_products, key, low, rows_dev):
-    blocks, slots = key.shape
-    row = pl.BlockSpec((1, 1, slots), lambda i: (i, 0, 0))
-    return pl.pallas_call(
-        functools.partial(collect_kernel, rows_dev // SUBKEYS),
-        grid=(blocks,),
-        in_specs=[pl.BlockSpec((FBLK, rows_dev), lambda i: (i, 0)), row, row],
-        out_specs=row,
-        out_shape=jax.ShapeDtypeStruct((blocks, 1, slots), jnp.float32),
-        name="collect",
-    )(grid_products, key[:, None], low[:, None])[:, 0]
+        functools.partial(read_kernel, sizes, blocks),
+        in_specs=[VMEM] * 4,
+        out_specs=[ANY, ANY, ANY, ANY, VMEM],
+        out_shape=[
+            shape((dps, cols, tokens, rows * width), low),
+            shape((dps, cols, tokens, rows_dev), low),
+            shape((dps, tokens, features), low),
+            shape((dps, tokens, features), low),
+            shape(meta.shape, meta.dtype),
+        ],
+        scratch_shapes=[
+            pltpu.VMEM(slots.shape, slots.dtype),
+            pltpu.VMEM((2, tokens, rows_dev), low),
+            pltpu.VMEM((2, tokens, features), low),
+            DMA, DMA, DMA, DMA,
+            DMA, DMA((dps,)),
+            DMA, DMA((dps, rows)),
+            DMA, DMA,
+            DMA, DMA((2,)), DMA, DMA, DMA,
+        ],
+        compiler_params=pltpu.CompilerParams(collective_id=6, has_side_effects=True),
+        name="read_memory",
+    )(grads, meta, slots, values)
+
+
+def back_kernel(
+    sizes, blocks, grads_all, own_part, other_part, meta_in, values_t,
+    memory, back, side_land, deep_land,
+    chunks, found, hots, mine, theirs, acc, side, total, deep,
+    gsem, osem, tsem, xsend, xrecv, zsend, zrecv, fsend, frecv, flocal, ssem, dsem,
+):
+    spot = here()
+    dp, row, col = spot
+    dps, rows, cols = sizes
+    tokens, width = memory.shape
+    areas = values_t.shape[1] // SUBKEYS
+    count = dps * rows * cols
+    me = index_of(spot, sizes)
+    greet_all(spot, sizes)
+
+    def source(turn):
+        return lax.rem(dp + 1 + turn, dps)
+
+    def load_parts(turn):
+        return (
+            pltpu.make_async_copy(own_part.at[source(turn)], mine, osem),
+            pltpu.make_async_copy(other_part.at[source(turn)], theirs, tsem),
+        )
+
+    def load_chunk(turn, kk):
+        return pltpu.make_async_copy(
+            grads_all.at[source(turn), 1 - col if kk == 0 else col], chunks.at[kk], gsem.at[kk]
+        )
+
+    def piece(turn, k):
+        left = pl.multiple_of(lax.rem(row + k, rows) * width, width)
+        return acc.at[turn, :, pl.ds(left, width)]
+
+    def combine(turn):
+        for copy in load_parts(turn):
+            copy.wait()
+        acc[turn] = (mine[...].astype(jnp.float32) + theirs[...].astype(jnp.float32)).astype(
+            jnp.bfloat16
+        )
+
+        @pl.when(turn + 1 < dps)
+        def _():
+            for copy in load_parts(turn + 1):
+                copy.start()
+
+        for k in range(1, rows):
+            remote(
+                piece(turn, k), side_land.at[turn, rows - k], xsend, xrecv.at[turn, rows - k],
+                (dp, lax.rem(row + k, rows), col),
+            ).start()
+
+    def row_total(turn):
+        copies = []
+        for k in range(1, rows):
+            arrived(side_land.at[turn, k], xrecv.at[turn, k])
+            copies.append(pltpu.make_async_copy(side_land.at[turn, k], side.at[k], ssem.at[k]))
+            copies[-1].start()
+        result = acc[turn, :, pl.ds(pl.multiple_of(row * width, width), width)].astype(jnp.float32)
+        for k in range(1, rows):
+            copies[k - 1].wait()
+            result = result + side[k].astype(jnp.float32)
+        return result
+
+    def deeper(turn):
+        total[turn] = row_total(turn).astype(jnp.bfloat16)
+        remote(
+            total.at[turn], deep_land.at[dps - 2 - turn], zsend, zrecv.at[dps - 2 - turn],
+            (source(turn), row, col),
+        ).start()
+
+    for copy in load_parts(0):
+        copy.start()
+    for kk in range(2):
+        load_chunk(0, kk).start()
+
+    def chunk(turn, kk):
+        source_dp = source(turn)
+        source_col = 1 - col if kk == 0 else col
+        keys = []
+        for block in range(blocks):
+            row_meta = slot_row(sizes, meta_in, source_dp, source_col, block)
+            keys.append(row_meta // SUBKEYS)
+            hots[block] = one_hot(row_meta % SUBKEYS, SUBKEYS)
+        load_chunk(turn, kk).wait()
+
+        def area_step(area, sums):
+            columns = pl.ds(pl.multiple_of(area * SUBKEYS, SUBKEYS), SUBKEYS)
+            grid = jnp.dot(
+                chunks[kk], values_t[:, columns], preferred_element_type=jnp.float32
+            ).astype(jnp.bfloat16)
+            new = []
+            for block in range(blocks):
+                product = jnp.dot(
+                    grid[block * FBLK : (block + 1) * FBLK],
+                    hots[block],
+                    preferred_element_type=jnp.float32,
+                )
+                spot_id = lax.broadcasted_iota(jnp.int32, product.shape, 0) + area * FBLK
+                new.append(
+                    sums[block]
+                    + jnp.sum(
+                        jnp.where(spot_id == keys[block], product, 0.0), axis=0, keepdims=True
+                    )
+                )
+            return tuple(new)
+
+        sums = lax.fori_loop(
+            0, areas, area_step, tuple(jnp.zeros(keys[0].shape, jnp.float32) for _ in range(blocks))
+        )
+
+        @pl.when(turn + 1 < dps)
+        def _():
+            load_chunk(turn + 1, kk).start()
+
+        for r in range(rows):
+            index = (source_dp * rows + r) * cols + source_col
+            for block in range(blocks):
+                found[index, block : block + 1, :] = sums[block][:, r * 128 : (r + 1) * 128]
+            away = remote(found.at[index], back.at[me], fsend, frecv, (source_dp, r, source_col))
+            own = jnp.logical_and(jnp.logical_and(source_dp == dp, row == r), source_col == col)
+            if kk == 0:
+                away.start()
+            else:
+                pl.when(jnp.logical_not(own))(away.start)
+                pl.when(own)(pltpu.make_async_copy(found.at[index], back.at[me], flocal).start)
+
+    def step(turn, carry):
+        @pl.when(2 * turn < dps)
+        def _():
+            combine(2 * turn)
+
+        @pl.when(turn > 0)
+        def _():
+            deeper(turn - 1)
+
+        chunk(turn, 0)
+
+        @pl.when(2 * turn + 1 < dps)
+        def _():
+            combine(2 * turn + 1)
+
+        chunk(turn, 1)
+        return carry
+
+    lax.fori_loop(0, dps, step, 0)
+    result = row_total(dps - 1)
+    for k in range(dps - 1):
+        arrived(deep_land.at[k], zrecv.at[k])
+        copy = pltpu.make_async_copy(deep_land.at[k], deep.at[k % 2], dsem.at[k % 2])
+        copy.start()
+        copy.wait()
+        result = result + deep[k % 2].astype(jnp.float32)
+    memory[...] = result
+    arrived(back.at[pl.ds(0, count - 1)], frecv)
+    arrived(back.at[0], flocal)
+    arrived(back.at[pl.ds(0, count - 1)], fsend)
+    arrived(side_land.at[:, pl.ds(0, rows - 1)], xsend)
+    arrived(deep_land.at[pl.ds(0, dps - 1)], zsend)
+
+
+def back_memory(sizes, grads_all, own_part, other_part, meta_in, values_t):
+    dps, rows, cols = sizes
+    _, _, tokens, features = grads_all.shape
+    width = features // rows
+    blocks = tokens // FBLK
+    count = dps * rows * cols
+    low, wide = jnp.bfloat16, jnp.float32
+    shape = jax.ShapeDtypeStruct
+    memory, back, _, _ = pl.pallas_call(
+        functools.partial(back_kernel, sizes, blocks),
+        in_specs=[ANY, ANY, ANY, VMEM, VMEM],
+        out_specs=[VMEM, VMEM, ANY, ANY],
+        out_shape=[
+            shape((tokens, width), wide),
+            shape((count, blocks, 128), wide),
+            shape((dps, rows, tokens, width), low),
+            shape((dps, tokens, width), low),
+        ],
+        scratch_shapes=[
+            pltpu.VMEM((2, tokens, features), low),
+            pltpu.VMEM((count, blocks, 128), wide),
+            pltpu.VMEM((blocks, SUBKEYS, rows * 128), low),
+            pltpu.VMEM((tokens, features), low),
+            pltpu.VMEM((tokens, features), low),
+            pltpu.VMEM((dps, tokens, features), low),
+            pltpu.VMEM((rows, tokens, width), low),
+            pltpu.VMEM((dps, tokens, width), low),
+            pltpu.VMEM((2, tokens, width), low),
+            DMA((2,)), DMA, DMA,
+            DMA, DMA((dps, rows)),
+            DMA, DMA((dps,)),
+            DMA, DMA, DMA, DMA((rows,)), DMA((2,)),
+        ],
+        compiler_params=pltpu.CompilerParams(collective_id=7, has_side_effects=True),
+        name="back_memory",
+    )(grads_all, own_part, other_part, meta_in, values_t)
+    return memory, back
 
 
 def unweigh_kernel(rows_dev, owners, back_ref, picks_ref, rank_ref, weights_ref, first_ref, second_ref):
@@ -741,66 +1089,29 @@
     )(back, flat[:, None, :], rank, weights)
 
 
-EVERYONE = ("dp", "row", "col")
-
-
-def exchange(operand):
-    return lax.all_to_all(operand, EVERYONE, split_axis=0, concat_axis=0, tiled=True)
-
-
-def by_block(arrived, dp_count, row_count, col_count):
-    _, blocks, cap = arrived.shape
-    wide = arrived.reshape(dp_count, row_count, col_count, blocks, cap)
-    return jnp.transpose(wide, (0, 2, 3, 1, 4)).reshape(
-        dp_count * col_count * blocks, row_count * cap
-    )
-
-
-def by_source(blocked, dp_count, row_count, col_count, blocks, cap):
-    wide = blocked.reshape(dp_count, col_count, blocks, row_count, cap)
-    return jnp.transpose(wide, (0, 3, 1, 2, 4)).reshape(
-        dp_count * row_count * col_count, blocks, cap
-    )
-
-
 def memory_all(query_rows, grad_memory, picks, subkeys, values):
-    dp_count = lax.axis_size("dp")
-    row_count = lax.axis_size("row")
-    col_count = lax.axis_size("col")
-    owners = dp_count * row_count * col_count
+    sizes = grid_sizes()
+    owners = sizes[0] * sizes[1] * sizes[2]
     rows_dev = values.shape[0]
     cap = FBLK * TOPK // owners
-    own_tokens = query_rows.shape[0]
-    blocks = own_tokens // FBLK
     head_id = lax.axis_index("row")
     keys_head = lax.dynamic_index_in_dim(subkeys, head_id, 0, keepdims=False)
     picks_head = lax.dynamic_index_in_dim(picks, head_id, 1, keepdims=False)
     flat = flat_picks(picks_head)
     rank, meta = route(flat, rows_dev, owners, cap)
-    sizes = (dp_count, row_count, col_count)
-    meta_in = by_block(exchange(jnp.swapaxes(meta, 0, 1)), *sizes)
-    key = meta_in // SUBKEYS
-    low = meta_in % SUBKEYS
     weights, slots = weigh(query_rows, keys_head, flat, rank, rows_dev, owners, cap)
-    weight_in = by_block(exchange(jnp.swapaxes(slots, 0, 1)), *sizes)
-    table = spread(key, low, weight_in, rows_dev)
-    partial = jnp.dot(table, values, preferred_element_type=jnp.float32).astype(jnp.bfloat16)
-    grid = partial.reshape(dp_count, col_count, own_tokens, row_count, -1)
-    grid = jnp.transpose(grid, (0, 3, 1, 2, 4)).reshape(owners, own_tokens, -1)
-    memory = lax.psum_scatter(grid, EVERYONE, scatter_dimension=0, tiled=True)[0]
-    memory = memory.astype(jnp.float32)
-    wide = lax.all_gather(grad_memory, "row", axis=1, tiled=True)
-    grad_all = lax.all_gather(wide, ("dp", "col"), axis=0, tiled=True)
-    grad_values = lax.dot_general(
-        table, grad_all, (((0,), (0,)), ((), ())), preferred_element_type=jnp.float32
-    )
-    products = lax.dot_general(
-        grad_all, values, (((1,), (1,)), ((), ())), preferred_element_type=jnp.float32
-    ).astype(jnp.bfloat16)
-    found = collect(products, key, low, rows_dev)
-    back = exchange(by_source(found, *sizes, blocks, cap))
+    spare = ((0, 0), (0, 0), (0, 128 - cap))
+    meta = jnp.pad(jnp.swapaxes(meta, 0, 1), spare, constant_values=-1)
+    slots = jnp.pad(jnp.swapaxes(slots, 0, 1).astype(jnp.float32), spare)
+    grads_all, table, own_part, other_part, meta_in = read_memory(
+        sizes, grad_memory, meta, slots, values
+    )
+    memory, back = back_memory(sizes, grads_all, own_part, other_part, meta_in, values.T)
+    grad_values = dense_tn(
+        table.reshape(-1, rows_dev), grads_all.reshape(-1, grads_all.shape[-1])
+    )
     first_t, second_t = unweigh(
-        jnp.transpose(back, (1, 2, 0)), flat, rank, weights, rows_dev, owners
+        jnp.transpose(back, (1, 2, 0))[:, :cap], flat, rank, weights, rows_dev, owners
     )
     grad_query = jnp.concatenate(
         [

time: 865 us -> 604 us (0.70)
  waiting for transfers between devices: 393 us -> 127 us
  Pallas kernels: 219 us -> 315 us
  matrix products: 138 us -> 87.7 us
  local copies, waits for them, and re-layouts: 43 us -> 23.9 us
  blocking collectives: 10.3 us -> 0 us
    reduce_scatter x1 -> x0, waiting for transfers between devices: 143 us -> none  [memory_all(): lax.psum_scatter(grid, EVERYONE, scatter_dimension=0, tiled=True)[0]]
    all_gather x2 -> x0, waiting for transfers between devices: 106 us -> none  [the longest x1 83.6 us: memory_all(): grad_all = lax.all_gather(wide, ('dp', 'col'), axis=0, tiled=True)]
    pallas_call x2, Pallas kernels: 49.9 us -> 146 us  [the longest x1 75.5 us: back_memory(): pl.pallas_call(functools.partial(back_kernel, sizes, blocks), in_specs=[A...]
    dot_general x3 -> x0, matrix products: 71.1 us -> none  [the longest x1 24.1 us: memory_all(): lax.dot_general(table, grad_all, (((0,), (0,)), ((), ())), preferred_elem...]
    reshape x5 -> x0, local copies, waits for them, and re-layouts: 22.9 us -> none  [the longest x2 22.8 us: memory_all(): grid = partial.reshape(dp_count, col_count, own_tokens, row_count, -1)]
    dot_general x7 -> x8, matrix products: 13.6 us -> 35.5 us  [dense_tn(): lax.dot_general(left, right, (((0,), (0,)), ((), ())), preferred_element_...]
    reduce_scatter x5, waiting for transfers between devices: 20.7 us -> 0.04 us  [col_sum(): lax.psum_scatter(grad.astype(low), 'col', scatter_dimension=dim, tiled=True)]
    all_gather x1, waiting for transfers between devices: 6.75 us -> 24.8 us  [per_device(): lax.all_gather(grad_keys, ('row', 'dp', 'col'), axis=0, tiled=True)]
  transfers between devices with their start and end apart: 13 -> 8, of which waited for: 9 -> 2; matrix products, arithmetic and copies ran while one was open for 9% -> 12% of each run, Pallas kernels for 8% -> 12%
where the time goes in v3:
time: 604 us; the launch traced here: 595 us
  Pallas kernels  315 us (52%)
  waiting for transfers between devices  127 us (21%)
  matrix products  87.7 us (15%)
  other arithmetic  24.4 us (4%)
  local copies, waits for them, and re-layouts  23.9 us (4%)
  between operations  16 us (3%)
    psum x1, waiting for transfers between devices, weight_sum(): return lax.psum(col_sum(grad, dim), 'dp').astype(jnp.float32)  102 us
    pallas_call x1, Pallas kernels, back_memory(): pl.pallas_call(functools.partial(back_kernel, sizes, blocks), in_specs=[A...  75.5 us
    pallas_call x1, Pallas kernels, read_memory(): pl.pallas_call(functools.partial(read_kernel, sizes, blocks), in_specs=[V...  70.7 us
    pallas_call x1, Pallas kernels, middle(): pl.pallas_call(functools.partial(middle_kernel, sizes), in_specs=[VMEM] *...  40.2 us
    dot_general x8, matrix products, dense_tn(): lax.dot_general(left, right, (((0,), (0,)), ((), ())), preferred_element_...  35.5 us
    pallas_call x1, Pallas kernels, join(): pl.pallas_call(functools.partial(join_kernel, sizes), in_specs=[VMEM] * 3...  32.5 us
    pallas_call x1, Pallas kernels, start_all(): pl.pallas_call(functools.partial(start_kernel, sizes), in_specs=[VMEM] *...  30.4 us
    pallas_call x1, Pallas kernels, last(): pl.pallas_call(functools.partial(last_kernel, sizes), in_specs=[VMEM] * 5...  25 us
  transfers between devices with their start and end apart: 8, of which 2 were waited for; matrix products, arithmetic and copies ran while one was open for 12% of the time, Pallas kernels for 12%

profile of v3, /device:TPU:0, one launch (start us, length us, event | category | flops | bytes accessed | tf_op | source)
XLA Modules:
  0.0 594.6 jit_solution(6803792677526395201)
XLA Ops:
  7.3 30.4 %start_all.1 = (bf16[512,1024]{1,0:T(8,128)(2,1)}, bf16[512,1024]{1,0:T(8,128)(2,1)}, bf16[3,1024,256]{2,1,0:T(8,128)(2,1)}, bf16[1024,1024]{1,0:T(8,128)(2,1)},...) custom-call(bf16[256,512]{1,0:T(8,128)(2,1)} %x.3, bf16[256,512]{1,0:T(8,128)(2,1)} %dy.1, ...), custom_call_target="tpu_custom_call" | custom-call | tf_op jit(solution)/shard_map/start_all/pallas_call | solution.py:243
  37.6 1.5 fusion
  39.2 2.8 fusion.12
  42.8 4.1 swap_tokens.1
  48.9 2.1 fusion.107
  50.9 2.0 fusion.106
  53.0 2.0 fusion.105
  55.0 2.1 fusion.104
  57.0 2.2 fusion.4
  65.6 1.4 convolution_convert_fusion.16
  69.1 6.5 %route.1 = (s32[4,1,4096]{2,1,0:T(1,128)}, s32[4,32,128]{2,1,0:T(8,128)}) custom-call(s32[4,1,4096]{2,1,0:T(1,128)} %bitcast.114), custom_call_target="tpu_custom_call" | custom-call | tf_op jit(solution)/shard_map/route/pallas_call | solution.py:561
  76.5 2.5 convolution_convert_fusion.3.part
  79.0 32.5 %join.1 = (f32[256,512]{1,0:T(8,128)}, bf16[512,1024]{1,0:T(8,128)(2,1)}) custom-call(bf16[512,1024]{1,0:T(8,128)(2,1)} %convolution_convert_fusion.3.part, bf16[256,512]{1,0:T(8,128)(2,1)} %x.3, bf16[1,512]{1,0:T(2,128)(2,1)} %broadcast_in_dim.16.gain), custom_call_target="tpu_custom_call" | custom-call | tf_op jit(solution)/shard_map/join/pallas_call | solution.py:349
  111.5 4.1 convolution_convert_fusion.2.query_ref
  115.7 12.9 %weigh.1 = (f32[4,32,128]{2,1,0:T(8,128)}, bf16[4,32,128]{2,1,0:T(8,128)(2,1)}) custom-call(bf16[512,1024]{1,0:T(8,128)(2,1)} %convolution_convert_fusion.2.query_ref, bf16[2,256,512]{2,1,0:T(8,128)(2,1)} %dynamic-slice_bitcast_fusion.keys_ref, s32[4,1,4096]{2,1,0:T(1,128)} %bitcast.115, s32[4,1,4096]{2,1,0:T(1,128)} %get-tuple-element.48.rank_ref), custom_call_target="tpu_custom_call" | custom-call | tf_op jit(solution)/shard_map/weigh/pallas_call | solution.py:612
  128.6 1.4 copy.89
  129.9 2.6 fusion.108
  133.2 6.4 %copy.60 = bf16[2048,1024]{0,1:T(8,128)(2,1)} copy(bf16[2048,1024]{1,0:T(8,128)(2,1)} %values.1) | data formatting | bytes 8388608 | tf_op args[11]
  139.6 2.9 multiply_convert_fusion.6
  142.5 70.7 %read_memory.1 = (bf16[4,2,512,1024]{3,2,1,0:T(8,128)(2,1)}, bf16[4,2,512,2048]{3,2,1,0:T(8,128)(2,1)}, bf16[4,512,1024]{2,1,0:T(8,128)(2,1)}, bf16[4,512,1024]{2,1,0:T(8,128)(2,1)}, s32[32,4,128]{2,1,0:T(4,128)}) custom-call(bf16[512,256]{1,0:T(8,128)(2,1)} %get-tuple-element.86.grads, s32[32,4,128]{2,1,0:T(4,128)} %bitcast.118, f32[32,4,128]{2,1,0:T(4,128)} %bitcast.117, ...), custom_call_target="tpu_custom_call" | custom-call | tf_op jit(solution)/shard_map/read_memory/pallas_call | solution.py:812
  213.2 75.5 %back_memory.1 = (f32[512,256]{1,0:T(8,128)}, f32[32,4,128]{2,1,0:T(4,128)}, bf16[4,4,512,256]{3,2,1,0:T(8,128)(2,1)}, bf16[4,512,256]{2,1,0:T(8,128)(2,1)}) custom-call(bf16[4,2,512,1024]{3,2,1,0:T(8,128)(2,1)} %get-tuple-element.50.grads_all, bf16[4,512,1024]{2,1,0:T(8,128)(2,1)} %get-tuple-element.51.own_part, ...), custom_call_target="tpu_custom_call" | custom-call | tf_op jit(solution)/shard_map/back_memory/pallas_call | solution.py:1006
  288.7 1.7 copy.61
  290.4 11.7 %unweigh.1 = (bf16[256,512]{1,0:T(8,128)(2,1)}, bf16[256,512]{1,0:T(8,128)(2,1)}) custom-call(f32[4,128,32]{2,1,0:T(8,128)} %bitcast.113, s32[4,1,4096]{2,1,0:T(1,128)} %bitcast.116, s32[4,1,4096]{2,1,0:T(1,128)} %get-tuple-element.48.rank_ref, f32[4,32,128]{2,1,0:T(8,128)} %get-tuple-element.55.weights_ref), custom_call_target="tpu_custom_call" | custom-call | tf_op jit(solution)/shard_map/unweigh/pallas_call | solution.py:1074
  302.1 1.5 fusion.16
  303.6 1.4 fusion.17
  307.1 1.8 multiply_convert_fusion.4
  308.9 1.4 convolution_convert_fusion.1.out_part
  310.7 1.3 fusion.35
  312.0 1.5 add_convert_fusion.1.part
  313.5 40.2 %middle.1 = (bf16[256,512]{1,0:T(8,128)(2,1)}, f32[256,512]{1,0:T(8,128)}, bf16[512,1024]{1,0:T(8,128)(2,1)}, f32[1,512]{1,0:T(1,128)}) custom-call(bf16[512,1024]{1,0:T(8,128)(2,1)} %add_convert_fusion.1.part, bf16[512,1024]{1,0:T(8,128)(2,1)} %convolution_convert_fusion.1.out_part, f32[256,512]{1,0:T(8,128)} %get-tuple-element.59.hidden, ...), custom_call_target="tpu_custom_call" | custom-call | tf_op jit(solution)/shard_map/middle/pallas_call | solution.py:420
  353.7 2.6 convolution_convert_fusion.7
  356.4 1.3 convolution_convert_fusion.6
  357.8 2.6 convolution_convert_fusion.5
  360.7 2.0 convolution_convert_fusion.15
  376.3 1.5 pad_maximum_fusion.src
  377.8 5.3 pair_sum.1
  385.9 1.3 pad_maximum_fusion.1
  388.0 2.6 convolution_convert_fusion
  392.1 1.5 fusion.41
  393.6 1.5 fusion.39
  395.1 2.7 add_convert_fusion.part
  397.9 25.0 %last.1 = (f32[256,512]{1,0:T(8,128)}, f32[2,8,128]{2,1,0:T(8,128)}) custom-call(bf16[512,1024]{1,0:T(8,128)(2,1)} %add_convert_fusion.part, bf16[256,512]{1,0:T(8,128)(2,1)} %x.3, f32[256,512]{1,0:T(8,128)} %get-tuple-element.62.above, bf16[1,512]{1,0:T(2,128)(2,1)} %broadcast_in_dim.17.gain, f32[1,512]{1,0:T(1,128)} %get-tuple-element.63.other_gain), custom_call_target="tpu_custom_call" | custom-call | tf_op jit(solution)/shard_map/last/pallas_call | solution.py:489
  424.3 24.1 %convolution_bitcast_fusion = f32[2048,1024]{1,0:T(8,128)} fusion(bf16[4,2,512,2048]{3,2,1,0:T(8,128)(2,1)} %get-tuple-element.66, bf16[4,2,512,1024]{3,2,1,0:T(8,128)(2,1)} %get-tuple-element.50.grads_all), kind=kOutput, calls=%fused_computation | convolution fusion | flops 17179869184 | bytes 33554432 | tf_op jit(solution)/shard_map/dot_general | solution.py:1203
  448.4 24.8 %all-gather.2.cloned.1.call-done = bf16[2048,512]{1,0:T(8,128)(2,1)} async-done(((bf16[64,512]{1,0:T(8,128)(2,1)}), bf16[2048,512]{1,0:T(8,128)(2,1)}) %all-gather.2.cloned.1.call-update) | async-done | bytes 2097168 | tf_op jit(solution)/shard_map/all_gather | solution.py:1292
  473.2 4.2 convert.67
  477.4 101.7 %all-reduce.3.cloned.1.call-done = (bf16[3,512,256]{2,1,0:T(8,128)(2,1)}, bf16[256,512]{1,0:T(8,128)(2,1)}, bf16[512,1024]{1,0:T(8,128)(2,1)}, bf16[512,256]{1,0:T(8,128)(2,1)}, bf16[256,512]{1,0:T(8,128)(2,1)}) async-done(((bf16[3,512,256]{2,1,0:T(8,128)(2,1)}, bf16[256,512]{1,0:T(8,128)(2,1)}, bf16[512,1024]{1,0:T(8,128)(2,1)}, bf16[512,256]{1,0:T(8,128)(2,1)}, bf16[256,512]{1,0:T(8,128)(2,1)}), ...) | async-done | bytes 2621456 | tf_op jit(solution)/shard_map/psum | solution.py:1279
  579.1 2.9 convert_element_type.152
  582.0 1.3 convert_element_type.148
  (171 shorter events, 38.9 us)
Async XLA Ops:
  7.2 68.5 %copy-start = (bf16[4,2,256,512]{3,2,1,0:T(8,128)(2,1)S(1)}, bf16[4,2,256,512]{3,2,1,0:T(8,128)(2,1)}, u32[]{:S(2)}) copy-start(bf16[4,2,256,512]{3,2,1,0:T(8,128)(2,1)} %param.23) | copy-start | bytes 6291460
  7.2 31.9 %copy-start.36 = (bf16[1024]{0:T(1024)(128)(2,1)S(1)}, bf16[1024]{0:T(1024)(128)(2,1)}, u32[]{:S(2)}) copy-start(bf16[1024]{0:T(1024)(128)(2,1)} %param.16) | copy-start | bytes 6148
  7.2 383.5 %reduce-scatter.17.cloned.1.call-start = ((), (), s32[]{:S(2)}) async-start(), calls=%async_computation.11 | async-start | bytes 589824 | tf_op jit(solution)/shard_map/reduce_scatter | solution.py:1288
  42.8 12.2 %copy-start.12 = (bf16[512,256]{1,0:T(8,128)(2,1)}, bf16[512,256]{1,0:T(8,128)(2,1)S(1)}, u32[]{:S(2)}) copy-start(bf16[512,256]{1,0:T(8,128)(2,1)S(1)} %slice_bitcast_fusion.2) | copy-start | bytes 786436
  48.1 321.6 %copy-start.10 = (bf16[1024,256]{1,0:T(8,128)(2,1)}, bf16[1024,256]{1,0:T(8,128)(2,1)S(1)}, u32[]{:S(2)}) copy-start(bf16[1024,256]{1,0:T(8,128)(2,1)S(1)} %get-tuple-element.75) | copy-start | bytes 1572868
  57.0 2.2 copy-start.4
  59.3 1.6 copy-start.6
  61.4 1.6 copy-start.8
  62.1 14.3 %copy-start.39 = (bf16[512,64]{0,1:T(8,128)(2,1)}, bf16[512,64]{0,1:T(8,128)(2,1)S(1)}, u32[]{:S(2)}) copy-start(bf16[512,64]{0,1:T(8,128)(2,1)S(1)} %convolution_convert_fusion.18) | copy-start | bytes 196612
  63.5 1.6 copy-start.2
  64.1 12.4 %copy-start.41 = (bf16[512,64]{0,1:T(8,128)(2,1)}, bf16[512,64]{0,1:T(8,128)(2,1)S(1)}, u32[]{:S(2)}) copy-start(bf16[512,64]{0,1:T(8,128)(2,1)S(1)} %convolution_convert_fusion.17) | copy-start | bytes 196612
  65.6 1.4 copy-start.37
  115.7 16.9 %copy-start.35 = (s32[4,32,128]{2,1,0:T(8,128)S(1)}, s32[4,32,128]{2,1,0:T(8,128)}, u32[]{:S(2)}) copy-start(s32[4,32,128]{2,1,0:T(8,128)} %get-tuple-element.46) | copy-start | bytes 196612
  302.1 3.8 copy-start.34
  305.9 118.3 %reduce-scatter.9.cloned.1.call-start = ((), (), s32[]{:S(2)}) async-start(), calls=%async_computation.7 | async-start | bytes 786432 | tf_op jit(solution)/shard_map/reduce_scatter | solution.py:1276
  307.1 1.8 copy-start.23
  307.1 3.2 copy-start.29
  307.1 3.6 copy-start.27
  307.1 3.6 copy-start.38
  308.9 3.1 copy-start.20
  313.5 40.2 %copy-start.40 = (bf16[512,64]{0,1:T(8,128)(2,1)S(1)}, bf16[512,64]{0,1:T(8,128)(2,1)}, u32[]{:S(2)}) copy-start(bf16[512,64]{0,1:T(8,128)(2,1)} %copy-done.39) | copy-start | bytes 196612
  313.5 40.2 %copy-start.42 = (bf16[512,64]{0,1:T(8,128)(2,1)S(1)}, bf16[512,64]{0,1:T(8,128)(2,1)}, u32[]{:S(2)}) copy-start(bf16[512,64]{0,1:T(8,128)(2,1)} %copy-done.41) | copy-start | bytes 196612
  313.5 40.2 %copy-start.43 = (bf16[512,64]{0,1:T(8,128)(2,1)S(1)}, bf16[512,64]{0,1:T(8,128)(2,1)}, u32[]{:S(2)}) copy-start(bf16[512,64]{0,1:T(8,128)(2,1)} %convolution_convert_fusion.16) | copy-start | bytes 196612
  353.7 2.7 copy-start.18
  353.7 2.7 copy-start.21
  356.3 67.9 %reduce-scatter.13.cloned.1.call-start = ((), (), s32[]{:S(2)}) async-start(), calls=%async_computation.9 | async-start | bytes 786432 | tf_op jit(solution)/shard_map/reduce_scatter | solution.py:1276
  357.7 5.0 copy-start.5
  357.8 66.5 %reduce-scatter.15.cloned.1.call-start = ((), (), s32[]{:S(2)}) async-start(), calls=%async_computation.10 | async-start | bytes 786432 | tf_op jit(solution)/shard_map/reduce_scatter | solution.py:1276
  360.5 63.8 %reduce-scatter.7.cloned.1.call-start = ((), (), s32[]{:S(2)}) async-start(), calls=%async_computation.6 | async-start | bytes 2359296 | tf_op jit(solution)/shard_map/reduce_scatter | solution.py:1276
  364.0 1.6 copy-start.7
  366.9 1.6 copy-start.9
  371.3 1.6 copy-start.3
  377.8 5.3 copy-start.11
  377.8 5.8 copy-start.17
  385.9 1.5 copy-start.19
  385.9 1.9 copy-start.25
  385.9 2.1 copy-start.28
  387.3 37.0 %reduce-scatter.11.cloned.1.call-start = ((), (), s32[]{:S(2)}) async-start(), calls=%async_computation.8 | async-start | bytes 3145728 | tf_op jit(solution)/shard_map/reduce_scatter | solution.py:1276
  390.6 3.0 copy-start.16
  390.6 82.6 %all-gather.2.cloned.1.call-start = ((), (), s32[]{:S(2)}) async-start(), calls=%async_computation.12 | async-start | bytes 2162688 | tf_op jit(solution)/shard_map/all_gather | solution.py:1292
  391.4 187.7 %all-reduce.3.cloned.1.call-start = ((), (), s32[]{:S(2)}) async-start(), calls=%async_computation.13 | async-start | bytes 5242880 | tf_op jit(solution)/shard_map/psum | solution.py:1279
  579.1 2.9 copy-start.22
  579.1 4.2 copy-start.32
  582.0 2.2 copy-start.31
  582.0 3.0 copy-start.30
  582.0 3.9 copy-start.33
  582.0 4.6 copy-start.26
  582.0 5.3 copy-start.1
  (4 other events, 4.8 us)
Sparse Core Ops, SparseCore 0:
  306.0 29.8 reduce-scatter.16
  356.4 7.0 reduce-scatter.8
  365.8 9.0 reduce-scatter.12
  377.0 9.0 reduce-scatter.14
  388.7 10.0 reduce-scatter.6
  401.5 11.0 reduce-scatter.10
  415.6 57.6 all-gather.1
  476.0 103.0 all-reduce.2

commit v4 on v3

--- a/solution.py
+++ b/solution.py
@@ -386,16 +386,250 @@
     return grad, jnp.sum(normed_grad * unit, axis=0, keepdims=True)
 
 
-def middle_kernel(
-    sizes, part, out_part, hidden, dy, gain, output, grad, grad_all, gain_grad,
-    landing, out_landing, mine, theirs, block, ssend, srecv, osend, orecv, gsend, grecv, psend, precv,
-):
+def slab(ref, dim, index, count):
+    size = ref.shape[dim] // count
+    window = [slice(None)] * len(ref.shape)
+    window[dim] = pl.ds(pl.multiple_of(index * size, size), size)
+    return ref.at[tuple(window)]
+
+
+def add_into(target, addend):
+    target[...] = (target[...].astype(jnp.float32) + addend[...].astype(jnp.float32)).astype(
+        target.dtype
+    )
+
+
+class PairSum:
+    def __init__(self, spot, sizes, terms, dims, halves, landings, send, recv):
+        self.col, self.cols = spot[2], sizes[2]
+        self.terms, self.dims, self.halves, self.landings = terms, dims, halves, landings
+        self.copies = [
+            remote(
+                slab(term, dim, 1 - spot[2], sizes[2]), landing, send.at[n], recv.at[n],
+                (spot[0], spot[1], 1 - spot[2]),
+            )
+            for n, (term, dim, landing) in enumerate(zip(terms, dims, landings))
+        ]
+
+    def start(self):
+        for copy in self.copies:
+            copy.start()
+
+    def finish(self):
+        for copy, term, dim, half, landing in zip(
+            self.copies, self.terms, self.dims, self.halves, self.landings
+        ):
+            copy.wait()
+            own = slab(term, dim, self.col, self.cols)
+            half[...] = (own[...].astype(jnp.float32) + landing[...].astype(jnp.float32)).astype(
+                half.dtype
+            )
+
+
+class LineReduce:
+    def __init__(self, spot, sizes, arrays, dims, below, above, sems):
+        self.spot, self.count = spot, sizes[0]
+        self.arrays, self.dims, self.below, self.above = arrays, dims, below, above
+        self.up_send, self.up_recv, self.down_send, self.down_recv = sems
+
+    def copy(self, n, k, up):
+        dp, row, col = self.spot
+        landing = self.below[n] if up else self.above[n]
+        send, recv = (
+            (self.up_send, self.up_recv) if up else (self.down_send, self.down_recv)
+        )
+        dim = self.dims[n]
+        return remote(
+            slab(self.arrays[n], dim, k, self.count),
+            slab(landing, dim, k, self.count),
+            send.at[n, k],
+            recv.at[n, k],
+            (jnp.clip(dp + (1 if up else -1), 0, self.count - 1), row, col),
+        )
+
+    def send(self, k, up):
+        for n in range(len(self.arrays)):
+            self.copy(n, k, up).start()
+
+    def start(self):
+        dp, last = self.spot[0], self.count - 1
+
+        @pl.when(dp == 0)
+        def _():
+            lax.fori_loop(0, last, lambda i, c: (self.send(last - i, True), c)[1], 0)
+
+        @pl.when(dp == last)
+        def _():
+            lax.fori_loop(0, last, lambda i, c: (self.send(i, False), c)[1], 0)
+
+    def take(self, k, up):
+        for n, (array, dim) in enumerate(zip(self.arrays, self.dims)):
+            landing = slab((self.below if up else self.above)[n], dim, k, self.count)
+            arrived(landing, (self.up_recv if up else self.down_recv).at[n, k])
+            add_into(slab(array, dim, k, self.count), landing)
+
+    def event(self, time):
+        dp, last = self.spot[0], self.count - 1
+
+        @pl.when(jnp.logical_and(dp > 0, time >= dp))
+        def _():
+            k = dp + last - time
+            self.take(k, True)
+            pl.when(k > dp)(lambda: self.send(k, True))
+
+        @pl.when(jnp.logical_and(dp < last, time >= last - dp))
+        def _():
+            k = time - (last - dp)
+            self.take(k, False)
+            pl.when(k < dp)(lambda: self.send(k, False))
+
+    def events(self):
+        lax.fori_loop(1, self.count, lambda time, c: (self.event(time), c)[1], 0)
+
+    def finish(self):
+        dp = self.spot[0]
+
+        def one(k, carry):
+            @pl.when(dp < k)
+            def _():
+                for n in range(len(self.arrays)):
+                    self.copy(n, k, True).wait_send()
+
+            @pl.when(dp > k)
+            def _():
+                for n in range(len(self.arrays)):
+                    self.copy(n, k, False).wait_send()
+
+            return carry
+
+        lax.fori_loop(0, self.count, one, 0)
+
+
+class LineGather:
+    def __init__(self, spot, sizes, arrays, dims, sems):
+        self.spot, self.count = spot, sizes[0]
+        self.arrays, self.dims = arrays, dims
+        self.up_send, self.down_send, self.recv = sems
+
+    def copy(self, n, k, up):
+        dp, row, col = self.spot
+        part = slab(self.arrays[n], self.dims[n], k, self.count)
+        return remote(
+            part,
+            part,
+            (self.up_send if up else self.down_send).at[n, k],
+            self.recv.at[n, k],
+            (jnp.clip(dp + (1 if up else -1), 0, self.count - 1), row, col),
+        )
+
+    def send(self, k, up):
+        dp = self.spot[0]
+
+        @pl.when(dp < self.count - 1 if up else dp > 0)
+        def _():
+            for n in range(len(self.arrays)):
+                self.copy(n, k, up).start()
+
+    def start(self):
+        self.send(self.spot[0], True)
+        self.send(self.spot[0], False)
+
+    def take(self, k):
+        for n, (array, dim) in enumerate(zip(self.arrays, self.dims)):
+            arrived(slab(array, dim, k, self.count), self.recv.at[n, k])
+
+    def event(self, time):
+        dp = self.spot[0]
+
+        @pl.when(dp - time >= 0)
+        def _():
+            self.take(dp - time)
+            self.send(dp - time, True)
+
+        @pl.when(dp + time < self.count)
+        def _():
+            self.take(dp + time)
+            self.send(dp + time, False)
+
+    def events(self):
+        lax.fori_loop(1, self.count, lambda time, c: (self.event(time), c)[1], 0)
+
+    def finish(self):
+        dp, last = self.spot[0], self.count - 1
+
+        def one(k, carry):
+            @pl.when(jnp.logical_and(k <= dp, dp < last))
+            def _():
+                for n in range(len(self.arrays)):
+                    self.copy(n, k, True).wait_send()
+
+            @pl.when(jnp.logical_and(k >= dp, dp > 0))
+            def _():
+                for n in range(len(self.arrays)):
+                    self.copy(n, k, False).wait_send()
+
+            return carry
+
+        lax.fori_loop(0, self.count, one, 0)
+
+
+def line_sems(sizes, arrays, kinds):
+    return [DMA((arrays, sizes[0])) for _ in range(kinds)]
+
+
+def greet_cross(spot, sizes):
+    barrier = pltpu.get_barrier_semaphore()
+    dp, row, col = spot
+    dps, rows, cols = sizes
+    for j in range(rows):
+        for k in range(cols):
+            if j + k > 0:
+                pl.semaphore_signal(
+                    barrier,
+                    inc=1,
+                    device_id=(dp, lax.rem(row + j, rows), lax.rem(col + k, cols)),
+                    device_id_type=MESH,
+                )
+    for j in (1, dps - 1):
+        pl.semaphore_signal(
+            barrier, inc=1, device_id=(lax.rem(dp + j, dps), row, col), device_id_type=MESH
+        )
+    pl.semaphore_wait(barrier, rows * cols + 1)
+
+
+FIRST_DIMS = (0, 0, 0, 0)
+FIRST_COLS = (0, 0, 1, 0)
+LAST_DIMS = (1, 0)
+LAST_COLS = (1, 1)
+
+
+def halved(shape, dim, cols):
+    shape = list(shape)
+    shape[dim] //= cols
+    return tuple(shape)
+
+
+def middle_kernel(sizes, *refs):
+    part, out_part, hidden, dy, gain = refs[:5]
+    terms = refs[5:9]
+    output, grad, grad_all, gain_grad = refs[9:13]
+    shards = refs[13:17]
+    landing, out_landing, mine, theirs, block = refs[17:22]
+    halves, pair_land, below, above = refs[22:26], refs[26:30], refs[30:34], refs[34:38]
+    (
+        ssend, srecv, osend, orecv, gsend, grecv, psend, precv, hsend, hrecv, *line
+    ) = refs[38:]
     spot = here()
-    greet_plane(spot, sizes)
+    greet_cross(spot, sizes)
     scatter = Scatter(spot, sizes, part, landing, ssend, srecv)
     scatter.start()
+    pair = PairSum(spot, sizes, terms, FIRST_COLS, halves, pair_land, hsend, hrecv)
+    pair.start()
     out_scatter = Scatter(spot, sizes, out_part, out_landing, osend, orecv)
     out_scatter.start()
+    pair.finish()
+    reduce = LineReduce(spot, sizes, halves, FIRST_DIMS, below, above, line)
+    reduce.start()
     scatter.wait()
     total, gains = norm_back(sizes, spot, landing, hidden, dy, gain, mine, theirs, psend, precv)
     gain_grad[...] = gains
@@ -403,30 +637,38 @@
     block[...] = total.astype(jnp.bfloat16)
     gather = Gather(spot, sizes, block, grad_all, gsend, grecv)
     gather.start()
+    reduce.event(1)
     out_scatter.wait()
     result = hidden[...]
     for q in range(sizes[1]):
         result = result + out_landing[q].astype(jnp.float32)
     output[...] = result.astype(jnp.bfloat16)
+    lax.fori_loop(2, sizes[0], lambda time, c: (reduce.event(time), c)[1], 0)
+    for half, dim, shard in zip(halves, FIRST_DIMS, shards):
+        shard[...] = slab(half, dim, spot[0], sizes[0])[...]
     scatter.wait_send()
     out_scatter.wait_send()
     gather.wait()
-
-
-def middle(sizes, part, out_part, hidden, dy, gain):
+    reduce.finish()
+
+
+def middle(sizes, part, out_part, hidden, dy, gain, terms):
     tokens, width = hidden.shape
-    rows = sizes[1]
+    dps, rows, cols = sizes
     low, wide = jnp.bfloat16, jnp.float32
+    halves = [halved(t.shape, d, cols) for t, d in zip(terms, FIRST_COLS)]
+    shards = [halved(h, d, dps) for h, d in zip(halves, FIRST_DIMS)]
     return pl.pallas_call(
         functools.partial(middle_kernel, sizes),
-        in_specs=[VMEM] * 5,
-        out_specs=[VMEM] * 4,
+        in_specs=[VMEM] * 9,
+        out_specs=[VMEM] * 8,
         out_shape=[
             jax.ShapeDtypeStruct((tokens, width), low),
             jax.ShapeDtypeStruct((tokens, width), wide),
             jax.ShapeDtypeStruct(part.shape, low),
             jax.ShapeDtypeStruct((1, width), wide),
-        ],
+        ]
+        + [jax.ShapeDtypeStruct(s, low) for s in shards],
         scratch_shapes=[
             pltpu.VMEM((rows, tokens, width), low),
             pltpu.VMEM((rows, tokens, width), low),
@@ -434,30 +676,99 @@
             pltpu.VMEM((2, tokens, 128), wide),
             pltpu.VMEM((tokens, width), low),
         ]
+        + [pltpu.VMEM(h, low) for h in halves] * 4
         + plane_sems(sizes) * 3
-        + [DMA, DMA],
+        + [DMA, DMA, DMA((4,)), DMA((4,))]
+        + line_sems(sizes, 4, 4),
         compiler_params=pltpu.CompilerParams(collective_id=4, has_side_effects=True),
         name="middle",
-    )(part, out_part, hidden, dy, gain[None])
-
-
-def last_kernel(
-    sizes, part, x, above, gain, other_gain, grad, gain_sums,
-    landing, mine, theirs, own_gain, gain_landing, ssend, srecv, psend, precv, bsend, brecv,
-):
+    )(part, out_part, hidden, dy, gain[None], *terms)
+
+
+def last_kernel(sizes, *refs):
+    part, x, above_grad, gain, other_gain = refs[:5]
+    shards, terms = refs[5:9], refs[9:11]
+    table, grads_all = refs[11:13]
+    grad, gain_sums, row_grads = refs[13:16]
+    firsts, lasts, keys_all = refs[16:20], refs[20:22], refs[22]
+    landing, mine, theirs, own_gain, gain_landing, tables, chunks = refs[23:30]
+    halves, pair_land, below, above = refs[30:32], refs[32:34], refs[34:36], refs[36:38]
+    (
+        ssend, srecv, psend, precv, bsend, brecv, hsend, hrecv, tsem, csem,
+        xsend, xrecv, kxsend, kxrecv, *line
+    ) = refs[38:]
     spot = here()
-    count = sizes[0] * sizes[1] * sizes[2]
+    dp, row, col = spot
+    dps, rows, cols = sizes
+    count = dps * rows * cols
     me = index_of(spot, sizes)
+    loads = dps * cols
+
+    def load(index):
+        slot = lax.rem(index, 2)
+        where = (lax.div(index, cols), lax.rem(index, cols))
+        return (
+            pltpu.make_async_copy(table.at[where], tables.at[slot], tsem.at[slot]),
+            pltpu.make_async_copy(grads_all.at[where], chunks.at[slot], csem.at[slot]),
+        )
+
+    for copy in load(0):
+        copy.start()
     greet_all(spot, sizes)
     scatter = Scatter(spot, sizes, part, landing, ssend, srecv)
     scatter.start()
+    pair = PairSum(spot, sizes, terms, LAST_COLS, halves, pair_land, hsend, hrecv)
+    pair.start()
+    for first, dim, shard in zip(firsts, FIRST_DIMS, shards):
+        slab(first, dim, dp, dps)[...] = shard[...]
+    gather = LineGather(spot, sizes, firsts, FIRST_DIMS, line[:3])
+    gather.start()
+    pair.finish()
+    reduce = LineReduce(spot, sizes, halves, LAST_DIMS, below, above, line[3:7])
+    reduce.start()
+
+    def product(index):
+        slot = lax.rem(index, 2)
+        for copy in load(index):
+            copy.wait()
+
+        @pl.when(index + 1 < loads)
+        def _():
+            for copy in load(index + 1):
+                copy.start()
+
+        def strip(n, carry):
+            columns = pl.ds(pl.multiple_of(n * 256, 256), 256)
+            term = lax.dot_general(
+                tables[slot, :, columns],
+                chunks[slot],
+                (((0,), (0,)), ((), ())),
+                preferred_element_type=jnp.float32,
+            )
+
+            @pl.when(index == 0)
+            def _():
+                row_grads[columns] = term
+
+            @pl.when(index > 0)
+            def _():
+                row_grads[columns] = row_grads[columns] + term
+
+            return carry
+
+        lax.fori_loop(0, tables.shape[2] // 256, strip, 0)
+
+    def products(first, end):
+        lax.fori_loop(first, end, lambda index, c: (product(index), c)[1], 0)
+
+    products(0, loads // 4)
     scatter.wait()
-    total, gains = norm_back(sizes, spot, landing, x, above, gain, mine, theirs, psend, precv)
+    total, gains = norm_back(sizes, spot, landing, x, above_grad, gain, mine, theirs, psend, precv)
     lines = gains.shape[1] // 128
-    for line in range(lines):
-        columns = slice(line * 128, (line + 1) * 128)
-        own_gain[line : line + 1] = gains[:, columns]
-        own_gain[lines + line : lines + line + 1] = other_gain[:, columns]
+    for line_index in range(lines):
+        columns = slice(line_index * 128, (line_index + 1) * 128)
+        own_gain[line_index : line_index + 1] = gains[:, columns]
+        own_gain[lines + line_index : lines + line_index + 1] = other_gain[:, columns]
 
     def tell(step, carry):
         device = device_of(lax.rem(me + step, count), sizes)
@@ -467,45 +778,102 @@
     lax.fori_loop(1, count, tell, 0)
     gain_landing[me] = own_gain[...]
     grad[...] = total
+    gather.event(1)
+    reduce.event(1)
+    products(loads // 4, loads // 2)
+    lax.fori_loop(2, dps, lambda time, c: (gather.event(time), reduce.event(time), c)[2], 0)
+    for first, half, dim in zip(lasts, halves, LAST_DIMS):
+        slab(first, dim, dp, dps)[...] = slab(half, dim, dp, dps)[...]
+    final = LineGather(spot, sizes, lasts, LAST_DIMS, line[7:10])
+    final.start()
+    keys = firsts[3]
+
+    def sideways(k):
+        return remote(
+            keys, keys_all.at[row, col], xsend, xrecv.at[rows - k],
+            (dp, lax.rem(row + k, rows), col),
+        )
+
+    def cross(src, k):
+        there = keys_all.at[lax.rem(row + k, rows), col]
+        return remote(src, there, kxsend, kxrecv, (dp, row, 1 - col))
+
+    for k in range(1, rows):
+        sideways(k).start()
+    cross(keys, 0).start()
+    keys_all[row, col] = keys[...]
+    products(loads // 2, 3 * loads // 4)
+    final.event(1)
+    for k in range(1, rows):
+        landed = keys_all.at[lax.rem(row + k, rows), col]
+        arrived(landed, xrecv.at[k])
+        cross(landed, k).start()
+    products(3 * loads // 4, loads)
+    lax.fori_loop(2, dps, lambda time, c: (final.event(time), c)[1], 0)
+    arrived(keys_all.at[:, 1 - col], kxrecv)
     scatter.wait_send()
     arrived(gain_landing.at[pl.ds(0, count - 1)], brecv)
-    for col in range(sizes[2]):
+    for c in range(cols):
 
         def add(index, sums):
-            return sums + gain_landing[index * sizes[2] + col]
-
-        gain_sums[col] = lax.fori_loop(
-            0, sizes[0] * sizes[1], add, jnp.zeros(own_gain.shape, jnp.float32)
-        )
+            return sums + gain_landing[index * cols + c]
+
+        gain_sums[c] = lax.fori_loop(0, dps * rows, add, jnp.zeros(own_gain.shape, jnp.float32))
     arrived(gain_landing.at[pl.ds(0, count - 1)], bsend)
-
-
-def last(sizes, part, x, above, gain, other_gain):
+    arrived(keys_all.at[:, col], kxsend)
+    arrived(keys_all.at[pl.ds(0, rows - 1), col], xsend)
+    gather.finish()
+    reduce.finish()
+    final.finish()
+
+
+def last(sizes, part, x, above, gain, other_gain, shards, terms, table, grads_all):
     tokens, width = x.shape
-    rows = sizes[1]
+    dps, rows, cols = sizes
     lines = 2 * width // 128
-    count = sizes[0] * sizes[1] * sizes[2]
-    wide = jnp.float32
+    count = dps * rows * cols
+    low, wide = jnp.bfloat16, jnp.float32
+    shape = jax.ShapeDtypeStruct
+
+    def grown(shard, dim):
+        full = list(shard.shape)
+        full[dim] *= dps
+        return tuple(full)
+
+    firsts = [grown(s, d) for s, d in zip(shards, FIRST_DIMS)]
+    halves = [halved(t.shape, d, cols) for t, d in zip(terms, LAST_COLS)]
+    rows_dev = table.shape[-1]
+    features = grads_all.shape[-1]
+    chunk = table.shape[2]
     return pl.pallas_call(
         functools.partial(last_kernel, sizes),
-        in_specs=[VMEM] * 5,
-        out_specs=[VMEM] * 2,
+        in_specs=[VMEM] * 11 + [ANY] * 2,
+        out_specs=[VMEM] * 10,
         out_shape=[
-            jax.ShapeDtypeStruct((tokens, width), wide),
-            jax.ShapeDtypeStruct((sizes[2], lines, 128), wide),
-        ],
+            shape((tokens, width), wide),
+            shape((cols, lines, 128), wide),
+            shape((rows_dev, features), wide),
+        ]
+        + [shape(s, low) for s in firsts + halves]
+        + [shape((rows, cols) + firsts[3], low)],
         scratch_shapes=[
-            pltpu.VMEM((rows, tokens, width), jnp.bfloat16),
+            pltpu.VMEM((rows, tokens, width), low),
             pltpu.VMEM((2, tokens, 128), wide),
             pltpu.VMEM((2, tokens, 128), wide),
             pltpu.VMEM((lines, 128), wide),
             pltpu.VMEM((count, lines, 128), wide),
+            pltpu.VMEM((2, chunk, rows_dev), low),
+            pltpu.VMEM((2, chunk, features), low),
         ]
+        + [pltpu.VMEM(h, low) for h in halves] * 4
         + plane_sems(sizes)
-        + [DMA, DMA, DMA, DMA],
+        + [DMA, DMA, DMA, DMA, DMA((2,)), DMA((2,)), DMA((2,)), DMA((2,))]
+        + [DMA, DMA((rows,)), DMA, DMA]
+        + line_sems(sizes, 4, 3)
+        + line_sems(sizes, 2, 7),
         compiler_params=pltpu.CompilerParams(collective_id=5, has_side_effects=True),
         name="last",
-    )(part, x, above, gain[None], other_gain)
+    )(part, x, above, gain[None], other_gain, *shards, *terms, table, grads_all)
 
 
 def allowed_mask(query_count, key_count, first_pos, prefix_len):
@@ -1107,9 +1475,6 @@
         sizes, grad_memory, meta, slots, values
     )
     memory, back = back_memory(sizes, grads_all, own_part, other_part, meta_in, values.T)
-    grad_values = dense_tn(
-        table.reshape(-1, rows_dev), grads_all.reshape(-1, grads_all.shape[-1])
-    )
     first_t, second_t = unweigh(
         jnp.transpose(back, (1, 2, 0))[:, :cap], flat, rank, weights, rows_dev, owners
     )
@@ -1128,7 +1493,7 @@
             jnp.dot(second_t, query_rows[:, HALF:], preferred_element_type=jnp.float32),
         ]
     )
-    return memory, grad_query, grad_values, grad_keys
+    return memory, grad_query, grad_keys, table, grads_all
 
 
 def head_scores(query_head, key_head, allowed):
@@ -1246,7 +1611,7 @@
     silu_gate = gate_value * sigmoid_gate
     grad_gated = dense_nt(dy_own, proj_w)
     grad_memory = (grad_gated * silu_gate).astype(low)
-    memory, grad_query, grad_values, grad_keys = memory_all(
+    memory, grad_query, grad_keys, table, grads_all = memory_all(
         query_rows, grad_memory, picks, subkeys, values
     )
     gated_value = (memory * silu_gate).astype(low)
@@ -1255,8 +1620,14 @@
         grad_gated * memory * sigmoid_gate * (1.0 + gate_value * (1.0 - sigmoid_gate))
     ).astype(low)
     grad_part = (dense_nt(grad_query, query_w) + dense_nt(grad_gate, gate_w)).astype(low)
-    output, grad_hidden, grad_hidden_all, gain_two_grad = middle(
-        sizes, grad_part, out_part, hidden, cotangent, gain_two
+    first_terms = [
+        dense_tn(normed_two, grad_query).astype(low),
+        dense_tn(normed_two, grad_gate).astype(low),
+        dense_tn(gated_value, dy_own).astype(low),
+        grad_keys.reshape(-1, HALF).astype(low),
+    ]
+    output, grad_hidden, grad_hidden_all, gain_two_grad, *shards = middle(
+        sizes, grad_part, out_part, hidden, cotangent, gain_two, first_terms
     )
     grad_attended = dense_nt(grad_hidden_all, attn_w).astype(low)
     grad_query_own, grad_kv_part = attend_backward(
@@ -1267,43 +1638,31 @@
     x_part = (
         dense_nt(grad_q, qkv_w[0]) + dense_nt(grad_kv[0], qkv_w[1]) + dense_nt(grad_kv[1], qkv_w[2])
     ).astype(low)
-    grad_inputs, gain_sums = last(sizes, x_part, inputs, grad_hidden, gain_one, gain_two_grad)
+    last_terms = [
+        jnp.stack([dense_tn(normed_one, part) for part in (grad_q, grad_kv[0], grad_kv[1])]).astype(low),
+        dense_tn(attended, grad_hidden_all).astype(low),
+    ]
+    (
+        grad_inputs, gain_sums, grad_values,
+        grad_w_query, grad_w_gate, grad_w_proj, _, grad_w_qkv, grad_w_attn_out, grad_subkeys,
+    ) = last(
+        sizes, x_part, inputs, grad_hidden, gain_one, gain_two_grad, shards, last_terms, table, grads_all
+    )
     gain_rows = gain_sums.reshape(sizes[2], 2, width_part)
     grad_gain_one = gain_rows[:, 0].reshape(-1)
     grad_gain_two = gain_rows[:, 1].reshape(-1)
 
-    def col_sum(grad, dim):
-        return lax.psum_scatter(grad.astype(low), "col", scatter_dimension=dim, tiled=True)
-
-    def weight_sum(grad, dim):
-        return lax.psum(col_sum(grad, dim), "dp").astype(jnp.float32)
-
-    grad_w_proj = weight_sum(dense_tn(gated_value, dy_own), 1)
-    grad_w_query = weight_sum(dense_tn(normed_two, grad_query), 0)
-    grad_w_gate = weight_sum(dense_tn(normed_two, grad_gate), 0)
-    grad_w_attn_out = weight_sum(dense_tn(attended, grad_hidden_all), 1)
-    grad_w_qkv = weight_sum(
-        jnp.stack([dense_tn(normed_one, part) for part in (grad_q, grad_kv[0], grad_kv[1])]), 1
-    )
-    grad_keys = lax.psum_scatter(
-        grad_keys.astype(low).reshape(-1, HALF), ("dp", "col"), scatter_dimension=0, tiled=True
-    )
-    grad_subkeys = (
-        lax.all_gather(grad_keys, ("row", "dp", "col"), axis=0, tiled=True)
-        .astype(jnp.float32)
-        .reshape(subkeys.shape)
-    )
     return (
         output,
         grad_inputs,
         grad_gain_one,
-        grad_w_qkv,
-        grad_w_attn_out,
+        grad_w_qkv.astype(jnp.float32),
+        grad_w_attn_out.astype(jnp.float32),
         grad_gain_two,
-        grad_w_query,
-        grad_w_gate,
-        grad_w_proj,
-        grad_subkeys,
+        grad_w_query.astype(jnp.float32),
+        grad_w_gate.astype(jnp.float32),
+        grad_w_proj.astype(jnp.float32),
+        grad_subkeys.astype(jnp.float32),
         grad_values,
     )
 

time: 604 us -> 492 us (0.81)
  waiting for transfers between devices: 127 us -> 0 us
  Pallas kernels: 315 us -> 377 us
  matrix products: 87.7 us -> 48.6 us
  between operations: 16 us -> 2.53 us
    psum x1 -> x0, waiting for transfers between devices: 102 us -> none  [weight_sum(): return lax.psum(col_sum(grad, dim), 'dp').astype(jnp.float32)]
    pallas_call x1, Pallas kernels: 25 us -> 81.2 us  [last(): pl.pallas_call(functools.partial(last_kernel, sizes), in_specs=[VMEM] * 1...]
    all_gather x1 -> x0, waiting for transfers between devices: 24.8 us -> none  [per_device(): lax.all_gather(grad_keys, ('row', 'dp', 'col'), axis=0, tiled=True)]
    dot_general x8 -> x7, matrix products: 35.5 us -> 11 us  [dense_tn(): lax.dot_general(left, right, (((0,), (0,)), ((), ())), preferred_element_...]
    convert_element_type x5 -> x6, other arithmetic: 6.69 us -> 12.2 us  [the longest x1 2.71 us: per_device(): grad_subkeys.astype(jnp.float32)]
    unnamed x91 -> x92, local copies, waits for them, and re-layouts: 13.1 us -> 17.5 us
  transfers between devices with their start and end apart: 8 -> 0, of which waited for: 2 -> 0; matrix products, arithmetic and copies ran while one was open for 12% -> 0% of each run, Pallas kernels for 12% -> 0%
where the time goes in v4:
time: 492 us; the launch traced here: 483 us
  Pallas kernels  377 us (77%)
  matrix products  48.6 us (10%)
  local copies, waits for them, and re-layouts  29.8 us (6%)
  other arithmetic  25.3 us (5%)
    pallas_call x1, Pallas kernels, last(): pl.pallas_call(functools.partial(last_kernel, sizes), in_specs=[VMEM] * 1...  81.2 us
    pallas_call x1, Pallas kernels, back_memory(): pl.pallas_call(functools.partial(back_kernel, sizes, blocks), in_specs=[A...  75.5 us
    pallas_call x1, Pallas kernels, read_memory(): pl.pallas_call(functools.partial(read_kernel, sizes, blocks), in_specs=[V...  70.7 us
    pallas_call x1, Pallas kernels, middle(): pl.pallas_call(functools.partial(middle_kernel, sizes), in_specs=[VMEM] *...  42.7 us
    pallas_call x1, Pallas kernels, join(): pl.pallas_call(functools.partial(join_kernel, sizes), in_specs=[VMEM] * 3...  32.5 us
    pallas_call x1, Pallas kernels, start_all(): pl.pallas_call(functools.partial(start_kernel, sizes), in_specs=[VMEM] *...  30.2 us
    unnamed x92, local copies, waits for them, and re-layouts  17.5 us
    pallas_call x1, Pallas kernels, weigh(): pl.pallas_call(functools.partial(weigh_kernel, rows_dev, owners, cap), gr...  12.4 us

profile of v4, /device:TPU:0, one launch (start us, length us, event | category | flops | bytes accessed | tf_op | source)
XLA Modules:
  0.0 482.9 jit_solution(12752147409109910591)
XLA Ops:
  6.3 6.5 %route.1 = (s32[4,1,4096]{2,1,0:T(1,128)}, s32[4,32,128]{2,1,0:T(8,128)}) custom-call(s32[4,1,4096]{2,1,0:T(1,128)} %bitcast.107), custom_call_target="tpu_custom_call" | custom-call | tf_op jit(solution)/shard_map/route/pallas_call | solution.py:929
  12.9 1.5 copy.85
  15.2 6.4 %copy.58 = bf16[2048,1024]{0,1:T(8,128)(2,1)} copy(bf16[2048,1024]{1,0:T(8,128)(2,1)} %values.1) | data formatting | bytes 8388608 | tf_op args[11]
  21.6 30.2 %start_all.1 = (bf16[512,1024]{1,0:T(8,128)(2,1)}, bf16[512,1024]{1,0:T(8,128)(2,1)}, bf16[3,1024,256]{2,1,0:T(8,128)(2,1)}, bf16[1024,1024]{1,0:T(8,128)(2,1)},...) custom-call(bf16[256,512]{1,0:T(8,128)(2,1)} %refs_1_.3, ...), custom_call_target="tpu_custom_call" | custom-call | tf_op jit(solution)/shard_map/start_all/pallas_call | solution.py:243
  51.9 1.5 fusion
  53.4 2.8 fusion.12
  56.2 0.9 slice.145.src
  57.1 4.0 swap_tokens.1
  61.0 1.3 slice_bitcast_fusion
  69.3 0.9 copy-done.4
  73.4 1.4 convolution_convert_fusion.3.part
  74.9 32.5 %join.1 = (f32[256,512]{1,0:T(8,128)}, bf16[512,1024]{1,0:T(8,128)(2,1)}) custom-call(bf16[512,1024]{1,0:T(8,128)(2,1)} %convolution_convert_fusion.3.part, bf16[256,512]{1,0:T(8,128)(2,1)} %refs_1_.3, bf16[1,512]{1,0:T(2,128)(2,1)} %broadcast_in_dim.16.gain.refs_4_), custom_call_target="tpu_custom_call" | custom-call | tf_op jit(solution)/shard_map/join/pallas_call | solution.py:349
  107.4 1.9 fusion.108
  109.4 1.4 multiply_convert_fusion.6
  110.8 1.0 copy-done.31
  111.8 2.2 convolution_convert_fusion.2.query_ref
  114.0 12.4 %weigh.1 = (f32[4,32,128]{2,1,0:T(8,128)}, bf16[4,32,128]{2,1,0:T(8,128)(2,1)}) custom-call(bf16[512,1024]{1,0:T(8,128)(2,1)} %convolution_convert_fusion.2.query_ref, bf16[2,256,512]{2,1,0:T(8,128)(2,1)} %dynamic-slice_bitcast_fusion.keys_ref, s32[4,1,4096]{2,1,0:T(1,128)} %bitcast.108, s32[4,1,4096]{2,1,0:T(1,128)} %get-tuple-element.59.rank_ref), custom_call_target="tpu_custom_call" | custom-call | tf_op jit(solution)/shard_map/weigh/pallas_call | solution.py:980
  126.4 1.4 copy.84
  127.8 70.7 %read_memory.1 = (bf16[4,2,512,1024]{3,2,1,0:T(8,128)(2,1)}, bf16[4,2,512,2048]{3,2,1,0:T(8,128)(2,1)}, bf16[4,512,1024]{2,1,0:T(8,128)(2,1)}, bf16[4,512,1024]{2,1,0:T(8,128)(2,1)}, s32[32,4,128]{2,1,0:T(4,128)}) custom-call(bf16[512,256]{1,0:T(8,128)(2,1)} %get-tuple-element.103.grads, s32[32,4,128]{2,1,0:T(4,128)} %bitcast.110, f32[32,4,128]{2,1,0:T(4,128)} %bitcast.111, ...), custom_call_target="tpu_custom_call" | custom-call | tf_op jit(solution)/shard_map/read_memory/pallas_call | solution.py:1180
  198.5 75.5 %back_memory.1 = (f32[512,256]{1,0:T(8,128)}, f32[32,4,128]{2,1,0:T(4,128)}, bf16[4,4,512,256]{3,2,1,0:T(8,128)(2,1)}, bf16[4,512,256]{2,1,0:T(8,128)(2,1)}) custom-call(bf16[4,2,512,1024]{3,2,1,0:T(8,128)(2,1)} %get-tuple-element.61.grads_all.refs_12_, bf16[4,512,1024]{2,1,0:T(8,128)(2,1)} %get-tuple-element.62.own_part, ...), custom_call_target="tpu_custom_call" | custom-call | tf_op jit(solution)/shard_map/back_memory/pallas_call | solution.py:1374
  274.1 2.4 multiply_convert_fusion.4
  276.5 1.3 convolution_convert_fusion.9.refs_7_
  277.8 0.8 copy.59
  278.6 11.7 %unweigh.1 = (bf16[256,512]{1,0:T(8,128)(2,1)}, bf16[256,512]{1,0:T(8,128)(2,1)}) custom-call(f32[4,128,32]{2,1,0:T(8,128)} %bitcast.106, s32[4,1,4096]{2,1,0:T(1,128)} %bitcast.109, s32[4,1,4096]{2,1,0:T(1,128)} %get-tuple-element.59.rank_ref, f32[4,32,128]{2,1,0:T(8,128)} %get-tuple-element.66.weights_ref), custom_call_target="tpu_custom_call" | custom-call | tf_op jit(solution)/shard_map/unweigh/pallas_call | solution.py:1442
  290.3 1.5 fusion.16
  291.8 1.6 fusion.17
  295.0 1.3 fusion.35
  296.3 1.5 add_convert_fusion.1.refs_0_
  297.8 1.3 convolution_convert_fusion.10.refs_6_
  299.1 2.6 convolution_convert_fusion.refs_5_
  301.7 1.4 convolution_convert_fusion.1.refs_1_
  303.1 42.7 %middle.1 = (bf16[256,512]{1,0:T(8,128)(2,1)}, f32[256,512]{1,0:T(8,128)}, bf16[512,1024]{1,0:T(8,128)(2,1)}, f32[1,512]{1,0:T(1,128)}, bf16[128,1024]{1,0:T(8,1...) custom-call(bf16[512,1024]{1,0:T(8,128)(2,1)} %add_convert_fusion.1.refs_0_, ...), custom_call_target="tpu_custom_call" | custom-call | tf_op jit(solution)/shard_map/middle/pallas_call | solution.py:661
  345.8 2.0 convolution_convert_fusion.13
  347.9 2.6 convolution_convert_fusion.5.refs_10_
  362.5 0.9 maximum_bitcast_fusion
  363.4 1.5 pad_maximum_fusion.src
  364.9 9.3 %pair_sum.1 = bf16[2,512,256]{2,1,0:T(8,128)(2,1)} custom-call(f32[2,1024,256]{2,1,0:T(8,128)} %pad_maximum_fusion.src), custom_call_target="tpu_custom_call" | custom-call | tf_op jit(solution)/shard_map/pair_sum/pallas_call | solution.py:304
  374.2 1.9 fusion.14
  377.5 1.3 pad_maximum_fusion.1.refs_9_
  380.4 1.5 add_convert_fusion.refs_0_
  382.0 81.2 %last.1 = (f32[256,512]{1,0:T(8,128)}, f32[2,8,128]{2,1,0:T(8,128)}, f32[2048,1024]{1,0:T(8,128)}, bf16[512,1024]{1,0:T(8,128)(2,1)}, bf16[512,256]{1,0:T(8,128)...) custom-call(bf16[512,1024]{1,0:T(8,128)(2,1)} %add_convert_fusion.re, ...), custom_call_target="tpu_custom_call" | custom-call | tf_op jit(solution)/shard_map/last/pallas_call | solution.py:848
  464.4 2.0 convert_element_type.154
  466.4 1.8 convert_element_type.156
  468.2 1.8 convert_element_type.157
  470.0 2.4 convert_element_type.153
  472.4 1.6 convert_element_type.155
  474.7 2.7 convert_element_type.158
  479.0 3.5 copy.92
  (147 shorter events, 36.1 us)
Async XLA Ops:
  0.6 13.7 %copy-start = (bf16[4,2,256,512]{3,2,1,0:T(8,128)(2,1)S(1)}, bf16[4,2,256,512]{3,2,1,0:T(8,128)(2,1)}, u32[]{:S(2)}) copy-start(bf16[4,2,256,512]{3,2,1,0:T(8,128)(2,1)} %param.23) | copy-start | bytes 6291460
  56.2 14.7 %copy-start.10 = (bf16[512,256]{1,0:T(8,128)(2,1)}, bf16[512,256]{1,0:T(8,128)(2,1)S(1)}, u32[]{:S(2)}) copy-start(bf16[512,256]{1,0:T(8,128)(2,1)S(1)} %slice_bitcast_fusion.2) | copy-start | bytes 786436
  63.1 1.3 copy-start.8
  65.2 7.6 %copy-start.34 = (bf16[512,64]{0,1:T(8,128)(2,1)}, bf16[512,64]{0,1:T(8,128)(2,1)S(1)}, u32[]{:S(2)}) copy-start(bf16[512,64]{0,1:T(8,128)(2,1)S(1)} %convolution_convert_fusion.16) | copy-start | bytes 196612
  66.0 1.3 copy-start.6
  67.9 4.9 %copy-start.36 = (bf16[512,64]{0,1:T(8,128)(2,1)}, bf16[512,64]{0,1:T(8,128)(2,1)S(1)}, u32[]{:S(2)}) copy-start(bf16[512,64]{0,1:T(8,128)(2,1)S(1)} %convolution_convert_fusion.17) | copy-start | bytes 196612
  68.8 1.4 copy-start.4
  70.9 2.0 copy-start.38
  71.7 1.4 copy-start.2
  72.2 1.3 copy-start.33
  73.4 35.9 %copy-start.40 = (bf16[512,64]{0,1:T(8,128)(2,1)}, bf16[512,64]{0,1:T(8,128)(2,1)S(1)}, u32[]{:S(2)}) copy-start(bf16[512,64]{0,1:T(8,128)(2,1)S(1)} %convolution_convert_fusion.19) | copy-start | bytes 196612
  107.4 2.0 copy-start.18
  107.4 2.0 copy-start.24
  109.4 1.4 copy-start.15
  109.4 1.4 copy-start.21
  109.4 2.4 copy-start.31
  274.1 2.4 copy-start.19
  274.1 3.7 copy-start.30
  290.3 3.9 copy-start.27
  290.3 4.3 copy-start.29
  291.8 3.2 copy-start.32
  295.0 1.3 copy-start.13
  295.0 1.3 copy-start.23
  296.3 1.5 copy-start.22
  299.1 2.6 copy-start.25
  303.1 44.7 %copy-start.35 = (bf16[512,64]{0,1:T(8,128)(2,1)S(1)}, bf16[512,64]{0,1:T(8,128)(2,1)}, u32[]{:S(2)}) copy-start(bf16[512,64]{0,1:T(8,128)(2,1)} %copy-done.34) | copy-start | bytes 196612
  303.1 44.7 %copy-start.37 = (bf16[512,64]{0,1:T(8,128)(2,1)S(1)}, bf16[512,64]{0,1:T(8,128)(2,1)}, u32[]{:S(2)}) copy-start(bf16[512,64]{0,1:T(8,128)(2,1)} %copy-done.36) | copy-start | bytes 196612
  303.1 44.8 %copy-start.39 = (bf16[512,64]{0,1:T(8,128)(2,1)S(1)}, bf16[512,64]{0,1:T(8,128)(2,1)}, u32[]{:S(2)}) copy-start(bf16[512,64]{0,1:T(8,128)(2,1)} %copy-done.38) | copy-start | bytes 196612
  303.1 44.8 %copy-start.41 = (bf16[512,64]{0,1:T(8,128)(2,1)S(1)}, bf16[512,64]{0,1:T(8,128)(2,1)}, u32[]{:S(2)}) copy-start(bf16[512,64]{0,1:T(8,128)(2,1)} %copy-done.40) | copy-start | bytes 196612
  345.8 4.7 copy-start.3
  347.9 3.2 copy-start.5
  350.5 1.6 copy-start.7
  351.1 1.8 copy-start.9
  354.3 1.0 copy-start.11
  364.9 9.3 %copy-start.20 = (bf16[512,1024]{1,0:T(8,128)(2,1)S(1)}, bf16[512,1024]{1,0:T(8,128)(2,1)}, u32[]{:S(2)}) copy-start(bf16[512,1024]{1,0:T(8,128)(2,1)} %get-tuple-element.53) | copy-start | bytes 3145732
  374.2 1.9 copy-start.14
  377.5 2.0 copy-start.16
  464.4 7.9 %copy-start.17 = (bf16[512,1024]{1,0:T(8,128)(2,1)S(1)}, bf16[512,1024]{1,0:T(8,128)(2,1)}, u32[]{:S(2)}) copy-start(bf16[512,1024]{1,0:T(8,128)(2,1)} %get-tuple-element.84) | copy-start | bytes 3145732
  464.4 14.5 %slice-start = ((s8[8388608]{0:T(1024)(128)(4,1)}), s8[4194304]{0:T(1024)(128)(4,1)S(1)}, s32[]{:S(2)}) async-start(s8[8388608]{0:T(1024)(128)(4,1)} %bitcast.103), calls=%async_computation | async-start | bytes 8388608
  472.4 2.3 copy-start.12
  474.7 2.7 copy-start.28
  474.7 3.4 copy-start.26
  474.7 4.2 slice-start.1
  479.0 3.5 copy-start.1

commit v5 on v4

--- a/solution.py
+++ b/solution.py
@@ -286,32 +286,6 @@
     )(src)
 
 
-def pair_sum_kernel(sizes, src, out, landing, send, recv):
-    spot = here()
-    dp, row, col = spot
-    greet_partner(spot, sizes)
-    size = landing.shape[1]
-    other = pl.multiple_of((1 - col) * size, size)
-    away = remote(src.at[:, pl.ds(other, size)], landing, send, recv, (dp, row, 1 - col))
-    away.start()
-    away.wait()
-    own = src[:, pl.ds(pl.multiple_of(col * size, size), size)]
-    out[...] = (own + landing[...]).astype(out.dtype)
-
-
-def pair_sum(sizes, src):
-    shape = (src.shape[0], src.shape[1] // sizes[2], src.shape[2])
-    return pl.pallas_call(
-        functools.partial(pair_sum_kernel, sizes),
-        in_specs=[VMEM],
-        out_specs=VMEM,
-        out_shape=jax.ShapeDtypeStruct(shape, jnp.bfloat16),
-        scratch_shapes=[pltpu.VMEM(shape, src.dtype), DMA, DMA],
-        compiler_params=pltpu.CompilerParams(collective_id=2, has_side_effects=True),
-        name="pair_sum",
-    )(src)
-
-
 def fold(column):
     return jnp.broadcast_to(column, (column.shape[0], 128))
 
@@ -610,23 +584,19 @@
 
 
 def middle_kernel(sizes, *refs):
-    part, out_part, hidden, dy, gain = refs[:5]
-    terms = refs[5:9]
-    output, grad, grad_all, gain_grad = refs[9:13]
-    shards = refs[13:17]
-    landing, out_landing, mine, theirs, block = refs[17:22]
-    halves, pair_land, below, above = refs[22:26], refs[26:30], refs[30:34], refs[34:38]
-    (
-        ssend, srecv, osend, orecv, gsend, grecv, psend, precv, hsend, hrecv, *line
-    ) = refs[38:]
+    part, hidden, dy, gain = refs[:4]
+    terms = refs[4:8]
+    grad, grad_all, gain_grad = refs[8:11]
+    shards = refs[11:15]
+    landing, mine, theirs, block = refs[15:19]
+    halves, pair_land, below, above = refs[19:23], refs[23:27], refs[27:31], refs[31:35]
+    ssend, srecv, gsend, grecv, psend, precv, hsend, hrecv, *line = refs[35:]
     spot = here()
     greet_cross(spot, sizes)
     scatter = Scatter(spot, sizes, part, landing, ssend, srecv)
     scatter.start()
     pair = PairSum(spot, sizes, terms, FIRST_COLS, halves, pair_land, hsend, hrecv)
     pair.start()
-    out_scatter = Scatter(spot, sizes, out_part, out_landing, osend, orecv)
-    out_scatter.start()
     pair.finish()
     reduce = LineReduce(spot, sizes, halves, FIRST_DIMS, below, above, line)
     reduce.start()
@@ -637,22 +607,15 @@
     block[...] = total.astype(jnp.bfloat16)
     gather = Gather(spot, sizes, block, grad_all, gsend, grecv)
     gather.start()
-    reduce.event(1)
-    out_scatter.wait()
-    result = hidden[...]
-    for q in range(sizes[1]):
-        result = result + out_landing[q].astype(jnp.float32)
-    output[...] = result.astype(jnp.bfloat16)
-    lax.fori_loop(2, sizes[0], lambda time, c: (reduce.event(time), c)[1], 0)
+    lax.fori_loop(1, sizes[0], lambda time, c: (reduce.event(time), c)[1], 0)
     for half, dim, shard in zip(halves, FIRST_DIMS, shards):
         shard[...] = slab(half, dim, spot[0], sizes[0])[...]
     scatter.wait_send()
-    out_scatter.wait_send()
     gather.wait()
     reduce.finish()
 
 
-def middle(sizes, part, out_part, hidden, dy, gain, terms):
+def middle(sizes, part, hidden, dy, gain, terms):
     tokens, width = hidden.shape
     dps, rows, cols = sizes
     low, wide = jnp.bfloat16, jnp.float32
@@ -660,10 +623,9 @@
     shards = [halved(h, d, dps) for h, d in zip(halves, FIRST_DIMS)]
     return pl.pallas_call(
         functools.partial(middle_kernel, sizes),
-        in_specs=[VMEM] * 9,
-        out_specs=[VMEM] * 8,
+        in_specs=[VMEM] * 8,
+        out_specs=[VMEM] * 7,
         out_shape=[
-            jax.ShapeDtypeStruct((tokens, width), low),
             jax.ShapeDtypeStruct((tokens, width), wide),
             jax.ShapeDtypeStruct(part.shape, low),
             jax.ShapeDtypeStruct((1, width), wide),
@@ -671,45 +633,51 @@
         + [jax.ShapeDtypeStruct(s, low) for s in shards],
         scratch_shapes=[
             pltpu.VMEM((rows, tokens, width), low),
-            pltpu.VMEM((rows, tokens, width), low),
             pltpu.VMEM((2, tokens, 128), wide),
             pltpu.VMEM((2, tokens, 128), wide),
             pltpu.VMEM((tokens, width), low),
         ]
         + [pltpu.VMEM(h, low) for h in halves] * 4
-        + plane_sems(sizes) * 3
+        + plane_sems(sizes) * 2
         + [DMA, DMA, DMA((4,)), DMA((4,))]
         + line_sems(sizes, 4, 4),
         compiler_params=pltpu.CompilerParams(collective_id=4, has_side_effects=True),
         name="middle",
-    )(part, out_part, hidden, dy, gain[None], *terms)
+    )(part, hidden, dy, gain[None], *terms)
 
 
 def last_kernel(sizes, *refs):
     part, x, above_grad, gain, other_gain = refs[:5]
-    shards, terms = refs[5:9], refs[9:11]
-    table, grads_all = refs[11:13]
-    grad, gain_sums, row_grads = refs[13:16]
-    firsts, lasts, keys_all = refs[16:20], refs[20:22], refs[22]
-    landing, mine, theirs, own_gain, gain_landing, tables, chunks = refs[23:30]
-    halves, pair_land, below, above = refs[30:32], refs[32:34], refs[34:36], refs[36:38]
+    keys, terms = refs[5], refs[6:8]
+    table, grads_all = refs[8:10]
+    grad, gain_sums, row_grads = refs[10:13]
+    lasts, keys_all = refs[13:15], refs[15]
+    landing, mine, theirs, own_gain, gain_landing, tables, chunks = refs[16:23]
+    halves, pair_land, below, above = refs[23:25], refs[25:27], refs[27:29], refs[29:31]
     (
         ssend, srecv, psend, precv, bsend, brecv, hsend, hrecv, tsem, csem,
         xsend, xrecv, kxsend, kxrecv, *line
-    ) = refs[38:]
+    ) = refs[31:]
     spot = here()
     dp, row, col = spot
     dps, rows, cols = sizes
     count = dps * rows * cols
     me = index_of(spot, sizes)
     loads = dps * cols
+    block = grads_all.shape[-1]
 
     def load(index):
         slot = lax.rem(index, 2)
         where = (lax.div(index, cols), lax.rem(index, cols))
         return (
             pltpu.make_async_copy(table.at[where], tables.at[slot], tsem.at[slot]),
-            pltpu.make_async_copy(grads_all.at[where], chunks.at[slot], csem.at[slot]),
+        ) + tuple(
+            pltpu.make_async_copy(
+                grads_all.at[where + (r,)],
+                chunks.at[slot, :, pl.ds(r * block, block)],
+                csem.at[slot, r],
+            )
+            for r in range(rows)
         )
 
     for copy in load(0):
@@ -719,13 +687,11 @@
     scatter.start()
     pair = PairSum(spot, sizes, terms, LAST_COLS, halves, pair_land, hsend, hrecv)
     pair.start()
-    for first, dim, shard in zip(firsts, FIRST_DIMS, shards):
-        slab(first, dim, dp, dps)[...] = shard[...]
-    gather = LineGather(spot, sizes, firsts, FIRST_DIMS, line[:3])
-    gather.start()
     pair.finish()
-    reduce = LineReduce(spot, sizes, halves, LAST_DIMS, below, above, line[3:7])
+    reduce = LineReduce(spot, sizes, halves, LAST_DIMS, below, above, line[:4])
     reduce.start()
+
+    wide_strip = min(512, tables.shape[2])
 
     def product(index):
         slot = lax.rem(index, 2)
@@ -738,7 +704,7 @@
                 copy.start()
 
         def strip(n, carry):
-            columns = pl.ds(pl.multiple_of(n * 256, 256), 256)
+            columns = pl.ds(pl.multiple_of(n * wide_strip, wide_strip), wide_strip)
             term = lax.dot_general(
                 tables[slot, :, columns],
                 chunks[slot],
@@ -756,10 +722,20 @@
 
             return carry
 
-        lax.fori_loop(0, tables.shape[2] // 256, strip, 0)
+        lax.fori_loop(0, tables.shape[2] // wide_strip, strip, 0)
 
     def products(first, end):
         lax.fori_loop(first, end, lambda index, c: (product(index), c)[1], 0)
+
+    def sideways(k):
+        return remote(
+            keys, keys_all.at[row, col], xsend, xrecv.at[rows - k],
+            (dp, lax.rem(row + k, rows), col),
+        )
+
+    def cross(src, k):
+        there = keys_all.at[lax.rem(row + k, rows), col]
+        return remote(src, there, kxsend, kxrecv, (dp, row, 1 - col))
 
     products(0, loads // 4)
     scatter.wait()
@@ -778,30 +754,17 @@
     lax.fori_loop(1, count, tell, 0)
     gain_landing[me] = own_gain[...]
     grad[...] = total
-    gather.event(1)
-    reduce.event(1)
-    products(loads // 4, loads // 2)
-    lax.fori_loop(2, dps, lambda time, c: (gather.event(time), reduce.event(time), c)[2], 0)
-    for first, half, dim in zip(lasts, halves, LAST_DIMS):
-        slab(first, dim, dp, dps)[...] = slab(half, dim, dp, dps)[...]
-    final = LineGather(spot, sizes, lasts, LAST_DIMS, line[7:10])
-    final.start()
-    keys = firsts[3]
-
-    def sideways(k):
-        return remote(
-            keys, keys_all.at[row, col], xsend, xrecv.at[rows - k],
-            (dp, lax.rem(row + k, rows), col),
-        )
-
-    def cross(src, k):
-        there = keys_all.at[lax.rem(row + k, rows), col]
-        return remote(src, there, kxsend, kxrecv, (dp, row, 1 - col))
-
     for k in range(1, rows):
         sideways(k).start()
     cross(keys, 0).start()
     keys_all[row, col] = keys[...]
+    reduce.event(1)
+    products(loads // 4, loads // 2)
+    lax.fori_loop(2, dps, lambda time, c: (reduce.event(time), c)[1], 0)
+    for first, half, dim in zip(lasts, halves, LAST_DIMS):
+        slab(first, dim, dp, dps)[...] = slab(half, dim, dp, dps)[...]
+    final = LineGather(spot, sizes, lasts, LAST_DIMS, line[4:7])
+    final.start()
     products(loads // 2, 3 * loads // 4)
     final.event(1)
     for k in range(1, rows):
@@ -822,12 +785,11 @@
     arrived(gain_landing.at[pl.ds(0, count - 1)], bsend)
     arrived(keys_all.at[:, col], kxsend)
     arrived(keys_all.at[pl.ds(0, rows - 1), col], xsend)
-    gather.finish()
     reduce.finish()
     final.finish()
 
 
-def last(sizes, part, x, above, gain, other_gain, shards, terms, table, grads_all):
+def last(sizes, part, x, above, gain, other_gain, keys, terms, table, grads_all):
     tokens, width = x.shape
     dps, rows, cols = sizes
     lines = 2 * width // 128
@@ -835,27 +797,21 @@
     low, wide = jnp.bfloat16, jnp.float32
     shape = jax.ShapeDtypeStruct
 
-    def grown(shard, dim):
-        full = list(shard.shape)
-        full[dim] *= dps
-        return tuple(full)
-
-    firsts = [grown(s, d) for s, d in zip(shards, FIRST_DIMS)]
     halves = [halved(t.shape, d, cols) for t, d in zip(terms, LAST_COLS)]
     rows_dev = table.shape[-1]
-    features = grads_all.shape[-1]
+    features = grads_all.shape[-1] * rows
     chunk = table.shape[2]
     return pl.pallas_call(
         functools.partial(last_kernel, sizes),
-        in_specs=[VMEM] * 11 + [ANY] * 2,
-        out_specs=[VMEM] * 10,
+        in_specs=[VMEM] * 8 + [ANY] * 2,
+        out_specs=[VMEM] * 6,
         out_shape=[
             shape((tokens, width), wide),
             shape((cols, lines, 128), wide),
             shape((rows_dev, features), wide),
         ]
-        + [shape(s, low) for s in firsts + halves]
-        + [shape((rows, cols) + firsts[3], low)],
+        + [shape(s, low) for s in halves]
+        + [shape((rows, cols) + keys.shape, low)],
         scratch_shapes=[
             pltpu.VMEM((rows, tokens, width), low),
             pltpu.VMEM((2, tokens, 128), wide),
@@ -867,13 +823,133 @@
         ]
         + [pltpu.VMEM(h, low) for h in halves] * 4
         + plane_sems(sizes)
-        + [DMA, DMA, DMA, DMA, DMA((2,)), DMA((2,)), DMA((2,)), DMA((2,))]
+        + [DMA, DMA, DMA, DMA, DMA((2,)), DMA((2,)), DMA((2,)), DMA((2, rows))]
         + [DMA, DMA((rows,)), DMA, DMA]
-        + line_sems(sizes, 4, 3)
         + line_sems(sizes, 2, 7),
         compiler_params=pltpu.CompilerParams(collective_id=5, has_side_effects=True),
         name="last",
-    )(part, x, above, gain[None], other_gain, *shards, *terms, table, grads_all)
+    )(part, x, above, gain[None], other_gain, keys, *terms, table, grads_all)
+
+
+def turn_kernel(sizes, *refs):
+    prefix, queries, kv, grad_out, log_sums, out_part, hidden = refs[:7]
+    shards = refs[7:11]
+    grad_q, grad_kv, output = refs[11:14]
+    firsts = refs[14:18]
+    totals, kv_landing, out_landing = refs[18:21]
+    osend, orecv, ksend, krecv, *line = refs[21:]
+    spot = here()
+    dp, row, col = spot
+    dps = sizes[0]
+    tokens, width = queries.shape
+    keys = kv.shape[1]
+    tile = tokens // 2
+    greet_cross(spot, sizes)
+    for first, dim, shard in zip(firsts, FIRST_DIMS, shards):
+        slab(first, dim, dp, dps)[...] = shard[...]
+    gather = LineGather(spot, sizes, firsts, FIRST_DIMS, line)
+    gather.start()
+    out_scatter = Scatter(spot, sizes, out_part, out_landing, osend, orecv)
+    out_scatter.start()
+    limit = prefix[0]
+    key_pos = lax.broadcasted_iota(jnp.int32, (keys, tile), 0)
+    lane = lax.broadcasted_iota(jnp.int32, (1, 2 * HDIM), 1)
+    sides = [
+        jnp.where(jnp.logical_and(lane >= a * HDIM, lane < (a + 1) * HDIM), 1.0, 0.0).astype(
+            jnp.bfloat16
+        )
+        for a in range(2)
+    ]
+
+    def unit(index, carry):
+        pair, part = lax.div(index, 2), lax.rem(index, 2)
+        lanes = pl.ds(pl.multiple_of(pair * 2 * HDIM, 2 * HDIM), 2 * HDIM)
+        lines = pl.ds(pl.multiple_of(part * tile, tile), tile)
+        query_pos = col * tokens + part * tile + lax.broadcasted_iota(jnp.int32, (1, tile), 1)
+        allowed = jnp.logical_or(key_pos <= query_pos, key_pos < limit)
+        q2, g2 = queries[lines, lanes], grad_out[lines, lanes]
+        k2, v2 = kv[0, :, lanes], kv[1, :, lanes]
+        dq = jnp.zeros((tile, 2 * HDIM), jnp.float32)
+        dk = jnp.zeros((keys, 2 * HDIM), jnp.float32)
+        dv = jnp.zeros((keys, 2 * HDIM), jnp.float32)
+        for a in range(2):
+            ka = k2 * sides[a]
+            scores = jnp.where(allowed, dense_nt(ka, q2) * HDIM ** (-0.5), -jnp.inf)
+            probs = jnp.exp(scores - log_sums[pl.ds(2 * pair + a, 1), lines])
+            grad_probs = dense_nt(v2 * sides[a], g2)
+            inner = jnp.sum(probs * grad_probs, axis=0, keepdims=True)
+            grad_scores = (probs * (grad_probs - inner)).astype(jnp.bfloat16)
+            dq = dq + dense_tn(grad_scores, ka)
+            dk = dk + dense(grad_scores, q2 * sides[a])
+            dv = dv + dense(probs.astype(jnp.bfloat16), g2 * sides[a])
+        grad_q[lines, lanes] = (dq * HDIM ** (-0.5)).astype(jnp.bfloat16)
+        dk = dk * HDIM ** (-0.5)
+
+        @pl.when(part == 0)
+        def _():
+            totals[0, :, lanes] = dk
+            totals[1, :, lanes] = dv
+
+        @pl.when(part > 0)
+        def _():
+            totals[0, :, lanes] = totals[0, :, lanes] + dk
+            totals[1, :, lanes] = totals[1, :, lanes] + dv
+
+        pl.when(index == 1)(lambda: gather.event(1))
+        pl.when(index == 3)(lambda: gather.event(2))
+        return carry
+
+    lax.fori_loop(0, 2 * width // (2 * HDIM), unit, 0)
+    size = kv_landing.shape[1]
+    other = pl.multiple_of((1 - col) * size, size)
+    away = remote(totals.at[:, pl.ds(other, size)], kv_landing, ksend, krecv, (dp, row, 1 - col))
+    away.start()
+    out_scatter.wait()
+    result = hidden[...]
+    for q in range(sizes[1]):
+        result = result + out_landing[q].astype(jnp.float32)
+    output[...] = result.astype(jnp.bfloat16)
+    away.wait()
+    own = totals[:, pl.ds(pl.multiple_of(col * size, size), size)]
+    grad_kv[...] = (own + kv_landing[...]).astype(jnp.bfloat16)
+    lax.fori_loop(3, dps, lambda time, c: (gather.event(time), c)[1], 0)
+    out_scatter.wait_send()
+    gather.finish()
+
+
+def turn(sizes, prefix, queries, kv, grad_out, log_sums, out_part, hidden, shards):
+    tokens, width = queries.shape
+    dps, rows, cols = sizes
+    low, wide = jnp.bfloat16, jnp.float32
+    shape = jax.ShapeDtypeStruct
+
+    def grown(shard, dim):
+        full = list(shard.shape)
+        full[dim] *= dps
+        return tuple(full)
+
+    firsts = [grown(s, d) for s, d in zip(shards, FIRST_DIMS)]
+    return pl.pallas_call(
+        functools.partial(turn_kernel, sizes),
+        in_specs=[pl.BlockSpec(memory_space=pltpu.SMEM)] + [VMEM] * 10,
+        out_specs=[VMEM] * 7,
+        out_shape=[
+            shape((tokens, width), low),
+            shape((2, tokens, width), low),
+            shape(hidden.shape, low),
+        ]
+        + [shape(s, low) for s in firsts],
+        scratch_shapes=[
+            pltpu.VMEM(kv.shape, wide),
+            pltpu.VMEM((2, tokens, width), wide),
+            pltpu.VMEM((rows,) + hidden.shape, low),
+        ]
+        + plane_sems(sizes)
+        + [DMA, DMA]
+        + line_sems(sizes, 4, 3),
+        compiler_params=pltpu.CompilerParams(collective_id=2, has_side_effects=True),
+        name="turn",
+    )(prefix, queries, kv, grad_out, log_sums, out_part, hidden, *shards)
 
 
 def allowed_mask(query_count, key_count, first_pos, prefix_len):
@@ -998,11 +1074,6 @@
     )(query_rows, keys_head, flat[:, None, :], rank)
 
 
-def own_block(tokens_ref, dp, col, row, width):
-    left = pl.multiple_of(row * width, width)
-    return tokens_ref.at[dp, col, :, pl.ds(left, width)]
-
-
 def send_rows(spot, sizes, src, landing, send, recv):
     count = sizes[0] * sizes[1] * sizes[2]
     me = index_of(spot, sizes)
@@ -1024,74 +1095,131 @@
     pieces = []
     for row in range(sizes[1]):
         index = (dp * sizes[1] + row) * sizes[2] + col
-        pieces.append(table[index, block : block + 1, :])
+        pieces.append(table[index, pl.ds(block, 1), :])
     return jnp.concatenate(pieces, axis=1)
 
 
-def read_kernel(
-    sizes, blocks, grads, meta, slots, values,
-    grads_all, table, own_part, other_part, meta_in,
-    slots_in, tables, parts, msend, mrecv, ssend, srecv, zsend, zrecv, xsend, xrecv, csend, crecv,
-    local, tsem, psem, qsend, qrecv,
+def nth_place(dp, q, dps):
+    twice = 2 * jnp.minimum(dp, dps - 1 - dp)
+    inside = q <= twice
+    distance = jnp.where(inside, lax.div(q + 1, 2), q - lax.div(twice, 2))
+    below = jnp.logical_or(
+        jnp.logical_and(inside, lax.rem(q, 2) == 1),
+        jnp.logical_and(jnp.logical_not(inside), dp > dps - 1 - dp),
+    )
+    return dp + jnp.where(below, -distance, distance), below
+
+
+def plane_neighbours(row, rows):
+    across = row + 1 - 2 * lax.rem(row, 2)
+    along = lax.rem(row + rows // 2, rows)
+    return across, along, lax.rem(across + rows // 2, rows)
+
+
+RING = 3
+
+
+def memory_kernel(
+    sizes, blocks, grads, meta, slots, values, values_t,
+    grads_all, table, other_part, memory, back,
+    meta_in, slots_in, tables, parts,
+    chunks, found, sums, grids, theirs, acc, first_land, side_land, deep_land, total,
+    msend, mrecv, ssend, srecv, zup, zdown, zrecv, wsend, wrecv, csend, crecv,
+    local, tsem, qsend, qrecv,
+    gsem, esem, hsend, hrecv, xsend, xrecv, dsend, drecv, fsend, frecv, flocal,
 ):
     spot = here()
     dp, row, col = spot
     dps, rows, cols = sizes
     tokens, width = grads.shape
+    half = tokens // 2
     areas = values.shape[0] // SUBKEYS
+    count = dps * rows * cols
+    me = index_of(spot, sizes)
+    across, along, opposite = plane_neighbours(row, rows)
+    first_half, second_half = pl.ds(0, half), pl.ds(half, half)
     greet_all(spot, sizes)
     send_rows(spot, sizes, meta, meta_in, msend, mrecv)
     send_rows(spot, sizes, slots, slots_in, ssend, srecv)
 
-    def block_at(j, k, c):
-        return own_block(grads_all, lax.rem(dp + j, dps), c, lax.rem(row + k, rows), width)
-
-    def cross(src, j, k):
-        remote(src, block_at(j, k, col), csend, crecv, (dp, row, 1 - col)).start()
-
-    def sideways(src, j):
-        for k in range(1, rows):
+    def place_of(u):
+        return nth_place(dp, dps - 1 - u, dps)[0]
+
+    def block_at(place, r, lines=slice(None)):
+        return grads_all.at[place, col, r, lines]
+
+    def cross(q, place, r, src=None):
+        there = block_at(place, r)
+        remote(there if src is None else src, there, csend, crecv.at[q], (dp, row, 1 - col)).start()
+
+    def line_copy(place, up, src=None):
+        there = block_at(place, row)
+        return remote(
+            there if src is None else src,
+            there,
+            (zup if up else zdown).at[place],
+            zrecv.at[place],
+            (jnp.clip(dp + (1 if up else -1), 0, dps - 1), row, col),
+        )
+
+    def sideways(q, place, src=None):
+        there = block_at(place, row)
+        for n, r in enumerate((across, along)):
             remote(
-                src, block_at(j, 0, col), xsend, xrecv.at[j, rows - k],
-                (dp, lax.rem(row + k, rows), col),
+                there if src is None else src, there, wsend, wrecv.at[q, n], (dp, r, col)
             ).start()
 
-    for k in range(1, dps):
-        remote(
-            grads, block_at(0, 0, col), zsend, zrecv.at[dps - k], (lax.rem(dp + k, dps), row, col)
-        ).start()
-    sideways(grads, 0)
-    cross(grads, 0, 0)
-    keep = pltpu.make_async_copy(grads, block_at(0, 0, col), local)
+    pl.when(dp < dps - 1)(lambda: line_copy(dp, True, grads).start())
+    pl.when(dp > 0)(lambda: line_copy(dp, False, grads).start())
+    sideways(0, dp, grads)
+    cross(0, dp, row, grads)
+    keep = pltpu.make_async_copy(grads, block_at(dp, row), local)
     keep.start()
 
-    def from_above(j):
-        src = block_at(j, 0, col)
-        arrived(src, zrecv.at[j])
-        sideways(src, j)
-        cross(src, j, 0)
-
-    def from_side(j):
-        for k in range(1, rows):
-            src = block_at(j, k, col)
-            arrived(src, xrecv.at[j, k])
-            cross(src, j, k)
+    def from_line(q):
+        place, below = nth_place(dp, q, dps)
+        arrived(block_at(place, row), zrecv.at[place])
+        pl.when(jnp.logical_and(below, dp < dps - 1))(lambda: line_copy(place, True).start())
+        pl.when(jnp.logical_and(jnp.logical_not(below), dp > 0))(
+            lambda: line_copy(place, False).start()
+        )
+        sideways(q, place)
+        cross(q, place, row)
+
+    def from_sides(q):
+        place, _ = nth_place(dp, q, dps)
+        for n, (r, other, lines) in enumerate(
+            ((across, along, first_half), (along, across, second_half))
+        ):
+            arrived(block_at(place, r), wrecv.at[q, n])
+            half = block_at(place, r, lines)
+            remote(half, half, wsend, wrecv.at[q, 2 + n], (dp, other, col)).start()
+            cross(q, place, r)
+
+    def from_opposite(q):
+        place, _ = nth_place(dp, q, dps)
+        for n, lines in enumerate((first_half, second_half)):
+            arrived(block_at(place, opposite, lines), wrecv.at[q, 2 + n])
+        cross(q, place, opposite)
 
     all_rows(meta_in, mrecv)
     all_rows(slots_in, srecv)
 
-    def chunk(turn, kk):
-        source_dp = lax.rem(dp + 1 + turn, dps)
-        source_col = 1 - col if kk == 0 else col
-        table_out = pltpu.make_async_copy(
-            tables.at[kk], table.at[source_dp, source_col], tsem.at[kk]
+    def write_places(chunk):
+        turn = lax.div(chunk, 2)
+        slot = lax.rem(chunk, 2)
+        return turn, slot, place_of(turn), jnp.where(slot == 0, 1 - col, col)
+
+    def table_copy(chunk):
+        _, slot, source_dp, source_col = write_places(chunk)
+        return pltpu.make_async_copy(
+            tables.at[slot], table.at[source_dp, source_col], tsem.at[slot]
         )
 
-        @pl.when(turn > 0)
-        def _():
-            table_out.wait()
-
-        for block in range(blocks):
+    def build(chunk):
+        turn, slot, source_dp, source_col = write_places(chunk)
+        pl.when(turn > 0)(lambda: table_copy(chunk).wait())
+        def one(block, carry):
             row_meta = slot_row(sizes, meta_in, source_dp, source_col, block)
             key = row_meta // SUBKEYS
             low = row_meta % SUBKEYS
@@ -1106,300 +1234,301 @@
             ).astype(jnp.bfloat16)
             for area in range(areas):
                 tables[
-                    kk,
-                    block * FBLK : (block + 1) * FBLK,
+                    slot,
+                    pl.ds(pl.multiple_of(block * FBLK, FBLK), FBLK),
                     area * SUBKEYS : (area + 1) * SUBKEYS,
                 ] = stacked[area * FBLK : (area + 1) * FBLK]
-        table_out.start()
-        if kk == 0:
-            part_out = remote(
-                parts.at[0], other_part.at[source_dp], qsend, qrecv, (dp, row, 1 - col)
-            )
-        else:
-            part_out = pltpu.make_async_copy(parts.at[1], own_part.at[source_dp], psem)
-
-        @pl.when(turn > 0)
-        def _():
-            if kk == 0:
-                part_out.wait_send()
-            else:
-                part_out.wait()
+            return carry
+
+        lax.fori_loop(0, blocks, one, 0)
+        table_copy(chunk).start()
+
+    def away(turn, source_dp):
+        return remote(parts.at[0], other_part.at[source_dp], qsend, qrecv.at[turn], (dp, row, 1 - col))
+
+    def multiply(chunk):
+        turn, slot, source_dp, _ = write_places(chunk)
+        later = turn > 0
+        pl.when(jnp.logical_and(later, slot == 0))(lambda: away(turn, source_dp).wait_send())
 
         def strip(n, carry):
-            columns = pl.ds(pl.multiple_of(n * 256, 256), 256)
-            parts[kk, :, columns] = jnp.dot(
-                tables[kk], values[:, columns], preferred_element_type=jnp.float32
+            columns = pl.ds(pl.multiple_of(n * 512, 512), 512)
+            parts[slot, :, columns] = jnp.dot(
+                tables[slot], values[:, columns], preferred_element_type=jnp.float32
             ).astype(jnp.bfloat16)
             return carry
 
-        lax.fori_loop(0, values.shape[1] // 256, strip, 0)
-        part_out.start()
-
-    def step(turn, carry):
-        chunk(turn, 0)
-
-        @pl.when(jnp.logical_and(turn > 0, 2 * turn < dps))
+        lax.fori_loop(0, values.shape[1] // 512, strip, 0)
+        pl.when(slot == 0)(lambda: away(turn, source_dp).start())
+
+    def load_part(u):
+        return pltpu.make_async_copy(other_part.at[place_of(u)], theirs, esem)
+
+    def strip(u, r, lines=slice(None)):
+        return acc.at[lax.rem(u, RING), lines, pl.ds(pl.multiple_of(r * width, width), width)]
+
+    lines_of = (pl.ds(0, half), pl.ds(half, half))
+
+    def halves(u):
+        return [
+            remote(
+                strip(u, opposite, lines_of[n]), first_land.at[u, n],
+                hsend.at[lax.rem(u, RING), n], hrecv.at[u, n], (dp, r, col),
+            )
+            for n, r in enumerate((across, along))
+        ]
+
+    def wholes(u):
+        return [
+            remote(
+                strip(u, r), side_land.at[u, n],
+                xsend.at[lax.rem(u, RING), n], xrecv.at[u, n], (dp, r, col),
+            )
+            for n, r in enumerate((across, along))
+        ]
+
+    def sent(u):
+        for copy in halves(u) + wholes(u):
+            copy.wait_send()
+
+    def combine(u):
+        arrived(other_part.at[place_of(u)], qrecv.at[u])
+        pl.when(u >= RING)(lambda: sent(u - RING))
+        load_part(u).start()
+        load_part(u).wait()
+        acc[lax.rem(u, RING)] = (
+            parts[1].astype(jnp.float32) + theirs[...].astype(jnp.float32)
+        ).astype(jnp.bfloat16)
+        for copy in halves(u):
+            copy.start()
+
+    def relay(u):
+        for n, r in enumerate((along, across)):
+            arrived(first_land.at[u, n], hrecv.at[u, n])
+            add_into(strip(u, r, lines_of[n]), first_land.at[u, n])
+        for copy in wholes(u):
+            copy.start()
+
+    def deep_copy(u):
+        place = place_of(u)
+        up = place > dp
+        target = jnp.where(up, dp + 1, dp - 1)
+        there = jnp.where(jnp.logical_and(jnp.logical_not(up), target == place), dps, place)
+        return remote(
+            total.at[u], deep_land.at[there], dsend.at[u], drecv.at[there],
+            (jnp.clip(target, 0, dps - 1), row, col),
+        )
+
+    def finish(u):
+        for n in range(2):
+            arrived(side_land.at[u, n], xrecv.at[u, n])
+        place = place_of(u)
+        result = (
+            strip(u, row)[...].astype(jnp.float32)
+            + side_land[u, 0].astype(jnp.float32)
+            + side_land[u, 1].astype(jnp.float32)
+        )
+        memory[...] = result
+
+        def more(index):
+            arrived(deep_land.at[index], drecv.at[index])
+            memory[...] = memory[...] + deep_land[index].astype(jnp.float32)
+
+        below = jnp.logical_and(place >= dp, dp > 0)
+        above = jnp.logical_and(place <= dp, dp < dps - 1)
+        pl.when(jnp.logical_or(below, jnp.logical_and(above, place < dp)))(lambda: more(place))
+        pl.when(jnp.logical_and(above, place == dp))(lambda: more(dps))
+
+        @pl.when(u < dps - 1)
         def _():
-            from_above(2 * turn)
-
-        @pl.when(turn > 0)
+            total[u] = memory[...].astype(jnp.bfloat16)
+            deep_copy(u).start()
+
+    def read_places(chunk):
+        slot = lax.rem(chunk, 2)
+        place = nth_place(dp, lax.div(chunk, 2), dps)[0]
+        return slot, place, jnp.where(slot == 0, col, 1 - col)
+
+    def load_chunk(chunk):
+        slot, source_dp, source_col = read_places(chunk)
+        return [
+            pltpu.make_async_copy(
+                grads_all.at[source_dp, source_col, r],
+                chunks.at[slot, :, pl.ds(r * width, width)],
+                gsem.at[slot, r],
+            )
+            for r in range(rows)
+        ]
+
+    def start_chunk(chunk):
+        slot, source_dp, source_col = read_places(chunk)
+
+        @pl.when(slot == 1)
         def _():
-            from_side(turn - 1)
-
-        chunk(turn, 1)
-
-        @pl.when(2 * turn + 1 < dps)
+            arrived(grads_all.at[source_dp, source_col], crecv.at[lax.div(chunk, 2)])
+
+        for copy in load_chunk(chunk):
+            copy.start()
+
+    wide_strip = min(512, areas * SUBKEYS)
+    per_strip = wide_strip // SUBKEYS
+
+    def search(chunk, part):
+        slot, source_dp, source_col = read_places(chunk)
+
+        @pl.when(part == 0)
         def _():
-            from_above(2 * turn + 1)
-
+            for copy in load_chunk(chunk):
+                copy.wait()
+
+            def strip(n, carry):
+                columns = pl.ds(pl.multiple_of(n * wide_strip, wide_strip), wide_strip)
+                grid = jnp.dot(
+                    chunks[slot], values_t[:, columns], preferred_element_type=jnp.float32
+                ).astype(jnp.bfloat16)
+                for area in range(per_strip):
+                    grids[n * per_strip + area] = grid[:, area * SUBKEYS : (area + 1) * SUBKEYS]
+                return carry
+
+            lax.fori_loop(0, areas // per_strip, strip, 0)
+
+            @pl.when(chunk + 2 < dps * cols)
+            def _():
+                start_chunk(chunk + 2)
+
+        @pl.when(part == 1)
+        def _():
+            def one(block, carry):
+                row_meta = slot_row(sizes, meta_in, source_dp, source_col, block)
+                lines = pl.ds(pl.multiple_of(block * FBLK, FBLK), FBLK)
+                stacked = grids[:, lines, :].reshape(areas * FBLK, SUBKEYS)
+                product = jnp.dot(
+                    stacked, one_hot(row_meta % SUBKEYS, SUBKEYS), preferred_element_type=jnp.float32
+                )
+                spot_id = lax.broadcasted_iota(jnp.int32, product.shape, 0)
+                sums[block] = jnp.sum(
+                    jnp.where(spot_id == row_meta // SUBKEYS, product, 0.0), axis=0, keepdims=True
+                )
+                return carry
+
+            lax.fori_loop(0, blocks, one, 0)
+
+            for r in range(rows):
+                index = (source_dp * rows + r) * cols + source_col
+                for block in range(blocks):
+                    found[index, block : block + 1, :] = sums[block, :, r * 128 : (r + 1) * 128]
+                away = remote(found.at[index], back.at[me], fsend, frecv, (source_dp, r, source_col))
+                own = jnp.logical_and(
+                    jnp.logical_and(source_dp == dp, row == r), source_col == col
+                )
+                pl.when(jnp.logical_not(own))(away.start)
+                pl.when(own)(pltpu.make_async_copy(found.at[index], back.at[me], flocal).start)
+
+    writes = 4 * dps
+
+    def poll(p, carry):
+        phase = lax.rem(p, 2)
+        writing = p < writes
+        pl.when(jnp.logical_and(writing, phase == 0))(lambda: build(lax.div(p, 2)))
+        pl.when(jnp.logical_and(writing, phase == 1))(lambda: multiply(lax.div(p, 2)))
+
+        @pl.when(p == writes)
+        def _():
+            keep.wait()
+            start_chunk(0)
+            start_chunk(1)
+
+        pl.when(p >= writes)(lambda: search(lax.div(p - writes, 2), phase))
+        turn, third = lax.div(p, 3), lax.rem(p, 3)
+        early = jnp.logical_and(third == 0, jnp.logical_and(turn > 0, turn + 1 < dps))
+        pl.when(p == 1)(lambda: from_line(1))
+        pl.when(early)(lambda: from_line(turn + 1))
+        pl.when(jnp.logical_and(third == 2, turn < dps))(lambda: from_sides(turn))
+        ready = jnp.logical_and(turn > 0, turn <= dps)
+        pl.when(jnp.logical_and(third == 1, ready))(lambda: from_opposite(turn - 1))
+        for event, delay in ((finish, FINISH_AT), (relay, RELAY_AT), (combine, COMBINE_AT)):
+            late = p - delay
+            now = jnp.logical_and(
+                jnp.logical_and(late >= 0, lax.rem(late, 4) == 0), late < 4 * dps
+            )
+            pl.when(now)(functools.partial(event, lax.div(late, 4)))
         return carry
 
-    lax.fori_loop(0, dps, step, 0)
-    from_side(dps - 1)
-    keep.wait()
-    for kk in range(2):
-        pltpu.make_async_copy(tables.at[kk], table.at[0, 0], tsem.at[kk]).wait()
-    pltpu.make_async_copy(parts.at[1], own_part.at[0], psem).wait()
-    remote(parts.at[0], other_part.at[0], qsend, qrecv, (dp, row, 1 - col)).wait_send()
-    arrived(other_part, qrecv)
-    arrived(grads_all.at[:, 0], crecv)
+    lax.fori_loop(0, 8 * dps, poll, 0)
+    for slot in range(2):
+        pltpu.make_async_copy(tables.at[slot], table.at[0, 0], tsem.at[slot]).wait()
+    away(0, 0).wait_send()
     arrived(grads_all.at[:, 0], csend)
-    arrived(grads_all.at[pl.ds(0, dps - 1), 0, :, pl.ds(0, width)], zsend)
-    arrived(grads_all.at[:, 0, :, pl.ds(0, (rows - 1) * width)], xsend)
+    arrived(grads_all.at[:, 0, pl.ds(0, rows - 1)], wsend)
     all_rows(meta_in, msend)
     all_rows(slots_in, ssend)
 
-
-def read_memory(sizes, grads, meta, slots, values):
+    def line_sent(k, carry):
+        pl.when(jnp.logical_and(k <= dp, dp < dps - 1))(lambda: line_copy(k, True).wait_send())
+        pl.when(jnp.logical_and(k >= dp, dp > 0))(lambda: line_copy(k, False).wait_send())
+        return carry
+
+    lax.fori_loop(0, dps, line_sent, 0)
+    arrived(back.at[pl.ds(0, count - 1)], frecv)
+    arrived(back.at[0], flocal)
+    arrived(back.at[pl.ds(0, count - 1)], fsend)
+    for u in range(max(0, dps - RING), dps):
+        sent(u)
+    lax.fori_loop(0, dps - 1, lambda u, c: (deep_copy(u).wait_send(), c)[1], 0)
+
+
+COMBINE_AT, RELAY_AT, FINISH_AT = 6, 9, 14
+
+
+def use_memory(sizes, grads, meta, slots, values, values_t):
     dps, rows, cols = sizes
     tokens, width = grads.shape
     rows_dev, features = values.shape
     blocks = tokens // FBLK
-    low = jnp.bfloat16
+    count = dps * rows * cols
+    low, wide = jnp.bfloat16, jnp.float32
     shape = jax.ShapeDtypeStruct
-    return pl.pallas_call(
-        functools.partial(read_kernel, sizes, blocks),
-        in_specs=[VMEM] * 4,
-        out_specs=[ANY, ANY, ANY, ANY, VMEM],
+    grads_all, table, _, memory, back = pl.pallas_call(
+        functools.partial(memory_kernel, sizes, blocks),
+        in_specs=[VMEM] * 5,
+        out_specs=[ANY] * 3 + [VMEM] * 2,
         out_shape=[
-            shape((dps, cols, tokens, rows * width), low),
+            shape((dps, cols, rows, tokens, width), low),
             shape((dps, cols, tokens, rows_dev), low),
             shape((dps, tokens, features), low),
-            shape((dps, tokens, features), low),
-            shape(meta.shape, meta.dtype),
+            shape((tokens, width), wide),
+            shape((count, blocks, 128), wide),
         ],
         scratch_shapes=[
+            pltpu.VMEM(meta.shape, meta.dtype),
             pltpu.VMEM(slots.shape, slots.dtype),
             pltpu.VMEM((2, tokens, rows_dev), low),
             pltpu.VMEM((2, tokens, features), low),
+            pltpu.VMEM((2, tokens, features), low),
+            pltpu.VMEM((count, blocks, 128), wide),
+            pltpu.VMEM((blocks, 1, rows * 128), wide),
+            pltpu.VMEM((rows_dev // SUBKEYS, tokens, SUBKEYS), low),
+            pltpu.VMEM((tokens, features), low),
+            pltpu.VMEM((RING, tokens, features), low),
+            pltpu.VMEM((dps, 2, tokens // 2, width), low),
+            pltpu.VMEM((dps, 2, tokens, width), low),
+            pltpu.VMEM((dps + 1, tokens, width), low),
+            pltpu.VMEM((dps, tokens, width), low),
             DMA, DMA, DMA, DMA,
+            DMA((dps,)), DMA((dps,)), DMA((dps,)),
+            DMA, DMA((dps, 4)),
             DMA, DMA((dps,)),
-            DMA, DMA((dps, rows)),
-            DMA, DMA,
-            DMA, DMA((2,)), DMA, DMA, DMA,
+            DMA, DMA((2,)), DMA, DMA((dps,)),
+            DMA((2, rows)), DMA,
+            DMA((RING, 2)), DMA((dps, 2)),
+            DMA((RING, 2)), DMA((dps, 2)),
+            DMA((dps,)), DMA((dps + 1,)),
+            DMA, DMA, DMA,
         ],
         compiler_params=pltpu.CompilerParams(collective_id=6, has_side_effects=True),
-        name="read_memory",
-    )(grads, meta, slots, values)
-
-
-def back_kernel(
-    sizes, blocks, grads_all, own_part, other_part, meta_in, values_t,
-    memory, back, side_land, deep_land,
-    chunks, found, hots, mine, theirs, acc, side, total, deep,
-    gsem, osem, tsem, xsend, xrecv, zsend, zrecv, fsend, frecv, flocal, ssem, dsem,
-):
-    spot = here()
-    dp, row, col = spot
-    dps, rows, cols = sizes
-    tokens, width = memory.shape
-    areas = values_t.shape[1] // SUBKEYS
-    count = dps * rows * cols
-    me = index_of(spot, sizes)
-    greet_all(spot, sizes)
-
-    def source(turn):
-        return lax.rem(dp + 1 + turn, dps)
-
-    def load_parts(turn):
-        return (
-            pltpu.make_async_copy(own_part.at[source(turn)], mine, osem),
-            pltpu.make_async_copy(other_part.at[source(turn)], theirs, tsem),
-        )
-
-    def load_chunk(turn, kk):
-        return pltpu.make_async_copy(
-            grads_all.at[source(turn), 1 - col if kk == 0 else col], chunks.at[kk], gsem.at[kk]
-        )
-
-    def piece(turn, k):
-        left = pl.multiple_of(lax.rem(row + k, rows) * width, width)
-        return acc.at[turn, :, pl.ds(left, width)]
-
-    def combine(turn):
-        for copy in load_parts(turn):
-            copy.wait()
-        acc[turn] = (mine[...].astype(jnp.float32) + theirs[...].astype(jnp.float32)).astype(
-            jnp.bfloat16
-        )
-
-        @pl.when(turn + 1 < dps)
-        def _():
-            for copy in load_parts(turn + 1):
-                copy.start()
-
-        for k in range(1, rows):
-            remote(
-                piece(turn, k), side_land.at[turn, rows - k], xsend, xrecv.at[turn, rows - k],
-                (dp, lax.rem(row + k, rows), col),
-            ).start()
-
-    def row_total(turn):
-        copies = []
-        for k in range(1, rows):
-            arrived(side_land.at[turn, k], xrecv.at[turn, k])
-            copies.append(pltpu.make_async_copy(side_land.at[turn, k], side.at[k], ssem.at[k]))
-            copies[-1].start()
-        result = acc[turn, :, pl.ds(pl.multiple_of(row * width, width), width)].astype(jnp.float32)
-        for k in range(1, rows):
-            copies[k - 1].wait()
-            result = result + side[k].astype(jnp.float32)
-        return result
-
-    def deeper(turn):
-        total[turn] = row_total(turn).astype(jnp.bfloat16)
-        remote(
-            total.at[turn], deep_land.at[dps - 2 - turn], zsend, zrecv.at[dps - 2 - turn],
-            (source(turn), row, col),
-        ).start()
-
-    for copy in load_parts(0):
-        copy.start()
-    for kk in range(2):
-        load_chunk(0, kk).start()
-
-    def chunk(turn, kk):
-        source_dp = source(turn)
-        source_col = 1 - col if kk == 0 else col
-        keys = []
-        for block in range(blocks):
-            row_meta = slot_row(sizes, meta_in, source_dp, source_col, block)
-            keys.append(row_meta // SUBKEYS)
-            hots[block] = one_hot(row_meta % SUBKEYS, SUBKEYS)
-        load_chunk(turn, kk).wait()
-
-        def area_step(area, sums):
-            columns = pl.ds(pl.multiple_of(area * SUBKEYS, SUBKEYS), SUBKEYS)
-            grid = jnp.dot(
-                chunks[kk], values_t[:, columns], preferred_element_type=jnp.float32
-            ).astype(jnp.bfloat16)
-            new = []
-            for block in range(blocks):
-                product = jnp.dot(
-                    grid[block * FBLK : (block + 1) * FBLK],
-                    hots[block],
-                    preferred_element_type=jnp.float32,
-                )
-                spot_id = lax.broadcasted_iota(jnp.int32, product.shape, 0) + area * FBLK
-                new.append(
-                    sums[block]
-                    + jnp.sum(
-                        jnp.where(spot_id == keys[block], product, 0.0), axis=0, keepdims=True
-                    )
-                )
-            return tuple(new)
-
-        sums = lax.fori_loop(
-            0, areas, area_step, tuple(jnp.zeros(keys[0].shape, jnp.float32) for _ in range(blocks))
-        )
-
-        @pl.when(turn + 1 < dps)
-        def _():
-            load_chunk(turn + 1, kk).start()
-
-        for r in range(rows):
-            index = (source_dp * rows + r) * cols + source_col
-            for block in range(blocks):
-                found[index, block : block + 1, :] = sums[block][:, r * 128 : (r + 1) * 128]
-            away = remote(found.at[index], back.at[me], fsend, frecv, (source_dp, r, source_col))
-            own = jnp.logical_and(jnp.logical_and(source_dp == dp, row == r), source_col == col)
-            if kk == 0:
-                away.start()
-            else:
-                pl.when(jnp.logical_not(own))(away.start)
-                pl.when(own)(pltpu.make_async_copy(found.at[index], back.at[me], flocal).start)
-
-    def step(turn, carry):
-        @pl.when(2 * turn < dps)
-        def _():
-            combine(2 * turn)
-
-        @pl.when(turn > 0)
-        def _():
-            deeper(turn - 1)
-
-        chunk(turn, 0)
-
-        @pl.when(2 * turn + 1 < dps)
-        def _():
-            combine(2 * turn + 1)
-
-        chunk(turn, 1)
-        return carry
-
-    lax.fori_loop(0, dps, step, 0)
-    result = row_total(dps - 1)
-    for k in range(dps - 1):
-        arrived(deep_land.at[k], zrecv.at[k])
-        copy = pltpu.make_async_copy(deep_land.at[k], deep.at[k % 2], dsem.at[k % 2])
-        copy.start()
-        copy.wait()
-        result = result + deep[k % 2].astype(jnp.float32)
-    memory[...] = result
-    arrived(back.at[pl.ds(0, count - 1)], frecv)
-    arrived(back.at[0], flocal)
-    arrived(back.at[pl.ds(0, count - 1)], fsend)
-    arrived(side_land.at[:, pl.ds(0, rows - 1)], xsend)
-    arrived(deep_land.at[pl.ds(0, dps - 1)], zsend)
-
-
-def back_memory(sizes, grads_all, own_part, other_part, meta_in, values_t):
-    dps, rows, cols = sizes
-    _, _, tokens, features = grads_all.shape
-    width = features // rows
-    blocks = tokens // FBLK
-    count = dps * rows * cols
-    low, wide = jnp.bfloat16, jnp.float32
-    shape = jax.ShapeDtypeStruct
-    memory, back, _, _ = pl.pallas_call(
-        functools.partial(back_kernel, sizes, blocks),
-        in_specs=[ANY, ANY, ANY, VMEM, VMEM],
-        out_specs=[VMEM, VMEM, ANY, ANY],
-        out_shape=[
-            shape((tokens, width), wide),
-            shape((count, blocks, 128), wide),
-            shape((dps, rows, tokens, width), low),
-            shape((dps, tokens, width), low),
-        ],
-        scratch_shapes=[
-            pltpu.VMEM((2, tokens, features), low),
-            pltpu.VMEM((count, blocks, 128), wide),
-            pltpu.VMEM((blocks, SUBKEYS, rows * 128), low),
-            pltpu.VMEM((tokens, features), low),
-            pltpu.VMEM((tokens, features), low),
-            pltpu.VMEM((dps, tokens, features), low),
-            pltpu.VMEM((rows, tokens, width), low),
-            pltpu.VMEM((dps, tokens, width), low),
-            pltpu.VMEM((2, tokens, width), low),
-            DMA((2,)), DMA, DMA,
-            DMA, DMA((dps, rows)),
-            DMA, DMA((dps,)),
-            DMA, DMA, DMA, DMA((rows,)), DMA((2,)),
-        ],
-        compiler_params=pltpu.CompilerParams(collective_id=7, has_side_effects=True),
-        name="back_memory",
-    )(grads_all, own_part, other_part, meta_in, values_t)
-    return memory, back
+        name="use_memory",
+    )(grads, meta, slots, values, values_t)
+    return grads_all, table, memory, back
 
 
 def unweigh_kernel(rows_dev, owners, back_ref, picks_ref, rank_ref, weights_ref, first_ref, second_ref):
@@ -1471,10 +1600,9 @@
     spare = ((0, 0), (0, 0), (0, 128 - cap))
     meta = jnp.pad(jnp.swapaxes(meta, 0, 1), spare, constant_values=-1)
     slots = jnp.pad(jnp.swapaxes(slots, 0, 1).astype(jnp.float32), spare)
-    grads_all, table, own_part, other_part, meta_in = read_memory(
-        sizes, grad_memory, meta, slots, values
-    )
-    memory, back = back_memory(sizes, grads_all, own_part, other_part, meta_in, values.T)
+    grads_all, table, memory, back = use_memory(
+        sizes, grad_memory, meta, slots, values, values.T
+    )
     first_t, second_t = unweigh(
         jnp.transpose(back, (1, 2, 0))[:, :cap], flat, rank, weights, rows_dev, owners
     )
@@ -1518,42 +1646,6 @@
         )
         log_sums.append(peak_score[:, 0] + jnp.log(row_sum[:, 0]))
     return (jnp.concatenate(outputs, axis=1), jnp.stack(log_sums))
-
-
-def attend_backward(queries, keys, values, allowed, log_sums, grad_out):
-    grad_queries = []
-    grad_keys = []
-    grad_values = []
-    for head_index in range(queries.shape[1] // HDIM):
-        columns = slice(head_index * HDIM, (head_index + 1) * HDIM)
-        query_head = queries[:, columns]
-        key_head = keys[:, columns]
-        value_head = values[:, columns]
-        grad_head = grad_out[:, columns]
-        scores = head_scores(query_head, key_head, allowed)
-        probabilities = jnp.exp(scores - log_sums[head_index][:, None])
-        grad_probs = jnp.einsum(
-            "qd,kd->qk", grad_head, value_head, preferred_element_type=jnp.float32
-        )
-        inner_sum = jnp.sum(probabilities * grad_probs, axis=1, keepdims=True)
-        grad_scores = (probabilities * (grad_probs - inner_sum)).astype(jnp.bfloat16)
-        grad_queries.append(
-            jnp.dot(grad_scores, key_head, preferred_element_type=jnp.float32) * HDIM ** (-0.5)
-        )
-        grad_keys.append(
-            jnp.einsum("qk,qd->kd", grad_scores, query_head, preferred_element_type=jnp.float32)
-            * HDIM ** (-0.5)
-        )
-        grad_values.append(
-            jnp.einsum(
-                "qk,qd->kd",
-                probabilities.astype(jnp.bfloat16),
-                grad_head,
-                preferred_element_type=jnp.float32,
-            )
-        )
-    stacked = jnp.stack([jnp.concatenate(grad_keys, axis=1), jnp.concatenate(grad_values, axis=1)])
-    return (jnp.concatenate(grad_queries, axis=1), stacked)
 
 
 def dense(left, right):
@@ -1626,15 +1718,13 @@
         dense_tn(gated_value, dy_own).astype(low),
         grad_keys.reshape(-1, HALF).astype(low),
     ]
-    output, grad_hidden, grad_hidden_all, gain_two_grad, *shards = middle(
-        sizes, grad_part, out_part, hidden, cotangent, gain_two, first_terms
+    grad_hidden, grad_hidden_all, gain_two_grad, *shards = middle(
+        sizes, grad_part, hidden, cotangent, gain_two, first_terms
     )
     grad_attended = dense_nt(grad_hidden_all, attn_w).astype(low)
-    grad_query_own, grad_kv_part = attend_backward(
-        qkv[0], kv_all[0], kv_all[1], allowed, log_sums, grad_attended
-    )
-    grad_kv = pair_sum(sizes, grad_kv_part)
-    grad_q = grad_query_own.astype(low)
+    grad_q, grad_kv, output, grad_w_query, grad_w_gate, grad_w_proj, grad_keys_half = turn(
+        sizes, prefix, qkv[0], kv_all, grad_attended, log_sums, out_part, hidden, shards
+    )
     x_part = (
         dense_nt(grad_q, qkv_w[0]) + dense_nt(grad_kv[0], qkv_w[1]) + dense_nt(grad_kv[1], qkv_w[2])
     ).astype(low)
@@ -1642,11 +1732,9 @@
         jnp.stack([dense_tn(normed_one, part) for part in (grad_q, grad_kv[0], grad_kv[1])]).astype(low),
         dense_tn(attended, grad_hidden_all).astype(low),
     ]
-    (
-        grad_inputs, gain_sums, grad_values,
-        grad_w_query, grad_w_gate, grad_w_proj, _, grad_w_qkv, grad_w_attn_out, grad_subkeys,
-    ) = last(
-        sizes, x_part, inputs, grad_hidden, gain_one, gain_two_grad, shards, last_terms, table, grads_all
+    grad_inputs, gain_sums, grad_values, grad_w_qkv, grad_w_attn_out, grad_subkeys = last(
+        sizes, x_part, inputs, grad_hidden, gain_one, gain_two_grad, grad_keys_half, last_terms,
+        table, grads_all,
     )
     gain_rows = gain_sums.reshape(sizes[2], 2, width_part)
     grad_gain_one = gain_rows[:, 0].reshape(-1)

time: 492 us -> 471 us (0.957)
  matrix products: 48.6 us -> 38.9 us
    dot_general x16 -> x0, matrix products: 9.52 us -> none  [the longest x4 3.07 us: attend_backward(): jnp.einsum('qd,kd->qk', grad_head, value_head, preferred_element_type=jnp...]
    pallas_call x4 -> x3, Pallas kernels: 237 us -> 228 us  [the longest x1 123 us: use_memory(): pl.pallas_call(functools.partial(memory_kernel, sizes, blocks), in_specs=...]
    pallas_call x1, Pallas kernels: 42.7 us -> 48.3 us  [middle(): pl.pallas_call(functools.partial(middle_kernel, sizes), in_specs=[VMEM] *...]
    unnamed x92 -> x70, local copies, waits for them, and re-layouts: 17.5 us -> 13.8 us
where the time goes in v5:
time: 471 us; the launch traced here: 462 us
  Pallas kernels  373 us (79%)
  matrix products  38.9 us (8%)
  local copies, waits for them, and re-layouts  26.2 us (6%)
  other arithmetic  21.5 us (5%)
    pallas_call x1, Pallas kernels, use_memory(): pl.pallas_call(functools.partial(memory_kernel, sizes, blocks), in_specs=...  123 us
    pallas_call x1, Pallas kernels, last(): pl.pallas_call(functools.partial(last_kernel, sizes), in_specs=[VMEM] * 8...  64.9 us
    pallas_call x1, Pallas kernels, middle(): pl.pallas_call(functools.partial(middle_kernel, sizes), in_specs=[VMEM] *...  48.3 us
    pallas_call x1, Pallas kernels, turn(): pl.pallas_call(functools.partial(turn_kernel, sizes), in_specs=[pl.BlockS...  39.3 us
    pallas_call x1, Pallas kernels, join(): pl.pallas_call(functools.partial(join_kernel, sizes), in_specs=[VMEM] * 3...  32.5 us
    pallas_call x1, Pallas kernels, start_all(): pl.pallas_call(functools.partial(start_kernel, sizes), in_specs=[VMEM] *...  30.2 us
    unnamed x70, local copies, waits for them, and re-layouts  13.8 us
    pallas_call x1, Pallas kernels, weigh(): pl.pallas_call(functools.partial(weigh_kernel, rows_dev, owners, cap), gr...  12.4 us

profile of v5, /device:TPU:0, one launch (start us, length us, event | category | flops | bytes accessed | tf_op | source)
XLA Modules:
  0.0 462.2 jit_solution(13643318439372570162)
XLA Ops:
  4.8 0.8 constant_dynamic-slice_fusion
  6.3 6.5 %route.1 = (s32[4,1,4096]{2,1,0:T(1,128)}, s32[4,32,128]{2,1,0:T(8,128)}) custom-call(s32[4,1,4096]{2,1,0:T(1,128)} %bitcast.99), custom_call_target="tpu_custom_call" | custom-call | tf_op jit(solution)/shard_map/route/pallas_call | solution.py:1005
  12.9 1.5 copy.49
  15.2 6.4 %copy.42 = bf16[2048,1024]{0,1:T(8,128)(2,1)} copy(bf16[2048,1024]{1,0:T(8,128)(2,1)} %values.1) | data formatting | bytes 8388608 | tf_op args[11]
  21.6 30.2 %start_all.1 = (bf16[512,1024]{1,0:T(8,128)(2,1)}, bf16[512,1024]{1,0:T(8,128)(2,1)}, bf16[3,1024,256]{2,1,0:T(8,128)(2,1)}, bf16[1024,1024]{1,0:T(8,128)(2,1)},...) custom-call(bf16[256,512]{1,0:T(8,128)(2,1)} %refs_1_.3, ...), custom_call_target="tpu_custom_call" | custom-call | tf_op jit(solution)/shard_map/start_all/pallas_call | solution.py:243
  51.9 1.5 fusion
  53.4 2.8 fusion.8
  56.2 0.9 slice.114.src
  57.1 4.0 swap_tokens.1.refs_2_
  61.0 1.3 slice_bitcast_fusion
  62.3 0.8 fusion.58
  66.4 0.8 fusion.60
  71.1 1.4 convolution_convert_fusion.3.part
  72.5 32.5 %join.1 = (f32[256,512]{1,0:T(8,128)}, bf16[512,1024]{1,0:T(8,128)(2,1)}) custom-call(bf16[512,1024]{1,0:T(8,128)(2,1)} %convolution_convert_fusion.3.part, bf16[256,512]{1,0:T(8,128)(2,1)} %refs_1_.3, bf16[1,512]{1,0:T(2,128)(2,1)} %broadcast_in_dim.12.gain.refs_3_), custom_call_target="tpu_custom_call" | custom-call | tf_op jit(solution)/shard_map/join/pallas_call | solution.py:323
  105.1 1.8 fusion.62
  106.9 1.4 multiply_convert_fusion.2
  109.1 2.2 convolution_convert_fusion.2.query_ref
  111.3 12.4 %weigh.1 = (f32[4,32,128]{2,1,0:T(8,128)}, bf16[4,32,128]{2,1,0:T(8,128)(2,1)}) custom-call(bf16[512,1024]{1,0:T(8,128)(2,1)} %convolution_convert_fusion.2.query_ref, bf16[2,256,512]{2,1,0:T(8,128)(2,1)} %dynamic-slice_bitcast_fusion.keys_ref, s32[4,1,4096]{2,1,0:T(1,128)} %bitcast.100, s32[4,1,4096]{2,1,0:T(1,128)} %get-tuple-element.59.rank_ref), custom_call_target="tpu_custom_call" | custom-call | tf_op jit(solution)/shard_map/weigh/pallas_call | solution.py:1056
  123.7 1.4 copy.48
  125.1 123.3 %use_memory.1 = (bf16[4,2,4,512,256]{4,3,2,1,0:T(8,128)(2,1)}, bf16[4,2,512,2048]{3,2,1,0:T(8,128)(2,1)}, bf16[4,512,1024]{2,1,0:T(8,128)(2,1)}, f32[512,256]{1,0:T(8,128)}, f32[32,4,128]{2,1,0:T(4,128)}) custom-call(bf16[512,256]{1,0:T(8,128)(2,1)} %get-tuple-element.103.grads, s32[32,4,128]{2,1,0:T(4,128)} %bitcast.102, f32[32,4,128]{2,1,0:T(4,128)} %bitcast.103, ...), custom_call_target="tpu_custom_call" | custom-call | tf_op jit(solution)/shard_map/use_memory/pallas_call | solution.py:1491
  248.4 2.2 multiply_convert_fusion
  250.7 1.3 convolution_convert_fusion.9.refs_6_
  252.0 0.8 copy.43
  252.8 11.7 %unweigh.1 = (bf16[256,512]{1,0:T(8,128)(2,1)}, bf16[256,512]{1,0:T(8,128)(2,1)}) custom-call(f32[4,128,32]{2,1,0:T(8,128)} %bitcast.98, s32[4,1,4096]{2,1,0:T(1,128)} %bitcast.101, s32[4,1,4096]{2,1,0:T(1,128)} %get-tuple-element.59.rank_ref, f32[4,32,128]{2,1,0:T(8,128)} %get-tuple-element.62.weights_ref), custom_call_target="tpu_custom_call" | custom-call | tf_op jit(solution)/shard_map/unweigh/pallas_call | solution.py:1571
  264.6 1.5 fusion.12
  266.0 1.6 fusion.13
  267.6 0.8 pad_maximum_fusion.4
  269.2 1.3 fusion.15
  270.5 1.5 add_convert_fusion.1.refs_0_
  272.0 1.3 convolution_convert_fusion.10.refs_5_
  273.3 2.6 convolution_convert_fusion.refs_4_
  275.9 48.3 %middle.1 = (f32[256,512]{1,0:T(8,128)}, bf16[512,1024]{1,0:T(8,128)(2,1)}, f32[1,512]{1,0:T(1,128)}, bf16[128,1024]{1,0:T(8,128)(2,1)}, bf16[128,256]{1,0:T(8,1...) custom-call(bf16[512,1024]{1,0:T(8,128)(2,1)} %add_convert_fusion.1.refs_0_, ...), custom_call_target="tpu_custom_call" | custom-call | tf_op jit(solution)/shard_map/middle/pallas_call | solution.py:624
  324.3 2.5 convolution_convert_fusion.13.refs_3_
  326.8 2.5 convolution_convert_fusion.5.refs_7_
  329.2 1.4 convolution_convert_fusion.1.refs_5_
  330.7 39.3 %turn.1 = (bf16[512,256]{1,0:T(8,128)(2,1)}, bf16[2,512,256]{2,1,0:T(8,128)(2,1)}, bf16[256,512]{1,0:T(8,128)(2,1)}, bf16[512,1024]{1,0:T(8,128)(2,1)}, bf16[512...) custom-call(s32[1]{0:T(128)} %copy.53.refs_0_, bf16[512,256]{1,0:T(8,128)(2,1)} %copy-done.12, ...), custom_call_target="tpu_custom_call" | custom-call | tf_op jit(solution)/shard_map/turn/pallas_call | solution.py:932
  370.0 1.8 convert_element_type.123
  371.8 1.9 convert_element_type.124
  373.6 1.6 fusion.9
  376.6 1.3 pad_maximum_fusion.refs_6_
  379.8 1.6 convert_element_type.122
  381.8 1.5 add_convert_fusion.refs_0_
  383.3 64.9 %last.1 = (f32[256,512]{1,0:T(8,128)}, f32[2,8,128]{2,1,0:T(8,128)}, f32[2048,1024]{1,0:T(8,128)}, bf16[3,512,256]{2,1,0:T(8,128)(2,1)}, bf16[256,512]{1,0:T(8,128)(2,1)}, /*index=5*/bf16[4,2,256,512]{3,2,1,0:T(8,128)(2,1)}) custom-call(bf16[512,1024]{1,0:T(8,128)(2,1)} %add_convert_fusion.refs_0_, bf16[256,512]{1,0:T(8,128)(2,1)} %refs_1_.3, ...), custom_call_target="tpu_custom_call" | custom-call | tf_op jit(solution)/shard_map/last/pallas_call | solution.py:804
  448.3 0.9 reshape.126
  449.7 1.9 convert_element_type.121
  451.6 2.6 convert_element_type.120
  454.1 2.6 convert_element_type.125
  458.2 3.5 copy.56
  (102 shorter events, 19.3 us)
Async XLA Ops:
  0.6 13.8 %copy-start = (bf16[4,2,256,512]{3,2,1,0:T(8,128)(2,1)S(1)}, bf16[4,2,256,512]{3,2,1,0:T(8,128)(2,1)}, u32[]{:S(2)}) copy-start(bf16[4,2,256,512]{3,2,1,0:T(8,128)(2,1)} %param.23) | copy-start | bytes 6291460
  56.2 12.3 %copy-start.12 = (bf16[512,256]{1,0:T(8,128)(2,1)}, bf16[512,256]{1,0:T(8,128)(2,1)S(1)}, u32[]{:S(2)}) copy-start(bf16[512,256]{1,0:T(8,128)(2,1)S(1)} %slice_bitcast_fusion.2.refs_1_) | copy-start | bytes 786436
  66.3 4.7 %copy-start.27 = (bf16[512,64]{0,1:T(8,128)(2,1)}, bf16[512,64]{0,1:T(8,128)(2,1)S(1)}, u32[]{:S(2)}) copy-start(bf16[512,64]{0,1:T(8,128)(2,1)S(1)} %convolution_convert_fusion.17) | copy-start | bytes 196612
  68.5 2.6 copy-start.29
  69.8 1.3 copy-start.25
  70.4 34.7 %copy-start.31 = (bf16[512,64]{0,1:T(8,128)(2,1)}, bf16[512,64]{0,1:T(8,128)(2,1)S(1)}, u32[]{:S(2)}) copy-start(bf16[512,64]{0,1:T(8,128)(2,1)S(1)} %convolution_convert_fusion.19) | copy-start | bytes 196612
  70.4 34.7 %copy-start.4 = (bf16[1024,256]{1,0:T(8,128)(2,1)S(1)}, bf16[1024,256]{1,0:T(8,128)(2,1)}, u32[]{:S(2)}) copy-start(bf16[1024,256]{1,0:T(8,128)(2,1)} %get-tuple-element.56) | copy-start | bytes 1572868
  105.0 1.8 copy-start.7
  105.1 1.8 copy-start.14
  106.9 1.4 copy-start.10
  106.9 2.2 copy-start.23
  248.4 2.3 copy-start.8
  248.4 3.5 copy-start.22
  264.5 3.9 copy-start.18
  264.5 4.3 copy-start.20
  266.0 3.2 copy-start.24
  269.2 1.3 copy-start.13
  270.5 1.5 copy-start.11
  275.9 48.4 %copy-start.26 = (bf16[256,1024]{1,0:T(8,128)(2,1)S(1)}, bf16[256,1024]{1,0:T(8,128)(2,1)}, u32[]{:S(2)}) copy-start(bf16[256,1024]{1,0:T(8,128)(2,1)} %get-tuple-element.54) | copy-start | bytes 1572868
  275.9 50.8 %copy-start.28 = (bf16[512,64]{0,1:T(8,128)(2,1)S(1)}, bf16[512,64]{0,1:T(8,128)(2,1)}, u32[]{:S(2)}) copy-start(bf16[512,64]{0,1:T(8,128)(2,1)} %copy-done.27) | copy-start | bytes 196612
  275.9 50.8 %copy-start.30 = (bf16[512,64]{0,1:T(8,128)(2,1)S(1)}, bf16[512,64]{0,1:T(8,128)(2,1)}, u32[]{:S(2)}) copy-start(bf16[512,64]{0,1:T(8,128)(2,1)} %copy-done.29) | copy-start | bytes 196612
  275.9 50.8 %copy-start.32 = (bf16[512,64]{0,1:T(8,128)(2,1)S(1)}, bf16[512,64]{0,1:T(8,128)(2,1)}, u32[]{:S(2)}) copy-start(bf16[512,64]{0,1:T(8,128)(2,1)} %copy-done.31) | copy-start | bytes 196612
  324.3 4.9 %copy-start.15 = (bf16[256,1024]{1,0:T(8,128)(2,1)S(1)}, bf16[256,1024]{1,0:T(8,128)(2,1)}, u32[]{:S(2)}) copy-start(bf16[256,1024]{1,0:T(8,128)(2,1)} %get-tuple-element.53) | copy-start | bytes 1572868
  330.6 43.0 %copy-start.9 = (bf16[512,1024]{1,0:T(8,128)(2,1)S(1)}, bf16[512,1024]{1,0:T(8,128)(2,1)}, u32[]{:S(2)}) copy-start(bf16[512,1024]{1,0:T(8,128)(2,1)} %get-tuple-element.51) | copy-start | bytes 3145732
  371.8 3.5 copy-start.17
  376.6 2.0 copy-start.5
  376.6 2.0 copy-start.21
  378.6 1.2 copy-start.6
  383.3 73.4 %copy-start.19 = (bf16[256,512]{1,0:T(8,128)(2,1)S(1)}, bf16[256,512]{1,0:T(8,128)(2,1)}, u32[]{:S(2)}) copy-start(bf16[256,512]{1,0:T(8,128)(2,1)} %get-tuple-element.116) | copy-start | bytes 786436
  448.2 5.9 %copy-start.3 = (bf16[4,2,256,512]{3,2,1,0:T(8,128)(2,1)S(1)}, bf16[4,2,256,512]{3,2,1,0:T(8,128)(2,1)}, u32[]{:S(2)}) copy-start(bf16[4,2,256,512]{3,2,1,0:T(8,128)(2,1)} %get-tuple-element.87) | copy-start | bytes 6291460
  449.7 7.7 %copy-start.16 = (f32[256,512]{1,0:T(8,128)S(1)}, f32[256,512]{1,0:T(8,128)}, u32[]{:S(2)}) copy-start(f32[256,512]{1,0:T(8,128)} %get-tuple-element.117) | copy-start | bytes 1572868
  451.6 6.7 %copy-start.2 = (f32[2048,1024]{1,0:T(8,128)S(1)}, f32[2048,1024]{1,0:T(8,128)}, u32[]{:S(2)}) copy-start(f32[2048,1024]{1,0:T(8,128)} %get-tuple-element.126) | copy-start | bytes 25165828
  458.2 3.5 copy-start.1

commit v6 on v5

--- a/solution.py
+++ b/solution.py
@@ -70,35 +70,36 @@
     pl.semaphore_wait(barrier, 1)
 
 
-def device_of(index, sizes):
-    _, rows, cols = sizes
-    return (
-        lax.div(index, rows * cols),
-        lax.rem(lax.div(index, cols), rows),
-        lax.rem(index, cols),
-    )
-
-
 def index_of(spot, sizes):
     return (spot[0] * sizes[1] + spot[1]) * sizes[2] + spot[2]
 
 
+def each_other(spot, sizes, action):
+    dp, row, col = spot
+    dps, rows, cols = sizes
+
+    def level(step, carry):
+        there = lax.rem(dp + step, dps)
+        for j in range(rows):
+            for k in range(cols):
+                device = (there, lax.rem(row + j, rows), lax.rem(col + k, cols))
+                if j + k > 0:
+                    action(device)
+                else:
+                    pl.when(step > 0)(functools.partial(action, device))
+        return carry
+
+    lax.fori_loop(0, dps, level, 0)
+
+
 def greet_all(spot, sizes):
     barrier = pltpu.get_barrier_semaphore()
-    count = sizes[0] * sizes[1] * sizes[2]
-    me = index_of(spot, sizes)
-
-    def greet(step, carry):
-        pl.semaphore_signal(
-            barrier,
-            inc=1,
-            device_id=device_of(lax.rem(me + step, count), sizes),
-            device_id_type=MESH,
-        )
-        return carry
-
-    lax.fori_loop(1, count, greet, 0)
-    pl.semaphore_wait(barrier, count - 1)
+
+    def greet(device):
+        pl.semaphore_signal(barrier, inc=1, device_id=device, device_id_type=MESH)
+
+    each_other(spot, sizes, greet)
+    pl.semaphore_wait(barrier, sizes[0] * sizes[1] * sizes[2] - 1)
 
 
 class Gather:
@@ -192,10 +193,10 @@
     return [DMA((rows,)), DMA((rows,))]
 
 
-def start_kernel(sizes, *refs):
-    x, dy, wqkv, wquery, wgate, wproj, wattn = refs[:7]
-    xs, dys, wqkv_all, wquery_all, wgate_all, wproj_all, wattn_all = refs[7:14]
-    xsend, xrecv, ysend, yrecv, wsend, wrecv, wlocal = refs[14:]
+def start_kernel(sizes, rows_dev, *refs):
+    x, dy, wqkv, wquery, wgate, wproj, wattn, picks = refs[:8]
+    xs, dys, wqkv_all, wquery_all, wgate_all, wproj_all, wattn_all, rank, meta = refs[8:17]
+    xsend, xrecv, ysend, yrecv, wsend, wrecv, wlocal = refs[17:]
     spot = here()
     dp, row, col = spot
     greet_plane(spot, sizes)
@@ -222,13 +223,21 @@
         away.start()
         own.start()
         copies += [away, own]
+
+    def one(block, carry):
+        rank[block], meta[block] = route_block(
+            picks[block], rows_dev, meta.shape[1], meta.shape[2]
+        )
+        return carry
+
+    lax.fori_loop(0, picks.shape[0], one, 0)
     for copy in copies:
         copy.wait()
     gather_x.wait()
     gather_y.wait()
 
 
-def start_all(sizes, x, dy, wqkv, wquery, wgate, wproj, wattn):
+def start_all(sizes, rows_dev, x, dy, wqkv, wquery, wgate, wproj, wattn, flat):
     tokens, width = x.shape
     half = sizes[1] // sizes[2]
     cols = sizes[2]
@@ -240,10 +249,12 @@
         return jax.ShapeDtypeStruct(tuple(shape), low)
 
     whole = jax.ShapeDtypeStruct((half * tokens, cols * width), low)
+    blocks, count = flat.shape
+    owners = sizes[0] * sizes[1] * sizes[2]
     return pl.pallas_call(
-        functools.partial(start_kernel, sizes),
-        in_specs=[VMEM] * 7,
-        out_specs=[ANY] * 7,
+        functools.partial(start_kernel, sizes, rows_dev),
+        in_specs=[VMEM] * 8,
+        out_specs=[ANY] * 7 + [VMEM] * 2,
         out_shape=[
             whole,
             whole,
@@ -252,11 +263,13 @@
             twice(wgate, 0),
             twice(wproj, 1),
             twice(wattn, 1),
+            jax.ShapeDtypeStruct((blocks, 1, count), jnp.int32),
+            jax.ShapeDtypeStruct((blocks, owners, count // owners), jnp.int32),
         ],
         scratch_shapes=plane_sems(sizes) * 2 + [DMA((5,))] * 3,
         compiler_params=pltpu.CompilerParams(collective_id=0, has_side_effects=True),
         name="start_all",
-    )(x, dy, wqkv, wquery, wgate, wproj, wattn)
+    )(x, dy, wqkv, wquery, wgate, wproj, wattn, flat[:, None])
 
 
 def swap_kernel(sizes, src, dst, send, recv, own):
@@ -571,8 +584,8 @@
     pl.semaphore_wait(barrier, rows * cols + 1)
 
 
-FIRST_DIMS = (0, 0, 0, 0)
-FIRST_COLS = (0, 0, 1, 0)
+FIRST_DIMS = (0, 0, 0)
+FIRST_COLS = (0, 1, 0)
 LAST_DIMS = (1, 0)
 LAST_COLS = (1, 1)
 
@@ -585,12 +598,12 @@
 
 def middle_kernel(sizes, *refs):
     part, hidden, dy, gain = refs[:4]
-    terms = refs[4:8]
-    grad, grad_all, gain_grad = refs[8:11]
-    shards = refs[11:15]
-    landing, mine, theirs, block = refs[15:19]
-    halves, pair_land, below, above = refs[19:23], refs[23:27], refs[27:31], refs[31:35]
-    ssend, srecv, gsend, grecv, psend, precv, hsend, hrecv, *line = refs[35:]
+    terms = refs[4:7]
+    grad, grad_all, gain_grad = refs[7:10]
+    shards = refs[10:13]
+    landing, mine, theirs, block = refs[13:17]
+    halves, pair_land, below, above = refs[17:20], refs[20:23], refs[23:26], refs[26:29]
+    ssend, srecv, gsend, grecv, psend, precv, hsend, hrecv, *line = refs[29:]
     spot = here()
     greet_cross(spot, sizes)
     scatter = Scatter(spot, sizes, part, landing, ssend, srecv)
@@ -623,8 +636,8 @@
     shards = [halved(h, d, dps) for h, d in zip(halves, FIRST_DIMS)]
     return pl.pallas_call(
         functools.partial(middle_kernel, sizes),
-        in_specs=[VMEM] * 8,
-        out_specs=[VMEM] * 7,
+        in_specs=[VMEM] * 7,
+        out_specs=[VMEM] * 6,
         out_shape=[
             jax.ShapeDtypeStruct((tokens, width), wide),
             jax.ShapeDtypeStruct(part.shape, low),
@@ -639,8 +652,8 @@
         ]
         + [pltpu.VMEM(h, low) for h in halves] * 4
         + plane_sems(sizes) * 2
-        + [DMA, DMA, DMA((4,)), DMA((4,))]
-        + line_sems(sizes, 4, 4),
+        + [DMA, DMA, DMA((3,)), DMA((3,))]
+        + line_sems(sizes, 3, 4),
         compiler_params=pltpu.CompilerParams(collective_id=4, has_side_effects=True),
         name="middle",
     )(part, hidden, dy, gain[None], *terms)
@@ -648,16 +661,16 @@
 
 def last_kernel(sizes, *refs):
     part, x, above_grad, gain, other_gain = refs[:5]
-    keys, terms = refs[5], refs[6:8]
-    table, grads_all = refs[8:10]
-    grad, gain_sums, row_grads = refs[10:13]
-    lasts, keys_all = refs[13:15], refs[15]
-    landing, mine, theirs, own_gain, gain_landing, tables, chunks = refs[16:23]
-    halves, pair_land, below, above = refs[23:25], refs[25:27], refs[27:29], refs[29:31]
+    keys, shard, terms = refs[5], refs[6], refs[7:9]
+    table, grads_all = refs[9:11]
+    grad, gain_sums, row_grads, first = refs[11:15]
+    lasts, keys_all = refs[15:17], refs[17]
+    landing, mine, theirs, own_gain, gain_landing, tables, chunks = refs[18:25]
+    halves, pair_land, below, above = refs[25:27], refs[27:29], refs[29:31], refs[31:33]
     (
         ssend, srecv, psend, precv, bsend, brecv, hsend, hrecv, tsem, csem,
         xsend, xrecv, kxsend, kxrecv, *line
-    ) = refs[31:]
+    ) = refs[33:]
     spot = here()
     dp, row, col = spot
     dps, rows, cols = sizes
@@ -687,6 +700,9 @@
     scatter.start()
     pair = PairSum(spot, sizes, terms, LAST_COLS, halves, pair_land, hsend, hrecv)
     pair.start()
+    slab(first, 0, dp, dps)[...] = shard[...]
+    gather = LineGather(spot, sizes, [first], [0], line[7:])
+    gather.start()
     pair.finish()
     reduce = LineReduce(spot, sizes, halves, LAST_DIMS, below, above, line[:4])
     reduce.start()
@@ -746,21 +762,20 @@
         own_gain[line_index : line_index + 1] = gains[:, columns]
         own_gain[lines + line_index : lines + line_index + 1] = other_gain[:, columns]
 
-    def tell(step, carry):
-        device = device_of(lax.rem(me + step, count), sizes)
+    def tell(device):
         remote(own_gain, gain_landing.at[me], bsend, brecv, device).start()
-        return carry
-
-    lax.fori_loop(1, count, tell, 0)
+
+    each_other(spot, sizes, tell)
     gain_landing[me] = own_gain[...]
     grad[...] = total
     for k in range(1, rows):
         sideways(k).start()
     cross(keys, 0).start()
     keys_all[row, col] = keys[...]
+    gather.event(1)
     reduce.event(1)
     products(loads // 4, loads // 2)
-    lax.fori_loop(2, dps, lambda time, c: (reduce.event(time), c)[1], 0)
+    lax.fori_loop(2, dps, lambda time, c: (gather.event(time), reduce.event(time), c)[2], 0)
     for first, half, dim in zip(lasts, halves, LAST_DIMS):
         slab(first, dim, dp, dps)[...] = slab(half, dim, dp, dps)[...]
     final = LineGather(spot, sizes, lasts, LAST_DIMS, line[4:7])
@@ -785,11 +800,12 @@
     arrived(gain_landing.at[pl.ds(0, count - 1)], bsend)
     arrived(keys_all.at[:, col], kxsend)
     arrived(keys_all.at[pl.ds(0, rows - 1), col], xsend)
+    gather.finish()
     reduce.finish()
     final.finish()
 
 
-def last(sizes, part, x, above, gain, other_gain, keys, terms, table, grads_all):
+def last(sizes, part, x, above, gain, other_gain, keys, shard, terms, table, grads_all):
     tokens, width = x.shape
     dps, rows, cols = sizes
     lines = 2 * width // 128
@@ -803,12 +819,13 @@
     chunk = table.shape[2]
     return pl.pallas_call(
         functools.partial(last_kernel, sizes),
-        in_specs=[VMEM] * 8 + [ANY] * 2,
-        out_specs=[VMEM] * 6,
+        in_specs=[VMEM] * 9 + [ANY] * 2,
+        out_specs=[VMEM] * 7,
         out_shape=[
             shape((tokens, width), wide),
             shape((cols, lines, 128), wide),
             shape((rows_dev, features), wide),
+            shape((shard.shape[0] * dps, shard.shape[1]), low),
         ]
         + [shape(s, low) for s in halves]
         + [shape((rows, cols) + keys.shape, low)],
@@ -825,19 +842,20 @@
         + plane_sems(sizes)
         + [DMA, DMA, DMA, DMA, DMA((2,)), DMA((2,)), DMA((2,)), DMA((2, rows))]
         + [DMA, DMA((rows,)), DMA, DMA]
-        + line_sems(sizes, 2, 7),
+        + line_sems(sizes, 2, 7)
+        + line_sems(sizes, 1, 3),
         compiler_params=pltpu.CompilerParams(collective_id=5, has_side_effects=True),
         name="last",
-    )(part, x, above, gain[None], other_gain, keys, *terms, table, grads_all)
+    )(part, x, above, gain[None], other_gain, keys, shard, *terms, table, grads_all)
 
 
 def turn_kernel(sizes, *refs):
     prefix, queries, kv, grad_out, log_sums, out_part, hidden = refs[:7]
-    shards = refs[7:11]
+    shards, term = refs[7:10], refs[10]
     grad_q, grad_kv, output = refs[11:14]
-    firsts = refs[14:18]
-    totals, kv_landing, out_landing = refs[18:21]
-    osend, orecv, ksend, krecv, *line = refs[21:]
+    firsts, term_shard = refs[14:17], refs[17]
+    totals, kv_landing, out_landing, half, pair_land, below, above = refs[18:25]
+    osend, orecv, ksend, krecv, hsend, hrecv, *line = refs[25:]
     spot = here()
     dp, row, col = spot
     dps = sizes[0]
@@ -847,10 +865,20 @@
     greet_cross(spot, sizes)
     for first, dim, shard in zip(firsts, FIRST_DIMS, shards):
         slab(first, dim, dp, dps)[...] = shard[...]
-    gather = LineGather(spot, sizes, firsts, FIRST_DIMS, line)
+    pair = PairSum(spot, sizes, [term], [0], [half], [pair_land], hsend, hrecv)
+    pair.start()
+    gather = LineGather(spot, sizes, firsts, FIRST_DIMS, line[:3])
     gather.start()
     out_scatter = Scatter(spot, sizes, out_part, out_landing, osend, orecv)
     out_scatter.start()
+    pair.finish()
+    reduce = LineReduce(spot, sizes, [half], [0], [below], [above], line[3:])
+    reduce.start()
+
+    def events(time):
+        gather.event(time)
+        reduce.event(time)
+
     limit = prefix[0]
     key_pos = lax.broadcasted_iota(jnp.int32, (keys, tile), 0)
     lane = lax.broadcasted_iota(jnp.int32, (1, 2 * HDIM), 1)
@@ -895,8 +923,8 @@
             totals[0, :, lanes] = totals[0, :, lanes] + dk
             totals[1, :, lanes] = totals[1, :, lanes] + dv
 
-        pl.when(index == 1)(lambda: gather.event(1))
-        pl.when(index == 3)(lambda: gather.event(2))
+        pl.when(index == 1)(lambda: events(1))
+        pl.when(index == 3)(lambda: events(2))
         return carry
 
     lax.fori_loop(0, 2 * width // (2 * HDIM), unit, 0)
@@ -912,12 +940,14 @@
     away.wait()
     own = totals[:, pl.ds(pl.multiple_of(col * size, size), size)]
     grad_kv[...] = (own + kv_landing[...]).astype(jnp.bfloat16)
-    lax.fori_loop(3, dps, lambda time, c: (gather.event(time), c)[1], 0)
+    lax.fori_loop(3, dps, lambda time, c: (events(time), c)[1], 0)
+    term_shard[...] = slab(half, 0, dp, dps)[...]
     out_scatter.wait_send()
     gather.finish()
-
-
-def turn(sizes, prefix, queries, kv, grad_out, log_sums, out_part, hidden, shards):
+    reduce.finish()
+
+
+def turn(sizes, prefix, queries, kv, grad_out, log_sums, out_part, hidden, shards, term):
     tokens, width = queries.shape
     dps, rows, cols = sizes
     low, wide = jnp.bfloat16, jnp.float32
@@ -929,6 +959,7 @@
         return tuple(full)
 
     firsts = [grown(s, d) for s, d in zip(shards, FIRST_DIMS)]
+    half = halved(term.shape, 0, cols)
     return pl.pallas_call(
         functools.partial(turn_kernel, sizes),
         in_specs=[pl.BlockSpec(memory_space=pltpu.SMEM)] + [VMEM] * 10,
@@ -938,18 +969,21 @@
             shape((2, tokens, width), low),
             shape(hidden.shape, low),
         ]
-        + [shape(s, low) for s in firsts],
+        + [shape(s, low) for s in firsts]
+        + [shape(halved(half, 0, dps), low)],
         scratch_shapes=[
             pltpu.VMEM(kv.shape, wide),
             pltpu.VMEM((2, tokens, width), wide),
             pltpu.VMEM((rows,) + hidden.shape, low),
         ]
+        + [pltpu.VMEM(half, low)] * 4
         + plane_sems(sizes)
-        + [DMA, DMA]
-        + line_sems(sizes, 4, 3),
+        + [DMA, DMA, DMA((1,)), DMA((1,))]
+        + line_sems(sizes, 3, 3)
+        + line_sems(sizes, 1, 4),
         compiler_params=pltpu.CompilerParams(collective_id=2, has_side_effects=True),
         name="turn",
-    )(prefix, queries, kv, grad_out, log_sums, out_part, hidden, *shards)
+    )(prefix, queries, kv, grad_out, log_sums, out_part, hidden, *shards, term)
 
 
 def allowed_mask(query_count, key_count, first_pos, prefix_len):
@@ -968,12 +1002,11 @@
     return jnp.where(hot, 1.0, 0.0).astype(jnp.bfloat16)
 
 
-def route_kernel(rows_dev, owners, cap, picks_ref, rank_ref, meta_ref):
+def route_block(picks, rows_dev, owners, cap):
     lane = lax.broadcasted_iota(jnp.int32, (FBLK, FBLK), 0)
     before = jnp.where(lane < lax.broadcasted_iota(jnp.int32, (FBLK, FBLK), 1), 1.0, 0.0).astype(
         jnp.bfloat16
     )
-    picks = picks_ref[0]
     owner = picks // rows_dev
     local = picks % rows_dev
     hot = one_hot(owner, owners)
@@ -986,7 +1019,6 @@
         ranks.append(jnp.sum(wide * (earlier + running), axis=0, keepdims=True))
         running = running + jnp.sum(wide, axis=1, keepdims=True)
     rank = jnp.concatenate(ranks, axis=1).astype(jnp.int32)
-    rank_ref[0] = rank
     slot_hot = one_hot(rank, cap)
     token = lax.broadcasted_iota(jnp.int32, picks.shape, 1) % FBLK
     outs = []
@@ -997,26 +1029,7 @@
                 scaled, slot_hot, (((1,), (1,)), ((), ())), preferred_element_type=jnp.float32
             ).astype(jnp.int32)
         )
-    meta_ref[0] = (outs[1] * FBLK + outs[2]) * SUBKEYS + outs[0]
-
-
-def route(flat, rows_dev, owners, cap):
-    blocks, count = flat.shape
-    rank, meta = pl.pallas_call(
-        functools.partial(route_kernel, rows_dev, owners, cap),
-        grid=(blocks,),
-        in_specs=[pl.BlockSpec((1, 1, count), lambda i: (i, 0, 0))],
-        out_specs=[
-            pl.BlockSpec((1, 1, count), lambda i: (i, 0, 0)),
-            pl.BlockSpec((1, owners, cap), lambda i: (i, 0, 0)),
-        ],
-        out_shape=[
-            jax.ShapeDtypeStruct((blocks, 1, count), jnp.int32),
-            jax.ShapeDtypeStruct((blocks, owners, cap), jnp.int32),
-        ],
-        name="route",
-    )(flat[:, None, :])
-    return rank, meta
+    return rank, (outs[1] * FBLK + outs[2]) * SUBKEYS + outs[0]
 
 
 def weigh_kernel(rows_dev, owners, cap, query_ref, keys_ref, picks_ref, rank_ref, weights_ref, slots_ref):
@@ -1075,15 +1088,12 @@
 
 
 def send_rows(spot, sizes, src, landing, send, recv):
-    count = sizes[0] * sizes[1] * sizes[2]
     me = index_of(spot, sizes)
 
-    def one(step, carry):
-        other = lax.rem(me + step, count)
-        remote(src.at[other], landing.at[me], send, recv, device_of(other, sizes)).start()
-        return carry
-
-    lax.fori_loop(1, count, one, 0)
+    def one(device):
+        remote(src.at[index_of(device, sizes)], landing.at[me], send, recv, device).start()
+
+    each_other(spot, sizes, one)
     landing[me] = src[me]
 
 
@@ -1120,9 +1130,9 @@
 
 
 def memory_kernel(
-    sizes, blocks, grads, meta, slots, values, values_t,
+    sizes, blocks, grads, meta, slots, values,
     grads_all, table, other_part, memory, back,
-    meta_in, slots_in, tables, parts,
+    meta_in, slots_in, values_t, tables, parts,
     chunks, found, sums, grids, theirs, acc, first_land, side_land, deep_land, total,
     msend, mrecv, ssend, srecv, zup, zdown, zrecv, wsend, wrecv, csend, crecv,
     local, tsem, qsend, qrecv,
@@ -1202,6 +1212,12 @@
             arrived(block_at(place, opposite, lines), wrecv.at[q, 2 + n])
         cross(q, place, opposite)
 
+    def turn_rows(n, carry):
+        lines = pl.ds(pl.multiple_of(n * 256, 256), 256)
+        values_t[:, lines] = values[lines].T
+        return carry
+
+    lax.fori_loop(0, values.shape[0] // 256, turn_rows, 0)
     all_rows(meta_in, mrecv)
     all_rows(slots_in, srecv)
 
@@ -1291,10 +1307,12 @@
         for copy in halves(u) + wholes(u):
             copy.wait_send()
 
+    def fetch(u):
+        arrived(other_part.at[place_of(u)], qrecv.at[u])
+        load_part(u).start()
+
     def combine(u):
-        arrived(other_part.at[place_of(u)], qrecv.at[u])
         pl.when(u >= RING)(lambda: sent(u - RING))
-        load_part(u).start()
         load_part(u).wait()
         acc[lax.rem(u, RING)] = (
             parts[1].astype(jnp.float32) + theirs[...].astype(jnp.float32)
@@ -1370,7 +1388,7 @@
         for copy in load_chunk(chunk):
             copy.start()
 
-    wide_strip = min(512, areas * SUBKEYS)
+    wide_strip = min(2048, areas * SUBKEYS)
     per_strip = wide_strip // SUBKEYS
 
     def search(chunk, part):
@@ -1440,13 +1458,11 @@
 
         pl.when(p >= writes)(lambda: search(lax.div(p - writes, 2), phase))
         turn, third = lax.div(p, 3), lax.rem(p, 3)
-        early = jnp.logical_and(third == 0, jnp.logical_and(turn > 0, turn + 1 < dps))
-        pl.when(p == 1)(lambda: from_line(1))
-        pl.when(early)(lambda: from_line(turn + 1))
-        pl.when(jnp.logical_and(third == 2, turn < dps))(lambda: from_sides(turn))
-        ready = jnp.logical_and(turn > 0, turn <= dps)
-        pl.when(jnp.logical_and(third == 1, ready))(lambda: from_opposite(turn - 1))
-        for event, delay in ((finish, FINISH_AT), (relay, RELAY_AT), (combine, COMBINE_AT)):
+        pl.when(jnp.logical_and(third == 2, turn + 1 < dps))(lambda: from_line(turn + 1))
+        for event, delay in ((from_sides, 1), (from_opposite, 2)):
+            now = jnp.logical_and(turn >= delay, turn < dps + delay)
+            pl.when(jnp.logical_and(third == 0, now))(functools.partial(event, turn - delay))
+        for event, delay in ((finish, FINISH_AT), (relay, RELAY_AT), (combine, COMBINE_AT), (fetch, FETCH_AT)):
             late = p - delay
             now = jnp.logical_and(
                 jnp.logical_and(late >= 0, lax.rem(late, 4) == 0), late < 4 * dps
@@ -1477,10 +1493,10 @@
     lax.fori_loop(0, dps - 1, lambda u, c: (deep_copy(u).wait_send(), c)[1], 0)
 
 
-COMBINE_AT, RELAY_AT, FINISH_AT = 6, 9, 14
-
-
-def use_memory(sizes, grads, meta, slots, values, values_t):
+FETCH_AT, COMBINE_AT, RELAY_AT, FINISH_AT = 5, 6, 10, 16
+
+
+def use_memory(sizes, grads, meta, slots, values):
     dps, rows, cols = sizes
     tokens, width = grads.shape
     rows_dev, features = values.shape
@@ -1490,7 +1506,7 @@
     shape = jax.ShapeDtypeStruct
     grads_all, table, _, memory, back = pl.pallas_call(
         functools.partial(memory_kernel, sizes, blocks),
-        in_specs=[VMEM] * 5,
+        in_specs=[VMEM] * 4,
         out_specs=[ANY] * 3 + [VMEM] * 2,
         out_shape=[
             shape((dps, cols, rows, tokens, width), low),
@@ -1502,6 +1518,7 @@
         scratch_shapes=[
             pltpu.VMEM(meta.shape, meta.dtype),
             pltpu.VMEM(slots.shape, slots.dtype),
+            pltpu.VMEM((features, rows_dev), low),
             pltpu.VMEM((2, tokens, rows_dev), low),
             pltpu.VMEM((2, tokens, features), low),
             pltpu.VMEM((2, tokens, features), low),
@@ -1527,7 +1544,7 @@
         ],
         compiler_params=pltpu.CompilerParams(collective_id=6, has_side_effects=True),
         name="use_memory",
-    )(grads, meta, slots, values, values_t)
+    )(grads, meta, slots, values)
     return grads_all, table, memory, back
 
 
@@ -1586,22 +1603,19 @@
     )(back, flat[:, None, :], rank, weights)
 
 
-def memory_all(query_rows, grad_memory, picks, subkeys, values):
+def memory_all(query_rows, grad_memory, flat, rank, meta, subkeys, values):
     sizes = grid_sizes()
     owners = sizes[0] * sizes[1] * sizes[2]
     rows_dev = values.shape[0]
     cap = FBLK * TOPK // owners
     head_id = lax.axis_index("row")
     keys_head = lax.dynamic_index_in_dim(subkeys, head_id, 0, keepdims=False)
-    picks_head = lax.dynamic_index_in_dim(picks, head_id, 1, keepdims=False)
-    flat = flat_picks(picks_head)
-    rank, meta = route(flat, rows_dev, owners, cap)
     weights, slots = weigh(query_rows, keys_head, flat, rank, rows_dev, owners, cap)
     spare = ((0, 0), (0, 0), (0, 128 - cap))
     meta = jnp.pad(jnp.swapaxes(meta, 0, 1), spare, constant_values=-1)
     slots = jnp.pad(jnp.swapaxes(slots, 0, 1).astype(jnp.float32), spare)
     grads_all, table, memory, back = use_memory(
-        sizes, grad_memory, meta, slots, values, values.T
+        sizes, grad_memory, meta, slots, values
     )
     first_t, second_t = unweigh(
         jnp.transpose(back, (1, 2, 0))[:, :cap], flat, rank, weights, rows_dev, owners
@@ -1685,8 +1699,9 @@
     gain_one = lax.dynamic_slice_in_dim(gain_attn, col_first, width_part)
     gain_two = lax.dynamic_slice_in_dim(gain_mem, col_first, width_part)
 
-    x_own, dy_own, qkv_w, query_w, gate_w, proj_w, attn_w = start_all(
-        sizes, inputs, cotangent, w_qkv, w_query, w_gate, w_proj, w_attn_out
+    flat = flat_picks(lax.dynamic_index_in_dim(picks, lax.axis_index("row"), 1, keepdims=False))
+    x_own, dy_own, qkv_w, query_w, gate_w, proj_w, attn_w, rank, meta = start_all(
+        sizes, values.shape[0], inputs, cotangent, w_qkv, w_query, w_gate, w_proj, w_attn_out, flat
     )
     residual = x_own.astype(jnp.float32)
     scale_one = lax.rsqrt(jnp.sum(residual * residual, axis=1, keepdims=True) / D + EPSILON)
@@ -1704,7 +1719,7 @@
     grad_gated = dense_nt(dy_own, proj_w)
     grad_memory = (grad_gated * silu_gate).astype(low)
     memory, grad_query, grad_keys, table, grads_all = memory_all(
-        query_rows, grad_memory, picks, subkeys, values
+        query_rows, grad_memory, flat, rank, meta, subkeys, values
     )
     gated_value = (memory * silu_gate).astype(low)
     out_part = dense(gated_value, proj_w).astype(low)
@@ -1712,8 +1727,8 @@
         grad_gated * memory * sigmoid_gate * (1.0 + gate_value * (1.0 - sigmoid_gate))
     ).astype(low)
     grad_part = (dense_nt(grad_query, query_w) + dense_nt(grad_gate, gate_w)).astype(low)
+    query_term = dense_tn(normed_two, grad_query).astype(low)
     first_terms = [
-        dense_tn(normed_two, grad_query).astype(low),
         dense_tn(normed_two, grad_gate).astype(low),
         dense_tn(gated_value, dy_own).astype(low),
         grad_keys.reshape(-1, HALF).astype(low),
@@ -1722,8 +1737,8 @@
         sizes, grad_part, hidden, cotangent, gain_two, first_terms
     )
     grad_attended = dense_nt(grad_hidden_all, attn_w).astype(low)
-    grad_q, grad_kv, output, grad_w_query, grad_w_gate, grad_w_proj, grad_keys_half = turn(
-        sizes, prefix, qkv[0], kv_all, grad_attended, log_sums, out_part, hidden, shards
+    grad_q, grad_kv, output, grad_w_gate, grad_w_proj, grad_keys_half, query_shard = turn(
+        sizes, prefix, qkv[0], kv_all, grad_attended, log_sums, out_part, hidden, shards, query_term
     )
     x_part = (
         dense_nt(grad_q, qkv_w[0]) + dense_nt(grad_kv[0], qkv_w[1]) + dense_nt(grad_kv[1], qkv_w[2])
@@ -1732,9 +1747,11 @@
         jnp.stack([dense_tn(normed_one, part) for part in (grad_q, grad_kv[0], grad_kv[1])]).astype(low),
         dense_tn(attended, grad_hidden_all).astype(low),
     ]
-    grad_inputs, gain_sums, grad_values, grad_w_qkv, grad_w_attn_out, grad_subkeys = last(
-        sizes, x_part, inputs, grad_hidden, gain_one, gain_two_grad, grad_keys_half, last_terms,
-        table, grads_all,
+    (
+        grad_inputs, gain_sums, grad_values, grad_w_query, grad_w_qkv, grad_w_attn_out, grad_subkeys,
+    ) = last(
+        sizes, x_part, inputs, grad_hidden, gain_one, gain_two_grad, grad_keys_half, query_shard,
+        last_terms, table, grads_all,
     )
     gain_rows = gain_sums.reshape(sizes[2], 2, width_part)
     grad_gain_one = gain_rows[:, 0].reshape(-1)

time: 471 us -> 442 us (0.938)
  Pallas kernels: 373 us -> 348 us
  other arithmetic: 21.5 us -> 16.3 us
    pallas_call x1, Pallas kernels: 123 us -> 112 us  [use_memory(): pl.pallas_call(functools.partial(memory_kernel, sizes, blocks), in_specs=...]
    pallas_call x1, Pallas kernels: 48.3 us -> 37.5 us  [middle(): pl.pallas_call(functools.partial(middle_kernel, sizes), in_specs=[VMEM] *...]
    unnamed x70 -> x93, local copies, waits for them, and re-layouts: 13.8 us -> 12.1 us
    pallas_call x3 -> x2, Pallas kernels: 102 us -> 102 us  [the longest x1 71.1 us: last(): pl.pallas_call(functools.partial(last_kernel, sizes), in_specs=[VMEM] * 9...]
where the time goes in v6:
time: 442 us; the launch traced here: 434 us
  Pallas kernels  348 us (79%)
  matrix products  43.1 us (10%)
  local copies, waits for them, and re-layouts  23.5 us (5%)
  other arithmetic  16.3 us (4%)
    pallas_call x1, Pallas kernels, use_memory(): pl.pallas_call(functools.partial(memory_kernel, sizes, blocks), in_specs=...  112 us
    pallas_call x1, Pallas kernels, last(): pl.pallas_call(functools.partial(last_kernel, sizes), in_specs=[VMEM] * 9...  71.1 us
    pallas_call x1, Pallas kernels, middle(): pl.pallas_call(functools.partial(middle_kernel, sizes), in_specs=[VMEM] *...  37.5 us
    pallas_call x1, Pallas kernels, turn(): pl.pallas_call(functools.partial(turn_kernel, sizes), in_specs=[pl.BlockS...  36.6 us
    pallas_call x1, Pallas kernels, join(): pl.pallas_call(functools.partial(join_kernel, sizes), in_specs=[VMEM] * 3...  32.5 us
    pallas_call x1, Pallas kernels, start_all(): pl.pallas_call(functools.partial(start_kernel, sizes, rows_dev), in_specs...  30.9 us
    pallas_call x1, Pallas kernels, weigh(): pl.pallas_call(functools.partial(weigh_kernel, rows_dev, owners, cap), gr...  12.4 us
    unnamed x93, local copies, waits for them, and re-layouts  12.1 us

profile of v6, /device:TPU:0, one launch (start us, length us, event | category | flops | bytes accessed | tf_op | source)
XLA Modules:
  0.0 433.7 jit_solution(6129649522962973638)
XLA Ops:
  0.7 1.0 constant_dynamic-slice_fusion
  2.3 30.9 %start_all.1 = (bf16[512,1024]{1,0:T(8,128)(2,1)}, bf16[512,1024]{1,0:T(8,128)(2,1)}, bf16[3,1024,256]{2,1,0:T(8,128)(2,1)}, bf16[1024,1024]{1,0:T(8,128)(2,1)},...) custom-call(bf16[256,512]{1,0:T(8,128)(2,1)} %refs_1_.3, ...), custom_call_target="tpu_custom_call" | custom-call | tf_op jit(solution)/shard_map/start_all/pallas_call | solution.py:254
  33.2 1.5 fusion
  34.8 2.8 fusion.8
  37.5 0.8 slice.114.src
  38.4 4.0 swap_tokens.1.refs_2_
  42.3 2.2 slice_bitcast_fusion
  45.3 1.8 fusion.61
  48.7 0.8 fusion.60
  50.8 0.8 fusion.59
  52.7 0.8 fusion.58
  55.1 1.4 convolution_convert_fusion.3.part
  57.2 32.5 %join.1 = (f32[256,512]{1,0:T(8,128)}, bf16[512,1024]{1,0:T(8,128)(2,1)}) custom-call(bf16[512,1024]{1,0:T(8,128)(2,1)} %convolution_convert_fusion.3.part, bf16[256,512]{1,0:T(8,128)(2,1)} %refs_1_.3, bf16[1,512]{1,0:T(2,128)(2,1)} %broadcast_in_dim.12.gain.refs_3_), custom_call_target="tpu_custom_call" | custom-call | tf_op jit(solution)/shard_map/join/pallas_call | solution.py:336
  89.8 4.1 convolution_convert_fusion.2.query_ref
  93.9 0.8 dynamic-slice_bitcast_fusion.keys_ref
  94.8 12.4 %weigh.1 = (f32[4,32,128]{2,1,0:T(8,128)}, bf16[4,32,128]{2,1,0:T(8,128)(2,1)}) custom-call(bf16[512,1024]{1,0:T(8,128)(2,1)} %convolution_convert_fusion.2.query_ref, bf16[2,256,512]{2,1,0:T(8,128)(2,1)} %dynamic-slice_bitcast_fusion.keys_ref, s32[4,1,4096]{2,1,0:T(1,128)} %bitcast.98, s32[4,1,4096]{2,1,0:T(1,128)} %get-tuple-element.59.rank_ref), custom_call_target="tpu_custom_call" | custom-call | tf_op jit(solution)/shard_map/weigh/pallas_call | solution.py:1069
  107.2 1.5 copy.45
  108.7 1.7 fusion.62
  110.4 1.4 multiply_convert_fusion.2
  112.4 111.8 %use_memory.1 = (bf16[4,2,4,512,256]{4,3,2,1,0:T(8,128)(2,1)}, bf16[4,2,512,2048]{3,2,1,0:T(8,128)(2,1)}, bf16[4,512,1024]{2,1,0:T(8,128)(2,1)}, f32[512,256]{1,0:T(8,128)}, f32[32,4,128]{2,1,0:T(4,128)}) custom-call(bf16[512,256]{1,0:T(8,128)(2,1)} %get-tuple-element.103.grads, s32[32,4,128]{2,1,0:T(4,128)} %bitcast.101, f32[32,4,128]{2,1,0:T(4,128)} %bitcast.100, ...), custom_call_target="tpu_custom_call" | custom-call | tf_op jit(solution)/shard_map/use_memory/pallas_call | solution.py:1507
  224.2 1.7 copy.40
  225.9 11.7 %unweigh.1 = (bf16[256,512]{1,0:T(8,128)(2,1)}, bf16[256,512]{1,0:T(8,128)(2,1)}) custom-call(f32[4,128,32]{2,1,0:T(8,128)} %bitcast.96, s32[4,1,4096]{2,1,0:T(1,128)} %bitcast.99, s32[4,1,4096]{2,1,0:T(1,128)} %get-tuple-element.59.rank_ref, f32[4,32,128]{2,1,0:T(8,128)} %get-tuple-element.62.weights_ref), custom_call_target="tpu_custom_call" | custom-call | tf_op jit(solution)/shard_map/unweigh/pallas_call | solution.py:1588
  237.6 1.5 fusion.12
  239.2 1.5 fusion.13
  240.7 0.8 pad_maximum_fusion.4
  241.9 1.3 convolution_convert_fusion.9.refs_5_
  243.1 1.3 convolution_convert_fusion.10.refs_4_
  244.4 1.1 convolution_convert_fusion.12
  245.9 3.2 fusion.15
  249.2 1.4 add_convert_fusion.1.refs_0_
  250.7 37.5 %middle.1 = (f32[256,512]{1,0:T(8,128)}, bf16[512,1024]{1,0:T(8,128)(2,1)}, f32[1,512]{1,0:T(1,128)}, bf16[128,256]{1,0:T(8,128)(2,1)}, bf16[64,512]{1,0:T(8,128)(2,1)}, /*index=5*/bf16[64,512]{1,0:T(8,128)(2,1)}) custom-call(bf16[512,1024]{1,0:T(8,128)(2,1)} %add_convert_fusion.1.refs_0_, f32[256,512]{1,0:T(8,128)} %get-tuple-element.66.refs_1_.refs_6_, ...), custom_call_target="tpu_custom_call" | custom-call | tf_op jit(solution)/shard_map/middle/pallas_call | solution.py:637
  288.2 2.5 convolution_convert_fusion.5.refs_8_
  290.7 2.6 convolution_convert_fusion.refs_10_
  293.3 1.4 convolution_convert_fusion.1.refs_5_
  295.4 1.2 convolution_convert_fusion.13.refs_3_
  296.6 36.6 %turn.1 = (bf16[512,256]{1,0:T(8,128)(2,1)}, bf16[2,512,256]{2,1,0:T(8,128)(2,1)}, bf16[256,512]{1,0:T(8,128)(2,1)}, bf16[512,256]{1,0:T(8,128)(2,1)}, bf16[256,...) custom-call(s32[1]{0:T(128)} %copy.50.refs_0_, bf16[512,256]{1,0:T(8,128)(2,1)} %copy-done.7, ...), custom_call_target="tpu_custom_call" | custom-call | tf_op jit(solution)/shard_map/turn/pallas_call | solution.py:963
  333.2 1.7 fusion.9
  336.2 1.3 pad_maximum_fusion.refs_7_
  339.6 1.5 add_convert_fusion.refs_0_
  341.8 71.1 %last.1 = (f32[256,512]{1,0:T(8,128)}, f32[2,8,128]{2,1,0:T(8,128)}, f32[2048,1024]{1,0:T(8,128)}, bf16[512,1024]{1,0:T(8,128)(2,1)}, bf16[3,512,256]{2,1,0:T(8,...) custom-call(bf16[512,1024]{1,0:T(8,128)(2,1)} %add_convert_fusion.refs_0_, ...), custom_call_target="tpu_custom_call" | custom-call | tf_op jit(solution)/shard_map/last/pallas_call | solution.py:820
  412.9 4.3 convert_element_type.125
  417.2 1.6 convert_element_type.122
  418.8 1.3 convert_element_type.120
  420.0 0.9 convert_element_type.121
  421.5 0.8 convert_element_type.123
  422.3 0.9 convert_element_type.124
  423.9 0.8 copy.52
  424.7 8.6 %copy.53 = f32[2048,1024]{1,0:T(8,128)} copy(f32[2048,1024]{1,0:T(8,128)} %get-tuple-element.126) | data formatting | bytes 16777216
  (124 shorter events, 14.3 us)
Async XLA Ops:
  0.6 93.3 %copy-start = (bf16[4,2,256,512]{3,2,1,0:T(8,128)(2,1)S(1)}, bf16[4,2,256,512]{3,2,1,0:T(8,128)(2,1)}, u32[]{:S(2)}) copy-start(bf16[4,2,256,512]{3,2,1,0:T(8,128)(2,1)} %param.23) | copy-start | bytes 6291460
  2.3 32.4 %copy-start.34 = (bf16[1024]{0:T(1024)(128)(2,1)S(1)}, bf16[1024]{0:T(1024)(128)(2,1)}, u32[]{:S(2)}) copy-start(bf16[1024]{0:T(1024)(128)(2,1)} %param.16) | copy-start | bytes 6148
  44.6 8.1 %copy-start.7 = (bf16[512,256]{1,0:T(8,128)(2,1)}, bf16[512,256]{1,0:T(8,128)(2,1)S(1)}, u32[]{:S(2)}) copy-start(bf16[512,256]{1,0:T(8,128)(2,1)S(1)} %slice_bitcast_fusion.2.refs_1_) | copy-start | bytes 786436
  45.3 2.3 copy-start.20
  47.6 1.0 copy-start.21
  50.8 4.1 copy-start.39
  52.7 2.1 copy-start.41
  54.1 1.0 copy-start.37
  54.1 2.5 copy-start.35
  54.8 39.1 %copy-start.43 = (bf16[512,64]{0,1:T(8,128)(2,1)}, bf16[512,64]{0,1:T(8,128)(2,1)S(1)}, u32[]{:S(2)}) copy-start(bf16[512,64]{0,1:T(8,128)(2,1)S(1)} %convolution_convert_fusion.16) | copy-start | bytes 196612
  93.9 14.8 %copy-start.2 = (bf16[1024,256]{1,0:T(8,128)(2,1)S(1)}, bf16[1024,256]{1,0:T(8,128)(2,1)}, u32[]{:S(2)}) copy-start(bf16[1024,256]{1,0:T(8,128)(2,1)} %get-tuple-element.56) | copy-start | bytes 1572868
  107.2 3.2 copy-start.5
  107.2 3.2 copy-start.14
  110.4 1.4 copy-start.32
  237.6 3.9 copy-start.22
  237.6 3.9 copy-start.24
  239.2 2.7 copy-start.6
  241.5 1.6 copy-start.9
  241.8 2.6 copy-start.11
  241.8 2.6 copy-start.30
  243.1 2.5 copy-start.27
  245.9 3.3 copy-start.16
  245.9 3.3 copy-start.12
  250.7 37.5 %copy-start.40 = (bf16[512,64]{0,1:T(8,128)(2,1)S(1)}, bf16[512,64]{0,1:T(8,128)(2,1)}, u32[]{:S(2)}) copy-start(bf16[512,64]{0,1:T(8,128)(2,1)} %copy-done.39) | copy-start | bytes 196612
  250.7 37.5 %copy-start.42 = (bf16[512,64]{0,1:T(8,128)(2,1)S(1)}, bf16[512,64]{0,1:T(8,128)(2,1)}, u32[]{:S(2)}) copy-start(bf16[512,64]{0,1:T(8,128)(2,1)} %copy-done.41) | copy-start | bytes 196612
  250.7 37.5 %copy-start.44 = (bf16[512,64]{0,1:T(8,128)(2,1)S(1)}, bf16[512,64]{0,1:T(8,128)(2,1)}, u32[]{:S(2)}) copy-start(bf16[512,64]{0,1:T(8,128)(2,1)} %copy-done.43) | copy-start | bytes 196612
  250.7 40.0 %copy-start.10 = (bf16[512,1024]{1,0:T(8,128)(2,1)S(1)}, bf16[512,1024]{1,0:T(8,128)(2,1)}, u32[]{:S(2)}) copy-start(bf16[512,1024]{1,0:T(8,128)(2,1)} %get-tuple-element.55) | copy-start | bytes 3145732
  250.7 40.0 %copy-start.17 = (bf16[512,512]{0,1:T(8,128)(2,1)S(1)}, bf16[512,512]{0,1:T(8,128)(2,1)}, u32[]{:S(2)}) copy-start(bf16[512,512]{0,1:T(8,128)(2,1)} %copy-done.16) | copy-start | bytes 1572868
  250.7 40.0 %copy-start.19 = (bf16[512,512]{0,1:T(8,128)(2,1)S(1)}, bf16[512,512]{0,1:T(8,128)(2,1)}, u32[]{:S(2)}) copy-start(bf16[512,512]{0,1:T(8,128)(2,1)} %convolution_convert_fusion.12) | copy-start | bytes 1572868
  290.7 2.7 copy-start.15
  290.7 4.7 %copy-start.36 = (bf16[512,1024]{1,0:T(8,128)(2,1)S(1)}, bf16[512,1024]{1,0:T(8,128)(2,1)}, u32[]{:S(2)}) copy-start(bf16[512,1024]{1,0:T(8,128)(2,1)} %get-tuple-element.67) | copy-start | bytes 3145732
  290.7 4.7 %copy-start.38 = (bf16[256,1024]{1,0:T(8,128)(2,1)S(1)}, bf16[256,1024]{1,0:T(8,128)(2,1)}, u32[]{:S(2)}) copy-start(bf16[256,1024]{1,0:T(8,128)(2,1)} %get-tuple-element.54) | copy-start | bytes 1572868
  296.6 36.6 %copy-start.8 = (bf16[512,1024]{1,0:T(8,128)(2,1)S(1)}, bf16[512,1024]{1,0:T(8,128)(2,1)}, u32[]{:S(2)}) copy-start(bf16[512,1024]{1,0:T(8,128)(2,1)} %get-tuple-element.51) | copy-start | bytes 3145732
  333.2 1.7 copy-start.23
  336.2 2.0 copy-start.3
  338.2 0.9 copy-start.31
  412.9 4.3 copy-start.4
  417.2 1.6 copy-start.13
  417.2 2.9 copy-start.28
  418.7 2.2 copy-start.33
  418.7 2.8 copy-start.26
  418.7 3.6 copy-start.25
  418.7 4.5 %copy-start.29 = (bf16[256,512]{1,0:T(8,128)(2,1)S(1)}, bf16[256,512]{1,0:T(8,128)(2,1)}, u32[]{:S(2)}) copy-start(bf16[256,512]{1,0:T(8,128)(2,1)} %get-tuple-element.116) | copy-start | bytes 786436
  418.7 5.2 %copy-start.18 = (f32[256,512]{1,0:T(8,128)S(1)}, f32[256,512]{1,0:T(8,128)}, u32[]{:S(2)}) copy-start(f32[256,512]{1,0:T(8,128)} %get-tuple-element.117) | copy-start | bytes 1572868
  424.7 8.6 %copy-start.1 = (bf16[4,2,256,512]{3,2,1,0:T(8,128)(2,1)S(1)}, bf16[4,2,256,512]{3,2,1,0:T(8,128)(2,1)}, u32[]{:S(2)}) copy-start(bf16[4,2,256,512]{3,2,1,0:T(8,128)(2,1)} %param.23) | copy-start | bytes 6291460

commit v7 on v6

--- a/solution.py
+++ b/solution.py
@@ -194,16 +194,14 @@
 
 
 def start_kernel(sizes, rows_dev, *refs):
-    x, dy, wqkv, wquery, wgate, wproj, wattn, picks = refs[:8]
-    xs, dys, wqkv_all, wquery_all, wgate_all, wproj_all, wattn_all, rank, meta = refs[8:17]
-    xsend, xrecv, ysend, yrecv, wsend, wrecv, wlocal = refs[17:]
+    x, wqkv, wquery, wgate, wproj, wattn, picks = refs[:7]
+    xs, wqkv_all, wquery_all, wgate_all, wproj_all, wattn_all, rank, meta = refs[7:15]
+    xsend, xrecv, wsend, wrecv, wlocal = refs[15:]
     spot = here()
     dp, row, col = spot
     greet_plane(spot, sizes)
     gather_x = Gather(spot, sizes, x, xs, xsend, xrecv)
-    gather_y = Gather(spot, sizes, dy, dys, ysend, yrecv)
     gather_x.start()
-    gather_y.start()
     copies = []
     for n, (src, dst, dim) in enumerate(
         (
@@ -234,10 +232,9 @@
     for copy in copies:
         copy.wait()
     gather_x.wait()
-    gather_y.wait()
-
-
-def start_all(sizes, rows_dev, x, dy, wqkv, wquery, wgate, wproj, wattn, flat):
+
+
+def start_all(sizes, rows_dev, x, wqkv, wquery, wgate, wproj, wattn, flat):
     tokens, width = x.shape
     half = sizes[1] // sizes[2]
     cols = sizes[2]
@@ -253,10 +250,9 @@
     owners = sizes[0] * sizes[1] * sizes[2]
     return pl.pallas_call(
         functools.partial(start_kernel, sizes, rows_dev),
-        in_specs=[VMEM] * 8,
-        out_specs=[ANY] * 7 + [VMEM] * 2,
+        in_specs=[VMEM] * 7,
+        out_specs=[ANY] * 6 + [VMEM] * 2,
         out_shape=[
-            whole,
             whole,
             twice(wqkv, 1),
             twice(wquery, 0),
@@ -266,37 +262,86 @@
             jax.ShapeDtypeStruct((blocks, 1, count), jnp.int32),
             jax.ShapeDtypeStruct((blocks, owners, count // owners), jnp.int32),
         ],
-        scratch_shapes=plane_sems(sizes) * 2 + [DMA((5,))] * 3,
+        scratch_shapes=plane_sems(sizes) + [DMA((5,))] * 3,
         compiler_params=pltpu.CompilerParams(collective_id=0, has_side_effects=True),
         name="start_all",
-    )(x, dy, wqkv, wquery, wgate, wproj, wattn, flat[:, None])
-
-
-def swap_kernel(sizes, src, dst, send, recv, own):
+    )(x, wqkv, wquery, wgate, wproj, wattn, flat[:, None])
+
+
+def lane_sides():
+    lane = lax.broadcasted_iota(jnp.int32, (1, 2 * HDIM), 1)
+    return [
+        jnp.where(jnp.logical_and(lane >= a * HDIM, lane < (a + 1) * HDIM), 1.0, 0.0).astype(
+            jnp.bfloat16
+        )
+        for a in range(2)
+    ]
+
+
+def attend_kernel(
+    sizes, prefix, qkv, dy, attended, log_sums, kv, dys, ysend, yrecv, send, recv, local
+):
     spot = here()
     dp, row, col = spot
-    greet_partner(spot, sizes)
-    size = src.shape[1]
-    there = dst.at[:, pl.ds(pl.multiple_of(col * size, size), size)]
-    away = remote(src, there, send, recv, (dp, row, 1 - col))
-    local = pltpu.make_async_copy(src, there, own)
+    greet_plane(spot, sizes)
+    _, tokens, width = qkv.shape
+    keys = kv.shape[1]
+    tile = tokens // 2
+    there = kv.at[:, pl.ds(pl.multiple_of(col * tokens, tokens), tokens)]
+    away = remote(qkv.at[pl.ds(1, 2)], there, send, recv, (dp, row, 1 - col))
+    home = pltpu.make_async_copy(qkv.at[pl.ds(1, 2)], there, local)
     away.start()
-    local.start()
+    home.start()
+    gather = Gather(spot, sizes, dy, dys, ysend, yrecv)
+    gather.start()
+    limit = prefix[0]
+    key_pos = lax.broadcasted_iota(jnp.int32, (keys, tile), 0)
+    sides = lane_sides()
     away.wait()
-    local.wait()
-
-
-def swap_tokens(sizes, src):
-    shape = (src.shape[0], src.shape[1] * sizes[2], src.shape[2])
+    home.wait()
+
+    def unit(index, carry):
+        pair, part = lax.div(index, 2), lax.rem(index, 2)
+        lanes = pl.ds(pl.multiple_of(pair * 2 * HDIM, 2 * HDIM), 2 * HDIM)
+        lines = pl.ds(pl.multiple_of(part * tile, tile), tile)
+        query_pos = col * tokens + part * tile + lax.broadcasted_iota(jnp.int32, (1, tile), 1)
+        allowed = jnp.logical_or(key_pos <= query_pos, key_pos < limit)
+        q2, k2, v2 = qkv[0, lines, lanes], kv[0, :, lanes], kv[1, :, lanes]
+        total = jnp.zeros((tile, 2 * HDIM), jnp.float32)
+        for a in range(2):
+            scores = jnp.where(allowed, dense_nt(k2 * sides[a], q2) * HDIM ** (-0.5), -jnp.inf)
+            peak = jnp.max(scores, axis=0, keepdims=True)
+            powers = jnp.exp(scores - peak)
+            power_sum = jnp.sum(powers, axis=0, keepdims=True)
+            probs = (powers / power_sum).astype(jnp.bfloat16)
+            total = total + dense_tn(probs, v2 * sides[a])
+            log_sums[pl.ds(2 * pair + a, 1), lines] = peak + jnp.log(power_sum)
+        attended[lines, lanes] = total.astype(jnp.bfloat16)
+        return carry
+
+    lax.fori_loop(0, 2 * width // (2 * HDIM), unit, 0)
+    gather.wait()
+
+
+def attend(sizes, prefix, qkv, dy):
+    _, tokens, width = qkv.shape
+    low, wide = jnp.bfloat16, jnp.float32
+    shape = jax.ShapeDtypeStruct
+    half = sizes[1] // sizes[2]
     return pl.pallas_call(
-        functools.partial(swap_kernel, sizes),
-        in_specs=[VMEM],
-        out_specs=VMEM,
-        out_shape=jax.ShapeDtypeStruct(shape, src.dtype),
-        scratch_shapes=[DMA, DMA, DMA],
+        functools.partial(attend_kernel, sizes),
+        in_specs=[pl.BlockSpec(memory_space=pltpu.SMEM), VMEM, VMEM],
+        out_specs=[VMEM, VMEM, VMEM, ANY],
+        out_shape=[
+            shape((tokens, width), low),
+            shape((width // HDIM, tokens), wide),
+            shape((2, tokens * sizes[2], width), low),
+            shape((half * dy.shape[0], sizes[2] * dy.shape[1]), low),
+        ],
+        scratch_shapes=plane_sems(sizes) + [DMA, DMA, DMA],
         compiler_params=pltpu.CompilerParams(collective_id=1, has_side_effects=True),
-        name="swap_tokens",
-    )(src)
+        name="attend",
+    )(prefix, qkv, dy)
 
 
 def fold(column):
@@ -665,12 +710,12 @@
     table, grads_all = refs[9:11]
     grad, gain_sums, row_grads, first = refs[11:15]
     lasts, keys_all = refs[15:17], refs[17]
-    landing, mine, theirs, own_gain, gain_landing, tables, chunks = refs[18:25]
-    halves, pair_land, below, above = refs[25:27], refs[27:29], refs[29:31], refs[31:33]
+    landing, mine, theirs, own_gain, gain_landing, tables, chunks, row_sums = refs[18:26]
+    halves, pair_land, below, above = refs[26:28], refs[28:30], refs[30:32], refs[32:34]
     (
         ssend, srecv, psend, precv, bsend, brecv, hsend, hrecv, tsem, csem,
         xsend, xrecv, kxsend, kxrecv, *line
-    ) = refs[33:]
+    ) = refs[34:]
     spot = here()
     dp, row, col = spot
     dps, rows, cols = sizes
@@ -730,11 +775,15 @@
 
             @pl.when(index == 0)
             def _():
-                row_grads[columns] = term
-
-            @pl.when(index > 0)
+                row_sums[columns] = term
+
+            @pl.when(jnp.logical_and(index > 0, index < loads - 1))
             def _():
-                row_grads[columns] = row_grads[columns] + term
+                row_sums[columns] = row_sums[columns] + term
+
+            @pl.when(index == loads - 1)
+            def _():
+                row_grads[columns] = (row_sums[columns] + term).astype(jnp.bfloat16)
 
             return carry
 
@@ -754,6 +803,8 @@
         return remote(src, there, kxsend, kxrecv, (dp, row, 1 - col))
 
     products(0, loads // 4)
+    gather.event(1)
+    reduce.event(1)
     scatter.wait()
     total, gains = norm_back(sizes, spot, landing, x, above_grad, gain, mine, theirs, psend, precv)
     lines = gains.shape[1] // 128
@@ -772,21 +823,26 @@
         sideways(k).start()
     cross(keys, 0).start()
     keys_all[row, col] = keys[...]
-    gather.event(1)
-    reduce.event(1)
     products(loads // 4, loads // 2)
-    lax.fori_loop(2, dps, lambda time, c: (gather.event(time), reduce.event(time), c)[2], 0)
+
+    def both(time):
+        gather.event(time)
+        reduce.event(time)
+
+    both(2)
+    products(loads // 2, 3 * loads // 4)
+    lax.fori_loop(3, dps, lambda time, c: (both(time), c)[1], 0)
     for first, half, dim in zip(lasts, halves, LAST_DIMS):
         slab(first, dim, dp, dps)[...] = slab(half, dim, dp, dps)[...]
     final = LineGather(spot, sizes, lasts, LAST_DIMS, line[4:7])
     final.start()
-    products(loads // 2, 3 * loads // 4)
+    products(3 * loads // 4, 7 * loads // 8)
     final.event(1)
     for k in range(1, rows):
         landed = keys_all.at[lax.rem(row + k, rows), col]
         arrived(landed, xrecv.at[k])
         cross(landed, k).start()
-    products(3 * loads // 4, loads)
+    products(7 * loads // 8, loads)
     lax.fori_loop(2, dps, lambda time, c: (final.event(time), c)[1], 0)
     arrived(keys_all.at[:, 1 - col], kxrecv)
     scatter.wait_send()
@@ -824,7 +880,7 @@
         out_shape=[
             shape((tokens, width), wide),
             shape((cols, lines, 128), wide),
-            shape((rows_dev, features), wide),
+            shape((rows_dev, features), low),
             shape((shard.shape[0] * dps, shard.shape[1]), low),
         ]
         + [shape(s, low) for s in halves]
@@ -837,6 +893,7 @@
             pltpu.VMEM((count, lines, 128), wide),
             pltpu.VMEM((2, chunk, rows_dev), low),
             pltpu.VMEM((2, chunk, features), low),
+            pltpu.VMEM((rows_dev, features), wide),
         ]
         + [pltpu.VMEM(h, low) for h in halves] * 4
         + plane_sems(sizes)
@@ -881,13 +938,7 @@
 
     limit = prefix[0]
     key_pos = lax.broadcasted_iota(jnp.int32, (keys, tile), 0)
-    lane = lax.broadcasted_iota(jnp.int32, (1, 2 * HDIM), 1)
-    sides = [
-        jnp.where(jnp.logical_and(lane >= a * HDIM, lane < (a + 1) * HDIM), 1.0, 0.0).astype(
-            jnp.bfloat16
-        )
-        for a in range(2)
-    ]
+    sides = lane_sides()
 
     def unit(index, carry):
         pair, part = lax.div(index, 2), lax.rem(index, 2)
@@ -984,12 +1035,6 @@
         compiler_params=pltpu.CompilerParams(collective_id=2, has_side_effects=True),
         name="turn",
     )(prefix, queries, kv, grad_out, log_sums, out_part, hidden, *shards, term)
-
-
-def allowed_mask(query_count, key_count, first_pos, prefix_len):
-    query_pos = first_pos + lax.iota(jnp.int32, query_count)
-    key_pos = lax.iota(jnp.int32, key_count)
-    return (key_pos[None, :] <= query_pos[:, None]) | (key_pos[None, :] < prefix_len)
 
 
 def flat_picks(picks_head):
@@ -1638,30 +1683,6 @@
     return memory, grad_query, grad_keys, table, grads_all
 
 
-def head_scores(query_head, key_head, allowed):
-    raw_scores = jnp.einsum(
-        "qd,kd->qk", query_head, key_head, preferred_element_type=jnp.float32
-    ) * HDIM ** (-0.5)
-    return jnp.where(allowed, raw_scores, -jnp.inf)
-
-
-def attend_forward(queries, keys, values, allowed):
-    outputs = []
-    log_sums = []
-    for head_index in range(queries.shape[1] // HDIM):
-        columns = slice(head_index * HDIM, (head_index + 1) * HDIM)
-        scores = head_scores(queries[:, columns], keys[:, columns], allowed)
-        peak_score = jnp.max(scores, axis=1, keepdims=True)
-        exp_scores = jnp.exp(scores - peak_score)
-        row_sum = jnp.sum(exp_scores, axis=1, keepdims=True)
-        probabilities = (exp_scores / row_sum).astype(jnp.bfloat16)
-        outputs.append(
-            jnp.dot(probabilities, values[:, columns], preferred_element_type=jnp.float32)
-        )
-        log_sums.append(peak_score[:, 0] + jnp.log(row_sum[:, 0]))
-    return (jnp.concatenate(outputs, axis=1), jnp.stack(log_sums))
-
-
 def dense(left, right):
     return jnp.dot(left, right, preferred_element_type=jnp.float32)
 
@@ -1692,25 +1713,20 @@
     low = jnp.bfloat16
     sizes = grid_sizes()
     width_part = inputs.shape[1]
-    own_tokens = picks.shape[0]
-    seq_tokens = own_tokens * sizes[2]
     col = lax.axis_index("col")
     col_first = col * width_part
     gain_one = lax.dynamic_slice_in_dim(gain_attn, col_first, width_part)
     gain_two = lax.dynamic_slice_in_dim(gain_mem, col_first, width_part)
 
     flat = flat_picks(lax.dynamic_index_in_dim(picks, lax.axis_index("row"), 1, keepdims=False))
-    x_own, dy_own, qkv_w, query_w, gate_w, proj_w, attn_w, rank, meta = start_all(
-        sizes, values.shape[0], inputs, cotangent, w_qkv, w_query, w_gate, w_proj, w_attn_out, flat
+    x_own, qkv_w, query_w, gate_w, proj_w, attn_w, rank, meta = start_all(
+        sizes, values.shape[0], inputs, w_qkv, w_query, w_gate, w_proj, w_attn_out, flat
     )
     residual = x_own.astype(jnp.float32)
     scale_one = lax.rsqrt(jnp.sum(residual * residual, axis=1, keepdims=True) / D + EPSILON)
     normed_one = (residual * scale_one * gain_attn.astype(jnp.float32)).astype(low)
     qkv = jnp.einsum("tc,jcf->jtf", normed_one, qkv_w, preferred_element_type=jnp.float32).astype(low)
-    kv_all = swap_tokens(sizes, qkv[1:])
-    allowed = allowed_mask(own_tokens, seq_tokens, col * own_tokens, prefix[0])
-    attended_sum, log_sums = attend_forward(qkv[0], kv_all[0], kv_all[1], allowed)
-    attended = attended_sum.astype(low)
+    attended, log_sums, kv_all, dy_own = attend(sizes, prefix, qkv, cotangent)
     hidden, normed_two = join(sizes, dense(attended, attn_w).astype(low), inputs, gain_two)
     query_rows = dense(normed_two, query_w).astype(low)
     gate_value = dense(normed_two, gate_w)
@@ -1768,7 +1784,7 @@
         grad_w_gate.astype(jnp.float32),
         grad_w_proj.astype(jnp.float32),
         grad_subkeys.astype(jnp.float32),
-        grad_values,
+        grad_values.astype(jnp.float32),
     )
 
 

time: 442 us -> 419 us (0.948)
  local copies, waits for them, and re-layouts: 23.5 us -> 13.2 us
  matrix products: 43.1 us -> 34.2 us
    pallas_call x1, Pallas kernels: 3.97 us -> 17.7 us  [attend(): pl.pallas_call(functools.partial(attend_kernel, sizes), in_specs=[pl.Bloc...]
    pallas_call x1, Pallas kernels: 30.9 us -> 19.4 us  [start_all(): pl.pallas_call(functools.partial(start_kernel, sizes, rows_dev), in_specs...]
    unnamed x93 -> x80, local copies, waits for them, and re-layouts: 12.1 us -> 3.63 us
    dot_general x8 -> x0, matrix products: 6.97 us -> none  [the longest x4 4.22 us: head_scores(): jnp.einsum('qd,kd->qk', query_head, key_head, preferred_element_type=jnp....]
    convert_element_type x0 -> x1, other arithmetic: none -> 4.44 us  [per_device(): grad_values.astype(jnp.float32)]
where the time goes in v7:
time: 419 us; the launch traced here: 414 us
  Pallas kernels  347 us (83%)
  matrix products  34.2 us (8%)
  other arithmetic  17.6 us (4%)
  local copies, waits for them, and re-layouts  13.2 us (3%)
    pallas_call x1, Pallas kernels, use_memory(): pl.pallas_call(functools.partial(memory_kernel, sizes, blocks), in_specs=...  112 us
    pallas_call x1, Pallas kernels, last(): pl.pallas_call(functools.partial(last_kernel, sizes), in_specs=[VMEM] * 9...  67.3 us
    pallas_call x1, Pallas kernels, middle(): pl.pallas_call(functools.partial(middle_kernel, sizes), in_specs=[VMEM] *...  37.4 us
    pallas_call x1, Pallas kernels, turn(): pl.pallas_call(functools.partial(turn_kernel, sizes), in_specs=[pl.BlockS...  36.6 us
    pallas_call x1, Pallas kernels, join(): pl.pallas_call(functools.partial(join_kernel, sizes), in_specs=[VMEM] * 3...  32.5 us
    pallas_call x1, Pallas kernels, start_all(): pl.pallas_call(functools.partial(start_kernel, sizes, rows_dev), in_specs...  19.4 us
    pallas_call x1, Pallas kernels, attend(): pl.pallas_call(functools.partial(attend_kernel, sizes), in_specs=[pl.Bloc...  17.7 us
    pallas_call x1, Pallas kernels, weigh(): pl.pallas_call(functools.partial(weigh_kernel, rows_dev, owners, cap), gr...  12.4 us

profile of v7, /device:TPU:0, one launch (start us, length us, event | category | flops | bytes accessed | tf_op | source)
XLA Modules:
  0.0 414.3 jit_solution(8057734841251190114)
XLA Ops:
  1.5 0.8 constant_dynamic-slice_fusion
  3.0 19.4 %start_all.1 = (bf16[512,1024]{1,0:T(8,128)(2,1)}, bf16[3,1024,256]{2,1,0:T(8,128)(2,1)}, bf16[1024,1024]{1,0:T(8,128)(2,1)}, bf16[1024,256]{1,0:T(8,128)(2,1)},...) custom-call(bf16[256,512]{1,0:T(8,128)(2,1)} %refs_1_.3, ...), custom_call_target="tpu_custom_call" | custom-call | tf_op jit(solution)/shard_map/start_all/pallas_call | solution.py:251
  22.5 1.5 fusion
  24.0 2.8 fusion.3.qkv
  26.8 0.7 slice_bitcast_fusion.refs_1_
  27.7 17.7 %attend.1 = (bf16[512,256]{1,0:T(8,128)(2,1)}, f32[4,512]{1,0:T(4,128)}, bf16[2,1024,256]{2,1,0:T(8,128)(2,1)}, bf16[512,1024]{1,0:T(8,128)(2,1)}) custom-call(s32[1]{0:T(128)S(6)} %copy.49.prefix.refs_0_, bf16[3,512,256]{2,1,0:T(8,128)(2,1)} %copy-done.6, bf16[256,512]{1,0:T(8,128)(2,1)} %refs_2_.3), custom_call_target="tpu_custom_call" | custom-call | tf_op jit(solution)/shard_map/attend/pallas_call | solution.py:331
  45.4 2.5 convolution_convert_fusion.3.part
  48.6 32.5 %join.1 = (f32[256,512]{1,0:T(8,128)}, bf16[512,1024]{1,0:T(8,128)(2,1)}) custom-call(bf16[512,1024]{1,0:T(8,128)(2,1)} %convolution_convert_fusion.3.part, bf16[256,512]{1,0:T(8,128)(2,1)} %refs_1_.3, bf16[1,512]{1,0:T(2,128)(2,1)} %broadcast_in_dim.4.gain.refs_3_), custom_call_target="tpu_custom_call" | custom-call | tf_op jit(solution)/shard_map/join/pallas_call | solution.py:381
  81.2 1.7 fusion.39
  83.0 2.5 multiply_convert_fusion.2
  85.5 0.7 copy.46
  86.2 2.2 convolution_convert_fusion.2.query_ref
  88.4 0.8 dynamic-slice_bitcast_fusion.keys_ref
  89.3 12.4 %weigh.1 = (f32[4,32,128]{2,1,0:T(8,128)}, bf16[4,32,128]{2,1,0:T(8,128)(2,1)}) custom-call(bf16[512,1024]{1,0:T(8,128)(2,1)} %convolution_convert_fusion.2.query_ref, bf16[2,256,512]{2,1,0:T(8,128)(2,1)} %dynamic-slice_bitcast_fusion.keys_ref, s32[4,1,4096]{2,1,0:T(1,128)} %bitcast.90, s32[4,1,4096]{2,1,0:T(1,128)} %get-tuple-element.64.rank_ref), custom_call_target="tpu_custom_call" | custom-call | tf_op jit(solution)/shard_map/weigh/pallas_call | solution.py:1114
  101.7 1.4 copy.45
  103.1 111.8 %use_memory.1 = (bf16[4,2,4,512,256]{4,3,2,1,0:T(8,128)(2,1)}, bf16[4,2,512,2048]{3,2,1,0:T(8,128)(2,1)}, bf16[4,512,1024]{2,1,0:T(8,128)(2,1)}, f32[512,256]{1,0:T(8,128)}, f32[32,4,128]{2,1,0:T(4,128)}) custom-call(bf16[512,256]{1,0:T(8,128)(2,1)} %get-tuple-element.99.grads, s32[32,4,128]{2,1,0:T(4,128)} %bitcast.92, f32[32,4,128]{2,1,0:T(4,128)} %bitcast.93, ...), custom_call_target="tpu_custom_call" | custom-call | tf_op jit(solution)/shard_map/use_memory/pallas_call | solution.py:1552
  214.9 1.7 copy.40
  216.6 11.7 %unweigh.1 = (bf16[256,512]{1,0:T(8,128)(2,1)}, bf16[256,512]{1,0:T(8,128)(2,1)}) custom-call(f32[4,128,32]{2,1,0:T(8,128)} %bitcast.88, s32[4,1,4096]{2,1,0:T(1,128)} %bitcast.91, s32[4,1,4096]{2,1,0:T(1,128)} %get-tuple-element.64.rank_ref, f32[4,32,128]{2,1,0:T(8,128)} %get-tuple-element.67.weights_ref), custom_call_target="tpu_custom_call" | custom-call | tf_op jit(solution)/shard_map/unweigh/pallas_call | solution.py:1633
  228.3 1.4 convolution_convert_fusion.11
  229.8 1.5 convolution_convert_fusion.12
  231.3 1.3 fusion.10
  233.0 1.5 add_convert_fusion.1.refs_0_
  234.5 1.3 convolution_convert_fusion.10.refs_4_
  235.8 1.3 convolution_convert_fusion.9.refs_5_
  237.7 0.8 pad_maximum_fusion.4
  238.5 37.4 %middle.1 = (f32[256,512]{1,0:T(8,128)}, bf16[512,1024]{1,0:T(8,128)(2,1)}, f32[1,512]{1,0:T(1,128)}, bf16[128,256]{1,0:T(8,128)(2,1)}, bf16[64,512]{1,0:T(8,128)(2,1)}, /*index=5*/bf16[64,512]{1,0:T(8,128)(2,1)}) custom-call(bf16[512,1024]{1,0:T(8,128)(2,1)} %add_convert_fusion.1.refs_0_, f32[256,512]{1,0:T(8,128)} %get-tuple-element.71.refs_1_.refs_6_, ...), custom_call_target="tpu_custom_call" | custom-call | tf_op jit(solution)/shard_map/middle/pallas_call | solution.py:682
  276.0 2.5 convolution_convert_fusion.13.refs_3_
  278.5 1.4 convolution_convert_fusion.1.refs_5_
  279.9 2.6 convolution_convert_fusion.refs_10_
  282.5 36.6 %turn.1 = (bf16[512,256]{1,0:T(8,128)(2,1)}, bf16[2,512,256]{2,1,0:T(8,128)(2,1)}, bf16[256,512]{1,0:T(8,128)(2,1)}, bf16[512,256]{1,0:T(8,128)(2,1)}, bf16[256,...) custom-call(s32[1]{0:T(128)S(6)} %copy.49.prefix.refs_0_, ...), custom_call_target="tpu_custom_call" | custom-call | tf_op jit(solution)/shard_map/turn/pallas_call | solution.py:1014
  319.2 1.7 fusion.16
  321.4 1.5 add_convert_fusion.refs_0_
  324.2 0.7 fusion.5
  325.2 0.7 fusion.4
  325.9 1.3 pad_maximum_fusion.refs_7_
  327.6 1.3 convolution_convert_fusion.5.refs_8_
  328.9 67.3 %last.1 = (f32[256,512]{1,0:T(8,128)}, f32[2,8,128]{2,1,0:T(8,128)}, bf16[2048,1024]{1,0:T(8,128)(2,1)}, bf16[512,1024]{1,0:T(8,128)(2,1)}, bf16[3,512,256]{2,1,...) custom-call(bf16[512,1024]{1,0:T(8,128)(2,1)} %add_convert_fusion.refs_0_, ...), custom_call_target="tpu_custom_call" | custom-call | tf_op jit(solution)/shard_map/last/pallas_call | solution.py:876
  396.3 0.8 reshape.45
  397.7 2.4 convert_element_type.105
  400.1 0.9 convert_element_type.106
  400.9 1.6 convert_element_type.107
  402.5 0.8 convert_element_type.108
  403.3 0.9 convert_element_type.109
  404.2 2.7 convert_element_type.110
  406.9 1.0 copy-done.2
  407.9 4.4 %convert_element_type.111 = f32[2048,1024]{1,0:T(8,128)} convert(bf16[2048,1024]{1,0:T(8,128)(2,1)S(1)} %copy-done.2) | non-fusion elementwise | flops 2097152 | bytes 12582912 | tf_op jit(solution)/shard_map/convert_element_type | solution.py:1787
  412.4 0.7 copy.50
  413.1 0.8 copy.51
  (91 shorter events, 5.8 us)
Async XLA Ops:
  0.6 87.8 %copy-start = (bf16[4,2,256,512]{3,2,1,0:T(8,128)(2,1)S(1)}, bf16[4,2,256,512]{3,2,1,0:T(8,128)(2,1)}, u32[]{:S(2)}) copy-start(bf16[4,2,256,512]{3,2,1,0:T(8,128)(2,1)} %param.23) | copy-start | bytes 6291460
  0.7 21.8 %copy-start.35 = (bf16[1024]{0:T(1024)(128)(2,1)S(1)}, bf16[1024]{0:T(1024)(128)(2,1)}, u32[]{:S(2)}) copy-start(bf16[1024]{0:T(1024)(128)(2,1)} %param.16) | copy-start | bytes 6148
  26.8 1.0 copy-start.6
  26.8 21.2 %copy-start.36 = (bf16[1024]{0:T(1024)(128)(2,1)S(1)}, bf16[1024]{0:T(1024)(128)(2,1)}, u32[]{:S(2)}) copy-start(bf16[1024]{0:T(1024)(128)(2,1)} %param.19) | copy-start | bytes 6148
  27.7 53.4 %copy-start.4 = (bf16[1024,256]{1,0:T(8,128)(2,1)S(1)}, bf16[1024,256]{1,0:T(8,128)(2,1)}, u32[]{:S(2)}) copy-start(bf16[1024,256]{1,0:T(8,128)(2,1)} %get-tuple-element.61) | copy-start | bytes 1572868
  81.2 1.8 copy-start.9
  82.9 2.6 copy-start.34
  83.0 3.2 copy-start.13
  83.0 3.2 copy-start.37
  228.3 3.0 copy-start.38
  229.8 2.8 copy-start.19
  231.3 1.3 copy-start.22
  231.3 1.3 copy-start.24
  231.3 1.4 copy-start.25
  233.0 1.5 copy-start.14
  234.4 1.3 copy-start.10
  234.4 2.6 copy-start.16
  234.4 2.6 copy-start.29
  234.5 2.9 copy-start.32
  237.7 38.3 %copy-start.18 = (bf16[256,1024]{1,0:T(8,128)(2,1)S(1)}, bf16[256,1024]{1,0:T(8,128)(2,1)}, u32[]{:S(2)}) copy-start(bf16[256,1024]{1,0:T(8,128)(2,1)} %get-tuple-element.59) | copy-start | bytes 1572868
  238.5 40.0 %copy-start.17 = (bf16[256,1024]{1,0:T(8,128)(2,1)S(1)}, bf16[256,1024]{1,0:T(8,128)(2,1)}, u32[]{:S(2)}) copy-start(bf16[256,1024]{1,0:T(8,128)(2,1)} %get-tuple-element.57) | copy-start | bytes 1572868
  275.9 4.0 copy-start.15
  275.9 4.0 copy-start.20
  275.9 4.0 copy-start.23
  319.1 1.8 copy-start.5
  319.1 1.8 copy-start.26
  321.4 2.2 copy-start.12
  324.2 1.0 copy-start.33
  325.8 1.3 copy-start.8
  325.8 1.8 copy-start.11
  396.2 3.8 copy-start.30
  396.2 4.7 %copy-start.7 = (bf16[512,1024]{1,0:T(8,128)(2,1)S(1)}, bf16[512,1024]{1,0:T(8,128)(2,1)}, u32[]{:S(2)}) copy-start(bf16[512,1024]{1,0:T(8,128)(2,1)} %get-tuple-element.90) | copy-start | bytes 3145732
  400.1 2.4 copy-start.28
  400.9 2.4 copy-start.27
  400.9 3.3 copy-start.3
  404.2 3.7 copy-start.2
  407.9 4.4 %copy-start.31 = (bf16[256,512]{1,0:T(8,128)(2,1)S(1)}, bf16[256,512]{1,0:T(8,128)(2,1)}, u32[]{:S(2)}) copy-start(bf16[256,512]{1,0:T(8,128)(2,1)} %get-tuple-element.112) | copy-start | bytes 786436
  407.9 5.2 %copy-start.21 = (f32[256,512]{1,0:T(8,128)S(1)}, f32[256,512]{1,0:T(8,128)}, u32[]{:S(2)}) copy-start(f32[256,512]{1,0:T(8,128)} %get-tuple-element.113) | copy-start | bytes 1572868
  407.9 5.9 %copy-start.1 = (bf16[4,2,256,512]{3,2,1,0:T(8,128)(2,1)S(1)}, bf16[4,2,256,512]{3,2,1,0:T(8,128)(2,1)}, u32[]{:S(2)}) copy-start(bf16[4,2,256,512]{3,2,1,0:T(8,128)(2,1)} %param.23) | copy-start | bytes 6291460

commit v8 on v7

--- a/solution.py
+++ b/solution.py
@@ -486,13 +486,8 @@
     def start(self):
         dp, last = self.spot[0], self.count - 1
 
-        @pl.when(dp == 0)
-        def _():
-            lax.fori_loop(0, last, lambda i, c: (self.send(last - i, True), c)[1], 0)
-
-        @pl.when(dp == last)
-        def _():
-            lax.fori_loop(0, last, lambda i, c: (self.send(i, False), c)[1], 0)
+        pl.when(dp == 0)(lambda: self.send(last, True))
+        pl.when(dp == last)(lambda: self.send(0, False))
 
     def take(self, k, up):
         for n, (array, dim) in enumerate(zip(self.arrays, self.dims)):
@@ -502,6 +497,8 @@
 
     def event(self, time):
         dp, last = self.spot[0], self.count - 1
+        pl.when(jnp.logical_and(dp == 0, time < last))(lambda: self.send(last - time, True))
+        pl.when(jnp.logical_and(dp == last, time < last))(lambda: self.send(time, False))
 
         @pl.when(jnp.logical_and(dp > 0, time >= dp))
         def _():
@@ -658,6 +655,7 @@
     pair.finish()
     reduce = LineReduce(spot, sizes, halves, FIRST_DIMS, below, above, line)
     reduce.start()
+    reduce.event(1)
     scatter.wait()
     total, gains = norm_back(sizes, spot, landing, hidden, dy, gain, mine, theirs, psend, precv)
     gain_grad[...] = gains
@@ -665,7 +663,7 @@
     block[...] = total.astype(jnp.bfloat16)
     gather = Gather(spot, sizes, block, grad_all, gsend, grecv)
     gather.start()
-    lax.fori_loop(1, sizes[0], lambda time, c: (reduce.event(time), c)[1], 0)
+    lax.fori_loop(2, sizes[0], lambda time, c: (reduce.event(time), c)[1], 0)
     for half, dim, shard in zip(halves, FIRST_DIMS, shards):
         shard[...] = slab(half, dim, spot[0], sizes[0])[...]
     scatter.wait_send()
@@ -802,9 +800,13 @@
         there = keys_all.at[lax.rem(row + k, rows), col]
         return remote(src, there, kxsend, kxrecv, (dp, row, 1 - col))
 
-    products(0, loads // 4)
-    gather.event(1)
-    reduce.event(1)
+    def both(time):
+        reduce.event(time)
+        gather.event(time)
+
+    products(0, loads // 8)
+    both(1)
+    products(loads // 8, loads // 4)
     scatter.wait()
     total, gains = norm_back(sizes, spot, landing, x, above_grad, gain, mine, theirs, psend, precv)
     lines = gains.shape[1] // 128
@@ -823,27 +825,23 @@
         sideways(k).start()
     cross(keys, 0).start()
     keys_all[row, col] = keys[...]
-    products(loads // 4, loads // 2)
-
-    def both(time):
-        gather.event(time)
-        reduce.event(time)
-
     both(2)
-    products(loads // 2, 3 * loads // 4)
+    products(loads // 4, 3 * loads // 8)
     lax.fori_loop(3, dps, lambda time, c: (both(time), c)[1], 0)
     for first, half, dim in zip(lasts, halves, LAST_DIMS):
         slab(first, dim, dp, dps)[...] = slab(half, dim, dp, dps)[...]
     final = LineGather(spot, sizes, lasts, LAST_DIMS, line[4:7])
     final.start()
-    products(3 * loads // 4, 7 * loads // 8)
+    products(3 * loads // 8, 5 * loads // 8)
     final.event(1)
     for k in range(1, rows):
         landed = keys_all.at[lax.rem(row + k, rows), col]
         arrived(landed, xrecv.at[k])
         cross(landed, k).start()
+    products(5 * loads // 8, 7 * loads // 8)
+    final.event(2)
     products(7 * loads // 8, loads)
-    lax.fori_loop(2, dps, lambda time, c: (final.event(time), c)[1], 0)
+    lax.fori_loop(3, dps, lambda time, c: (final.event(time), c)[1], 0)
     arrived(keys_all.at[:, 1 - col], kxrecv)
     scatter.wait_send()
     arrived(gain_landing.at[pl.ds(0, count - 1)], brecv)
@@ -974,8 +972,8 @@
             totals[0, :, lanes] = totals[0, :, lanes] + dk
             totals[1, :, lanes] = totals[1, :, lanes] + dv
 
-        pl.when(index == 1)(lambda: events(1))
-        pl.when(index == 3)(lambda: events(2))
+        pl.when(index == 0)(lambda: events(1))
+        pl.when(index == 2)(lambda: events(2))
         return carry
 
     lax.fori_loop(0, 2 * width // (2 * HDIM), unit, 0)
@@ -1077,39 +1075,46 @@
     return rank, (outs[1] * FBLK + outs[2]) * SUBKEYS + outs[0]
 
 
-def weigh_kernel(rows_dev, owners, cap, query_ref, keys_ref, picks_ref, rank_ref, weights_ref, slots_ref):
+def pick_rows(table, index):
+    inner = index % 8
+    outer = index // 8
+    result = jnp.zeros(index.shape, jnp.float32)
+    for group in range(SUBKEYS // 8):
+        rows = table[group * 8 : (group + 1) * 8]
+        found = [
+            jnp.take_along_axis(rows, inner[n * 8 : (n + 1) * 8], axis=0)
+            for n in range(index.shape[0] // 8)
+        ]
+        result = jnp.where(outer == group, jnp.concatenate(found, axis=0), result)
+    return result
+
+
+def weigh_kernel(
+    rows_dev, owners, cap, query_ref, keys_ref, picks_ref, square_ref, rank_ref, weights_ref, slots_ref
+):
     picks = picks_ref[0]
+    square = square_ref[0]
     first = lax.dot_general(
         keys_ref[0], query_ref[:, :HALF], (((1,), (1,)), ((), ())), preferred_element_type=jnp.float32
     )
     second = lax.dot_general(
         keys_ref[1], query_ref[:, HALF:], (((1,), (1,)), ((), ())), preferred_element_type=jnp.float32
     )
-    upper = picks // SUBKEYS
-    lower = picks % SUBKEYS
-    key_id = lax.broadcasted_iota(jnp.int32, (SUBKEYS, FBLK), 0)
-    rows = []
-    for pick in range(TOPK):
-        columns = slice(pick * FBLK, (pick + 1) * FBLK)
-        chosen = jnp.where(key_id == upper[:, columns], first, 0.0) + jnp.where(
-            key_id == lower[:, columns], second, 0.0
-        )
-        rows.append(jnp.sum(chosen, axis=0, keepdims=True))
-    scores = jnp.concatenate(rows, axis=0)
+    scores = pick_rows(first, square // SUBKEYS) + pick_rows(second, square % SUBKEYS)
     powers = jnp.exp(scores - jnp.max(scores, axis=0, keepdims=True))
     weights = powers / jnp.sum(powers, axis=0, keepdims=True)
     weights_ref[0] = weights
     flat = jnp.concatenate([weights[pick : pick + 1] for pick in range(TOPK)], axis=1)
     scaled = one_hot(picks // rows_dev, owners) * flat.astype(jnp.bfloat16)
     slots_ref[0] = lax.dot_general(
+        one_hot(rank_ref[0], cap),
         scaled,
-        one_hot(rank_ref[0], cap),
         (((1,), (1,)), ((), ())),
         preferred_element_type=jnp.float32,
-    ).astype(jnp.bfloat16)
-
-
-def weigh(query_rows, keys_head, flat, rank, rows_dev, owners, cap):
+    )
+
+
+def weigh(query_rows, keys_head, flat, square, rank, rows_dev, owners, cap):
     blocks, count = flat.shape
     return pl.pallas_call(
         functools.partial(weigh_kernel, rows_dev, owners, cap),
@@ -1118,18 +1123,19 @@
             pl.BlockSpec((FBLK, 2 * HALF), lambda i: (i, 0)),
             pl.BlockSpec((2, SUBKEYS, HALF), lambda i: (0, 0, 0)),
             pl.BlockSpec((1, 1, count), lambda i: (i, 0, 0)),
+            pl.BlockSpec((1, TOPK, FBLK), lambda i: (i, 0, 0)),
             pl.BlockSpec((1, 1, count), lambda i: (i, 0, 0)),
         ],
         out_specs=[
             pl.BlockSpec((1, TOPK, FBLK), lambda i: (i, 0, 0)),
-            pl.BlockSpec((1, owners, cap), lambda i: (i, 0, 0)),
+            pl.BlockSpec((1, cap, owners), lambda i: (i, 0, 0)),
         ],
         out_shape=[
             jax.ShapeDtypeStruct((blocks, TOPK, FBLK), jnp.float32),
-            jax.ShapeDtypeStruct((blocks, owners, cap), jnp.bfloat16),
+            jax.ShapeDtypeStruct((blocks, cap, owners), jnp.float32),
         ],
         name="weigh",
-    )(query_rows, keys_head, flat[:, None, :], rank)
+    )(query_rows, keys_head, flat[:, None, :], square, rank)
 
 
 def send_rows(spot, sizes, src, landing, send, recv):
@@ -1615,16 +1621,23 @@
     grads = weights * (grads - jnp.sum(weights * grads, axis=0, keepdims=True))
     upper = picks // SUBKEYS
     lower = picks % SUBKEYS
-    key_id = lax.broadcasted_iota(jnp.int32, (SUBKEYS, FBLK), 0)
-    first = jnp.zeros((SUBKEYS, FBLK), jnp.float32)
-    second = jnp.zeros((SUBKEYS, FBLK), jnp.float32)
-    for pick in range(TOPK):
-        columns = slice(pick * FBLK, (pick + 1) * FBLK)
-        value = grads[pick : pick + 1]
-        first = first + jnp.where(key_id == upper[:, columns], value, 0.0)
-        second = second + jnp.where(key_id == lower[:, columns], value, 0.0)
-    first_ref[...] = first.astype(jnp.bfloat16)
-    second_ref[...] = second.astype(jnp.bfloat16)
+    tile = 64
+
+    def some_keys(index, carry):
+        lines = pl.ds(pl.multiple_of(index * tile, tile), tile)
+        key_id = lax.broadcasted_iota(jnp.int32, (tile, FBLK), 0) + index * tile
+        first = jnp.zeros((tile, FBLK), jnp.float32)
+        second = jnp.zeros((tile, FBLK), jnp.float32)
+        for pick in range(TOPK):
+            columns = slice(pick * FBLK, (pick + 1) * FBLK)
+            value = grads[pick : pick + 1]
+            first = first + jnp.where(key_id == upper[:, columns], value, 0.0)
+            second = second + jnp.where(key_id == lower[:, columns], value, 0.0)
+        first_ref[lines] = first.astype(jnp.bfloat16)
+        second_ref[lines] = second.astype(jnp.bfloat16)
+        return carry
+
+    lax.fori_loop(0, SUBKEYS // tile, some_keys, 0)
 
 
 def unweigh(back, flat, rank, weights, rows_dev, owners):
@@ -1655,10 +1668,11 @@
     cap = FBLK * TOPK // owners
     head_id = lax.axis_index("row")
     keys_head = lax.dynamic_index_in_dim(subkeys, head_id, 0, keepdims=False)
-    weights, slots = weigh(query_rows, keys_head, flat, rank, rows_dev, owners, cap)
+    square = flat.reshape(-1, TOPK, FBLK)
+    weights, slots = weigh(query_rows, keys_head, flat, square, rank, rows_dev, owners, cap)
     spare = ((0, 0), (0, 0), (0, 128 - cap))
     meta = jnp.pad(jnp.swapaxes(meta, 0, 1), spare, constant_values=-1)
-    slots = jnp.pad(jnp.swapaxes(slots, 0, 1).astype(jnp.float32), spare)
+    slots = jnp.pad(jnp.transpose(slots, (2, 0, 1)), spare)
     grads_all, table, memory, back = use_memory(
         sizes, grad_memory, meta, slots, values
     )

time: 419 us -> 404 us (0.964)
  Pallas kernels: 347 us -> 336 us
    pallas_call x1, Pallas kernels: 12.4 us -> 6.08 us  [weigh(): pl.pallas_call(functools.partial(weigh_kernel, rows_dev, owners, cap), gr...]
where the time goes in v8:
time: 404 us; the launch traced here: 403 us
  Pallas kernels  336 us (83%)
  matrix products  34.2 us (8%)
  other arithmetic  17.6 us (4%)
  local copies, waits for them, and re-layouts  13.5 us (3%)
    pallas_call x1, Pallas kernels, use_memory(): pl.pallas_call(functools.partial(memory_kernel, sizes, blocks), in_specs=...  112 us
    pallas_call x1, Pallas kernels, last(): pl.pallas_call(functools.partial(last_kernel, sizes), in_specs=[VMEM] * 9...  65.8 us
    pallas_call x1, Pallas kernels, middle(): pl.pallas_call(functools.partial(middle_kernel, sizes), in_specs=[VMEM] *...  37.4 us
    pallas_call x1, Pallas kernels, turn(): pl.pallas_call(functools.partial(turn_kernel, sizes), in_specs=[pl.BlockS...  36.3 us
    pallas_call x1, Pallas kernels, join(): pl.pallas_call(functools.partial(join_kernel, sizes), in_specs=[VMEM] * 3...  32.5 us
    pallas_call x1, Pallas kernels, start_all(): pl.pallas_call(functools.partial(start_kernel, sizes, rows_dev), in_specs...  19.4 us
    pallas_call x1, Pallas kernels, attend(): pl.pallas_call(functools.partial(attend_kernel, sizes), in_specs=[pl.Bloc...  17.7 us
    dot_general x7, matrix products, dense_nt(): lax.dot_general(left, right, (((1,), (1,)), ((), ())), preferred_element_...  11.5 us

profile of v8, /device:TPU:0, one launch (start us, length us, event | category | flops | bytes accessed | tf_op | source)
XLA Modules:
  0.0 403.4 jit_solution(15888806165521724750)
XLA Ops:
  1.5 0.8 constant_dynamic-slice_fusion
  3.0 19.4 %start_all.1 = (bf16[512,1024]{1,0:T(8,128)(2,1)}, bf16[3,1024,256]{2,1,0:T(8,128)(2,1)}, bf16[1024,1024]{1,0:T(8,128)(2,1)}, bf16[1024,256]{1,0:T(8,128)(2,1)},...) custom-call(bf16[256,512]{1,0:T(8,128)(2,1)} %refs_1_.3, ...), custom_call_target="tpu_custom_call" | custom-call | tf_op jit(solution)/shard_map/start_all/pallas_call | solution.py:251
  22.5 1.5 fusion
  24.0 2.8 fusion.3.qkv
  26.8 0.7 slice_bitcast_fusion.refs_1_
  27.7 17.7 %attend.1 = (bf16[512,256]{1,0:T(8,128)(2,1)}, f32[4,512]{1,0:T(4,128)}, bf16[2,1024,256]{2,1,0:T(8,128)(2,1)}, bf16[512,1024]{1,0:T(8,128)(2,1)}) custom-call(s32[1]{0:T(128)S(6)} %copy.44.prefix.refs_0_, bf16[3,512,256]{2,1,0:T(8,128)(2,1)} %copy-done.6, bf16[256,512]{1,0:T(8,128)(2,1)} %refs_2_.3), custom_call_target="tpu_custom_call" | custom-call | tf_op jit(solution)/shard_map/attend/pallas_call | solution.py:331
  45.4 2.5 convolution_convert_fusion.3.part
  48.6 32.5 %join.1 = (f32[256,512]{1,0:T(8,128)}, bf16[512,1024]{1,0:T(8,128)(2,1)}) custom-call(bf16[512,1024]{1,0:T(8,128)(2,1)} %convolution_convert_fusion.3.part, bf16[256,512]{1,0:T(8,128)(2,1)} %refs_1_.3, bf16[1,512]{1,0:T(2,128)(2,1)} %broadcast_in_dim.4.gain.refs_3_), custom_call_target="tpu_custom_call" | custom-call | tf_op jit(solution)/shard_map/join/pallas_call | solution.py:381
  81.2 1.8 fusion.39
  83.0 2.5 multiply_convert_fusion.2
  85.5 0.7 copy.40
  86.2 2.2 convolution_convert_fusion.2.query_ref
  88.4 0.8 dynamic-slice_bitcast_fusion.keys_ref
  89.3 6.1 %weigh.1 = (f32[4,32,128]{2,1,0:T(8,128)}, f32[4,128,32]{2,1,0:T(8,128)}) custom-call(bf16[512,1024]{1,0:T(8,128)(2,1)} %convolution_convert_fusion.2.query_ref, bf16[2,256,512]{2,1,0:T(8,128)(2,1)} %dynamic-slice_bitcast_fusion.keys_ref, s32[4,1,4096]{2,1,0:T(1,128)} %bitcast.90, s32[4,32,128]{2,1,0:T(8,128)} %bitcast.91, ...), custom_call_target="tpu_custom_call" | custom-call | tf_op jit(solution)/shard_map/weigh/pallas_call | solution.py:1119
  95.4 1.7 copy.33
  97.0 111.8 %use_memory.1 = (bf16[4,2,4,512,256]{4,3,2,1,0:T(8,128)(2,1)}, bf16[4,2,512,2048]{3,2,1,0:T(8,128)(2,1)}, bf16[4,512,1024]{2,1,0:T(8,128)(2,1)}, f32[512,256]{1,0:T(8,128)}, f32[32,4,128]{2,1,0:T(4,128)}) custom-call(bf16[512,256]{1,0:T(8,128)(2,1)} %get-tuple-element.101.grads, s32[32,4,128]{2,1,0:T(4,128)} %bitcast.95, f32[32,4,128]{2,1,0:T(4,128)} %bitcast.94, ...), custom_call_target="tpu_custom_call" | custom-call | tf_op jit(solution)/shard_map/use_memory/pallas_call | solution.py:1558
  208.8 1.7 copy.34
  210.5 9.2 %unweigh.1 = (bf16[256,512]{1,0:T(8,128)(2,1)}, bf16[256,512]{1,0:T(8,128)(2,1)}) custom-call(f32[4,128,32]{2,1,0:T(8,128)} %bitcast.93, s32[4,1,4096]{2,1,0:T(1,128)} %bitcast.92, s32[4,1,4096]{2,1,0:T(1,128)} %get-tuple-element.64.rank_ref, f32[4,32,128]{2,1,0:T(8,128)} %get-tuple-element.67.weights_ref), custom_call_target="tpu_custom_call" | custom-call | tf_op jit(solution)/shard_map/unweigh/pallas_call | solution.py:1646
  219.7 1.4 convolution_convert_fusion.11
  221.2 1.5 convolution_convert_fusion.12
  222.7 1.3 fusion.10
  224.4 1.5 add_convert_fusion.1.refs_0_
  225.9 1.3 convolution_convert_fusion.10.refs_4_
  227.2 1.3 convolution_convert_fusion.9.refs_5_
  229.1 0.8 pad_maximum_fusion.4
  229.9 37.4 %middle.1 = (f32[256,512]{1,0:T(8,128)}, bf16[512,1024]{1,0:T(8,128)(2,1)}, f32[1,512]{1,0:T(1,128)}, bf16[128,256]{1,0:T(8,128)(2,1)}, bf16[64,512]{1,0:T(8,128)(2,1)}, /*index=5*/bf16[64,512]{1,0:T(8,128)(2,1)}) custom-call(bf16[512,1024]{1,0:T(8,128)(2,1)} %add_convert_fusion.1.refs_0_, f32[256,512]{1,0:T(8,128)} %get-tuple-element.71.refs_1_.refs_6_, ...), custom_call_target="tpu_custom_call" | custom-call | tf_op jit(solution)/shard_map/middle/pallas_call | solution.py:680
  267.3 2.5 convolution_convert_fusion.13.refs_3_
  269.9 1.4 convolution_convert_fusion.1.refs_5_
  271.3 2.6 convolution_convert_fusion.refs_10_
  273.9 36.3 %turn.1 = (bf16[512,256]{1,0:T(8,128)(2,1)}, bf16[2,512,256]{2,1,0:T(8,128)(2,1)}, bf16[256,512]{1,0:T(8,128)(2,1)}, bf16[512,256]{1,0:T(8,128)(2,1)}, bf16[256,...) custom-call(s32[1]{0:T(128)S(6)} %copy.44.prefix.refs_0_, ...), custom_call_target="tpu_custom_call" | custom-call | tf_op jit(solution)/shard_map/turn/pallas_call | solution.py:1012
  310.3 1.7 fusion.16
  312.5 1.5 add_convert_fusion.refs_0_
  315.3 0.7 fusion.5
  316.3 0.7 fusion.4
  317.0 1.3 pad_maximum_fusion.refs_7_
  318.7 1.3 convolution_convert_fusion.5.refs_8_
  320.0 65.8 %last.1 = (f32[256,512]{1,0:T(8,128)}, f32[2,8,128]{2,1,0:T(8,128)}, bf16[2048,1024]{1,0:T(8,128)(2,1)}, bf16[512,1024]{1,0:T(8,128)(2,1)}, bf16[3,512,256]{2,1,...) custom-call(bf16[512,1024]{1,0:T(8,128)(2,1)} %add_convert_fusion.refs_0_, ...), custom_call_target="tpu_custom_call" | custom-call | tf_op jit(solution)/shard_map/last/pallas_call | solution.py:874
  385.8 0.8 reshape.45
  387.2 2.4 convert_element_type.98
  389.6 0.9 convert_element_type.99
  390.5 1.6 convert_element_type.100
  392.1 0.8 convert_element_type.101
  392.9 0.9 convert_element_type.102
  393.8 2.7 convert_element_type.103
  396.5 1.0 copy-done.2
  397.5 4.4 %convert_element_type.104 = f32[2048,1024]{1,0:T(8,128)} convert(bf16[2048,1024]{1,0:T(8,128)(2,1)S(1)} %copy-done.2) | non-fusion elementwise | flops 2097152 | bytes 12582912 | tf_op jit(solution)/shard_map/convert_element_type | solution.py:1801
  401.9 0.7 copy.45
  402.6 0.8 copy.46
  (91 shorter events, 5.8 us)
Async XLA Ops:
  0.6 87.8 %copy-start = (bf16[4,2,256,512]{3,2,1,0:T(8,128)(2,1)S(1)}, bf16[4,2,256,512]{3,2,1,0:T(8,128)(2,1)}, u32[]{:S(2)}) copy-start(bf16[4,2,256,512]{3,2,1,0:T(8,128)(2,1)} %param.23) | copy-start | bytes 6291460
  0.7 21.8 %copy-start.35 = (bf16[1024]{0:T(1024)(128)(2,1)S(1)}, bf16[1024]{0:T(1024)(128)(2,1)}, u32[]{:S(2)}) copy-start(bf16[1024]{0:T(1024)(128)(2,1)} %param.16) | copy-start | bytes 6148
  26.8 1.0 copy-start.6
  26.8 21.2 %copy-start.36 = (bf16[1024]{0:T(1024)(128)(2,1)S(1)}, bf16[1024]{0:T(1024)(128)(2,1)}, u32[]{:S(2)}) copy-start(bf16[1024]{0:T(1024)(128)(2,1)} %param.19) | copy-start | bytes 6148
  27.7 53.4 %copy-start.4 = (bf16[1024,256]{1,0:T(8,128)(2,1)S(1)}, bf16[1024,256]{1,0:T(8,128)(2,1)}, u32[]{:S(2)}) copy-start(bf16[1024,256]{1,0:T(8,128)(2,1)} %get-tuple-element.61) | copy-start | bytes 1572868
  81.2 1.8 copy-start.9
  82.9 2.6 copy-start.34
  83.0 3.2 copy-start.14
  83.0 3.2 copy-start.37
  219.7 2.9 copy-start.38
  221.2 2.8 copy-start.19
  222.7 1.3 copy-start.22
  222.7 1.3 copy-start.24
  222.7 1.4 copy-start.25
  224.4 1.5 copy-start.15
  225.8 1.3 copy-start.10
  225.8 2.6 copy-start.12
  225.8 2.6 copy-start.29
  225.9 2.9 copy-start.32
  229.1 38.3 %copy-start.18 = (bf16[256,1024]{1,0:T(8,128)(2,1)S(1)}, bf16[256,1024]{1,0:T(8,128)(2,1)}, u32[]{:S(2)}) copy-start(bf16[256,1024]{1,0:T(8,128)(2,1)} %get-tuple-element.59) | copy-start | bytes 1572868
  229.9 40.0 %copy-start.17 = (bf16[256,1024]{1,0:T(8,128)(2,1)S(1)}, bf16[256,1024]{1,0:T(8,128)(2,1)}, u32[]{:S(2)}) copy-start(bf16[256,1024]{1,0:T(8,128)(2,1)} %get-tuple-element.57) | copy-start | bytes 1572868
  267.3 4.0 copy-start.16
  267.3 4.0 copy-start.20
  267.3 4.0 copy-start.23
  310.2 1.8 copy-start.5
  310.3 1.8 copy-start.26
  312.5 2.2 copy-start.13
  315.3 1.0 copy-start.33
  316.9 1.3 copy-start.8
  317.0 1.8 copy-start.11
  385.8 3.8 copy-start.30
  385.8 4.7 %copy-start.7 = (bf16[512,1024]{1,0:T(8,128)(2,1)S(1)}, bf16[512,1024]{1,0:T(8,128)(2,1)}, u32[]{:S(2)}) copy-start(bf16[512,1024]{1,0:T(8,128)(2,1)} %get-tuple-element.90) | copy-start | bytes 3145732
  389.6 2.4 copy-start.28
  390.5 2.4 copy-start.27
  390.5 3.3 copy-start.3
  393.8 3.7 copy-start.2
  397.5 4.4 %copy-start.31 = (bf16[256,512]{1,0:T(8,128)(2,1)S(1)}, bf16[256,512]{1,0:T(8,128)(2,1)}, u32[]{:S(2)}) copy-start(bf16[256,512]{1,0:T(8,128)(2,1)} %get-tuple-element.114) | copy-start | bytes 786436
  397.5 5.2 %copy-start.21 = (f32[256,512]{1,0:T(8,128)S(1)}, f32[256,512]{1,0:T(8,128)}, u32[]{:S(2)}) copy-start(f32[256,512]{1,0:T(8,128)} %get-tuple-element.115) | copy-start | bytes 1572868
  397.5 5.9 %copy-start.1 = (bf16[4,2,256,512]{3,2,1,0:T(8,128)(2,1)S(1)}, bf16[4,2,256,512]{3,2,1,0:T(8,128)(2,1)}, u32[]{:S(2)}) copy-start(bf16[4,2,256,512]{3,2,1,0:T(8,128)(2,1)} %param.23) | copy-start | bytes 6291460

commit v9 on v8

--- a/solution.py
+++ b/solution.py
@@ -1138,6 +1138,12 @@
     )(query_rows, keys_head, flat[:, None, :], square, rank)
 
 
+def short_hot(row_values, size):
+    short = jnp.int16
+    hot = lax.broadcasted_iota(short, (size, row_values.shape[1]), 0) == row_values.astype(short)
+    return jnp.where(hot, jnp.ones((), jnp.bfloat16), jnp.zeros((), jnp.bfloat16))
+
+
 def send_rows(spot, sizes, src, landing, send, recv):
     me = index_of(spot, sizes)
 
@@ -1291,11 +1297,12 @@
             key = row_meta // SUBKEYS
             low = row_meta % SUBKEYS
             weight = slot_row(sizes, slots_in, source_dp, source_col, block)
-            at_key = lax.broadcasted_iota(jnp.int32, (areas * FBLK, key.shape[1]), 0) == key
-            left = jnp.where(at_key, weight, 0.0).astype(jnp.bfloat16)
+            short = jnp.int16
+            at_key = lax.broadcasted_iota(short, (areas * FBLK, key.shape[1]), 0) == key.astype(short)
+            left = jnp.where(at_key, weight.astype(jnp.bfloat16), jnp.zeros((), jnp.bfloat16))
             stacked = lax.dot_general(
                 left,
-                one_hot(low, SUBKEYS),
+                short_hot(low, SUBKEYS),
                 (((1,), (1,)), ((), ())),
                 preferred_element_type=jnp.float32,
             ).astype(jnp.bfloat16)
@@ -1472,7 +1479,7 @@
                 lines = pl.ds(pl.multiple_of(block * FBLK, FBLK), FBLK)
                 stacked = grids[:, lines, :].reshape(areas * FBLK, SUBKEYS)
                 product = jnp.dot(
-                    stacked, one_hot(row_meta % SUBKEYS, SUBKEYS), preferred_element_type=jnp.float32
+                    stacked, short_hot(row_meta % SUBKEYS, SUBKEYS), preferred_element_type=jnp.float32
                 )
                 spot_id = lax.broadcasted_iota(jnp.int32, product.shape, 0)
                 sums[block] = jnp.sum(
@@ -1607,10 +1614,10 @@
     rest = back - high.astype(jnp.float32)
     middle = rest.astype(jnp.bfloat16)
     lowest = (rest - middle.astype(jnp.float32)).astype(jnp.bfloat16)
-    spread_back = (
-        jnp.dot(high, hot, preferred_element_type=jnp.float32)
-        + jnp.dot(middle, hot, preferred_element_type=jnp.float32)
-        + jnp.dot(lowest, hot, preferred_element_type=jnp.float32)
+    spread_back = jnp.dot(
+        jnp.concatenate([high, middle, lowest], axis=1),
+        jnp.concatenate([hot, hot, hot], axis=0),
+        preferred_element_type=jnp.float32,
     )
     slot = lax.broadcasted_iota(jnp.int32, spread_back.shape, 0)
     flat = jnp.sum(jnp.where(slot == rank_ref[0], spread_back, 0.0), axis=0, keepdims=True)

time: 404 us -> 402 us (level)
  no operation moved by 1% of the time
where the time goes in v9:
time: 402 us; the launch traced here: 401 us
  Pallas kernels  334 us (83%)
  matrix products  34.2 us (9%)
  other arithmetic  17.6 us (4%)
  local copies, waits for them, and re-layouts  13.5 us (3%)
    pallas_call x1, Pallas kernels, use_memory(): pl.pallas_call(functools.partial(memory_kernel, sizes, blocks), in_specs=...  111 us
    pallas_call x1, Pallas kernels, last(): pl.pallas_call(functools.partial(last_kernel, sizes), in_specs=[VMEM] * 9...  65.8 us
    pallas_call x1, Pallas kernels, middle(): pl.pallas_call(functools.partial(middle_kernel, sizes), in_specs=[VMEM] *...  37.4 us
    pallas_call x1, Pallas kernels, turn(): pl.pallas_call(functools.partial(turn_kernel, sizes), in_specs=[pl.BlockS...  36.3 us
    pallas_call x1, Pallas kernels, join(): pl.pallas_call(functools.partial(join_kernel, sizes), in_specs=[VMEM] * 3...  32.5 us
    pallas_call x1, Pallas kernels, start_all(): pl.pallas_call(functools.partial(start_kernel, sizes, rows_dev), in_specs...  19.4 us
    pallas_call x1, Pallas kernels, attend(): pl.pallas_call(functools.partial(attend_kernel, sizes), in_specs=[pl.Bloc...  17.7 us
    dot_general x7, matrix products, dense_nt(): lax.dot_general(left, right, (((1,), (1,)), ((), ())), preferred_element_...  11.5 us

profile of v9, /device:TPU:0, one launch (start us, length us, event | category | flops | bytes accessed | tf_op | source)
XLA Modules:
  0.0 401.3 jit_solution(16843065409139810411)
XLA Ops:
  1.5 0.8 constant_dynamic-slice_fusion
  3.0 19.4 %start_all.1 = (bf16[512,1024]{1,0:T(8,128)(2,1)}, bf16[3,1024,256]{2,1,0:T(8,128)(2,1)}, bf16[1024,1024]{1,0:T(8,128)(2,1)}, bf16[1024,256]{1,0:T(8,128)(2,1)},...) custom-call(bf16[256,512]{1,0:T(8,128)(2,1)} %refs_1_.3, ...), custom_call_target="tpu_custom_call" | custom-call | tf_op jit(solution)/shard_map/start_all/pallas_call | solution.py:251
  22.5 1.5 fusion
  24.0 2.8 fusion.3.qkv
  26.8 0.7 slice_bitcast_fusion.refs_1_
  27.7 17.7 %attend.1 = (bf16[512,256]{1,0:T(8,128)(2,1)}, f32[4,512]{1,0:T(4,128)}, bf16[2,1024,256]{2,1,0:T(8,128)(2,1)}, bf16[512,1024]{1,0:T(8,128)(2,1)}) custom-call(s32[1]{0:T(128)S(6)} %copy.44.prefix.refs_0_, bf16[3,512,256]{2,1,0:T(8,128)(2,1)} %copy-done.6, bf16[256,512]{1,0:T(8,128)(2,1)} %refs_2_.3), custom_call_target="tpu_custom_call" | custom-call | tf_op jit(solution)/shard_map/attend/pallas_call | solution.py:331
  45.4 2.5 convolution_convert_fusion.3.part
  48.6 32.5 %join.1 = (f32[256,512]{1,0:T(8,128)}, bf16[512,1024]{1,0:T(8,128)(2,1)}) custom-call(bf16[512,1024]{1,0:T(8,128)(2,1)} %convolution_convert_fusion.3.part, bf16[256,512]{1,0:T(8,128)(2,1)} %refs_1_.3, bf16[1,512]{1,0:T(2,128)(2,1)} %broadcast_in_dim.4.gain.refs_3_), custom_call_target="tpu_custom_call" | custom-call | tf_op jit(solution)/shard_map/join/pallas_call | solution.py:381
  81.2 1.8 fusion.39
  83.0 2.5 multiply_convert_fusion.2
  85.5 0.7 copy.40
  86.2 2.2 convolution_convert_fusion.2.query_ref
  88.4 0.8 dynamic-slice_bitcast_fusion.keys_ref
  89.3 6.1 %weigh.1 = (f32[4,32,128]{2,1,0:T(8,128)}, f32[4,128,32]{2,1,0:T(8,128)}) custom-call(bf16[512,1024]{1,0:T(8,128)(2,1)} %convolution_convert_fusion.2.query_ref, bf16[2,256,512]{2,1,0:T(8,128)(2,1)} %dynamic-slice_bitcast_fusion.keys_ref, s32[4,1,4096]{2,1,0:T(1,128)} %bitcast.90, s32[4,32,128]{2,1,0:T(8,128)} %bitcast.91, ...), custom_call_target="tpu_custom_call" | custom-call | tf_op jit(solution)/shard_map/weigh/pallas_call | solution.py:1119
  95.4 1.7 copy.33
  97.0 111.4 %use_memory.1 = (bf16[4,2,4,512,256]{4,3,2,1,0:T(8,128)(2,1)}, bf16[4,2,512,2048]{3,2,1,0:T(8,128)(2,1)}, bf16[4,512,1024]{2,1,0:T(8,128)(2,1)}, f32[512,256]{1,0:T(8,128)}, f32[32,4,128]{2,1,0:T(4,128)}) custom-call(bf16[512,256]{1,0:T(8,128)(2,1)} %get-tuple-element.101.grads, s32[32,4,128]{2,1,0:T(4,128)} %bitcast.95, f32[32,4,128]{2,1,0:T(4,128)} %bitcast.94, ...), custom_call_target="tpu_custom_call" | custom-call | tf_op jit(solution)/shard_map/use_memory/pallas_call | solution.py:1565
  208.5 1.7 copy.34
  210.1 7.4 %unweigh.1 = (bf16[256,512]{1,0:T(8,128)(2,1)}, bf16[256,512]{1,0:T(8,128)(2,1)}) custom-call(f32[4,128,32]{2,1,0:T(8,128)} %bitcast.93, s32[4,1,4096]{2,1,0:T(1,128)} %bitcast.92, s32[4,1,4096]{2,1,0:T(1,128)} %get-tuple-element.64.rank_ref, f32[4,32,128]{2,1,0:T(8,128)} %get-tuple-element.67.weights_ref), custom_call_target="tpu_custom_call" | custom-call | tf_op jit(solution)/shard_map/unweigh/pallas_call | solution.py:1653
  217.6 1.4 convolution_convert_fusion.11
  219.0 1.5 convolution_convert_fusion.12
  220.6 1.3 fusion.10
  222.2 1.5 add_convert_fusion.1.refs_0_
  223.7 1.3 convolution_convert_fusion.10.refs_4_
  225.0 1.3 convolution_convert_fusion.9.refs_5_
  226.9 0.8 pad_maximum_fusion.4
  227.8 37.4 %middle.1 = (f32[256,512]{1,0:T(8,128)}, bf16[512,1024]{1,0:T(8,128)(2,1)}, f32[1,512]{1,0:T(1,128)}, bf16[128,256]{1,0:T(8,128)(2,1)}, bf16[64,512]{1,0:T(8,128)(2,1)}, /*index=5*/bf16[64,512]{1,0:T(8,128)(2,1)}) custom-call(bf16[512,1024]{1,0:T(8,128)(2,1)} %add_convert_fusion.1.refs_0_, f32[256,512]{1,0:T(8,128)} %get-tuple-element.71.refs_1_.refs_6_, ...), custom_call_target="tpu_custom_call" | custom-call | tf_op jit(solution)/shard_map/middle/pallas_call | solution.py:680
  265.2 2.5 convolution_convert_fusion.13.refs_3_
  267.8 1.4 convolution_convert_fusion.1.refs_5_
  269.2 2.6 convolution_convert_fusion.refs_10_
  271.8 36.3 %turn.1 = (bf16[512,256]{1,0:T(8,128)(2,1)}, bf16[2,512,256]{2,1,0:T(8,128)(2,1)}, bf16[256,512]{1,0:T(8,128)(2,1)}, bf16[512,256]{1,0:T(8,128)(2,1)}, bf16[256,...) custom-call(s32[1]{0:T(128)S(6)} %copy.44.prefix.refs_0_, ...), custom_call_target="tpu_custom_call" | custom-call | tf_op jit(solution)/shard_map/turn/pallas_call | solution.py:1012
  308.2 1.7 fusion.16
  310.4 1.5 add_convert_fusion.refs_0_
  313.2 0.7 fusion.5
  314.2 0.7 fusion.4
  314.8 1.3 pad_maximum_fusion.refs_7_
  316.6 1.3 convolution_convert_fusion.5.refs_8_
  317.9 65.8 %last.1 = (f32[256,512]{1,0:T(8,128)}, f32[2,8,128]{2,1,0:T(8,128)}, bf16[2048,1024]{1,0:T(8,128)(2,1)}, bf16[512,1024]{1,0:T(8,128)(2,1)}, bf16[3,512,256]{2,1,...) custom-call(bf16[512,1024]{1,0:T(8,128)(2,1)} %add_convert_fusion.refs_0_, ...), custom_call_target="tpu_custom_call" | custom-call | tf_op jit(solution)/shard_map/last/pallas_call | solution.py:874
  383.7 0.8 reshape.45
  385.1 2.4 convert_element_type.98
  387.5 0.9 convert_element_type.99
  388.4 1.6 convert_element_type.100
  390.0 0.8 convert_element_type.101
  390.8 0.9 convert_element_type.102
  391.6 2.7 convert_element_type.103
  394.4 1.0 copy-done.2
  395.4 4.4 %convert_element_type.104 = f32[2048,1024]{1,0:T(8,128)} convert(bf16[2048,1024]{1,0:T(8,128)(2,1)S(1)} %copy-done.2) | non-fusion elementwise | flops 2097152 | bytes 12582912 | tf_op jit(solution)/shard_map/convert_element_type | solution.py:1808
  399.8 0.7 copy.45
  400.5 0.8 copy.46
  (91 shorter events, 5.8 us)
Async XLA Ops:
  0.6 87.8 %copy-start = (bf16[4,2,256,512]{3,2,1,0:T(8,128)(2,1)S(1)}, bf16[4,2,256,512]{3,2,1,0:T(8,128)(2,1)}, u32[]{:S(2)}) copy-start(bf16[4,2,256,512]{3,2,1,0:T(8,128)(2,1)} %param.23) | copy-start | bytes 6291460
  0.7 21.8 %copy-start.35 = (bf16[1024]{0:T(1024)(128)(2,1)S(1)}, bf16[1024]{0:T(1024)(128)(2,1)}, u32[]{:S(2)}) copy-start(bf16[1024]{0:T(1024)(128)(2,1)} %param.16) | copy-start | bytes 6148
  26.8 1.0 copy-start.6
  26.8 21.2 %copy-start.36 = (bf16[1024]{0:T(1024)(128)(2,1)S(1)}, bf16[1024]{0:T(1024)(128)(2,1)}, u32[]{:S(2)}) copy-start(bf16[1024]{0:T(1024)(128)(2,1)} %param.19) | copy-start | bytes 6148
  27.7 53.4 %copy-start.4 = (bf16[1024,256]{1,0:T(8,128)(2,1)S(1)}, bf16[1024,256]{1,0:T(8,128)(2,1)}, u32[]{:S(2)}) copy-start(bf16[1024,256]{1,0:T(8,128)(2,1)} %get-tuple-element.61) | copy-start | bytes 1572868
  81.2 1.8 copy-start.9
  82.9 2.6 copy-start.34
  83.0 3.2 copy-start.14
  83.0 3.2 copy-start.37
  217.6 2.9 copy-start.38
  219.0 2.8 copy-start.19
  220.5 1.3 copy-start.22
  220.5 1.3 copy-start.24
  220.5 1.4 copy-start.25
  222.2 1.5 copy-start.15
  223.7 1.3 copy-start.10
  223.7 2.6 copy-start.12
  223.7 2.6 copy-start.29
  223.7 2.9 copy-start.32
  226.9 38.3 %copy-start.18 = (bf16[256,1024]{1,0:T(8,128)(2,1)S(1)}, bf16[256,1024]{1,0:T(8,128)(2,1)}, u32[]{:S(2)}) copy-start(bf16[256,1024]{1,0:T(8,128)(2,1)} %get-tuple-element.59) | copy-start | bytes 1572868
  227.8 40.0 %copy-start.17 = (bf16[256,1024]{1,0:T(8,128)(2,1)S(1)}, bf16[256,1024]{1,0:T(8,128)(2,1)}, u32[]{:S(2)}) copy-start(bf16[256,1024]{1,0:T(8,128)(2,1)} %get-tuple-element.57) | copy-start | bytes 1572868
  265.2 4.0 copy-start.16
  265.2 4.0 copy-start.20
  265.2 4.0 copy-start.23
  308.1 1.8 copy-start.5
  308.1 1.8 copy-start.26
  310.4 2.2 copy-start.13
  313.2 1.0 copy-start.33
  314.8 1.3 copy-start.8
  314.8 1.8 copy-start.11
  383.7 3.8 copy-start.30
  383.7 4.7 %copy-start.7 = (bf16[512,1024]{1,0:T(8,128)(2,1)S(1)}, bf16[512,1024]{1,0:T(8,128)(2,1)}, u32[]{:S(2)}) copy-start(bf16[512,1024]{1,0:T(8,128)(2,1)} %get-tuple-element.90) | copy-start | bytes 3145732
  387.5 2.4 copy-start.28
  388.4 2.4 copy-start.27
  388.4 3.3 copy-start.3
  391.6 3.7 copy-start.2
  395.3 4.4 %copy-start.31 = (bf16[256,512]{1,0:T(8,128)(2,1)S(1)}, bf16[256,512]{1,0:T(8,128)(2,1)}, u32[]{:S(2)}) copy-start(bf16[256,512]{1,0:T(8,128)(2,1)} %get-tuple-element.114) | copy-start | bytes 786436
  395.4 5.2 %copy-start.21 = (f32[256,512]{1,0:T(8,128)S(1)}, f32[256,512]{1,0:T(8,128)}, u32[]{:S(2)}) copy-start(f32[256,512]{1,0:T(8,128)} %get-tuple-element.115) | copy-start | bytes 1572868
  395.4 5.9 %copy-start.1 = (bf16[4,2,256,512]{3,2,1,0:T(8,128)(2,1)S(1)}, bf16[4,2,256,512]{3,2,1,0:T(8,128)(2,1)}, u32[]{:S(2)}) copy-start(bf16[4,2,256,512]{3,2,1,0:T(8,128)(2,1)} %param.23) | copy-start | bytes 6291460
